TPU v7x, 32 devices: a 4x4x1 block of a 4x4x8 slice. The times are simulated.
32 devices in a mesh: dp: 1 (over z), tp: 4 (over y), fsdp: 8 (over x, core).
Axes of the slice: x: 4, y: 4, z: 1, core: 2. Of those that a mesh axis runs over, the one named last changes fastest.
The devices are a block of a 4x4x8 slice.
Arguments:
- tokens: bfloat16 [8, 4096, 3072], P(('dp', 'fsdp'))
- positions: int32 [8, 4096], P(('dp', 'fsdp'))
- valid_len: int32 [8], P(('dp', 'fsdp'))
- w_query: bfloat16 [3072, 3072], P('fsdp', 'tp')
- w_key: bfloat16 [3072, 1024], P('fsdp', 'tp')
- w_value: bfloat16 [3072, 1024], P('fsdp', 'tp')
- w_out: bfloat16 [3072, 3072], P('tp', 'fsdp')
- w_gate: bfloat16 [3072, 8192], P('fsdp', 'tp')
- w_up: bfloat16 [3072, 8192], P('fsdp', 'tp')
- w_down: bfloat16 [8192, 3072], P('tp', 'fsdp')
- norm_attn: bfloat16 [3072], replicated
- norm_mlp: bfloat16 [3072], replicated
Outputs:
- output 1: bfloat16 [8, 4096, 3072], P(('dp', 'fsdp'))
- output 2: bfloat16 [8, 4096, 8, 128], P(('dp', 'fsdp'), None, 'tp')
- output 3: bfloat16 [8, 4096, 8, 128], P(('dp', 'fsdp'), None, 'tp')
All inputs are finite; a program needn't handle non-finite values.
Results may differ from a plain program's by a relative error of at most 0.0131316.
Values are sent between devices in bfloat16 or wider.
A program may use at most 768 MiB of HBM per device.

v0:
```python
import math
import jax
import jax.numpy as jnp
from jax import lax
from jax.sharding import PartitionSpec as P

HEAD_DIM = 128
Q_BLOCK = 256
ROPE_THETA = 500000.0
NORM_EPS = 1e-5
SCORE_SCALE = HEAD_DIM ** -0.5


def rope_freqs():
    half_idx = jnp.arange(HEAD_DIM // 2, dtype=jnp.float32)
    inv_freq = jnp.power(ROPE_THETA, -2.0 * half_idx / HEAD_DIM)
    wave_len = 2.0 * math.pi / inv_freq
    smooth = (8192.0 / wave_len - 1.0) / 3.0
    blended = (1.0 - smooth) * inv_freq / 8.0 + smooth * inv_freq
    return jnp.where(wave_len < 2048.0, inv_freq, jnp.where(wave_len > 8192.0, inv_freq / 8.0, blended))


def rms_norm(values, gain_vec):
    vals_f32 = values.astype(jnp.float32)
    inv_rms = lax.rsqrt(jnp.mean(vals_f32 * vals_f32, axis=-1, keepdims=True) + NORM_EPS)
    return (vals_f32 * inv_rms * gain_vec.astype(jnp.float32)).astype(jnp.bfloat16)


def rotate(proj_val, cos_t, sin_t):
    half_dim = proj_val.shape[-1] // 2
    lead_half = proj_val[..., :half_dim]
    tail_half = proj_val[..., half_dim:]
    return jnp.concatenate([lead_half * cos_t - tail_half * sin_t, tail_half * cos_t + lead_half * sin_t], axis=-1)


def attention(q_rot, k_rot, v_cache, valid_len):
    seq_len = q_rot.shape[1]
    block_len = min(seq_len, Q_BLOCK)
    pieces = []
    for block_idx in range(seq_len // block_len):
        first_row = block_idx * block_len
        end_row = first_row + block_len
        scores = jnp.einsum('bqkgd,bskd->bkgqs', q_rot[:, first_row:end_row], k_rot[:, :end_row], preferred_element_type=jnp.float32) * SCORE_SCALE
        q_index = jnp.arange(first_row, end_row)[:, None]
        k_index = jnp.arange(end_row)[None, :]
        allowed = (k_index <= q_index)[None] & (k_index[None] < valid_len[:, None, None])
        scores = jnp.where(allowed[:, None, None], scores, -jnp.inf)
        attn_prob = jax.nn.softmax(scores, axis=-1).astype(jnp.bfloat16)
        pieces.append(jnp.einsum('bkgqs,bskd->bqkgd', attn_prob, v_cache[:, :end_row], preferred_element_type=jnp.float32).astype(jnp.bfloat16))
    return jnp.concatenate(pieces, axis=1)


def rope_attend(q_proj, k_proj, v_proj, positions, valid_len):
    batch_loc, seq_len = positions.shape
    kv_count = k_proj.shape[-1] // HEAD_DIM
    q_count = q_proj.shape[-1] // HEAD_DIM
    angles = positions.astype(jnp.float32)[:, :, None] * rope_freqs()
    cos_t = jnp.cos(angles)[:, :, None, :]
    sin_t = jnp.sin(angles)[:, :, None, :]
    q_rot = rotate(q_proj.reshape(batch_loc, seq_len, q_count, HEAD_DIM), cos_t, sin_t).astype(jnp.bfloat16)
    q_rot = q_rot.reshape(batch_loc, seq_len, kv_count, q_count // kv_count, HEAD_DIM)
    k_rot = rotate(k_proj.reshape(batch_loc, seq_len, kv_count, HEAD_DIM), cos_t, sin_t).astype(jnp.bfloat16)
    v_cache = v_proj.astype(jnp.bfloat16).reshape(batch_loc, seq_len, kv_count, HEAD_DIM)
    attn_out = attention(q_rot, k_rot, v_cache, valid_len).reshape(batch_loc, seq_len, q_count * HEAD_DIM)
    return attn_out, k_rot, v_cache


def solution(mesh):
    batch_axes = ('dp', 'fsdp')
    in_specs = (P(batch_axes, None, None), P(batch_axes, None), P(batch_axes),
                P('fsdp', 'tp'), P('fsdp', 'tp'), P('fsdp', 'tp'), P('tp', 'fsdp'),
                P('fsdp', 'tp'), P('fsdp', 'tp'), P('tp', 'fsdp'), P(None), P(None))
    out_specs = (P(batch_axes, None, None), P(batch_axes, None, 'tp', None), P(batch_axes, None, 'tp', None))

    def local_layer(tokens, positions, valid_len, w_query, w_key, w_value, w_out, w_gate, w_up, w_down, norm_attn, norm_mlp):
        h_in = rms_norm(tokens, norm_attn)
        full_q = lax.all_gather(w_query, 'fsdp', axis=0, tiled=True)
        full_k = lax.all_gather(w_key, 'fsdp', axis=0, tiled=True)
        full_v = lax.all_gather(w_value, 'fsdp', axis=0, tiled=True)
        q_proj = jnp.einsum('btd,dk->btk', h_in, full_q, preferred_element_type=jnp.float32)
        k_proj = jnp.einsum('btd,dk->btk', h_in, full_k, preferred_element_type=jnp.float32)
        v_proj = jnp.einsum('btd,dk->btk', h_in, full_v, preferred_element_type=jnp.float32)
        attn_out, k_rot, v_cache = rope_attend(q_proj, k_proj, v_proj, positions, valid_len)
        full_o = lax.all_gather(w_out, 'fsdp', axis=1, tiled=True)
        y_part = jnp.einsum('btk,kd->btd', attn_out, full_o, preferred_element_type=jnp.float32).astype(jnp.bfloat16)
        y_attn = lax.psum(y_part, 'tp')
        resid_mid = (tokens.astype(jnp.float32) + y_attn.astype(jnp.float32)).astype(jnp.bfloat16)
        h_mlp = rms_norm(resid_mid, norm_mlp)
        full_gate = lax.all_gather(w_gate, 'fsdp', axis=0, tiled=True)
        full_up = lax.all_gather(w_up, 'fsdp', axis=0, tiled=True)
        gate_val = jnp.einsum('btd,df->btf', h_mlp, full_gate, preferred_element_type=jnp.float32)
        up_val = jnp.einsum('btd,df->btf', h_mlp, full_up, preferred_element_type=jnp.float32)
        hidden_act = (jax.nn.silu(gate_val) * up_val).astype(jnp.bfloat16)
        full_down = lax.all_gather(w_down, 'fsdp', axis=1, tiled=True)
        down_part = jnp.einsum('btf,fd->btd', hidden_act, full_down, preferred_element_type=jnp.float32).astype(jnp.bfloat16)
        down_val = lax.psum(down_part, 'tp')
        hidden_out = (resid_mid.astype(jnp.float32) + down_val.astype(jnp.float32)).astype(jnp.bfloat16)
        return hidden_out, k_rot, v_cache

    return jax.shard_map(local_layer, mesh=mesh, in_specs=in_specs, out_specs=out_specs, check_vma=False)
```

profile of v0, /device:TPU:97, one launch (start us, length us, event | category | flops | bytes accessed | tf_op | source)
XLA Modules:
  0.0 1637.4 jit_solution(9907982843976481446)
XLA Ops:
  11.2 10.3 fusion
  54.9 12.1 fusion.66
  68.8 13.9 fusion.69
  82.6 9.8 all-gather.12.cloned.1.call-done
  99.0 25.0 %fusion.50 = f32[1,4096,6,128]{1,3,2,0:T(8,128)S(1)} fusion(bf16[6,128,3072]{2,1,0:T(8,128)(2,1)} %bitcast.967, bf16[1,4096,3072]{2,1,0:T(8,128)(2,1)} %param.12, f32[3072]{0:T(1024)} %copy-done.49, f32[4096]{0:T(1024)S(1)} %add_rsqrt_fusion.1), kind=kOutput, calls=%fused_computation.95 | convolution fusion | flops 19377684480 | bytes 42496000 | tf_op jit(solution)/shard_map/btd,dk->btk/dot_general | solution.py:80
  199.2 10.0 fusion.25
  209.2 9.9 fusion.23
  219.1 10.8 fusion.21
  229.9 11.0 fusion.20
  311.8 9.0 fusion.220
  320.8 9.5 fusion.24
  330.3 9.9 fusion.214
  340.3 10.4 fusion.22
  350.7 10.2 fusion.208
  360.9 9.4 fusion.19
  370.3 10.9 fusion.202
  381.2 11.5 fusion.17
  392.8 12.2 fusion.196
  405.1 11.7 fusion.18
  416.8 11.2 fusion.15
  428.0 10.7 fusion.16
  438.7 11.9 fusion.190
  450.6 12.6 fusion.184
  463.2 27.2 %convert_bitcast_fusion.1 = bf16[1,4096,3072]{2,1,0:T(8,128)(2,1)} fusion(bf16[4096,768]{0,1:T(8,128)(2,1)} %bitcast.190, bf16[768,3072]{1,0:T(8,128)(2,1)} %all-gather.14.cloned.1.call-done), kind=kOutput, calls=%fused_computation.24 | convolution fusion | flops 19339935744 | bytes 36175872 | tf_op jit(solution)/shard_map/btk,kd->btd/dot_general | solution.py:85
  492.8 422.2 %all-reduce.3.cloned.1.call-done = bf16[1,4096,3072]{2,1,0:T(8,128)(2,1)} async-done(((bf16[1,4096,3072]{2,1,0:T(8,128)(2,1)}), bf16[1,4096,3072]{2,1,0:T(8,128)(2,1)}) %all-reduce.3.cloned.1.call-update) | async-done | bytes 25165840 | tf_op jit(solution)/shard_map/psum | solution.py:86
  915.0 25.7 %fusion.4 = (f32[4096]{0:T(1024)S(1)}, bf16[1,4096,3072]{2,1,0:T(8,128)(2,1)}) fusion(bf16[1,4096,3072]{2,1,0:T(8,128)(2,1)} %all-reduce.3.cloned.1.call-done, bf16[1,4096,3072]{2,1,0:T(8,128)(2,1)} %param.12), kind=kLoop, calls=%fused_computation.10 | loop fusion | flops 88076288 | bytes 75513856 | tf_op jit(solution)/shard_map/reduce_sum | solution.py:25
  940.7 41.1 %all-gather.16.cloned.1.call-done = bf16[3072,2048]{1,0:T(8,128)(2,1)} async-done(((bf16[384,2048]{1,0:T(8,128)(2,1)}), bf16[3072,2048]{1,0:T(8,128)(2,1)}) %all-gather.16.cloned.1.call-update) | async-done | bytes 12582928 | tf_op jit(solution)/shard_map/all_gather | solution.py:89
  981.8 63.6 %fusion.54 = f32[4096,2048]{1,0:T(8,128)} fusion(bf16[3072,2048]{1,0:T(8,128)(2,1)} %all-gather.16.cloned.1.call-done, bf16[1,4096,3072]{2,1,0:T(8,128)(2,1)} %get-tuple-element.7, f32[3072]{0:T(1024)S(1)} %convert_element_type.341, f32[4096]{0:T(1024)S(1)} %add_rsqrt_fusion), kind=kOutput, calls=%fused_computation.96 | convolution fusion | flops 51589939200 | bytes 71331840 | tf_op jit(solution)/shard_map/btd,df->btf/dot_general | solution.py:91
  1048.6 64.0 %multiply_convert_fusion = bf16[4096,2048]{1,0:T(8,128)(2,1)} fusion(f32[4096,2048]{1,0:T(8,128)} %fusion.54, bf16[3072,2048]{1,0:T(8,128)(2,1)} %all-gather.18.cloned.1.call-done, bf16[1,4096,3072]{2,1,0:T(8,128)(2,1)} %get-tuple-element.7, f32[3072]{0:T(1024)S(1)} %convert_element_type.341, f32[4096]{0:T(1024)S(1)} %add_rsqrt_fusion), kind=kOutput, calls=%fused_computation.14 | convolution fusion | flops 51640270848 | bytes 88109056 | tf_op jit(solution)/shard_map/btd,df->btf/dot_general | solution.py:92
  1115.2 60.3 %convert_bitcast_fusion = bf16[1,4096,3072]{2,1,0:T(8,128)(2,1)} fusion(bf16[4096,2048]{1,0:T(8,128)(2,1)} %multiply_convert_fusion, bf16[2048,3072]{1,0:T(8,128)(2,1)} %all-gather.20.cloned.1.call-done), kind=kOutput, calls=%fused_computation.23 | convolution fusion | flops 51552190464 | bytes 54525952 | tf_op jit(solution)/shard_map/btf,fd->btd/dot_general | solution.py:95
  1189.5 411.0 %all-reduce.5.cloned.1.call-done = bf16[1,4096,3072]{2,1,0:T(8,128)(2,1)} async-done(((bf16[1,4096,3072]{2,1,0:T(8,128)(2,1)}), bf16[1,4096,3072]{2,1,0:T(8,128)(2,1)}) %all-reduce.5.cloned.1.call-update) | async-done | bytes 25165840 | tf_op jit(solution)/shard_map/psum | solution.py:96
  1600.5 29.8 %fusion.7 = bf16[1,4096,3072]{2,1,0:T(8,128)(2,1)} fusion(bf16[1,4096,3072]{2,1,0:T(8,128)(2,1)} %get-tuple-element.7, bf16[1,4096,3072]{2,1,0:T(8,128)(2,1)} %all-reduce.5.cloned.1.call-done), kind=kLoop, calls=%fused_computation.13 | loop fusion | flops 50331648 | bytes 75497472 | tf_op jit(solution)/shard_map/convert_element_type | solution.py:97
  (264 shorter events, 212.8 us)
Async XLA Ops:
  7.2 45.2 %all-gather.10.cloned.1.call-start = ((), (), s32[]{:S(2)}) async-start(), calls=%async_computation.1 | async-start | bytes 1769472 | tf_op jit(solution)/shard_map/all_gather | solution.py:78
  8.0 60.8 %all-gather.8.cloned.1.call-start = ((), (), s32[]{:S(2)}) async-start(), calls=%async_computation | async-start | bytes 1769472 | tf_op jit(solution)/shard_map/all_gather | solution.py:79
  8.8 83.6 %all-gather.12.cloned.1.call-start = ((), (), s32[]{:S(2)}) async-start(), calls=%async_computation.2 | async-start | bytes 5308416 | tf_op jit(solution)/shard_map/all_gather | solution.py:77
  9.6 453.6 %all-gather.14.cloned.1.call-start = ((), (), s32[]{:S(2)}) async-start(), calls=%async_computation.3 | async-start | bytes 5308416 | tf_op jit(solution)/shard_map/all_gather | solution.py:84
  10.2 904.8 %all-reduce.3.cloned.1.call-start = ((), (), s32[]{:S(2)}) async-start(), calls=%async_computation.4 | async-start | bytes 50331648 | tf_op jit(solution)/shard_map/psum | solution.py:86
  11.2 43.8 %copy-start.49 = (f32[3072]{0:T(1024)}, f32[3072]{0:T(1024)S(1)}, u32[]{:S(2)}) copy-start(f32[3072]{0:T(1024)S(1)} %convert_element_type.268) | copy-start | bytes 36868
  11.2 10.4 copy-start.48
  68.8 161.1 %copy-start.1 = (bf16[1,4096,2,64]{1,3,2,0:T(8,128)(2,1)}, bf16[1,4096,2,64]{1,3,2,0:T(8,128)(2,1)S(1)}, u32[]{:S(2)}) copy-start(bf16[1,4096,2,64]{1,3,2,0:T(8,128)(2,1)S(1)} %get-tuple-element.10) | copy-start | bytes 3145732
  152.0 96.2 %copy-start.41 = (f32[2,3,256]{2,1,0:T(4,128)}, f32[2,3,256]{2,1,0:T(4,128)S(1)}, u32[]{:S(2)}) copy-start(f32[2,3,256]{2,1,0:T(4,128)S(1)} %get-tuple-element.18) | copy-start | bytes 18436
  199.2 10.0 copy-start.12
  219.1 10.8 copy-start.7
  268.6 10.9 slice-start.6
  330.3 10.0 copy-start.14
  330.3 10.0 copy-start.40
  340.3 10.4 copy-start.34
  350.7 10.2 copy-start.13
  350.7 10.2 copy-start.39
  370.3 11.0 copy-start.11
  370.3 11.0 copy-start.37
  381.2 23.8 %slice-start.2 = ((s8[6291456]{0:T(1024)(128)(4,1)}), s8[4194304]{0:T(1024)(128)(4,1)S(1)}, s32[]{:S(2)}) async-start(s8[6291456]{0:T(1024)(128)(4,1)} %bitcast.948), calls=%async_computation.11 | async-start | bytes 8388608
  381.2 23.8 %slice-start.4 = ((s8[6291456]{0:T(1024)(128)(4,1)}), s8[4194304]{0:T(1024)(128)(4,1)S(1)}, s32[]{:S(2)}) async-start(s8[6291456]{0:T(1024)(128)(4,1)} %bitcast.950), calls=%async_computation.13 | async-start | bytes 8388608
  392.7 12.3 slice-start.3
  392.8 12.3 slice-start.5
  392.8 12.3 copy-start.2
  392.8 12.3 copy-start.5
  392.8 12.3 copy-start.9
  416.8 11.2 copy-start.8
  416.8 11.2 copy-start.38
  490.5 491.3 %all-gather.16.cloned.1.call-start = ((), (), s32[]{:S(2)}) async-start(), calls=%async_computation.5 | async-start | bytes 14155776 | tf_op jit(solution)/shard_map/all_gather | solution.py:89
  491.1 557.5 %all-gather.18.cloned.1.call-start = ((), (), s32[]{:S(2)}) async-start(), calls=%async_computation.6 | async-start | bytes 14155776 | tf_op jit(solution)/shard_map/all_gather | solution.py:90
  491.9 623.3 %all-gather.20.cloned.1.call-start = ((), (), s32[]{:S(2)}) async-start(), calls=%async_computation.7 | async-start | bytes 14155776 | tf_op jit(solution)/shard_map/all_gather | solution.py:94
  492.7 1107.8 %all-reduce.5.cloned.1.call-start = ((), (), s32[]{:S(2)}) async-start(), calls=%async_computation.8 | async-start | bytes 50331648 | tf_op jit(solution)/shard_map/psum | solution.py:96
  (47 other events, 256.1 us)
Sparse Core Ops, SparseCore 0:
  9.6 26.0 all-gather.9
  37.3 21.9 all-gather.7
  60.8 31.5 all-gather.11
  93.9 31.3 all-gather.13
  490.6 424.3 all-reduce.2
  916.5 65.2 all-gather.15
  983.4 65.1 all-gather.17
  1050.2 64.9 all-gather.19
  1175.7 424.7 all-reduce.4
where the time goes:
time: 1650 us; the launch traced here: 1640 us
  waiting for transfers between devices  895 us (54%)
  matrix products  493 us (30%)
  other arithmetic  196 us (12%)
  local copies, waits for them, and re-layouts  37.4 us (2%)
    psum x1, waiting for transfers between devices, local_layer(): y_attn = lax.psum(y_part, 'tp')  422 us
    psum x1, waiting for transfers between devices, local_layer(): down_val = lax.psum(down_part, 'tp')  411 us
    dot_general x16, matrix products, attention(): jnp.einsum('bkgqs,bskd->bqkgd', attn_prob, v_cache[:, :end_row], preferre...  117 us
    dot_general x16, matrix products, attention(): jnp.einsum('bqkgd,bskd->bkgqs', q_rot[:, first_row:end_row], k_rot[:, :en...  109 us
    reduce_sum x16, other arithmetic, attention(): attn_prob = jax.nn.softmax(scores, axis=-1).astype(jnp.bfloat16)  92.5 us
    dot_general x1, matrix products, local_layer(): jnp.einsum('btd,df->btf', h_mlp, full_up, preferred_element_type=jnp.floa...  64 us
    dot_general x1, matrix products, local_layer(): jnp.einsum('btd,df->btf', h_mlp, full_gate, preferred_element_type=jnp.fl...  63.6 us
    dot_general x1, matrix products, local_layer(): jnp.einsum('btf,fd->btd', hidden_act, full_down, preferred_element_type=j...  60.3 us
  transfers between devices with their start and end apart: 9, of which 6 were waited for; matrix products, arithmetic and copies ran while one was open for 37% of the time, Pallas kernels for 0%

commit v1 on v0

v1 whole, which is shorter than its diff:
```python
import functools
import math
import jax
import jax.numpy as jnp
from jax import lax
from jax.experimental import pallas as pl
from jax.experimental.pallas import tpu as pltpu
from jax.sharding import PartitionSpec as P

HEAD_DIM = 128
ROPE_THETA = 500000.0
NORM_EPS = 1e-5
EXP2_SCALE = HEAD_DIM ** -0.5 * math.log2(math.e)
N_CALLS = 2
VMEM_LIMIT = 60 * 1024 * 1024


def rope_freqs():
    half_idx = jnp.arange(HEAD_DIM // 2, dtype=jnp.float32)
    inv_freq = jnp.power(ROPE_THETA, -2.0 * half_idx / HEAD_DIM)
    wave_len = 2.0 * math.pi / inv_freq
    smooth = (8192.0 / wave_len - 1.0) / 3.0
    blended = (1.0 - smooth) * inv_freq / 8.0 + smooth * inv_freq
    return jnp.where(wave_len < 2048.0, inv_freq, jnp.where(wave_len > 8192.0, inv_freq / 8.0, blended))


def params(**kw):
    return pltpu.CompilerParams(vmem_limit_bytes=VMEM_LIMIT, **kw)


def cost(flops, nbytes):
    return pl.CostEstimate(flops=flops, bytes_accessed=nbytes, transcendentals=0)


def norm_rows(vals_f32, gain):
    inv = lax.rsqrt(jnp.mean(vals_f32 * vals_f32, axis=-1, keepdims=True) + NORM_EPS)
    return (vals_f32 * inv * gain).astype(jnp.bfloat16)


def qkv_kernel(n_q, n_kv, x_ref, g_ref, w_ref, cos_ref, sin_ref, q_ref, k_ref, v_ref):
    h = norm_rows(x_ref[...].astype(jnp.float32), g_ref[...].astype(jnp.float32))
    cos_t, sin_t = cos_ref[...], sin_ref[...]
    for g in range(n_kv):
        per = n_q // n_kv
        for kind in range(2):
            if kind == 0:
                lo, cnt = g * per, per
            else:
                lo, cnt = n_q + g, 1
            y = jnp.dot(h, w_ref[:, lo * HEAD_DIM:(lo + cnt) * HEAD_DIM], preferred_element_type=jnp.float32)
            for i in range(cnt):
                a = y[:, i * HEAD_DIM:(i + 1) * HEAD_DIM]
                r = (a * cos_t + pltpu.roll(a, HEAD_DIM // 2, 1) * sin_t).astype(jnp.bfloat16)
                if kind == 0:
                    q_ref[lo + i] = r
                else:
                    k_ref[:, g * HEAD_DIM:(g + 1) * HEAD_DIM] = r
    base = (n_q + n_kv) * HEAD_DIM
    v_ref[...] = jnp.dot(h, w_ref[:, base:base + n_kv * HEAD_DIM], preferred_element_type=jnp.float32).astype(jnp.bfloat16)


def qkv_call(x, gain, w, cos_t, sin_t, n_q, n_kv):
    s, d = x.shape
    bm = min(512, s)
    n = w.shape[1]
    row = lambda i: (i, 0)
    return pl.pallas_call(
        functools.partial(qkv_kernel, n_q, n_kv),
        grid=(s // bm,),
        in_specs=[pl.BlockSpec((bm, d), row), pl.BlockSpec((1, d), lambda i: (0, 0)), pl.BlockSpec((d, n), lambda i: (0, 0)),
                  pl.BlockSpec((bm, HEAD_DIM), row), pl.BlockSpec((bm, HEAD_DIM), row)],
        out_specs=[pl.BlockSpec((n_q, bm, HEAD_DIM), lambda i: (0, i, 0)),
                   pl.BlockSpec((bm, n_kv * HEAD_DIM), row), pl.BlockSpec((bm, n_kv * HEAD_DIM), row)],
        out_shape=[jax.ShapeDtypeStruct((n_q, s, HEAD_DIM), jnp.bfloat16),
                   jax.ShapeDtypeStruct((s, n_kv * HEAD_DIM), jnp.bfloat16),
                   jax.ShapeDtypeStruct((s, n_kv * HEAD_DIM), jnp.bfloat16)],
        compiler_params=params(),
        cost_estimate=cost(2 * s * d * n, 2 * s * d + 2 * d * n + 2 * s * n),
        name="qkv",
    )(x, gain, w, cos_t, sin_t)


def att_kernel(bq, bk, per, first, len_ref, q_ref, k_ref, v_ref, o_ref, m_ref, l_ref, acc_ref):
    row0 = first + pl.program_id(1) * bq
    valid = len_ref[0]
    m_ref[...] = jnp.full_like(m_ref, -jnp.inf)
    l_ref[...] = jnp.zeros_like(l_ref)
    acc_ref[...] = jnp.zeros_like(acc_ref)
    reps = bk // HEAD_DIM

    def step(j, masked):
        k0 = pl.multiple_of(j * bk, bk)
        k_blk = k_ref[pl.ds(k0, bk), :]
        v_blk = v_ref[pl.ds(k0, bk), :]
        if masked:
            kid = k0 + lax.broadcasted_iota(jnp.int32, (bq, bk), 1)
            qid = row0 + lax.broadcasted_iota(jnp.int32, (bq, bk), 0)
            allowed = (kid <= qid) & (kid < valid)
        for h in range(per):
            sc = lax.dot_general(q_ref[h], k_blk, (((1,), (1,)), ((), ())), preferred_element_type=jnp.float32)
            if masked:
                sc = jnp.where(allowed, sc, -jnp.inf)
            m_old = m_ref[h]
            m_new = jnp.maximum(m_old, jnp.max(sc, axis=1, keepdims=True))
            p = jnp.exp2((sc - jnp.tile(m_new, (1, reps))) * EXP2_SCALE)
            alpha = jnp.exp2((m_old - m_new) * EXP2_SCALE)
            l_ref[h] = l_ref[h] * alpha + jnp.sum(p, axis=1, keepdims=True)
            acc_ref[h] = acc_ref[h] * alpha + jnp.dot(p.astype(jnp.bfloat16), v_blk, preferred_element_type=jnp.float32)
            m_ref[h] = m_new

    n_full = jnp.minimum((row0 + 1) // bk, valid // bk)
    n_end = jnp.minimum((row0 + bq + bk - 1) // bk, (valid + bk - 1) // bk)

    def full(j, _):
        step(j, False)
        return 0

    def part(j, _):
        step(j, True)
        return 0

    lax.fori_loop(0, n_full, full, 0)
    lax.fori_loop(n_full, n_end, part, 0)
    for h in range(per):
        o_ref[:, h * HEAD_DIM:(h + 1) * HEAD_DIM] = (acc_ref[h] / l_ref[h]).astype(jnp.bfloat16)


def att_call(q, k, v, valid_len, call):
    n_q, s, _ = q.shape
    n_kv = k.shape[1] // HEAD_DIM
    per = n_q // n_kv
    rows = s // N_CALLS
    bq = min(256, rows)
    bk = min(512, s)
    first = call * rows
    off = first // bq
    frac = (2 * call + 1) / N_CALLS ** 2
    kernel = functools.partial(att_kernel, bq, bk, per, first)
    args = [valid_len, q, k, v]
    in_specs = [pl.BlockSpec(memory_space=pltpu.SMEM),
                pl.BlockSpec((per, bq, HEAD_DIM), lambda g, i: (g, off + i, 0)),
                pl.BlockSpec((s, HEAD_DIM), lambda g, i: (0, g)),
                pl.BlockSpec((s, HEAD_DIM), lambda g, i: (0, g))]
    return pl.pallas_call(
        kernel,
        grid=(n_kv, rows // bq),
        in_specs=in_specs,
        out_specs=pl.BlockSpec((bq, per * HEAD_DIM), lambda g, i: (i, g)),
        out_shape=jax.ShapeDtypeStruct((rows, n_q * HEAD_DIM), jnp.bfloat16),
        scratch_shapes=[pltpu.VMEM((per, bq, HEAD_DIM), jnp.float32)] * 3,
        compiler_params=params(),
        cost_estimate=cost(int(8 * frac * n_q * s * s * HEAD_DIM), 4 * n_q * s * HEAD_DIM),
        name="attention",
    )(*args)


def out_kernel(n_src, bn, idx_ref, *refs):
    o_refs = refs[:n_src]
    w_ref, x_ref, g_ref, r_ref, u_ref, y_ref = refs[n_src:]
    d = x_ref.shape[1]

    @pl.loop(0, d // bn)
    def _(n):
        acc = None
        for s in range(n_src):
            col = pl.multiple_of(idx_ref[1 + s] * d + n * bn, bn)
            part = jnp.dot(o_refs[s][...], w_ref[:, pl.ds(col, bn)], preferred_element_type=jnp.float32)
            acc = part if acc is None else acc + part
        col = pl.multiple_of(n * bn, bn)
        y_ref[:, pl.ds(col, bn)] = (x_ref[:, pl.ds(col, bn)].astype(jnp.float32) + acc).astype(jnp.bfloat16)

    r_ref[...] = y_ref[...]
    u_ref[...] = norm_rows(y_ref[...].astype(jnp.float32), g_ref[...].astype(jnp.float32))


def out_call(idx, o_pieces, w, x, gain, sub, n_tp):
    n_src = len(o_pieces)
    rows, ko = o_pieces[0].shape
    d = x.shape[1]
    bn = min(512, d)
    row = lambda i, idx: (i, 0)
    fixed = lambda i, idx: (0, 0)
    return pl.pallas_call(
        functools.partial(out_kernel, n_src, bn),
        grid_spec=pltpu.PrefetchScalarGridSpec(
            num_scalar_prefetch=1,
            grid=(rows // sub,),
            in_specs=[pl.BlockSpec((sub, ko), row)] * n_src + [
                pl.BlockSpec(w.shape, fixed, pipeline_mode=pl.Buffered(1)),
                pl.BlockSpec((sub, d), lambda i, idx: (i * n_tp + idx[0], 0)),
                pl.BlockSpec((1, d), fixed)],
            out_specs=[pl.BlockSpec((sub, d), row), pl.BlockSpec((sub, d), row)],
            scratch_shapes=[pltpu.VMEM((sub, d), jnp.bfloat16)]),
        out_shape=[jax.ShapeDtypeStruct((rows, d), jnp.bfloat16)] * 2,
        compiler_params=params(),
        cost_estimate=cost(2 * rows * d * ko * n_src, 2 * w.size + 8 * rows * d),
        name="w_out",
    )(idx, *o_pieces, w, x, gain)


def gu_kernel(bm, u_ref, g_ref, up_ref, a_ref):
    rows = u_ref.shape[0]

    @pl.loop(0, rows // bm)
    def _(m):
        r = pl.ds(pl.multiple_of(m * bm, bm), bm)
        u = u_ref[r, :]
        gate = jnp.dot(u, g_ref[0], preferred_element_type=jnp.float32)
        up = jnp.dot(u, up_ref[0], preferred_element_type=jnp.float32)
        a_ref[r, :] = (jax.nn.silu(gate) * up).astype(jnp.bfloat16)


def gu_call(u, w):
    rows, d = u.shape
    n_src, _, two = w.shape
    half = two // 2
    bn = min(512, half)
    nb = half // bn
    bm = min(256, rows)
    return pl.pallas_call(
        functools.partial(gu_kernel, bm),
        grid=(n_src, nb),
        in_specs=[pl.BlockSpec((rows, d), lambda j, n: (0, 0), pipeline_mode=pl.Buffered(1)),
                  pl.BlockSpec((1, d, bn), lambda j, n: (j, 0, n)),
                  pl.BlockSpec((1, d, bn), lambda j, n: (j, 0, nb + n))],
        out_specs=pl.BlockSpec((rows, bn), lambda j, n: (0, j * nb + n)),
        out_shape=jax.ShapeDtypeStruct((rows, n_src * half), jnp.bfloat16),
        compiler_params=params(),
        cost_estimate=cost(2 * rows * d * n_src * two, 2 * w.size + 2 * rows * d + 2 * rows * n_src * half),
        name="gate_up",
    )(u, w, w)


def down_kernel(bm, parts, *refs):
    a_refs = refs[:parts]
    w_ref, r_ref, o_ref, acc_ref = refs[parts:]
    j = pl.program_id(1)
    kp = a_refs[0].shape[1]
    rows = acc_ref.shape[0]

    @pl.when(j == 0)
    def _():
        acc_ref[...] = r_ref[...].astype(jnp.float32)

    @pl.loop(0, rows // bm)
    def _(m):
        r = pl.ds(pl.multiple_of(m * bm, bm), bm)
        acc = acc_ref[r, :]
        for p in range(parts):
            acc = acc + jnp.dot(a_refs[p][r, :], w_ref[p * kp:(p + 1) * kp, :], preferred_element_type=jnp.float32)
        acc_ref[r, :] = acc

    @pl.when(j == pl.num_programs(1) - 1)
    def _():
        o_ref[...] = acc_ref[...].astype(jnp.bfloat16)


def down_call(a_parts, w, resid, n_src, chunk, n_chunks):
    rows, d = resid.shape
    rows //= n_chunks
    parts = len(a_parts)
    kj = w.shape[0]
    kp = kj // parts
    bn = min(1024, d)
    nb = d // bn
    bm = min(256, rows)
    return pl.pallas_call(
        functools.partial(down_kernel, bm, parts),
        grid=(nb, n_src),
        in_specs=[pl.BlockSpec((rows, kp), lambda n, j: (chunk, j))] * parts + [
            pl.BlockSpec((kj, bn), lambda n, j: (0, j * nb + n)),
            pl.BlockSpec((rows, bn), lambda n, j: (chunk, n))],
        out_specs=pl.BlockSpec((rows, bn), lambda n, j: (0, n)),
        out_shape=jax.ShapeDtypeStruct((rows, d), jnp.bfloat16),
        scratch_shapes=[pltpu.VMEM((rows, bn), jnp.float32)],
        compiler_params=params(),
        cost_estimate=cost(2 * rows * d * kj * n_src, 2 * w.size + 4 * rows * d),
        name="down",
    )(*a_parts, w, resid)


def solution(mesh):
    batch_axes = ('dp', 'fsdp')
    n_tp = mesh.shape['tp']
    n_fs = mesh.shape['fsdp']
    in_specs = (P(batch_axes, None, None), P(batch_axes, None), P(batch_axes),
                P('fsdp', 'tp'), P('fsdp', 'tp'), P('fsdp', 'tp'), P('tp', 'fsdp'),
                P('fsdp', 'tp'), P('fsdp', 'tp'), P('tp', 'fsdp'), P(None), P(None))
    out_specs = (P(batch_axes, None, None), P(batch_axes, None, 'tp', None), P(batch_axes, None, 'tp', None))

    def local_layer(tokens, positions, valid_len, w_query, w_key, w_value, w_out, w_gate, w_up, w_down, norm_attn, norm_mlp):
        _, seq, d = tokens.shape
        x = tokens.reshape(seq, d)
        n_q = w_query.shape[1] // HEAD_DIM
        n_kv = w_key.shape[1] // HEAD_DIM
        sub = seq // (n_tp * N_CALLS)
        me = lax.axis_index('tp')
        both = ('tp', 'fsdp')

        w_qkv = lax.all_gather(jnp.concatenate([w_query, w_key, w_value], axis=1), 'fsdp', axis=0, tiled=True)
        full_o = lax.all_gather(w_out, both, axis=1, tiled=True)
        fl = w_gate.shape[1]
        gu_parts = []
        for p in range(2):
            cut = slice(p * fl // 2, (p + 1) * fl // 2)
            local = jnp.concatenate([w_gate[:, cut], w_up[:, cut]], axis=1)
            gu_parts.append(lax.all_gather(local, both, axis=0, tiled=True).reshape(n_tp, d, fl))
        full_d = lax.all_gather(w_down, both, axis=1, tiled=True)

        angles = positions.reshape(seq, 1).astype(jnp.float32) * rope_freqs()[None, :]
        cos_h, sin_h = jnp.cos(angles), jnp.sin(angles)
        cos_t = jnp.concatenate([cos_h, cos_h], axis=1)
        sin_t = jnp.concatenate([-sin_h, sin_h], axis=1)
        q, k, v = qkv_call(x, norm_attn.reshape(1, d), w_qkv, cos_t, sin_t, n_q, n_kv)

        pieces = [[] for _ in range(n_tp)]
        for call in range(N_CALLS):
            o = att_call(q, k, v, valid_len, call)
            for s in range(n_tp):
                blk = lax.dynamic_slice_in_dim(o, (me + s) % n_tp * sub, sub, axis=0)
                if s:
                    blk = lax.ppermute(blk, 'tp', [(i, (i + s) % n_tp) for i in range(n_tp)])
                pieces[s].append(blk)
        o_pieces = [jnp.concatenate(p, axis=0) for p in pieces]
        idx = jnp.stack([me] + [(me - s) % n_tp for s in range(n_tp)]).astype(jnp.int32)
        resid, u = out_call(idx, o_pieces, full_o, x, norm_mlp.reshape(1, d), sub, n_tp)

        a_parts = [gu_call(u, w) for w in gu_parts]
        outs = []
        for c in range(N_CALLS):
            part = down_call(a_parts, full_d, resid, n_tp, c, N_CALLS)
            outs.append(lax.all_gather(part, 'tp', axis=0, tiled=True))
        hidden = jnp.concatenate(outs, axis=0).reshape(1, seq, d)
        return hidden, k.reshape(1, seq, n_kv, HEAD_DIM), v.reshape(1, seq, n_kv, HEAD_DIM)

    return jax.shard_map(local_layer, mesh=mesh, in_specs=in_specs, out_specs=out_specs, check_vma=False)
```

time: 1650 us -> 998 us (0.60)
  matrix products: 493 us -> 0 us
  Pallas kernels: 0 us -> 421 us
  waiting for transfers between devices: 895 us -> 493 us
  other arithmetic: 196 us -> 44.6 us
  local copies, waits for them, and re-layouts: 37.4 us -> 16.3 us
    psum x2 -> x0, waiting for transfers between devices: 833 us -> none  [the longest x1 422 us: local_layer(): y_attn = lax.psum(y_part, 'tp')]
    dot_general x39 -> x0, matrix products: 493 us -> none  [the longest x16 117 us: attention(): jnp.einsum('bkgqs,bskd->bqkgd', attn_prob, v_cache[:, :end_row], preferre...]
    pallas_call x0 -> x8, Pallas kernels: none -> 421 us  [the longest x2 127 us: gu_call(): pl.pallas_call(functools.partial(gu_kernel, bm), grid=(n_src, nb), in_spe...]
    all_gather x7, waiting for transfers between devices: 56.8 us -> 397 us  [the longest x2 193 us: local_layer(): outs.append(lax.all_gather(part, 'tp', axis=0, tiled=True))]
    reduce_sum x18 -> x0, other arithmetic: 129 us -> none  [the longest x16 92.5 us: attention(): attn_prob = jax.nn.softmax(scores, axis=-1).astype(jnp.bfloat16)]
    ppermute x0 -> x6, waiting for transfers between devices: none -> 94.3 us  [local_layer(): blk = lax.ppermute(blk, 'tp', [(i, (i + s) % n_tp) for i in range(n_tp)])]
    convert_element_type x4 -> x1, other arithmetic: 30.5 us -> 0.01 us  [local_layer(): positions.reshape(seq, 1).astype(jnp.float32) * rope_freqs()[None, :]]
    and x16 -> x0, other arithmetic: 26.2 us -> none  [attention(): (k_index <= q_index)[None] & (k_index[None] < valid_len[:, None, None])]
  transfers between devices with their start and end apart: 9 -> 13, of which waited for: 6 -> 9; matrix products, arithmetic and copies ran while one was open for 37% -> 4% of each run, Pallas kernels for 0% -> 38%
where the time goes in v1:
time: 998 us; the launch traced here: 997 us
  waiting for transfers between devices  493 us (49%)
  Pallas kernels  421 us (42%)
  other arithmetic  44.6 us (4%)
  local copies, waits for them, and re-layouts  16.3 us (2%)
  between operations  15 us (2%)
    all_gather x2, waiting for transfers between devices, local_layer(): outs.append(lax.all_gather(part, 'tp', axis=0, tiled=True))  193 us
    pallas_call x2, Pallas kernels, gu_call(): pl.pallas_call(functools.partial(gu_kernel, bm), grid=(n_src, nb), in_spe...  127 us
    pallas_call x2, Pallas kernels, att_call(): pl.pallas_call(kernel, grid=(n_kv, rows // bq), in_specs=in_specs, out_sp...  125 us
    all_gather x1, waiting for transfers between devices, local_layer(): full_d = lax.all_gather(w_down, both, axis=1, tiled=True)  102 us
    ppermute x6, waiting for transfers between devices, local_layer(): blk = lax.ppermute(blk, 'tp', [(i, (i + s) % n_tp) for i in range(n_tp)])  94.3 us
    pallas_call x2, Pallas kernels, down_call(): pl.pallas_call(functools.partial(down_kernel, bm, parts), grid=(nb, n_src...  74.6 us
    all_gather x2, waiting for transfers between devices, local_layer(): lax.all_gather(local, both, axis=0, tiled=True).reshape(n_tp, d, fl)  71.3 us
    pallas_call x1, Pallas kernels, qkv_call(): pl.pallas_call(functools.partial(qkv_kernel, n_q, n_kv), grid=(s // bm,),...  58.3 us
  transfers between devices with their start and end apart: 13, of which 9 were waited for; matrix products, arithmetic and copies ran while one was open for 4% of the time, Pallas kernels for 38%

profile of v1, /device:TPU:97, one launch (start us, length us, event | category | flops | bytes accessed | tf_op | source)
XLA Modules:
  0.0 997.4 jit_solution(12851028977308326940)
XLA Ops:
  7.3 2.4 pad_maximum_fusion.8
  10.6 1.7 fusion.1
  13.7 1.3 pad_maximum_fusion.6
  17.2 7.5 fusion
  24.7 3.2 pad_maximum_fusion
  27.9 31.4 %all-gather.8.cloned.1.call-done.w_ref = bf16[3072,1280]{1,0:T(8,128)(2,1)} async-done(((bf16[384,1280]{1,0:T(8,128)(2,1)}), bf16[3072,1280]{1,0:T(8,128)(2,1)}) %all-gather.8.cloned.1.call-update) | async-done | bytes 7864336 | tf_op jit(solution)/shard_map/all_gather | solution.py:300
  59.3 58.3 %qkv.1 = (bf16[6,4096,128]{2,1,0:T(8,128)(2,1)}, bf16[4096,256]{1,0:T(8,128)(2,1)}, bf16[4096,256]{1,0:T(8,128)(2,1)}) custom-call(bf16[4096,3072]{1,0:T(8,128)(2,1)} %bitcast.16, bf16[1,3072]{1,0:T(2,128)(2,1)} %reshape.61.g_ref, bf16[3072,1280]{1,0:T(8,128)(2,1)} %all-gather.8.cloned.1.call-done.w_ref, f32[4096,128]{1,0:T(8,128)} %get-tuple-element.28.cos_ref, ...), custom_call_target="tpu_custom_call" | custom-call | flops 32212254720 | bytes 43515904 | tf_op jit(solution)/shard_map/qkv/pallas_call | solution.py:67
  117.6 49.2 %attention.2 = bf16[2048,768]{1,0:T(8,128)(2,1)} custom-call(s32[1]{0:T(128)S(6)} %copy.15.len_ref, bf16[6,4096,128]{2,1,0:T(8,128)(2,1)} %get-tuple-element.8.q_ref, bf16[4096,256]{1,0:T(8,128)(2,1)} %get-tuple-element.9.k_ref, bf16[4096,256]{1,0:T(8,128)(2,1)} %get-tuple-element.10.v_ref), custom_call_target="tpu_custom_call" | custom-call | flops 25769803776 | bytes 12582912 | tf_op jit(solution)/shard_map/attention/pallas_call | solution.py:144
  166.8 3.3 constant_dynamic-slice_fusion.1
  170.1 2.4 collective-permute-start.4
  172.5 75.5 %attention.3 = bf16[2048,768]{1,0:T(8,128)(2,1)} custom-call(s32[1]{0:T(128)S(6)} %copy.15.len_ref, bf16[6,4096,128]{2,1,0:T(8,128)(2,1)} %get-tuple-element.8.q_ref, bf16[4096,256]{1,0:T(8,128)(2,1)} %get-tuple-element.9.k_ref, bf16[4096,256]{1,0:T(8,128)(2,1)} %get-tuple-element.10.v_ref), custom_call_target="tpu_custom_call" | custom-call | flops 77309411328 | bytes 12582912 | tf_op jit(solution)/shard_map/attention/pallas_call | solution.py:144
  248.0 3.3 constant_dynamic-slice_fusion
  252.1 2.7 collective-permute-start.3
  258.3 21.2 %collective-permute-done.5 = bf16[512,768]{1,0:T(8,128)(2,1)} collective-permute-done((bf16[512,768]{1,0:T(8,128)(2,1)}, bf16[512,768]{1,0:T(8,128)(2,1)}, u32[]{:S(2)}, u32[]{:S(2)}) %collective-permute-start.5) | collective-permute-done | bytes 786464 | tf_op jit(solution)/shard_map/ppermute | solution.py:322
  279.4 2.4 pad_maximum_fusion.5.refs_3_
  281.8 26.8 %collective-permute-done.3 = bf16[512,768]{1,0:T(8,128)(2,1)} collective-permute-done((bf16[512,768]{1,0:T(8,128)(2,1)}, bf16[512,768]{1,0:T(8,128)(2,1)}, u32[]{:S(2)}, u32[]{:S(2)}) %collective-permute-start.3) | collective-permute-done | bytes 786464 | tf_op jit(solution)/shard_map/ppermute | solution.py:322
  308.6 2.6 pad_maximum_fusion.4.refs_2_
  311.2 27.5 %collective-permute-done = bf16[512,768]{1,0:T(8,128)(2,1)S(1)} collective-permute-done((bf16[512,768]{1,0:T(8,128)(2,1)}, bf16[512,768]{1,0:T(8,128)(2,1)S(1)}, u32[]{:S(2)}, u32[]{:S(2)}) %collective-permute-start) | collective-permute-done | bytes 786464 | tf_op jit(solution)/shard_map/ppermute | solution.py:322
  338.7 18.8 %collective-permute-done.1 = bf16[512,768]{1,0:T(8,128)(2,1)} collective-permute-done((bf16[512,768]{1,0:T(8,128)(2,1)}, bf16[512,768]{1,0:T(8,128)(2,1)}, u32[]{:S(2)}, u32[]{:S(2)}) %collective-permute-start.1) | collective-permute-done | bytes 786464 | tf_op jit(solution)/shard_map/ppermute | solution.py:322
  357.5 2.4 pad_maximum_fusion.3.refs_1_
  359.9 36.7 %w_out.1 = (bf16[1024,3072]{1,0:T(8,128)(2,1)}, bf16[1024,3072]{1,0:T(8,128)(2,1)}) custom-call(s32[5]{0:T(128)} %stack.23.idx_ref, bf16[1024,768]{1,0:T(8,128)(2,1)} %pad_maximum_fusion.2.refs_0_, bf16[1024,768]{1,0:T(8,128)(2,1)} %pad_maximum_fusion.3.refs_1_, bf16[1024,768]{1,0:T(8,128)(2,1)} %pad_maximum_fusion.4.refs_2_, ...), custom_call_target="tpu_custom_call" | custom-call | flops 19327352832 | bytes 44040192 | tf_op jit(solution)/shard_map/w_out/pallas_call | solution.py:183
  396.6 63.4 %gate_up.3.refs_1_ = bf16[1024,4096]{1,0:T(8,128)(2,1)} custom-call(bf16[1024,3072]{1,0:T(8,128)(2,1)} %get-tuple-element.11.u_ref, bf16[4,3072,2048]{2,1,0:T(8,128)(2,1)} %bitcast.12, bf16[4,3072,2048]{2,1,0:T(8,128)(2,1)} %bitcast.13), custom_call_target="tpu_custom_call" | custom-call | flops 51539607552 | bytes 65011712 | tf_op jit(solution)/shard_map/gate_up/pallas_call | solution.py:220
  460.0 71.3 %all-gather.12.cloned.1.call-done = bf16[12288,2048]{1,0:T(8,128)(2,1)} async-done(((bf16[384,2048]{1,0:T(8,128)(2,1)}), bf16[12288,2048]{1,0:T(8,128)(2,1)}) %all-gather.12.cloned.1.call-update) | async-done | bytes 50331664 | tf_op jit(solution)/shard_map/all_gather | solution.py:307
  531.3 63.2 %gate_up.2.refs_0_ = bf16[1024,4096]{1,0:T(8,128)(2,1)} custom-call(bf16[1024,3072]{1,0:T(8,128)(2,1)} %get-tuple-element.11.u_ref, bf16[4,3072,2048]{2,1,0:T(8,128)(2,1)} %bitcast.14, bf16[4,3072,2048]{2,1,0:T(8,128)(2,1)} %bitcast.15), custom_call_target="tpu_custom_call" | custom-call | flops 51539607552 | bytes 65011712 | tf_op jit(solution)/shard_map/gate_up/pallas_call | solution.py:220
  594.5 102.2 %all-gather.16.cloned.1.call-done.refs_2_ = bf16[2048,12288]{1,0:T(8,128)(2,1)} async-done(((bf16[2048,384]{1,0:T(8,128)(2,1)}), bf16[2048,12288]{1,0:T(8,128)(2,1)}) %all-gather.16.cloned.1.call-update) | async-done | bytes 50331664 | tf_op jit(solution)/shard_map/all_gather | solution.py:308
  696.7 37.3 %down.2 = bf16[512,3072]{1,0:T(8,128)(2,1)} custom-call(bf16[1024,4096]{1,0:T(8,128)(2,1)} %gate_up.2.refs_0_, bf16[1024,4096]{1,0:T(8,128)(2,1)} %gate_up.3.refs_1_, bf16[2048,12288]{1,0:T(8,128)(2,1)} %all-gather.16.cloned.1.call-done.refs_2_, bf16[1024,3072]{1,0:T(8,128)(2,1)} %get-tuple-element.12.refs_3_), custom_call_target="tpu_custom_call" | custom-call | flops 25769803776 | bytes 56623104 | tf_op jit(solution)/shard_map/down/pallas_call | solution.py:267
  734.1 37.3 %down.3 = bf16[512,3072]{1,0:T(8,128)(2,1)} custom-call(bf16[1024,4096]{1,0:T(8,128)(2,1)} %gate_up.2.refs_0_, bf16[1024,4096]{1,0:T(8,128)(2,1)} %gate_up.3.refs_1_, bf16[2048,12288]{1,0:T(8,128)(2,1)} %all-gather.16.cloned.1.call-done.refs_2_, bf16[1024,3072]{1,0:T(8,128)(2,1)} %get-tuple-element.12.refs_3_), custom_call_target="tpu_custom_call" | custom-call | flops 25769803776 | bytes 56623104 | tf_op jit(solution)/shard_map/down/pallas_call | solution.py:267
  771.5 4.1 reshape.66
  775.7 2.0 reshape.67
  777.7 73.4 %all-gather.18.cloned.1.call-done = bf16[2048,3072]{1,0:T(8,128)(2,1)} async-done(((bf16[512,3072]{1,0:T(8,128)(2,1)}), bf16[2048,3072]{1,0:T(8,128)(2,1)}) %all-gather.18.cloned.1.call-update) | async-done | bytes 12582928 | tf_op jit(solution)/shard_map/all_gather | solution.py:332
  851.1 119.1 %all-gather.20.cloned.1.call-done = bf16[2048,3072]{1,0:T(8,128)(2,1)} async-done(((bf16[512,3072]{1,0:T(8,128)(2,1)}), bf16[2048,3072]{1,0:T(8,128)(2,1)}) %all-gather.20.cloned.1.call-update) | async-done | bytes 12582928 | tf_op jit(solution)/shard_map/all_gather | solution.py:332
  970.2 20.4 %maximum_bitcast_fusion = bf16[1,4096,3072]{2,1,0:T(8,128)(2,1)} fusion(bf16[2048,3072]{1,0:T(8,128)(2,1)} %all-gather.20.cloned.1.call-done, bf16[2048,3072]{1,0:T(8,128)(2,1)} %all-gather.18.cloned.1.call-done), kind=kLoop, calls=%fused_computation | loop fusion | flops 50331648 | bytes 50331648 | tf_op jit(solution)/shard_map/reshape | solution.py:333
  (39 shorter events, 8.2 us)
Async XLA Ops:
  7.2 3.4 copy-start.1
  7.2 52.1 %all-gather.8.cloned.1.call-start = ((), (), s32[]{:S(2)}) async-start(), calls=%async_computation | async-start | bytes 8847360 | tf_op jit(solution)/shard_map/all_gather | solution.py:300
  9.7 350.2 %all-gather.10.cloned.1.call-start = ((), (), s32[]{:S(2)}) async-start(), calls=%async_computation.1 | async-start | bytes 19464192 | tf_op jit(solution)/shard_map/all_gather | solution.py:301
  10.5 386.1 %all-gather.14.cloned.1.call-start = ((), (), s32[]{:S(2)}) async-start(), calls=%async_computation.3 | async-start | bytes 51904512 | tf_op jit(solution)/shard_map/all_gather | solution.py:307
  13.6 517.7 %all-gather.12.cloned.1.call-start = ((), (), s32[]{:S(2)}) async-start(), calls=%async_computation.2 | async-start | bytes 51904512 | tf_op jit(solution)/shard_map/all_gather | solution.py:307
  15.0 0.8 copy-start.2
  15.0 0.9 copy-start.3
  15.1 681.6 %all-gather.16.cloned.1.call-start = ((), (), s32[]{:S(2)}) async-start(), calls=%async_computation.4 | async-start | bytes 51904512 | tf_op jit(solution)/shard_map/all_gather | solution.py:308
  15.8 835.4 %all-gather.18.cloned.1.call-start = ((), (), s32[]{:S(2)}) async-start(), calls=%async_computation.5 | async-start | bytes 15728640 | tf_op jit(solution)/shard_map/all_gather | solution.py:332
  170.1 85.7 %collective-permute-start.4 = (bf16[512,768]{1,0:T(8,128)(2,1)}, bf16[512,768]{1,0:T(8,128)(2,1)S(1)}, u32[]{:S(2)}, u32[]{:S(2)}) collective-permute-start(bf16[512,768]{1,0:T(8,128)(2,1)} %get-tuple-element.13), channel_id=1, source_target_pairs={{0,24},{8,0},{16,8},{24,16},{1,25},{9,1},{17,9},{25,17},{2,26},{10... | collective-permute-start | bytes 2359304 | tf_op jit(solution)/shard_map/ppermute | solution.py:322
  248.0 7.8 copy-start.4
  251.3 28.1 %collective-permute-start.5 = (bf16[512,768]{1,0:T(8,128)(2,1)}, bf16[512,768]{1,0:T(8,128)(2,1)}, u32[]{:S(2)}, u32[]{:S(2)}) collective-permute-start(bf16[512,768]{1,0:T(8,128)(2,1)} %get-tuple-element.17), channel_id=1, source_target_pairs={{0,24},{8,0},{16,8},{24,16},{1,25},{9,1},{17,9},{25,17},{2,26},{10... | collective-permute-start | bytes 2359304 | tf_op jit(solution)/shard_map/ppermute | solution.py:322
  251.9 29.9 %collective-permute-start.2 = (bf16[512,768]{1,0:T(8,128)(2,1)}, bf16[512,768]{1,0:T(8,128)(2,1)}, u32[]{:S(2)}, u32[]{:S(2)}) collective-permute-start(bf16[512,768]{1,0:T(8,128)(2,1)} %get-tuple-element.14), channel_id=1, source_target_pairs={{0,16},{8,24},{16,0},{24,8},{1,17},{9,25},{17,1},{25,9},{2,18},{10... | collective-permute-start | bytes 2359304 | tf_op jit(solution)/shard_map/ppermute | solution.py:322
  252.1 56.4 %collective-permute-start.3 = (bf16[512,768]{1,0:T(8,128)(2,1)}, bf16[512,768]{1,0:T(8,128)(2,1)}, u32[]{:S(2)}, u32[]{:S(2)}) collective-permute-start(bf16[512,768]{1,0:T(8,128)(2,1)} %get-tuple-element.18), channel_id=1, source_target_pairs={{0,16},{8,24},{16,0},{24,8},{1,17},{9,25},{17,1},{25,9},{2,18},{10... | collective-permute-start | bytes 2359304 | tf_op jit(solution)/shard_map/ppermute | solution.py:322
  254.9 83.9 %collective-permute-start = (bf16[512,768]{1,0:T(8,128)(2,1)}, bf16[512,768]{1,0:T(8,128)(2,1)S(1)}, u32[]{:S(2)}, u32[]{:S(2)}) collective-permute-start(bf16[512,768]{1,0:T(8,128)(2,1)} %get-tuple-element.15), channel_id=1, source_target_pairs={{0,8},{8,16},{16,24},{24,0},{1,9},{9,17},{17,25},{25,1},{2,10},{10... | collective-permute-start | bytes 2359304 | tf_op jit(solution)/shard_map/ppermute | solution.py:322
  255.8 101.8 %collective-permute-start.1 = (bf16[512,768]{1,0:T(8,128)(2,1)}, bf16[512,768]{1,0:T(8,128)(2,1)}, u32[]{:S(2)}, u32[]{:S(2)}) collective-permute-start(bf16[512,768]{1,0:T(8,128)(2,1)} %get-tuple-element.19), channel_id=1, source_target_pairs={{0,8},{8,16},{16,24},{24,0},{1,9},{9,17},{17,25},{25,1},{2,10},{10... | collective-permute-start | bytes 2359304 | tf_op jit(solution)/shard_map/ppermute | solution.py:322
  734.1 236.1 %all-gather.20.cloned.1.call-start = ((), (), s32[]{:S(2)}) async-start(), calls=%async_computation.6 | async-start | bytes 15728640 | tf_op jit(solution)/shard_map/all_gather | solution.py:332
  771.5 4.1 copy-start
Sparse Core Ops, SparseCore 0:
  10.2 49.0 all-gather.7
  61.3 79.4 all-gather.9
  142.8 235.6 all-gather.13
  380.5 150.7 all-gather.11
  533.1 163.5 all-gather.15
  734.2 116.8 all-gather.17
  852.7 117.4 all-gather.19

commit v2 on v1

--- a/solution.py
+++ b/solution.py
@@ -5,14 +5,15 @@
 from jax import lax
 from jax.experimental import pallas as pl
 from jax.experimental.pallas import tpu as pltpu
-from jax.sharding import PartitionSpec as P
+from jax.sharding import Mesh, PartitionSpec as P
+
 
 HEAD_DIM = 128
 ROPE_THETA = 500000.0
 NORM_EPS = 1e-5
 EXP2_SCALE = HEAD_DIM ** -0.5 * math.log2(math.e)
 N_CALLS = 2
-VMEM_LIMIT = 60 * 1024 * 1024
+VMEM_LIMIT = 67043328
 
 
 def rope_freqs():
@@ -231,16 +232,24 @@
     )(u, w, w)
 
 
-def down_kernel(bm, parts, *refs):
+def down_kernel(bm, parts, own, *refs):
     a_refs = refs[:parts]
-    w_ref, r_ref, o_ref, acc_ref = refs[parts:]
+    w_ref = refs[parts]
+    rest = refs[parts + 1:]
+    acc_ref = rest[-1]
     j = pl.program_id(1)
     kp = a_refs[0].shape[1]
     rows = acc_ref.shape[0]
+    half = rows // 2
 
     @pl.when(j == 0)
     def _():
-        acc_ref[...] = r_ref[...].astype(jnp.float32)
+        if own:
+            for h in range(2):
+                r = slice(h * half, (h + 1) * half)
+                acc_ref[r, :] = rest[0][r, :].astype(jnp.float32) + rest[1 + h][...].astype(jnp.float32)
+        else:
+            acc_ref[...] = jnp.zeros_like(acc_ref)
 
     @pl.loop(0, rows // bm)
     def _(m):
@@ -252,41 +261,64 @@
 
     @pl.when(j == pl.num_programs(1) - 1)
     def _():
-        o_ref[...] = acc_ref[...].astype(jnp.bfloat16)
-
-
-def down_call(a_parts, w, resid, n_src, chunk, n_chunks):
-    rows, d = resid.shape
-    rows //= n_chunks
+        if own:
+            rest[3][...] = acc_ref[...].astype(jnp.bfloat16)
+        else:
+            for h in range(2):
+                rest[h][...] = acc_ref[h * half:(h + 1) * half, :].astype(jnp.bfloat16)
+
+
+def down_call(a_parts, w, rows, chunk, resid=None, partials=()):
+    kj = w.shape[0]
     parts = len(a_parts)
-    kj = w.shape[0]
     kp = kj // parts
+    n_src = a_parts[0].shape[1] // kp
+    d = w.shape[1] // n_src
+    own = resid is not None
     bn = min(1024, d)
     nb = d // bn
     bm = min(256, rows)
-    return pl.pallas_call(
-        functools.partial(down_kernel, bm, parts),
+    args = [*a_parts, w]
+    in_specs = [pl.BlockSpec((rows, kp), lambda n, j: (chunk, j))] * parts + [pl.BlockSpec((kj, bn), lambda n, j: (0, j * nb + n))]
+    col = lambda n, j: (0, n)
+    if own:
+        args += [resid, *partials]
+        in_specs += [pl.BlockSpec((rows, bn), lambda n, j: (chunk, n))] + [pl.BlockSpec((rows // 2, bn), col)] * 2
+        out_specs = pl.BlockSpec((rows, bn), col)
+        out_shape = jax.ShapeDtypeStruct((rows, d), jnp.bfloat16)
+    else:
+        out_specs = [pl.BlockSpec((rows // 2, bn), col)] * 2
+        out_shape = [jax.ShapeDtypeStruct((rows // 2, d), jnp.bfloat16)] * 2
+    return pl.pallas_call(
+        functools.partial(down_kernel, bm, parts, own),
         grid=(nb, n_src),
-        in_specs=[pl.BlockSpec((rows, kp), lambda n, j: (chunk, j))] * parts + [
-            pl.BlockSpec((kj, bn), lambda n, j: (0, j * nb + n)),
-            pl.BlockSpec((rows, bn), lambda n, j: (chunk, n))],
-        out_specs=pl.BlockSpec((rows, bn), lambda n, j: (0, n)),
-        out_shape=jax.ShapeDtypeStruct((rows, d), jnp.bfloat16),
+        in_specs=in_specs,
+        out_specs=out_specs,
+        out_shape=out_shape,
         scratch_shapes=[pltpu.VMEM((rows, bn), jnp.float32)],
         compiler_params=params(),
         cost_estimate=cost(2 * rows * d * kj * n_src, 2 * w.size + 4 * rows * d),
         name="down",
-    )(*a_parts, w, resid)
+    )(*args)
+
+
+def after(val, *deps):
+    return lax.optimization_barrier((val, *deps))[0]
 
 
 def solution(mesh):
-    batch_axes = ('dp', 'fsdp')
     n_tp = mesh.shape['tp']
     n_fs = mesh.shape['fsdp']
+    mesh2 = Mesh(mesh.devices.reshape(mesh.shape['dp'], n_tp // 2, 2, n_fs), ('dp', 'ta', 'tb', 'fsdp'))
+    tp = ('ta', 'tb')
+    batch_axes = ('dp', 'fsdp')
     in_specs = (P(batch_axes, None, None), P(batch_axes, None), P(batch_axes),
-                P('fsdp', 'tp'), P('fsdp', 'tp'), P('fsdp', 'tp'), P('tp', 'fsdp'),
-                P('fsdp', 'tp'), P('fsdp', 'tp'), P('tp', 'fsdp'), P(None), P(None))
-    out_specs = (P(batch_axes, None, None), P(batch_axes, None, 'tp', None), P(batch_axes, None, 'tp', None))
+                P('fsdp', tp), P('fsdp', tp), P('fsdp', tp), P(tp, 'fsdp'),
+                P('fsdp', tp), P('fsdp', tp), P(tp, 'fsdp'), P(None), P(None))
+    out_specs = (P(batch_axes, None, None), P(batch_axes, None, tp, None), P(batch_axes, None, tp, None))
+
+    def shift(val, s):
+        return lax.ppermute(val, tp, [(i, (i + s) % n_tp) for i in range(n_tp)])
 
     def local_layer(tokens, positions, valid_len, w_query, w_key, w_value, w_out, w_gate, w_up, w_down, norm_attn, norm_mlp):
         _, seq, d = tokens.shape
@@ -294,18 +326,17 @@
         n_q = w_query.shape[1] // HEAD_DIM
         n_kv = w_key.shape[1] // HEAD_DIM
         sub = seq // (n_tp * N_CALLS)
-        me = lax.axis_index('tp')
-        both = ('tp', 'fsdp')
+        me = lax.axis_index(tp)
 
         w_qkv = lax.all_gather(jnp.concatenate([w_query, w_key, w_value], axis=1), 'fsdp', axis=0, tiled=True)
-        full_o = lax.all_gather(w_out, both, axis=1, tiled=True)
+        full_o = lax.all_gather(w_out, ('ta', 'tb', 'fsdp'), axis=1, tiled=True)
         fl = w_gate.shape[1]
         gu_parts = []
         for p in range(2):
             cut = slice(p * fl // 2, (p + 1) * fl // 2)
             local = jnp.concatenate([w_gate[:, cut], w_up[:, cut]], axis=1)
-            gu_parts.append(lax.all_gather(local, both, axis=0, tiled=True).reshape(n_tp, d, fl))
-        full_d = lax.all_gather(w_down, both, axis=1, tiled=True)
+            gu_parts.append(lax.all_gather(local, ('ta', 'fsdp'), axis=0, tiled=True).reshape(n_tp // 2, d, fl))
+        full_d = lax.all_gather(w_down, ('ta', 'fsdp'), axis=1, tiled=True)
 
         angles = positions.reshape(seq, 1).astype(jnp.float32) * rope_freqs()[None, :]
         cos_h, sin_h = jnp.cos(angles), jnp.sin(angles)
@@ -315,22 +346,39 @@
 
         pieces = [[] for _ in range(n_tp)]
         for call in range(N_CALLS):
-            o = att_call(q, k, v, valid_len, call)
+            o = att_call(after(q, *[p[0] for p in pieces[:call]]), k, v, valid_len, call)
             for s in range(n_tp):
                 blk = lax.dynamic_slice_in_dim(o, (me + s) % n_tp * sub, sub, axis=0)
                 if s:
-                    blk = lax.ppermute(blk, 'tp', [(i, (i + s) % n_tp) for i in range(n_tp)])
+                    blk = shift(blk, s)
                 pieces[s].append(blk)
         o_pieces = [jnp.concatenate(p, axis=0) for p in pieces]
         idx = jnp.stack([me] + [(me - s) % n_tp for s in range(n_tp)]).astype(jnp.int32)
         resid, u = out_call(idx, o_pieces, full_o, x, norm_mlp.reshape(1, d), sub, n_tp)
 
-        a_parts = [gu_call(u, w) for w in gu_parts]
+        u4 = u.reshape(N_CALLS, 2, sub // 2, d)
+        u_prev = shift(u4[:, 0], 1)
+        u_next = shift(u4[:, 1], -1)
+        a_own = [gu_call(u, gu_parts[0])]
+        a_own.append(gu_call(after(u, a_own[0]), gu_parts[1]))
+        u_prev, u_next = lax.optimization_barrier((u_prev, u_next, a_own[1]))[:2]
+        u_recv = jnp.stack([u_prev, u_next], axis=1).reshape(u.shape)
+        a_recv = [gu_call(u_recv, gu_parts[0])]
+        a_recv.append(gu_call(after(u_recv, a_recv[0]), gu_parts[1]))
+        partials = []
+        order = a_recv[1]
+        for c in range(N_CALLS):
+            p_prev, p_next = down_call([after(a_recv[0], order), a_recv[1]], full_d, sub, c)
+            order = p_prev
+            b_next = shift(p_prev, -1)
+            b_prev = shift(p_next, 1)
+            partials.append((b_next, b_prev))
         outs = []
         for c in range(N_CALLS):
-            part = down_call(a_parts, full_d, resid, n_tp, c, N_CALLS)
-            outs.append(lax.all_gather(part, 'tp', axis=0, tiled=True))
+            mine = down_call([after(a_own[0], order), a_own[1]], full_d, sub, c, resid, partials[c])
+            order = mine
+            outs.append(lax.all_gather(after(mine, *outs), tp, axis=0, tiled=True))
         hidden = jnp.concatenate(outs, axis=0).reshape(1, seq, d)
         return hidden, k.reshape(1, seq, n_kv, HEAD_DIM), v.reshape(1, seq, n_kv, HEAD_DIM)
 
-    return jax.shard_map(local_layer, mesh=mesh, in_specs=in_specs, out_specs=out_specs, check_vma=False)
+    return jax.shard_map(local_layer, mesh=mesh2, in_specs=in_specs, out_specs=out_specs, check_vma=False)

time: 998 us -> 1060 us (1.062)
  Pallas kernels: 421 us -> 444 us
  waiting for transfers between devices: 493 us -> 507 us
    ppermute x6 -> x12, waiting for transfers between devices: 94.3 us -> 108 us  [shift(): return lax.ppermute(val, tp, [(i, (i + s) % n_tp) for i in range(n_tp)])]
    pallas_call x2 -> x4, Pallas kernels: 127 us -> 138 us  [gu_call(): pl.pallas_call(functools.partial(gu_kernel, bm), grid=(n_src, nb), in_spe...]
    pallas_call x2 -> x4, Pallas kernels: 74.6 us -> 86 us  [down_call(): pl.pallas_call(functools.partial(down_kernel, bm, parts, own), grid=(nb,...]
  transfers between devices with their start and end apart: 13 -> 19, of which waited for: 9 -> 13; matrix products, arithmetic and copies ran while one was open for 4% -> 5% of each run, Pallas kernels for 38% -> 38%
where the time goes in v2:
time: 1060 us
  waiting for transfers between devices  507 us (48%)
  Pallas kernels  444 us (42%)
  other arithmetic  50.9 us (5%)
  local copies, waits for them, and re-layouts  25.2 us (2%)
  between operations  15 us (1%)
  starting transfers between devices  13 us (1%)
    all_gather x2, waiting for transfers between devices, local_layer(): outs.append(lax.all_gather(after(mine, *outs), tp, axis=0, tiled=True))  164 us
    all_gather x2, waiting for transfers between devices, local_layer(): lax.all_gather(local, ('ta', 'fsdp'), axis=0, tiled=True)  139 us
    pallas_call x4, Pallas kernels, gu_call(): pl.pallas_call(functools.partial(gu_kernel, bm), grid=(n_src, nb), in_spe...  138 us
    pallas_call x2, Pallas kernels, att_call(): pl.pallas_call(kernel, grid=(n_kv, rows // bq), in_specs=in_specs, out_sp...  125 us
    ppermute x12, waiting for transfers between devices, shift(): return lax.ppermute(val, tp, [(i, (i + s) % n_tp) for i in range(n_tp)])  108 us
    pallas_call x4, Pallas kernels, down_call(): pl.pallas_call(functools.partial(down_kernel, bm, parts, own), grid=(nb,...  86 us
    all_gather x1, waiting for transfers between devices, local_layer(): full_d = lax.all_gather(w_down, ('ta', 'fsdp'), axis=1, tiled=True)  63.3 us
    pallas_call x1, Pallas kernels, qkv_call(): pl.pallas_call(functools.partial(qkv_kernel, n_q, n_kv), grid=(s // bm,),...  58.2 us
  transfers between devices with their start and end apart: 19, of which 13 were waited for; matrix products, arithmetic and copies ran while one was open for 5% of the time, Pallas kernels for 38%

profile of v2, /device:TPU:97, one launch (start us, length us, event | category | flops | bytes accessed | tf_op | source)
XLA Modules:
  0.0 1055.4 jit_solution(15300105914335556196)
XLA Ops:
  17.2 7.5 fusion
  24.7 3.2 pad_maximum_fusion.1
  27.9 31.6 %all-gather.8.cloned.1.call-done.w_ref = bf16[3072,1280]{1,0:T(8,128)(2,1)} async-done(((bf16[384,1280]{1,0:T(8,128)(2,1)}), bf16[3072,1280]{1,0:T(8,128)(2,1)}) %all-gather.8.cloned.1.call-update) | async-done | bytes 7864336 | tf_op jit(solution)/shard_map/all_gather | solution.py:331
  59.5 58.2 %qkv.1 = (bf16[6,4096,128]{2,1,0:T(8,128)(2,1)}, bf16[4096,256]{1,0:T(8,128)(2,1)}, bf16[4096,256]{1,0:T(8,128)(2,1)}) custom-call(bf16[4096,3072]{1,0:T(8,128)(2,1)} %bitcast.27, bf16[1,3072]{1,0:T(2,128)(2,1)} %reshape.67.g_ref, bf16[3072,1280]{1,0:T(8,128)(2,1)} %all-gather.8.cloned.1.call-done.w_ref, f32[4096,128]{1,0:T(8,128)} %get-tuple-element.58.cos_ref, ...), custom_call_target="tpu_custom_call" | custom-call | flops 32212254720 | bytes 43515904 | tf_op jit(solution)/shard_map/qkv/pallas_call | solution.py:68
  117.7 49.1 %attention.2 = bf16[2048,768]{1,0:T(8,128)(2,1)} custom-call(s32[1]{0:T(128)S(6)} %copy.19.len_ref, bf16[6,4096,128]{2,1,0:T(8,128)(2,1)} %get-tuple-element.25.q_ref, bf16[4096,256]{1,0:T(8,128)(2,1)} %get-tuple-element.23.k_ref, bf16[4096,256]{1,0:T(8,128)(2,1)} %get-tuple-element.24.v_ref), custom_call_target="tpu_custom_call" | custom-call | flops 25769803776 | bytes 12582912 | tf_op jit(solution)/shard_map/attention/pallas_call | solution.py:145
  166.8 3.6 constant_dynamic-slice_fusion.1
  170.4 75.6 %attention.3 = bf16[2048,768]{1,0:T(8,128)(2,1)} custom-call(s32[1]{0:T(128)S(6)} %copy.19.len_ref, bf16[6,4096,128]{2,1,0:T(8,128)(2,1)} %get-tuple-element.25.q_ref, bf16[4096,256]{1,0:T(8,128)(2,1)} %get-tuple-element.23.k_ref, bf16[4096,256]{1,0:T(8,128)(2,1)} %get-tuple-element.24.v_ref), custom_call_target="tpu_custom_call" | custom-call | flops 77309411328 | bytes 12582912 | tf_op jit(solution)/shard_map/attention/pallas_call | solution.py:145
  246.0 3.3 constant_dynamic-slice_fusion
  256.1 13.5 %collective-permute-done.1 = bf16[512,768]{1,0:T(8,128)(2,1)} collective-permute-done((bf16[512,768]{1,0:T(8,128)(2,1)S(1)}, bf16[512,768]{1,0:T(8,128)(2,1)}, u32[]{:S(2)}, u32[]{:S(2)}) %collective-permute-start.1) | collective-permute-done | bytes 786464 | tf_op jit(solution)/shard_map/ppermute | solution.py:321
  272.3 5.7 collective-permute-done
  280.6 5.4 collective-permute-done.3
  286.1 8.5 collective-permute-done.2
  299.3 37.3 %w_out.1 = (bf16[1024,3072]{1,0:T(8,128)(2,1)}, bf16[1024,3072]{1,0:T(8,128)(2,1)}) custom-call(s32[5]{0:T(128)} %stack.32.idx_ref, bf16[1024,768]{1,0:T(8,128)(2,1)} %pad_maximum_fusion.3.refs_0_, bf16[1024,768]{1,0:T(8,128)(2,1)} %pad_maximum_fusion.4.refs_1_, bf16[1024,768]{1,0:T(8,128)(2,1)} %pad_maximum_fusion.5.refs_2_, ...), custom_call_target="tpu_custom_call" | custom-call | flops 19327352832 | bytes 44040192 | tf_op jit(solution)/shard_map/w_out/pallas_call | solution.py:184
  336.6 6.1 slice_bitcast_fusion
  345.4 34.6 %gate_up.4.refs_0_ = bf16[1024,2048]{1,0:T(8,128)(2,1)} custom-call(bf16[1024,3072]{1,0:T(8,128)(2,1)} %get-tuple-element.27.u_ref, bf16[2,3072,2048]{2,1,0:T(8,128)(2,1)} %bitcast.29, bf16[2,3072,2048]{2,1,0:T(8,128)(2,1)} %bitcast.30), custom_call_target="tpu_custom_call" | custom-call | flops 25769803776 | bytes 35651584 | tf_op jit(solution)/shard_map/gate_up/pallas_call | solution.py:221
  380.0 139.2 %all-gather.14.cloned.1.call-done = bf16[6144,2048]{1,0:T(8,128)(2,1)} async-done(((bf16[384,2048]{1,0:T(8,128)(2,1)}), bf16[6144,2048]{1,0:T(8,128)(2,1)}) %all-gather.14.cloned.1.call-update) | async-done | bytes 25165840 | tf_op jit(solution)/shard_map/all_gather | solution.py:338
  519.1 34.4 %gate_up.5.refs_1_ = bf16[1024,2048]{1,0:T(8,128)(2,1)} custom-call(bf16[1024,3072]{1,0:T(8,128)(2,1)} %get-tuple-element.27.u_ref, bf16[2,3072,2048]{2,1,0:T(8,128)(2,1)} %bitcast.33, bf16[2,3072,2048]{2,1,0:T(8,128)(2,1)} %bitcast.34), custom_call_target="tpu_custom_call" | custom-call | flops 25769803776 | bytes 35651584 | tf_op jit(solution)/shard_map/gate_up/pallas_call | solution.py:221
  553.6 6.3 pad_maximum_fusion
  559.9 34.6 %gate_up.6.refs_0_ = bf16[1024,2048]{1,0:T(8,128)(2,1)} custom-call(bf16[1024,3072]{1,0:T(8,128)(2,1)} %bitcast.24, bf16[2,3072,2048]{2,1,0:T(8,128)(2,1)} %bitcast.31, bf16[2,3072,2048]{2,1,0:T(8,128)(2,1)} %bitcast.32), custom_call_target="tpu_custom_call" | custom-call | flops 25769803776 | bytes 35651584 | tf_op jit(solution)/shard_map/gate_up/pallas_call | solution.py:221
  594.5 34.5 %gate_up.7.refs_1_ = bf16[1024,2048]{1,0:T(8,128)(2,1)} custom-call(bf16[1024,3072]{1,0:T(8,128)(2,1)} %bitcast.25, bf16[2,3072,2048]{2,1,0:T(8,128)(2,1)} %bitcast.35, bf16[2,3072,2048]{2,1,0:T(8,128)(2,1)} %bitcast.36), custom_call_target="tpu_custom_call" | custom-call | flops 25769803776 | bytes 35651584 | tf_op jit(solution)/shard_map/gate_up/pallas_call | solution.py:221
  629.0 63.3 %all-gather.16.cloned.1.call-done.refs_2_ = bf16[2048,6144]{1,0:T(8,128)(2,1)} async-done(((bf16[2048,384]{1,0:T(8,128)(2,1)}), bf16[2048,6144]{1,0:T(8,128)(2,1)}) %all-gather.16.cloned.1.call-update) | async-done | bytes 25165840 | tf_op jit(solution)/shard_map/all_gather | solution.py:339
  692.3 20.9 %down.4 = (bf16[256,3072]{1,0:T(8,128)(2,1)}, bf16[256,3072]{1,0:T(8,128)(2,1)}) custom-call(bf16[1024,2048]{1,0:T(8,128)(2,1)} %gate_up.6.refs_0_, bf16[1024,2048]{1,0:T(8,128)(2,1)} %gate_up.7.refs_1_, bf16[2048,6144]{1,0:T(8,128)(2,1)} %all-gather.16.cloned.1.call-done.refs_2_), custom_call_target="tpu_custom_call" | custom-call | flops 12884901888 | bytes 31457280 | tf_op jit(solution)/shard_map/down/pallas_call | solution.py:292
  714.6 20.8 %down.5 = (bf16[256,3072]{1,0:T(8,128)(2,1)}, bf16[256,3072]{1,0:T(8,128)(2,1)}) custom-call(bf16[1024,2048]{1,0:T(8,128)(2,1)} %gate_up.6.refs_0_, bf16[1024,2048]{1,0:T(8,128)(2,1)} %gate_up.7.refs_1_, bf16[2048,6144]{1,0:T(8,128)(2,1)} %all-gather.16.cloned.1.call-done.refs_2_), custom_call_target="tpu_custom_call" | custom-call | flops 12884901888 | bytes 31457280 | tf_op jit(solution)/shard_map/down/pallas_call | solution.py:292
  735.4 13.8 %collective-permute-done.8.refs_4_ = bf16[256,3072]{1,0:T(8,128)(2,1)} collective-permute-done((bf16[256,3072]{1,0:T(8,128)(2,1)}, bf16[256,3072]{1,0:T(8,128)(2,1)}, u32[]{:S(2)}, u32[]{:S(2)}) %collective-permute-start.8) | collective-permute-done | bytes 1572896 | tf_op jit(solution)/shard_map/ppermute | solution.py:321
  751.0 22.0 %down.6 = bf16[512,3072]{1,0:T(8,128)(2,1)} custom-call(bf16[1024,2048]{1,0:T(8,128)(2,1)} %gate_up.4.refs_0_, bf16[1024,2048]{1,0:T(8,128)(2,1)} %gate_up.5.refs_1_, bf16[2048,6144]{1,0:T(8,128)(2,1)} %all-gather.16.cloned.1.call-done.refs_2_, bf16[1024,3072]{1,0:T(8,128)(2,1)} %get-tuple-element.36.refs_3_, ...), custom_call_target="tpu_custom_call" | custom-call | flops 12884901888 | bytes 31457280 | tf_op jit(solution)/shard_map/down/pallas_call | solution.py:292
  775.9 56.2 %collective-permute-done.10.refs_4_ = bf16[256,3072]{1,0:T(8,128)(2,1)S(1)} collective-permute-done((bf16[256,3072]{1,0:T(8,128)(2,1)S(1)}, bf16[256,3072]{1,0:T(8,128)(2,1)S(1)}, u32[]{:S(2)}, u32[]{:S(2)}) %collective-permute-start.10) | collective-permute-done | bytes 1572896 | tf_op jit(solution)/shard_map/ppermute | solution.py:321
  833.2 2.8 collective-permute-done.11.refs_5_
  836.1 22.4 %down.7 = bf16[512,3072]{1,0:T(8,128)(2,1)} custom-call(bf16[1024,2048]{1,0:T(8,128)(2,1)} %gate_up.4.refs_0_, bf16[1024,2048]{1,0:T(8,128)(2,1)} %gate_up.5.refs_1_, bf16[2048,6144]{1,0:T(8,128)(2,1)} %all-gather.16.cloned.1.call-done.refs_2_, bf16[1024,3072]{1,0:T(8,128)(2,1)} %get-tuple-element.36.refs_3_, bf16[256,3072]{1,0:T(8,128)(2,1)} %copy-done.8, ...), custom_call_target="tpu_custom_call" | custom-call | flops 12884901888 | bytes 31457280 | tf_op jit(solution)/shard_map/down/pallas_call | solution.py:292
  858.4 55.4 %all-gather.18.cloned.1.call-done = bf16[2048,3072]{1,0:T(8,128)(2,1)} async-done(((bf16[512,3072]{1,0:T(8,128)(2,1)}), bf16[2048,3072]{1,0:T(8,128)(2,1)}) %all-gather.18.cloned.1.call-update) | async-done | bytes 12582928 | tf_op jit(solution)/shard_map/all_gather | solution.py:380
  913.9 4.1 reshape.74
  920.0 108.2 %all-gather.20.cloned.1.call-done = bf16[2048,3072]{1,0:T(8,128)(2,1)} async-done(((bf16[512,3072]{1,0:T(8,128)(2,1)}), bf16[2048,3072]{1,0:T(8,128)(2,1)}) %all-gather.20.cloned.1.call-update) | async-done | bytes 12582928 | tf_op jit(solution)/shard_map/all_gather | solution.py:380
  1028.2 20.4 %maximum_bitcast_fusion = bf16[1,4096,3072]{2,1,0:T(8,128)(2,1)} fusion(bf16[2048,3072]{1,0:T(8,128)(2,1)} %all-gather.20.cloned.1.call-done, bf16[2048,3072]{1,0:T(8,128)(2,1)} %all-gather.18.cloned.1.call-done), kind=kLoop, calls=%fused_computation | loop fusion | flops 50331648 | bytes 50331648 | tf_op jit(solution)/shard_map/reshape | solution.py:381
  (65 shorter events, 38.1 us)
Async XLA Ops:
  7.2 3.4 copy-start.2
  7.2 52.3 %all-gather.8.cloned.1.call-start = ((), (), s32[]{:S(2)}) async-start(), calls=%async_computation | async-start | bytes 8847360 | tf_op jit(solution)/shard_map/all_gather | solution.py:331
  9.7 289.6 %all-gather.10.cloned.1.call-start = ((), (), s32[]{:S(2)}) async-start(), calls=%async_computation.1 | async-start | bytes 19464192 | tf_op jit(solution)/shard_map/all_gather | solution.py:332
  10.5 334.8 %all-gather.12.cloned.1.call-start = ((), (), s32[]{:S(2)}) async-start(), calls=%async_computation.2 | async-start | bytes 26738688 | tf_op jit(solution)/shard_map/all_gather | solution.py:338
  13.7 505.4 %all-gather.14.cloned.1.call-start = ((), (), s32[]{:S(2)}) async-start(), calls=%async_computation.3 | async-start | bytes 26738688 | tf_op jit(solution)/shard_map/all_gather | solution.py:338
  15.0 1.5 copy-start.4
  15.0 2.1 copy-start.3
  15.1 677.2 %all-gather.16.cloned.1.call-start = ((), (), s32[]{:S(2)}) async-start(), calls=%async_computation.4 | async-start | bytes 26738688 | tf_op jit(solution)/shard_map/all_gather | solution.py:339
  15.8 898.1 %all-gather.18.cloned.1.call-start = ((), (), s32[]{:S(2)}) async-start(), calls=%async_computation.5 | async-start | bytes 15728640 | tf_op jit(solution)/shard_map/all_gather | solution.py:380
  246.0 23.9 %copy-start.5 = (bf16[3072]{0:T(1024)(128)(2,1)S(1)}, bf16[3072]{0:T(1024)(128)(2,1)}, u32[]{:S(2)}) copy-start(bf16[3072]{0:T(1024)(128)(2,1)} %param.23) | copy-start | bytes 18436
  246.0 25.1 %copy-start = (bf16[512,768]{1,0:T(8,128)(2,1)S(1)}, bf16[512,768]{1,0:T(8,128)(2,1)}, u32[]{:S(2)}) copy-start(bf16[512,768]{1,0:T(8,128)(2,1)} %get-tuple-element.46) | copy-start | bytes 2359300
  249.3 20.3 %collective-permute-start.1 = (bf16[512,768]{1,0:T(8,128)(2,1)S(1)}, bf16[512,768]{1,0:T(8,128)(2,1)}, u32[]{:S(2)}, u32[]{:S(2)}) collective-permute-start(bf16[512,768]{1,0:T(8,128)(2,1)S(1)} %get-tuple-element.49), channel_id=1, source_target_pairs={{0,8},{8,16},{16,24},{24,0},{1,9},{9,17},{17,25},{25,1},{2,10},{10... | collective-permute-start | bytes 2359304 | tf_op jit(solution)/shard_map/ppermute | solution.py:321
  250.4 27.6 %collective-permute-start = (bf16[512,768]{1,0:T(8,128)(2,1)}, bf16[512,768]{1,0:T(8,128)(2,1)}, u32[]{:S(2)}, u32[]{:S(2)}) collective-permute-start(bf16[512,768]{1,0:T(8,128)(2,1)} %get-tuple-element.45), channel_id=1, source_target_pairs={{0,8},{8,16},{16,24},{24,0},{1,9},{9,17},{17,25},{25,1},{2,10},{10... | collective-permute-start | bytes 2359304 | tf_op jit(solution)/shard_map/ppermute | solution.py:321
  251.7 34.4 %collective-permute-start.3 = (bf16[512,768]{1,0:T(8,128)(2,1)}, bf16[512,768]{1,0:T(8,128)(2,1)S(1)}, u32[]{:S(2)}, u32[]{:S(2)}) collective-permute-start(bf16[512,768]{1,0:T(8,128)(2,1)} %get-tuple-element.48), channel_id=1, source_target_pairs={{0,16},{8,24},{16,0},{24,8},{1,17},{9,25},{17,1},{25,9},{2,18},{10... | collective-permute-start | bytes 2359304 | tf_op jit(solution)/shard_map/ppermute | solution.py:321
  253.2 41.4 %collective-permute-start.2 = (bf16[512,768]{1,0:T(8,128)(2,1)}, bf16[512,768]{1,0:T(8,128)(2,1)}, u32[]{:S(2)}, u32[]{:S(2)}) collective-permute-start(bf16[512,768]{1,0:T(8,128)(2,1)} %get-tuple-element.44), channel_id=1, source_target_pairs={{0,16},{8,24},{16,0},{24,8},{1,17},{9,25},{17,1},{25,9},{2,18},{10... | collective-permute-start | bytes 2359304 | tf_op jit(solution)/shard_map/ppermute | solution.py:321
  254.7 42.3 %collective-permute-start.5 = (bf16[512,768]{1,0:T(8,128)(2,1)}, bf16[512,768]{1,0:T(8,128)(2,1)S(1)}, u32[]{:S(2)}, u32[]{:S(2)}) collective-permute-start(bf16[512,768]{1,0:T(8,128)(2,1)} %get-tuple-element.47), channel_id=1, source_target_pairs={{0,24},{8,0},{16,8},{24,16},{1,25},{9,1},{17,9},{25,17},{2,26},{10... | collective-permute-start | bytes 2359304 | tf_op jit(solution)/shard_map/ppermute | solution.py:321
  269.6 27.4 %collective-permute-start.4 = (bf16[512,768]{1,0:T(8,128)(2,1)}, bf16[512,768]{1,0:T(8,128)(2,1)}, u32[]{:S(2)}, u32[]{:S(2)}) collective-permute-start(bf16[512,768]{1,0:T(8,128)(2,1)} %get-tuple-element.43), channel_id=1, source_target_pairs={{0,24},{8,0},{16,8},{24,16},{1,25},{9,1},{17,9},{25,17},{2,26},{10... | collective-permute-start | bytes 2359304 | tf_op jit(solution)/shard_map/ppermute | solution.py:321
  342.7 210.9 %collective-permute-start.6 = (bf16[2,256,3072]{2,1,0:T(8,128)(2,1)}, bf16[2,256,3072]{2,1,0:T(8,128)(2,1)}, u32[]{:S(2)}, u32[]{:S(2)}) collective-permute-start(bf16[2,256,3072]{2,1,0:T(8,128)(2,1)} %get-tuple-element.42), channel_id=1, source_target_pairs={{0,8},{8,16},{16,24},{24,0},{1,9},{9,17},{17,25},{25,1},{2,10},{10... | collective-permute-start | bytes 9437192 | tf_op jit(solution)/shard_map/ppermute | solution.py:321
  342.7 210.9 %collective-permute-start.7 = (bf16[2,256,3072]{2,1,0:T(8,128)(2,1)}, bf16[2,256,3072]{2,1,0:T(8,128)(2,1)}, u32[]{:S(2)}, u32[]{:S(2)}) collective-permute-start(bf16[2,256,3072]{2,1,0:T(8,128)(2,1)} %get-tuple-element.41), channel_id=1, source_target_pairs={{0,24},{8,0},{16,8},{24,16},{1,25},{9,1},{17,9},{25,17},{2,26},{10... | collective-permute-start | bytes 9437192 | tf_op jit(solution)/shard_map/ppermute | solution.py:321
  713.2 36.0 %collective-permute-start.8 = (bf16[256,3072]{1,0:T(8,128)(2,1)}, bf16[256,3072]{1,0:T(8,128)(2,1)}, u32[]{:S(2)}, u32[]{:S(2)}) collective-permute-start(bf16[256,3072]{1,0:T(8,128)(2,1)} %get-tuple-element.32), channel_id=1, source_target_pairs={{0,24},{8,0},{16,8},{24,16},{1,25},{9,1},{17,9},{25,17},{2,26},{10... | collective-permute-start | bytes 4718600 | tf_op jit(solution)/shard_map/ppermute | solution.py:321
  714.0 36.9 %collective-permute-start.9 = (bf16[256,3072]{1,0:T(8,128)(2,1)}, bf16[256,3072]{1,0:T(8,128)(2,1)}, u32[]{:S(2)}, u32[]{:S(2)}) collective-permute-start(bf16[256,3072]{1,0:T(8,128)(2,1)} %get-tuple-element.37), channel_id=1, source_target_pairs={{0,8},{8,16},{16,24},{24,0},{1,9},{9,17},{17,25},{25,1},{2,10},{10... | collective-permute-start | bytes 4718600 | tf_op jit(solution)/shard_map/ppermute | solution.py:321
  773.0 1.4 copy-start.7
  773.0 1.9 copy-start.6
  773.1 255.2 %all-gather.20.cloned.1.call-start = ((), (), s32[]{:S(2)}) async-start(), calls=%async_computation.6 | async-start | bytes 15728640 | tf_op jit(solution)/shard_map/all_gather | solution.py:380
  774.4 57.7 %collective-permute-start.10 = (bf16[256,3072]{1,0:T(8,128)(2,1)S(1)}, bf16[256,3072]{1,0:T(8,128)(2,1)S(1)}, u32[]{:S(2)}, u32[]{:S(2)}) collective-permute-start(bf16[256,3072]{1,0:T(8,128)(2,1)S(1)} %copy-done.7), channel_id=1, source_target_pairs={{0,24},{8,0},{16,8},{24,16},{1,25},{9,1},{17,9},{25,17},{2,26},{10... | collective-permute-start | bytes 4718600 | tf_op jit(solution)/shard_map/ppermute | solution.py:321
  774.9 61.2 %collective-permute-start.11 = (bf16[256,3072]{1,0:T(8,128)(2,1)S(1)}, bf16[256,3072]{1,0:T(8,128)(2,1)}, u32[]{:S(2)}, u32[]{:S(2)}) collective-permute-start(bf16[256,3072]{1,0:T(8,128)(2,1)S(1)} %copy-done.6), channel_id=1, source_target_pairs={{0,8},{8,16},{16,24},{24,0},{1,9},{9,17},{17,25},{25,1},{2,10},{10... | collective-permute-start | bytes 4718600 | tf_op jit(solution)/shard_map/ppermute | solution.py:321
  832.1 1.1 copy-start.8
  913.9 4.1 copy-start.1
Sparse Core Ops, SparseCore 0:
  10.2 49.2 all-gather.7
  61.5 80.3 all-gather.9
  144.1 179.0 all-gather.11
  325.3 193.7 all-gather.13
  521.1 171.1 all-gather.15
  773.2 140.5 all-gather.17
  915.4 112.8 all-gather.19

commit v3 on v2

--- a/solution.py
+++ b/solution.py
@@ -38,76 +38,120 @@
     return (vals_f32 * inv * gain).astype(jnp.bfloat16)
 
 
-def qkv_kernel(n_q, n_kv, x_ref, g_ref, w_ref, cos_ref, sin_ref, q_ref, k_ref, v_ref):
-    h = norm_rows(x_ref[...].astype(jnp.float32), g_ref[...].astype(jnp.float32))
+def norm_kernel(x_ref, g_ref, h_ref):
+    h_ref[...] = norm_rows(x_ref[...].astype(jnp.float32), g_ref[...].astype(jnp.float32))
+
+
+def norm_call(x, gain):
+    s, d = x.shape
+    bm = min(256, s)
+    return pl.pallas_call(
+        norm_kernel,
+        grid=(s // bm,),
+        in_specs=[pl.BlockSpec((bm, d), lambda i: (i, 0)), pl.BlockSpec((1, d), lambda i: (0, 0))],
+        out_specs=pl.BlockSpec((bm, d), lambda i: (i, 0)),
+        out_shape=jax.ShapeDtypeStruct((s, d), jnp.bfloat16),
+        compiler_params=params(),
+        cost_estimate=cost(8 * s * d, 4 * s * d),
+        name="norm",
+    )(x, gain)
+
+
+def qkv_kernel(n_q, n_kv, h_ref, w_ref, cos_ref, sin_ref, q_ref, k_ref, v_ref, vt_ref):
+    h = h_ref[...]
     cos_t, sin_t = cos_ref[...], sin_ref[...]
-    for g in range(n_kv):
-        per = n_q // n_kv
-        for kind in range(2):
-            if kind == 0:
-                lo, cnt = g * per, per
+    n_heads = n_q + 2 * n_kv
+    for lo in range(0, n_heads, 2):
+        y = jnp.dot(h, w_ref[:, lo * HEAD_DIM:(lo + 2) * HEAD_DIM], preferred_element_type=jnp.float32)
+        for i in range(lo, lo + 2):
+            a = y[:, (i - lo) * HEAD_DIM:(i - lo + 1) * HEAD_DIM]
+            if i >= n_q + n_kv:
+                cols = slice((i - n_q - n_kv) * HEAD_DIM, (i - n_q - n_kv + 1) * HEAD_DIM)
+                v_ref[:, cols] = a.astype(jnp.bfloat16)
+                vt_ref[cols, :] = a.T.astype(jnp.bfloat16)
+                continue
+            r = (a * cos_t + pltpu.roll(a, HEAD_DIM // 2, 1) * sin_t).astype(jnp.bfloat16)
+            if i < n_q:
+                q_ref[i] = r
             else:
-                lo, cnt = n_q + g, 1
-            y = jnp.dot(h, w_ref[:, lo * HEAD_DIM:(lo + cnt) * HEAD_DIM], preferred_element_type=jnp.float32)
-            for i in range(cnt):
-                a = y[:, i * HEAD_DIM:(i + 1) * HEAD_DIM]
-                r = (a * cos_t + pltpu.roll(a, HEAD_DIM // 2, 1) * sin_t).astype(jnp.bfloat16)
-                if kind == 0:
-                    q_ref[lo + i] = r
-                else:
-                    k_ref[:, g * HEAD_DIM:(g + 1) * HEAD_DIM] = r
-    base = (n_q + n_kv) * HEAD_DIM
-    v_ref[...] = jnp.dot(h, w_ref[:, base:base + n_kv * HEAD_DIM], preferred_element_type=jnp.float32).astype(jnp.bfloat16)
-
-
-def qkv_call(x, gain, w, cos_t, sin_t, n_q, n_kv):
-    s, d = x.shape
+                k_ref[:, (i - n_q) * HEAD_DIM:(i - n_q + 1) * HEAD_DIM] = r
+
+
+def qkv_call(h, w, cos_t, sin_t, n_q, n_kv):
+    s, d = h.shape
     bm = min(512, s)
     n = w.shape[1]
     row = lambda i: (i, 0)
     return pl.pallas_call(
         functools.partial(qkv_kernel, n_q, n_kv),
         grid=(s // bm,),
-        in_specs=[pl.BlockSpec((bm, d), row), pl.BlockSpec((1, d), lambda i: (0, 0)), pl.BlockSpec((d, n), lambda i: (0, 0)),
+        in_specs=[pl.BlockSpec((bm, d), row), pl.BlockSpec((d, n), lambda i: (0, 0), pipeline_mode=pl.Buffered(1)),
                   pl.BlockSpec((bm, HEAD_DIM), row), pl.BlockSpec((bm, HEAD_DIM), row)],
         out_specs=[pl.BlockSpec((n_q, bm, HEAD_DIM), lambda i: (0, i, 0)),
-                   pl.BlockSpec((bm, n_kv * HEAD_DIM), row), pl.BlockSpec((bm, n_kv * HEAD_DIM), row)],
+                   pl.BlockSpec((bm, n_kv * HEAD_DIM), row), pl.BlockSpec((bm, n_kv * HEAD_DIM), row),
+                   pl.BlockSpec((n_kv * HEAD_DIM, bm), lambda i: (0, i))],
         out_shape=[jax.ShapeDtypeStruct((n_q, s, HEAD_DIM), jnp.bfloat16),
                    jax.ShapeDtypeStruct((s, n_kv * HEAD_DIM), jnp.bfloat16),
-                   jax.ShapeDtypeStruct((s, n_kv * HEAD_DIM), jnp.bfloat16)],
+                   jax.ShapeDtypeStruct((s, n_kv * HEAD_DIM), jnp.bfloat16),
+                   jax.ShapeDtypeStruct((n_kv * HEAD_DIM, s), jnp.bfloat16)],
         compiler_params=params(),
         cost_estimate=cost(2 * s * d * n, 2 * s * d + 2 * d * n + 2 * s * n),
         name="qkv",
-    )(x, gain, w, cos_t, sin_t)
-
-
-def att_kernel(bq, bk, per, first, len_ref, q_ref, k_ref, v_ref, o_ref, m_ref, l_ref, acc_ref):
+    )(h, w, cos_t, sin_t)
+
+
+def att_kernel(bq, bk, per, first, len_ref, q_ref, k_ref, vt_ref, o_ref, s_ref, p_ref, m_ref, l_ref, alpha_ref, acc_ref):
     row0 = first + pl.program_id(1) * bq
     valid = len_ref[0]
+    last = k_ref.shape[0] // bk - 1
     m_ref[...] = jnp.full_like(m_ref, -jnp.inf)
     l_ref[...] = jnp.zeros_like(l_ref)
+    alpha_ref[...] = jnp.zeros_like(alpha_ref)
     acc_ref[...] = jnp.zeros_like(acc_ref)
-    reps = bk // HEAD_DIM
+    p_ref[...] = jnp.zeros_like(p_ref)
+
+    def scores(j, h):
+        k_blk = k_ref[pl.ds(pl.multiple_of(j * bk, bk), bk), :]
+        s_ref[h] = lax.dot_general(k_blk, q_ref[h], (((1,), (1,)), ((), ())), preferred_element_type=jnp.float32)
+
+    def values(j, h):
+        vt_blk = vt_ref[:, pl.ds(pl.multiple_of(j * bk, bk), bk)]
+        acc_ref[h] = acc_ref[h] * alpha_ref[h] + jnp.dot(vt_blk, p_ref[h], preferred_element_type=jnp.float32)
+
+    tall = min(32, bk)
+
+    def softmax(j, h, masked):
+        m_old = m_ref[h]
+        m8 = None
+        for c in range(bk // tall):
+            r = slice(c * tall, (c + 1) * tall)
+            sc = s_ref[h, r, :]
+            if masked:
+                kid = j * bk + c * tall + lax.broadcasted_iota(jnp.int32, (tall, bq), 0)
+                qid = row0 + lax.broadcasted_iota(jnp.int32, (tall, bq), 1)
+                sc = jnp.where((kid <= qid) & (kid < valid), sc, -jnp.inf)
+                s_ref[h, r, :] = sc
+            top = jnp.max(sc.reshape(tall // 8, 8, bq), axis=0)
+            m8 = top if m8 is None else jnp.maximum(m8, top)
+        m_new = jnp.maximum(m_old, jnp.max(m8, axis=0, keepdims=True))
+        m_rows = jnp.broadcast_to(m_new, (8, bq))[None]
+        l8 = None
+        for c in range(bk // tall):
+            r = slice(c * tall, (c + 1) * tall)
+            p = jnp.exp2((s_ref[h, r, :].reshape(tall // 8, 8, bq) - m_rows) * EXP2_SCALE)
+            tot = jnp.sum(p, axis=0)
+            l8 = tot if l8 is None else l8 + tot
+            p_ref[h, r, :] = p.reshape(tall, bq).astype(jnp.bfloat16)
+        alpha = jnp.exp2((m_old - m_new) * EXP2_SCALE)
+        l_ref[h] = l_ref[h] * alpha + jnp.sum(l8, axis=0, keepdims=True)
+        alpha_ref[h] = alpha
+        m_ref[h] = m_new
 
     def step(j, masked):
-        k0 = pl.multiple_of(j * bk, bk)
-        k_blk = k_ref[pl.ds(k0, bk), :]
-        v_blk = v_ref[pl.ds(k0, bk), :]
-        if masked:
-            kid = k0 + lax.broadcasted_iota(jnp.int32, (bq, bk), 1)
-            qid = row0 + lax.broadcasted_iota(jnp.int32, (bq, bk), 0)
-            allowed = (kid <= qid) & (kid < valid)
         for h in range(per):
-            sc = lax.dot_general(q_ref[h], k_blk, (((1,), (1,)), ((), ())), preferred_element_type=jnp.float32)
-            if masked:
-                sc = jnp.where(allowed, sc, -jnp.inf)
-            m_old = m_ref[h]
-            m_new = jnp.maximum(m_old, jnp.max(sc, axis=1, keepdims=True))
-            p = jnp.exp2((sc - jnp.tile(m_new, (1, reps))) * EXP2_SCALE)
-            alpha = jnp.exp2((m_old - m_new) * EXP2_SCALE)
-            l_ref[h] = l_ref[h] * alpha + jnp.sum(p, axis=1, keepdims=True)
-            acc_ref[h] = acc_ref[h] * alpha + jnp.dot(p.astype(jnp.bfloat16), v_blk, preferred_element_type=jnp.float32)
-            m_ref[h] = m_new
+            values(jnp.maximum(j - 1, 0), h)
+            softmax(j, h, masked)
+            scores(jnp.minimum(j + 1, last), h)
 
     n_full = jnp.minimum((row0 + 1) // bk, valid // bk)
     n_end = jnp.minimum((row0 + bq + bk - 1) // bk, (valid + bk - 1) // bk)
@@ -120,39 +164,40 @@
         step(j, True)
         return 0
 
+    for h in range(per):
+        scores(0, h)
     lax.fori_loop(0, n_full, full, 0)
     lax.fori_loop(n_full, n_end, part, 0)
     for h in range(per):
-        o_ref[:, h * HEAD_DIM:(h + 1) * HEAD_DIM] = (acc_ref[h] / l_ref[h]).astype(jnp.bfloat16)
-
-
-def att_call(q, k, v, valid_len, call):
+        values(n_end - 1, h)
+        o_ref[:, h * HEAD_DIM:(h + 1) * HEAD_DIM] = (acc_ref[h] / l_ref[h]).T.astype(jnp.bfloat16)
+
+
+def att_call(q, k, vt, valid_len, call):
     n_q, s, _ = q.shape
     n_kv = k.shape[1] // HEAD_DIM
     per = n_q // n_kv
     rows = s // N_CALLS
-    bq = min(256, rows)
+    bq = min(512, rows)
     bk = min(512, s)
     first = call * rows
     off = first // bq
     frac = (2 * call + 1) / N_CALLS ** 2
-    kernel = functools.partial(att_kernel, bq, bk, per, first)
-    args = [valid_len, q, k, v]
-    in_specs = [pl.BlockSpec(memory_space=pltpu.SMEM),
-                pl.BlockSpec((per, bq, HEAD_DIM), lambda g, i: (g, off + i, 0)),
-                pl.BlockSpec((s, HEAD_DIM), lambda g, i: (0, g)),
-                pl.BlockSpec((s, HEAD_DIM), lambda g, i: (0, g))]
-    return pl.pallas_call(
-        kernel,
+    return pl.pallas_call(
+        functools.partial(att_kernel, bq, bk, per, first),
         grid=(n_kv, rows // bq),
-        in_specs=in_specs,
+        in_specs=[pl.BlockSpec(memory_space=pltpu.SMEM),
+                  pl.BlockSpec((per, bq, HEAD_DIM), lambda g, i: (g, off + i, 0)),
+                  pl.BlockSpec((s, HEAD_DIM), lambda g, i: (0, g)),
+                  pl.BlockSpec((HEAD_DIM, s), lambda g, i: (g, 0))],
         out_specs=pl.BlockSpec((bq, per * HEAD_DIM), lambda g, i: (i, g)),
         out_shape=jax.ShapeDtypeStruct((rows, n_q * HEAD_DIM), jnp.bfloat16),
-        scratch_shapes=[pltpu.VMEM((per, bq, HEAD_DIM), jnp.float32)] * 3,
+        scratch_shapes=[pltpu.VMEM((per, bk, bq), jnp.float32), pltpu.VMEM((per, bk, bq), jnp.bfloat16)]
+        + [pltpu.VMEM((per, 1, bq), jnp.float32)] * 3 + [pltpu.VMEM((per, HEAD_DIM, bq), jnp.float32)],
         compiler_params=params(),
         cost_estimate=cost(int(8 * frac * n_q * s * s * HEAD_DIM), 4 * n_q * s * HEAD_DIM),
         name="attention",
-    )(*args)
+    )(valid_len, q, k, vt)
 
 
 def out_kernel(n_src, bn, idx_ref, *refs):
@@ -206,15 +251,14 @@
     def _(m):
         r = pl.ds(pl.multiple_of(m * bm, bm), bm)
         u = u_ref[r, :]
-        gate = jnp.dot(u, g_ref[0], preferred_element_type=jnp.float32)
-        up = jnp.dot(u, up_ref[0], preferred_element_type=jnp.float32)
+        gate = jnp.dot(u, g_ref[...], preferred_element_type=jnp.float32)
+        up = jnp.dot(u, up_ref[...], preferred_element_type=jnp.float32)
         a_ref[r, :] = (jax.nn.silu(gate) * up).astype(jnp.bfloat16)
 
 
-def gu_call(u, w):
+def gu_call(u, w, n_src):
     rows, d = u.shape
-    n_src, _, two = w.shape
-    half = two // 2
+    half = w.shape[1] // (2 * n_src)
     bn = min(512, half)
     nb = half // bn
     bm = min(256, rows)
@@ -222,12 +266,12 @@
         functools.partial(gu_kernel, bm),
         grid=(n_src, nb),
         in_specs=[pl.BlockSpec((rows, d), lambda j, n: (0, 0), pipeline_mode=pl.Buffered(1)),
-                  pl.BlockSpec((1, d, bn), lambda j, n: (j, 0, n)),
-                  pl.BlockSpec((1, d, bn), lambda j, n: (j, 0, nb + n))],
+                  pl.BlockSpec((d, bn), lambda j, n: (0, 2 * j * nb + n)),
+                  pl.BlockSpec((d, bn), lambda j, n: (0, (2 * j + 1) * nb + n))],
         out_specs=pl.BlockSpec((rows, bn), lambda j, n: (0, j * nb + n)),
         out_shape=jax.ShapeDtypeStruct((rows, n_src * half), jnp.bfloat16),
         compiler_params=params(),
-        cost_estimate=cost(2 * rows * d * n_src * two, 2 * w.size + 2 * rows * d + 2 * rows * n_src * half),
+        cost_estimate=cost(4 * rows * d * n_src * half, 2 * w.size + 2 * rows * d + 2 * rows * n_src * half),
         name="gate_up",
     )(u, w, w)
 
@@ -268,18 +312,17 @@
                 rest[h][...] = acc_ref[h * half:(h + 1) * half, :].astype(jnp.bfloat16)
 
 
-def down_call(a_parts, w, rows, chunk, resid=None, partials=()):
-    kj = w.shape[0]
+def down_call(a_parts, w, n_src, rows, chunk, resid=None, partials=()):
+    d = w.shape[1]
     parts = len(a_parts)
+    kj = w.shape[0] // n_src
     kp = kj // parts
-    n_src = a_parts[0].shape[1] // kp
-    d = w.shape[1] // n_src
     own = resid is not None
     bn = min(1024, d)
     nb = d // bn
     bm = min(256, rows)
     args = [*a_parts, w]
-    in_specs = [pl.BlockSpec((rows, kp), lambda n, j: (chunk, j))] * parts + [pl.BlockSpec((kj, bn), lambda n, j: (0, j * nb + n))]
+    in_specs = [pl.BlockSpec((rows, kp), lambda n, j: (chunk, j))] * parts + [pl.BlockSpec((kj, bn), lambda n, j: (j, n))]
     col = lambda n, j: (0, n)
     if own:
         args += [resid, *partials]
@@ -331,51 +374,63 @@
         w_qkv = lax.all_gather(jnp.concatenate([w_query, w_key, w_value], axis=1), 'fsdp', axis=0, tiled=True)
         full_o = lax.all_gather(w_out, ('ta', 'tb', 'fsdp'), axis=1, tiled=True)
         fl = w_gate.shape[1]
-        gu_parts = []
+        n_src = 2
+        swaps = []
         for p in range(2):
             cut = slice(p * fl // 2, (p + 1) * fl // 2)
             local = jnp.concatenate([w_gate[:, cut], w_up[:, cut]], axis=1)
-            gu_parts.append(lax.all_gather(local, ('ta', 'fsdp'), axis=0, tiled=True).reshape(n_tp // 2, d, fl))
-        full_d = lax.all_gather(w_down, ('ta', 'fsdp'), axis=1, tiled=True)
+            swaps.append((local, shift(local, 2)))
+        swaps.append((w_down, shift(w_down, 2)))
+
+        def joined(p, axis, *deps):
+            return jnp.concatenate([after(swaps[p][0], *deps), swaps[p][1]], axis=axis)
 
         angles = positions.reshape(seq, 1).astype(jnp.float32) * rope_freqs()[None, :]
         cos_h, sin_h = jnp.cos(angles), jnp.sin(angles)
         cos_t = jnp.concatenate([cos_h, cos_h], axis=1)
         sin_t = jnp.concatenate([-sin_h, sin_h], axis=1)
-        q, k, v = qkv_call(x, norm_attn.reshape(1, d), w_qkv, cos_t, sin_t, n_q, n_kv)
+        h = norm_call(x, norm_attn.reshape(1, d))
+        q, k, v, vt = qkv_call(h, w_qkv, cos_t, sin_t, n_q, n_kv)
 
         pieces = [[] for _ in range(n_tp)]
+        gu_parts = []
+        o = q
         for call in range(N_CALLS):
-            o = att_call(after(q, *[p[0] for p in pieces[:call]]), k, v, valid_len, call)
+            gu_parts.append(joined(call, 1, o))
+            o = att_call(after(q, gu_parts[call], o), k, vt, valid_len, call)
             for s in range(n_tp):
                 blk = lax.dynamic_slice_in_dim(o, (me + s) % n_tp * sub, sub, axis=0)
                 if s:
                     blk = shift(blk, s)
                 pieces[s].append(blk)
+        d_part = joined(2, 0, o)
+        gu_full = [lax.all_gather(w, 'fsdp', axis=0, tiled=True) for w in gu_parts]
+        full_d = lax.all_gather(d_part, 'fsdp', axis=1, tiled=True)
         o_pieces = [jnp.concatenate(p, axis=0) for p in pieces]
+        o_pieces[0] = after(o_pieces[0], d_part)
         idx = jnp.stack([me] + [(me - s) % n_tp for s in range(n_tp)]).astype(jnp.int32)
         resid, u = out_call(idx, o_pieces, full_o, x, norm_mlp.reshape(1, d), sub, n_tp)
 
         u4 = u.reshape(N_CALLS, 2, sub // 2, d)
         u_prev = shift(u4[:, 0], 1)
         u_next = shift(u4[:, 1], -1)
-        a_own = [gu_call(u, gu_parts[0])]
-        a_own.append(gu_call(after(u, a_own[0]), gu_parts[1]))
+        a_own = [gu_call(u, gu_full[0], n_src)]
+        a_own.append(gu_call(after(u, a_own[0]), gu_full[1], n_src))
         u_prev, u_next = lax.optimization_barrier((u_prev, u_next, a_own[1]))[:2]
         u_recv = jnp.stack([u_prev, u_next], axis=1).reshape(u.shape)
-        a_recv = [gu_call(u_recv, gu_parts[0])]
-        a_recv.append(gu_call(after(u_recv, a_recv[0]), gu_parts[1]))
+        a_recv = [gu_call(u_recv, gu_full[0], n_src)]
+        a_recv.append(gu_call(after(u_recv, a_recv[0]), gu_full[1], n_src))
         partials = []
         order = a_recv[1]
         for c in range(N_CALLS):
-            p_prev, p_next = down_call([after(a_recv[0], order), a_recv[1]], full_d, sub, c)
+            p_prev, p_next = down_call([after(a_recv[0], order), a_recv[1]], full_d, n_src, sub, c)
             order = p_prev
             b_next = shift(p_prev, -1)
             b_prev = shift(p_next, 1)
             partials.append((b_next, b_prev))
         outs = []
         for c in range(N_CALLS):
-            mine = down_call([after(a_own[0], order), a_own[1]], full_d, sub, c, resid, partials[c])
+            mine = down_call([after(a_own[0], order), a_own[1]], full_d, n_src, sub, c, resid, partials[c])
             order = mine
             outs.append(lax.all_gather(after(mine, *outs), tp, axis=0, tiled=True))
         hidden = jnp.concatenate(outs, axis=0).reshape(1, seq, d)

time: 1060 us -> 900 us (0.85)
  waiting for transfers between devices: 507 us -> 351 us
  Pallas kernels: 444 us -> 418 us
  local copies, waits for them, and re-layouts: 25.2 us -> 37.2 us
  starting transfers between devices: 13 us -> 23.8 us
    all_gather x3, waiting for transfers between devices: 202 us -> 38.9 us  [the longest x2 29.5 us: local_layer(): gu_full = [lax.all_gather(w, 'fsdp', axis=0, tiled=True) for w in gu_parts]]
    ppermute x12 -> x15, waiting for transfers between devices: 108 us -> 144 us  [shift(): return lax.ppermute(val, tp, [(i, (i + s) % n_tp) for i in range(n_tp)])]
    all_gather x1, waiting for transfers between devices: 31.6 us -> 0.7 us  [local_layer(): lax.all_gather(jnp.concatenate([w_query, w_key, w_value], axis=1), 'fsdp'...]
    pallas_call x1, Pallas kernels: 58.2 us -> 41.2 us  [qkv_call(): pl.pallas_call(functools.partial(qkv_kernel, n_q, n_kv), grid=(s // bm,),...]
    pallas_call x2 -> x3, Pallas kernels: 125 us -> 111 us  [the longest x2 83.9 us: att_call(): pl.pallas_call(functools.partial(att_kernel, bq, bk, per, first), grid=(n...]
    ppermute x12 -> x15, starting transfers between devices: 12.5 us -> 23.1 us  [shift(): return lax.ppermute(val, tp, [(i, (i + s) % n_tp) for i in range(n_tp)])]
  transfers between devices with their start and end apart: 19 -> 22, of which waited for: 13 -> 14; matrix products, arithmetic and copies ran while one was open for 5% -> 7% of each run, Pallas kernels for 38% -> 42%
where the time goes in v3:
time: 900 us; the launch traced here: 899 us
  Pallas kernels  418 us (46%)
  waiting for transfers between devices  351 us (39%)
  other arithmetic  53.7 us (6%)
  local copies, waits for them, and re-layouts  37.2 us (4%)
  starting transfers between devices  23.8 us (3%)
  between operations  15 us (2%)
    all_gather x2, waiting for transfers between devices, local_layer(): outs.append(lax.all_gather(after(mine, *outs), tp, axis=0, tiled=True))  167 us
    ppermute x15, waiting for transfers between devices, shift(): return lax.ppermute(val, tp, [(i, (i + s) % n_tp) for i in range(n_tp)])  144 us
    pallas_call x4, Pallas kernels, gu_call(): pl.pallas_call(functools.partial(gu_kernel, bm), grid=(n_src, nb), in_spe...  139 us
    pallas_call x4, Pallas kernels, down_call(): pl.pallas_call(functools.partial(down_kernel, bm, parts, own), grid=(nb,...  85.8 us
    pallas_call x2, Pallas kernels, att_call(): pl.pallas_call(functools.partial(att_kernel, bq, bk, per, first), grid=(n...  83.9 us
    pallas_call x1, Pallas kernels, qkv_call(): pl.pallas_call(functools.partial(qkv_kernel, n_q, n_kv), grid=(s // bm,),...  41.2 us
    pallas_call x1, Pallas kernels, out_call(): pl.pallas_call(functools.partial(out_kernel, n_src, bn), grid_spec=pltpu....  40.8 us
    all_gather x2, waiting for transfers between devices, local_layer(): gu_full = [lax.all_gather(w, 'fsdp', axis=0, tiled=True) for w in gu_parts]  29.5 us
  transfers between devices with their start and end apart: 22, of which 14 were waited for; matrix products, arithmetic and copies ran while one was open for 7% of the time, Pallas kernels for 42%

profile of v3, /device:TPU:97, one launch (start us, length us, event | category | flops | bytes accessed | tf_op | source)
XLA Modules:
  0.0 899.0 jit_solution(8212142249764757656)
XLA Ops:
  13.6 4.8 collective-permute-start
  19.6 27.5 %norm.1.h_ref = bf16[4096,3072]{1,0:T(8,128)(2,1)} custom-call(bf16[4096,3072]{1,0:T(8,128)(2,1)} %bitcast.21, bf16[1,3072]{1,0:T(2,128)(2,1)} %reshape.61.g_ref), custom_call_target="tpu_custom_call" | custom-call | flops 100663296 | bytes 50331648 | tf_op jit(solution)/shard_map/norm/pallas_call | solution.py:48
  47.2 8.2 fusion
  59.2 41.2 %qkv.1 = (bf16[6,4096,128]{2,1,0:T(8,128)(2,1)}, bf16[4096,256]{1,0:T(8,128)(2,1)}, bf16[4096,256]{1,0:T(8,128)(2,1)}, bf16[256,4096]{1,0:T(8,128)(2,1)}) custom-call(bf16[4096,3072]{1,0:T(8,128)(2,1)} %norm.1.h_ref, bf16[3072,1280]{1,0:T(8,128)(2,1)} %all-gather.8.cloned.1.call-done.w_ref, f32[4096,128]{1,0:T(8,128)} %get-tuple-element.70.cos_ref, ...), custom_call_target="tpu_custom_call" | custom-call | flops 32212254720 | bytes 43515904 | tf_op jit(solution)/shard_map/qkv/pallas_call | solution.py:85
  111.5 35.5 %attention.2 = bf16[2048,768]{1,0:T(8,128)(2,1)} custom-call(s32[1]{0:T(128)S(6)} %copy.22.len_ref, bf16[6,4096,128]{2,1,0:T(8,128)(2,1)} %get-tuple-element.34.q_ref, bf16[4096,256]{1,0:T(8,128)(2,1)} %get-tuple-element.31.k_ref, bf16[256,4096]{1,0:T(8,128)(2,1)} %get-tuple-element.32.vt_ref), custom_call_target="tpu_custom_call" | custom-call | flops 25769803776 | bytes 12582912 | tf_op jit(solution)/shard_map/attention/pallas_call | solution.py:186
  148.5 20.2 %collective-permute-done.1 = bf16[384,2048]{1,0:T(8,128)(2,1)} collective-permute-done((bf16[384,2048]{1,0:T(8,128)(2,1)}, bf16[384,2048]{1,0:T(8,128)(2,1)}, u32[]{:S(2)}, u32[]{:S(2)}) %collective-permute-start.1) | collective-permute-done | bytes 1572896 | tf_op jit(solution)/shard_map/ppermute | solution.py:364
  174.6 48.4 %attention.3 = bf16[2048,768]{1,0:T(8,128)(2,1)} custom-call(s32[1]{0:T(128)S(6)} %copy.22.len_ref, bf16[6,4096,128]{2,1,0:T(8,128)(2,1)} %get-tuple-element.34.q_ref, bf16[4096,256]{1,0:T(8,128)(2,1)} %get-tuple-element.31.k_ref, bf16[256,4096]{1,0:T(8,128)(2,1)} %get-tuple-element.32.vt_ref), custom_call_target="tpu_custom_call" | custom-call | flops 77309411328 | bytes 12582912 | tf_op jit(solution)/shard_map/attention/pallas_call | solution.py:186
  228.3 3.4 constant_dynamic-slice_fusion
  233.2 3.8 collective-permute-start.6
  238.8 5.3 collective-permute-done.4
  246.6 14.3 %collective-permute-done.3 = bf16[512,768]{1,0:T(8,128)(2,1)} collective-permute-done((bf16[512,768]{1,0:T(8,128)(2,1)}, bf16[512,768]{1,0:T(8,128)(2,1)}, u32[]{:S(2)}, u32[]{:S(2)}) %collective-permute-start.3) | collective-permute-done | bytes 786464 | tf_op jit(solution)/shard_map/ppermute | solution.py:364
  263.3 15.4 %collective-permute-done.5 = bf16[512,768]{1,0:T(8,128)(2,1)} collective-permute-done((bf16[512,768]{1,0:T(8,128)(2,1)}, bf16[512,768]{1,0:T(8,128)(2,1)}, u32[]{:S(2)}, u32[]{:S(2)}) %collective-permute-start.5) | collective-permute-done | bytes 786464 | tf_op jit(solution)/shard_map/ppermute | solution.py:364
  281.4 14.6 %collective-permute-done.7 = bf16[512,768]{1,0:T(8,128)(2,1)} collective-permute-done((bf16[512,768]{1,0:T(8,128)(2,1)}, bf16[512,768]{1,0:T(8,128)(2,1)}, u32[]{:S(2)}, u32[]{:S(2)}) %collective-permute-start.7) | collective-permute-done | bytes 786464 | tf_op jit(solution)/shard_map/ppermute | solution.py:364
  298.4 40.8 %w_out.1 = (bf16[1024,3072]{1,0:T(8,128)(2,1)}, bf16[1024,3072]{1,0:T(8,128)(2,1)}) custom-call(s32[5]{0:T(128)} %stack.32.idx_ref, bf16[1024,768]{1,0:T(8,128)(2,1)} %pad_maximum_fusion.5.refs_0_, bf16[1024,768]{1,0:T(8,128)(2,1)} %pad_maximum_fusion.6.refs_1_, bf16[1024,768]{1,0:T(8,128)(2,1)} %pad_maximum_fusion.7.refs_2_, ...), custom_call_target="tpu_custom_call" | custom-call | flops 19327352832 | bytes 44040192 | tf_op jit(solution)/shard_map/w_out/pallas_call | solution.py:229
  339.1 6.1 slice_bitcast_fusion
  348.8 34.8 %gate_up.4.refs_0_ = bf16[1024,2048]{1,0:T(8,128)(2,1)} custom-call(bf16[1024,3072]{1,0:T(8,128)(2,1)} %get-tuple-element.38.u_ref, bf16[3072,4096]{1,0:T(8,128)(2,1)} %all-gather.12.cloned.1.call-done.g_ref.up_ref, bf16[3072,4096]{1,0:T(8,128)(2,1)} %all-gather.12.cloned.1.call-done.g_ref.up_ref), custom_call_target="tpu_custom_call" | custom-call | flops 25769803776 | bytes 35651584 | tf_op jit(solution)/shard_map/gate_up/pallas_call | solution.py:265
  383.6 29.5 %all-gather.14.cloned.1.call-done.g_ref.up_ref = bf16[3072,4096]{1,0:T(8,128)(2,1)} async-done(((bf16[384,4096]{1,0:T(8,128)(2,1)}), bf16[3072,4096]{1,0:T(8,128)(2,1)}) %all-gather.14.cloned.1.call-update) | async-done | bytes 25165840 | tf_op jit(solution)/shard_map/all_gather | solution.py:407
  413.0 34.6 %gate_up.5.refs_1_ = bf16[1024,2048]{1,0:T(8,128)(2,1)} custom-call(bf16[1024,3072]{1,0:T(8,128)(2,1)} %get-tuple-element.38.u_ref, bf16[3072,4096]{1,0:T(8,128)(2,1)} %all-gather.14.cloned.1.call-done.g_ref.up_ref, bf16[3072,4096]{1,0:T(8,128)(2,1)} %all-gather.14.cloned.1.call-done.g_ref.up_ref), custom_call_target="tpu_custom_call" | custom-call | flops 25769803776 | bytes 35651584 | tf_op jit(solution)/shard_map/gate_up/pallas_call | solution.py:265
  447.6 6.2 pad_maximum_fusion
  453.8 34.8 %gate_up.6.refs_0_ = bf16[1024,2048]{1,0:T(8,128)(2,1)} custom-call(bf16[1024,3072]{1,0:T(8,128)(2,1)} %bitcast.24, bf16[3072,4096]{1,0:T(8,128)(2,1)} %all-gather.12.cloned.1.call-done.g_ref.up_ref, bf16[3072,4096]{1,0:T(8,128)(2,1)} %all-gather.12.cloned.1.call-done.g_ref.up_ref), custom_call_target="tpu_custom_call" | custom-call | flops 25769803776 | bytes 35651584 | tf_op jit(solution)/shard_map/gate_up/pallas_call | solution.py:265
  488.6 34.9 %gate_up.7.refs_1_ = bf16[1024,2048]{1,0:T(8,128)(2,1)} custom-call(bf16[1024,3072]{1,0:T(8,128)(2,1)} %bitcast.25, bf16[3072,4096]{1,0:T(8,128)(2,1)} %all-gather.14.cloned.1.call-done.g_ref.up_ref, bf16[3072,4096]{1,0:T(8,128)(2,1)} %all-gather.14.cloned.1.call-done.g_ref.up_ref), custom_call_target="tpu_custom_call" | custom-call | flops 25769803776 | bytes 35651584 | tf_op jit(solution)/shard_map/gate_up/pallas_call | solution.py:265
  523.4 9.5 %all-gather.16.cloned.1.call-done.refs_2_ = bf16[4096,3072]{1,0:T(8,128)(2,1)} async-done(((bf16[4096,384]{1,0:T(8,128)(2,1)}), bf16[4096,3072]{1,0:T(8,128)(2,1)}) %all-gather.16.cloned.1.call-update) | async-done | bytes 25165840 | tf_op jit(solution)/shard_map/all_gather | solution.py:408
  532.9 20.9 %down.4 = (bf16[256,3072]{1,0:T(8,128)(2,1)}, bf16[256,3072]{1,0:T(8,128)(2,1)}) custom-call(bf16[1024,2048]{1,0:T(8,128)(2,1)} %gate_up.6.refs_0_, bf16[1024,2048]{1,0:T(8,128)(2,1)} %gate_up.7.refs_1_, bf16[4096,3072]{1,0:T(8,128)(2,1)} %all-gather.16.cloned.1.call-done.refs_2_), custom_call_target="tpu_custom_call" | custom-call | flops 12884901888 | bytes 31457280 | tf_op jit(solution)/shard_map/down/pallas_call | solution.py:335
  556.3 20.8 %down.5 = (bf16[256,3072]{1,0:T(8,128)(2,1)}, bf16[256,3072]{1,0:T(8,128)(2,1)}) custom-call(bf16[1024,2048]{1,0:T(8,128)(2,1)} %gate_up.6.refs_0_, bf16[1024,2048]{1,0:T(8,128)(2,1)} %gate_up.7.refs_1_, bf16[4096,3072]{1,0:T(8,128)(2,1)} %all-gather.16.cloned.1.call-done.refs_2_), custom_call_target="tpu_custom_call" | custom-call | flops 12884901888 | bytes 31457280 | tf_op jit(solution)/shard_map/down/pallas_call | solution.py:335
  577.1 13.0 %collective-permute-done.11.refs_4_ = bf16[256,3072]{1,0:T(8,128)(2,1)} collective-permute-done((bf16[256,3072]{1,0:T(8,128)(2,1)}, bf16[256,3072]{1,0:T(8,128)(2,1)}, u32[]{:S(2)}, u32[]{:S(2)}) %collective-permute-start.11) | collective-permute-done | bytes 1572896 | tf_op jit(solution)/shard_map/ppermute | solution.py:364
  593.2 21.9 %down.6 = bf16[512,3072]{1,0:T(8,128)(2,1)} custom-call(bf16[1024,2048]{1,0:T(8,128)(2,1)} %gate_up.4.refs_0_, bf16[1024,2048]{1,0:T(8,128)(2,1)} %gate_up.5.refs_1_, bf16[4096,3072]{1,0:T(8,128)(2,1)} %all-gather.16.cloned.1.call-done.refs_2_, bf16[1024,3072]{1,0:T(8,128)(2,1)} %get-tuple-element.47.refs_3_, ...), custom_call_target="tpu_custom_call" | custom-call | flops 12884901888 | bytes 31457280 | tf_op jit(solution)/shard_map/down/pallas_call | solution.py:335
  618.0 54.8 %collective-permute-done.13.refs_4_ = bf16[256,3072]{1,0:T(8,128)(2,1)S(1)} collective-permute-done((bf16[256,3072]{1,0:T(8,128)(2,1)S(1)}, bf16[256,3072]{1,0:T(8,128)(2,1)S(1)}, u32[]{:S(2)}, u32[]{:S(2)}) %collective-permute-start.13) | collective-permute-done | bytes 1572896 | tf_op jit(solution)/shard_map/ppermute | solution.py:364
  676.8 22.2 %down.7 = bf16[512,3072]{1,0:T(8,128)(2,1)} custom-call(bf16[1024,2048]{1,0:T(8,128)(2,1)} %gate_up.4.refs_0_, bf16[1024,2048]{1,0:T(8,128)(2,1)} %gate_up.5.refs_1_, bf16[4096,3072]{1,0:T(8,128)(2,1)} %all-gather.16.cloned.1.call-done.refs_2_, bf16[1024,3072]{1,0:T(8,128)(2,1)} %get-tuple-element.47.refs_3_, bf16[256,3072]{1,0:T(8,128)(2,1)} %copy-done.12, ...), custom_call_target="tpu_custom_call" | custom-call | flops 12884901888 | bytes 31457280 | tf_op jit(solution)/shard_map/down/pallas_call | solution.py:335
  699.1 56.9 %all-gather.18.cloned.1.call-done = bf16[2048,3072]{1,0:T(8,128)(2,1)} async-done(((bf16[512,3072]{1,0:T(8,128)(2,1)}), bf16[2048,3072]{1,0:T(8,128)(2,1)}) %all-gather.18.cloned.1.call-update) | async-done | bytes 12582928 | tf_op jit(solution)/shard_map/all_gather | solution.py:435
  756.1 4.0 reshape.66
  762.0 109.8 %all-gather.20.cloned.1.call-done = bf16[2048,3072]{1,0:T(8,128)(2,1)} async-done(((bf16[512,3072]{1,0:T(8,128)(2,1)}), bf16[2048,3072]{1,0:T(8,128)(2,1)}) %all-gather.20.cloned.1.call-update) | async-done | bytes 12582928 | tf_op jit(solution)/shard_map/all_gather | solution.py:435
  871.8 20.4 %maximum_bitcast_fusion = bf16[1,4096,3072]{2,1,0:T(8,128)(2,1)} fusion(bf16[2048,3072]{1,0:T(8,128)(2,1)} %all-gather.20.cloned.1.call-done, bf16[2048,3072]{1,0:T(8,128)(2,1)} %all-gather.18.cloned.1.call-done), kind=kLoop, calls=%fused_computation | loop fusion | flops 50331648 | bytes 50331648 | tf_op jit(solution)/shard_map/reshape | solution.py:436
  (86 shorter events, 65.7 us)
Async XLA Ops:
  7.2 3.5 copy-start.5
  7.2 3.5 copy-start.6
  7.2 52.0 %all-gather.8.cloned.1.call-start = ((), (), s32[]{:S(2)}) async-start(), calls=%async_computation | async-start | bytes 8847360 | tf_op jit(solution)/shard_map/all_gather | solution.py:374
  9.8 288.5 %all-gather.10.cloned.1.call-start = ((), (), s32[]{:S(2)}) async-start(), calls=%async_computation.1 | async-start | bytes 19464192 | tf_op jit(solution)/shard_map/all_gather | solution.py:375
  10.7 338.1 %all-gather.12.cloned.1.call-start = ((), (), s32[]{:S(2)}) async-start(), calls=%async_computation.2 | async-start | bytes 28311552 | tf_op jit(solution)/shard_map/all_gather | solution.py:407
  12.2 6.2 copy-start.8
  12.2 6.8 copy-start.7
  13.6 88.4 %collective-permute-start = (bf16[384,2048]{1,0:T(8,128)(2,1)}, bf16[384,2048]{1,0:T(8,128)(2,1)}, u32[]{:S(2)}, u32[]{:S(2)}) collective-permute-start(bf16[384,2048]{1,0:T(8,128)(2,1)} %pad_maximum_fusion.3), channel_id=1, source_target_pairs={{0,16},{8,24},{16,0},{24,8},{1,17},{9,25},{17,1},{25,9},{2,18},{10... | collective-permute-start | bytes 4718600 | tf_op jit(solution)/shard_map/ppermute | solution.py:364
  105.2 307.9 %all-gather.14.cloned.1.call-start = ((), (), s32[]{:S(2)}) async-start(), calls=%async_computation.3 | async-start | bytes 28311552 | tf_op jit(solution)/shard_map/all_gather | solution.py:407
  108.1 60.7 %collective-permute-start.1 = (bf16[384,2048]{1,0:T(8,128)(2,1)}, bf16[384,2048]{1,0:T(8,128)(2,1)}, u32[]{:S(2)}, u32[]{:S(2)}) collective-permute-start(bf16[384,2048]{1,0:T(8,128)(2,1)} %pad_maximum_fusion.4), channel_id=1, source_target_pairs={{0,16},{8,24},{16,0},{24,8},{1,17},{9,25},{17,1},{25,9},{2,18},{10... | collective-permute-start | bytes 4718600 | tf_op jit(solution)/shard_map/ppermute | solution.py:364
  170.3 1.6 copy-start.1
  172.0 361.0 %all-gather.16.cloned.1.call-start = ((), (), s32[]{:S(2)}) async-start(), calls=%async_computation.4 | async-start | bytes 28311552 | tf_op jit(solution)/shard_map/all_gather | solution.py:408
  172.0 52.7 %collective-permute-start.2 = (bf16[2048,384]{1,0:T(8,128)(2,1)}, bf16[2048,384]{1,0:T(8,128)(2,1)}, u32[]{:S(2)}, u32[]{:S(2)}) collective-permute-start(bf16[2048,384]{1,0:T(8,128)(2,1)} %param.21), channel_id=1, source_target_pairs={{0,16},{8,24},{16,0},{24,8},{1,17},{9,25},{17,1},{25,9},{2,18},{10... | collective-permute-start | bytes 4718600 | tf_op jit(solution)/shard_map/ppermute | solution.py:364
  226.5 1.6 copy-start.2
  228.2 527.8 %all-gather.18.cloned.1.call-start = ((), (), s32[]{:S(2)}) async-start(), calls=%async_computation.5 | async-start | bytes 15728640 | tf_op jit(solution)/shard_map/all_gather | solution.py:435
  228.3 3.4 copy-start.3
  231.7 12.5 %copy-start.9 = (bf16[3072]{0:T(1024)(128)(2,1)S(1)}, bf16[3072]{0:T(1024)(128)(2,1)}, u32[]{:S(2)}) copy-start(bf16[3072]{0:T(1024)(128)(2,1)} %param.23) | copy-start | bytes 18436
  231.7 12.5 %collective-permute-start.4 = (bf16[512,768]{1,0:T(8,128)(2,1)S(1)}, bf16[512,768]{1,0:T(8,128)(2,1)S(1)}, u32[]{:S(2)}, u32[]{:S(2)}) collective-permute-start(bf16[512,768]{1,0:T(8,128)(2,1)S(1)} %get-tuple-element.61), channel_id=1, source_target_pairs={{0,8},{8,16},{16,24},{24,0},{1,9},{9,17},{17,25},{25,1},{2,10},{10... | collective-permute-start | bytes 2359304 | tf_op jit(solution)/shard_map/ppermute | solution.py:364
  233.2 27.8 %collective-permute-start.3 = (bf16[512,768]{1,0:T(8,128)(2,1)}, bf16[512,768]{1,0:T(8,128)(2,1)}, u32[]{:S(2)}, u32[]{:S(2)}) collective-permute-start(bf16[512,768]{1,0:T(8,128)(2,1)} %get-tuple-element.57), channel_id=1, source_target_pairs={{0,8},{8,16},{16,24},{24,0},{1,9},{9,17},{17,25},{25,1},{2,10},{10... | collective-permute-start | bytes 2359304 | tf_op jit(solution)/shard_map/ppermute | solution.py:364
  233.2 30.1 %collective-permute-start.6 = (bf16[512,768]{1,0:T(8,128)(2,1)}, bf16[512,768]{1,0:T(8,128)(2,1)}, u32[]{:S(2)}, u32[]{:S(2)}) collective-permute-start(bf16[512,768]{1,0:T(8,128)(2,1)} %get-tuple-element.60), channel_id=1, source_target_pairs={{0,16},{8,24},{16,0},{24,8},{1,17},{9,25},{17,1},{25,9},{2,18},{10... | collective-permute-start | bytes 2359304 | tf_op jit(solution)/shard_map/ppermute | solution.py:364
  237.0 41.7 %collective-permute-start.5 = (bf16[512,768]{1,0:T(8,128)(2,1)}, bf16[512,768]{1,0:T(8,128)(2,1)}, u32[]{:S(2)}, u32[]{:S(2)}) collective-permute-start(bf16[512,768]{1,0:T(8,128)(2,1)} %get-tuple-element.56), channel_id=1, source_target_pairs={{0,16},{8,24},{16,0},{24,8},{1,17},{9,25},{17,1},{25,9},{2,18},{10... | collective-permute-start | bytes 2359304 | tf_op jit(solution)/shard_map/ppermute | solution.py:364
  237.0 44.3 %collective-permute-start.8 = (bf16[512,768]{1,0:T(8,128)(2,1)}, bf16[512,768]{1,0:T(8,128)(2,1)S(1)}, u32[]{:S(2)}, u32[]{:S(2)}) collective-permute-start(bf16[512,768]{1,0:T(8,128)(2,1)} %get-tuple-element.59), channel_id=1, source_target_pairs={{0,24},{8,0},{16,8},{24,16},{1,25},{9,1},{17,9},{25,17},{2,26},{10... | collective-permute-start | bytes 2359304 | tf_op jit(solution)/shard_map/ppermute | solution.py:364
  244.2 51.8 %collective-permute-start.7 = (bf16[512,768]{1,0:T(8,128)(2,1)}, bf16[512,768]{1,0:T(8,128)(2,1)}, u32[]{:S(2)}, u32[]{:S(2)}) collective-permute-start(bf16[512,768]{1,0:T(8,128)(2,1)} %get-tuple-element.55), channel_id=1, source_target_pairs={{0,24},{8,0},{16,8},{24,16},{1,25},{9,1},{17,9},{25,17},{2,26},{10... | collective-permute-start | bytes 2359304 | tf_op jit(solution)/shard_map/ppermute | solution.py:364
  345.2 102.4 %collective-permute-start.9 = (bf16[2,256,3072]{2,1,0:T(8,128)(2,1)}, bf16[2,256,3072]{2,1,0:T(8,128)(2,1)}, u32[]{:S(2)}, u32[]{:S(2)}) collective-permute-start(bf16[2,256,3072]{2,1,0:T(8,128)(2,1)} %get-tuple-element.54), channel_id=1, source_target_pairs={{0,8},{8,16},{16,24},{24,0},{1,9},{9,17},{17,25},{25,1},{2,10},{10... | collective-permute-start | bytes 9437192 | tf_op jit(solution)/shard_map/ppermute | solution.py:364
  347.9 99.7 %collective-permute-start.10 = (bf16[2,256,3072]{2,1,0:T(8,128)(2,1)}, bf16[2,256,3072]{2,1,0:T(8,128)(2,1)}, u32[]{:S(2)}, u32[]{:S(2)}) collective-permute-start(bf16[2,256,3072]{2,1,0:T(8,128)(2,1)} %get-tuple-element.53), channel_id=1, source_target_pairs={{0,24},{8,0},{16,8},{24,16},{1,25},{9,1},{17,9},{25,17},{2,26},{10... | collective-permute-start | bytes 9437192 | tf_op jit(solution)/shard_map/ppermute | solution.py:364
  553.8 36.3 %collective-permute-start.11 = (bf16[256,3072]{1,0:T(8,128)(2,1)}, bf16[256,3072]{1,0:T(8,128)(2,1)}, u32[]{:S(2)}, u32[]{:S(2)}) collective-permute-start(bf16[256,3072]{1,0:T(8,128)(2,1)} %get-tuple-element.43), channel_id=1, source_target_pairs={{0,24},{8,0},{16,8},{24,16},{1,25},{9,1},{17,9},{25,17},{2,26},{10... | collective-permute-start | bytes 4718600 | tf_op jit(solution)/shard_map/ppermute | solution.py:364
  556.3 36.9 %collective-permute-start.12 = (bf16[256,3072]{1,0:T(8,128)(2,1)}, bf16[256,3072]{1,0:T(8,128)(2,1)}, u32[]{:S(2)}, u32[]{:S(2)}) collective-permute-start(bf16[256,3072]{1,0:T(8,128)(2,1)} %get-tuple-element.48), channel_id=1, source_target_pairs={{0,8},{8,16},{16,24},{24,0},{1,9},{9,17},{17,25},{25,1},{2,10},{10... | collective-permute-start | bytes 4718600 | tf_op jit(solution)/shard_map/ppermute | solution.py:364
  615.2 1.9 copy-start.10
  615.2 256.6 %all-gather.20.cloned.1.call-start = ((), (), s32[]{:S(2)}) async-start(), calls=%async_computation.6 | async-start | bytes 15728640 | tf_op jit(solution)/shard_map/all_gather | solution.py:435
  616.6 56.3 %collective-permute-start.13 = (bf16[256,3072]{1,0:T(8,128)(2,1)S(1)}, bf16[256,3072]{1,0:T(8,128)(2,1)S(1)}, u32[]{:S(2)}, u32[]{:S(2)}) collective-permute-start(bf16[256,3072]{1,0:T(8,128)(2,1)S(1)} %copy-done.11), channel_id=1, source_target_pairs={{0,24},{8,0},{16,8},{24,16},{1,25},{9,1},{17,9},{25,17},{2,26},{10... | collective-permute-start | bytes 4718600 | tf_op jit(solution)/shard_map/ppermute | solution.py:364
  617.0 59.8 %collective-permute-start.14 = (bf16[256,3072]{1,0:T(8,128)(2,1)S(1)}, bf16[256,3072]{1,0:T(8,128)(2,1)}, u32[]{:S(2)}, u32[]{:S(2)}) collective-permute-start(bf16[256,3072]{1,0:T(8,128)(2,1)S(1)} %copy-done.10), channel_id=1, source_target_pairs={{0,8},{8,16},{16,24},{24,0},{1,9},{9,17},{17,25},{25,1},{2,10},{10... | collective-permute-start | bytes 4718600 | tf_op jit(solution)/shard_map/ppermute | solution.py:364
  699.1 61.0 %copy-start.4 = (bf16[4096,256]{1,0:T(8,128)(2,1)S(1)}, bf16[4096,256]{1,0:T(8,128)(2,1)}, u32[]{:S(2)}) copy-start(bf16[4096,256]{1,0:T(8,128)(2,1)} %get-tuple-element.52) | copy-start | bytes 6291460
  (3 other events, 4.2 us)
Sparse Core Ops, SparseCore 0:
  10.0 49.2 all-gather.7
  61.2 112.5 all-gather.9
  175.4 117.4 all-gather.11
  294.4 118.5 all-gather.13
  414.5 118.4 all-gather.15
  615.4 140.5 all-gather.17
  757.6 114.2 all-gather.19

commit v4 on v3

--- a/solution.py
+++ b/solution.py
@@ -200,98 +200,124 @@
     )(valid_len, q, k, vt)
 
 
-def out_kernel(n_src, bn, idx_ref, *refs):
+def out_kernel(n_src, idx_ref, *refs):
     o_refs = refs[:n_src]
-    w_ref, x_ref, g_ref, r_ref, u_ref, y_ref = refs[n_src:]
-    d = x_ref.shape[1]
-
-    @pl.loop(0, d // bn)
-    def _(n):
-        acc = None
+    w_ref, x_ref, g_ref, r_ref, ua_ref, ub_ref, o_all, y_ref = refs[n_src:]
+    ko = o_refs[0].shape[1]
+    n = pl.program_id(0)
+    bn = w_ref.shape[1]
+    half = ua_ref.shape[0]
+
+    @pl.when(n == 0)
+    def _():
         for s in range(n_src):
-            col = pl.multiple_of(idx_ref[1 + s] * d + n * bn, bn)
-            part = jnp.dot(o_refs[s][...], w_ref[:, pl.ds(col, bn)], preferred_element_type=jnp.float32)
-            acc = part if acc is None else acc + part
-        col = pl.multiple_of(n * bn, bn)
-        y_ref[:, pl.ds(col, bn)] = (x_ref[:, pl.ds(col, bn)].astype(jnp.float32) + acc).astype(jnp.bfloat16)
-
-    r_ref[...] = y_ref[...]
-    u_ref[...] = norm_rows(y_ref[...].astype(jnp.float32), g_ref[...].astype(jnp.float32))
-
-
-def out_call(idx, o_pieces, w, x, gain, sub, n_tp):
+            o_all[:, s * ko:(s + 1) * ko] = o_refs[s][...]
+
+    acc = jnp.dot(o_all[...], w_ref[...], preferred_element_type=jnp.float32)
+    col = pl.ds(pl.multiple_of(n * bn, bn), bn)
+    y_ref[:, col] = (x_ref[:, col].astype(jnp.float32) + acc).astype(jnp.bfloat16)
+
+    @pl.when(n == pl.num_programs(0) - 1)
+    def _():
+        r_ref[...] = y_ref[...]
+        u = norm_rows(y_ref[...].astype(jnp.float32), g_ref[...].astype(jnp.float32))
+        ua_ref[...] = u[:half]
+        ub_ref[...] = u[half:]
+
+
+def out_call(idx, o_pieces, w, x, gain):
     n_src = len(o_pieces)
     rows, ko = o_pieces[0].shape
     d = x.shape[1]
     bn = min(512, d)
-    row = lambda i, idx: (i, 0)
-    fixed = lambda i, idx: (0, 0)
-    return pl.pallas_call(
-        functools.partial(out_kernel, n_src, bn),
+    fixed = lambda n, idx: (0, 0)
+    half = jax.ShapeDtypeStruct((rows // 2, d), jnp.bfloat16)
+    return pl.pallas_call(
+        functools.partial(out_kernel, n_src),
         grid_spec=pltpu.PrefetchScalarGridSpec(
             num_scalar_prefetch=1,
-            grid=(rows // sub,),
-            in_specs=[pl.BlockSpec((sub, ko), row)] * n_src + [
-                pl.BlockSpec(w.shape, fixed, pipeline_mode=pl.Buffered(1)),
-                pl.BlockSpec((sub, d), lambda i, idx: (i * n_tp + idx[0], 0)),
+            grid=(d // bn,),
+            in_specs=[pl.BlockSpec((rows, ko), fixed)] * n_src + [
+                pl.BlockSpec((n_src * ko, bn), lambda n, idx: (0, n)),
+                pl.BlockSpec((rows, d), lambda n, idx: (idx[0], 0)),
                 pl.BlockSpec((1, d), fixed)],
-            out_specs=[pl.BlockSpec((sub, d), row), pl.BlockSpec((sub, d), row)],
-            scratch_shapes=[pltpu.VMEM((sub, d), jnp.bfloat16)]),
-        out_shape=[jax.ShapeDtypeStruct((rows, d), jnp.bfloat16)] * 2,
+            out_specs=[pl.BlockSpec((rows, d), fixed), pl.BlockSpec((rows // 2, d), fixed), pl.BlockSpec((rows // 2, d), fixed)],
+            scratch_shapes=[pltpu.VMEM((rows, n_src * ko), jnp.bfloat16), pltpu.VMEM((rows, d), jnp.bfloat16)]),
+        out_shape=[jax.ShapeDtypeStruct((rows, d), jnp.bfloat16), half, half],
         compiler_params=params(),
         cost_estimate=cost(2 * rows * d * ko * n_src, 2 * w.size + 8 * rows * d),
         name="w_out",
     )(idx, *o_pieces, w, x, gain)
 
 
-def gu_kernel(bm, u_ref, g_ref, up_ref, a_ref):
-    rows = u_ref.shape[0]
+def gu_kernel(bm, n_u, *refs):
+    u_refs = refs[:n_u]
+    g_ref, up_ref, a_ref, u_all, sem = refs[n_u:]
+    rows = u_all.shape[0]
+    piece = rows // n_u
+
+    @pl.when((pl.program_id(0) == 0) & (pl.program_id(1) == 0))
+    def _():
+        copies = [pltpu.make_async_copy(u_refs[i], u_all.at[i * piece:(i + 1) * piece, :], sem.at[i]) for i in range(n_u)]
+        for c in copies:
+            c.start()
+        for c in copies:
+            c.wait()
 
     @pl.loop(0, rows // bm)
     def _(m):
         r = pl.ds(pl.multiple_of(m * bm, bm), bm)
-        u = u_ref[r, :]
+        u = u_all[r, :]
         gate = jnp.dot(u, g_ref[...], preferred_element_type=jnp.float32)
         up = jnp.dot(u, up_ref[...], preferred_element_type=jnp.float32)
         a_ref[r, :] = (jax.nn.silu(gate) * up).astype(jnp.bfloat16)
 
 
-def gu_call(u, w, n_src):
-    rows, d = u.shape
+def gu_call(us, w, n_src):
+    n_u = len(us)
+    rows, d = us[0].shape
+    rows *= n_u
     half = w.shape[1] // (2 * n_src)
     bn = min(512, half)
     nb = half // bn
     bm = min(256, rows)
     return pl.pallas_call(
-        functools.partial(gu_kernel, bm),
+        functools.partial(gu_kernel, bm, n_u),
         grid=(n_src, nb),
-        in_specs=[pl.BlockSpec((rows, d), lambda j, n: (0, 0), pipeline_mode=pl.Buffered(1)),
-                  pl.BlockSpec((d, bn), lambda j, n: (0, 2 * j * nb + n)),
-                  pl.BlockSpec((d, bn), lambda j, n: (0, (2 * j + 1) * nb + n))],
+        in_specs=[pl.BlockSpec(memory_space=pl.ANY)] * n_u + [
+            pl.BlockSpec((d, bn), lambda j, n: (0, 2 * j * nb + n)),
+            pl.BlockSpec((d, bn), lambda j, n: (0, (2 * j + 1) * nb + n))],
         out_specs=pl.BlockSpec((rows, bn), lambda j, n: (0, j * nb + n)),
         out_shape=jax.ShapeDtypeStruct((rows, n_src * half), jnp.bfloat16),
+        scratch_shapes=[pltpu.VMEM((rows, d), jnp.bfloat16), pltpu.SemaphoreType.DMA((n_u,))],
         compiler_params=params(),
         cost_estimate=cost(4 * rows * d * n_src * half, 2 * w.size + 2 * rows * d + 2 * rows * n_src * half),
         name="gate_up",
-    )(u, w, w)
-
-
-def down_kernel(bm, parts, own, *refs):
+    )(*us, w, w)
+
+
+def down_kernel(bm, parts, own, n_f, blk, n_blk, *refs):
     a_refs = refs[:parts]
     w_ref = refs[parts]
     rest = refs[parts + 1:]
     acc_ref = rest[-1]
-    j = pl.program_id(1)
+    j = pl.program_id(0)
     kp = a_refs[0].shape[1]
-    rows = acc_ref.shape[0]
-    half = rows // 2
+    rows, cols = acc_ref.shape
+    lanes = cols // n_f
 
     @pl.when(j == 0)
     def _():
         if own:
-            for h in range(2):
-                r = slice(h * half, (h + 1) * half)
-                acc_ref[r, :] = rest[0][r, :].astype(jnp.float32) + rest[1 + h][...].astype(jnp.float32)
+            quarter = rows // (2 * N_CALLS)
+            for c in range(N_CALLS):
+                for h in range(2):
+                    r = slice((2 * c + h) * quarter, (2 * c + h + 1) * quarter)
+                    for f in range(n_f):
+                        src = slice((f * n_blk + blk) * lanes, (f * n_blk + blk + 1) * lanes)
+                        dst = slice(f * lanes, (f + 1) * lanes)
+                        part = rest[N_CALLS + h][c * quarter:(c + 1) * quarter, dst].astype(jnp.float32)
+                        acc_ref[r, dst] = rest[c][h * quarter:(h + 1) * quarter, src].astype(jnp.float32) + part
         else:
             acc_ref[...] = jnp.zeros_like(acc_ref)
 
@@ -303,46 +329,85 @@
             acc = acc + jnp.dot(a_refs[p][r, :], w_ref[p * kp:(p + 1) * kp, :], preferred_element_type=jnp.float32)
         acc_ref[r, :] = acc
 
-    @pl.when(j == pl.num_programs(1) - 1)
+    @pl.when(j == pl.num_programs(0) - 1)
     def _():
         if own:
-            rest[3][...] = acc_ref[...].astype(jnp.bfloat16)
+            rest[N_CALLS + 2][...] = acc_ref[...].astype(jnp.bfloat16)
         else:
             for h in range(2):
-                rest[h][...] = acc_ref[h * half:(h + 1) * half, :].astype(jnp.bfloat16)
-
-
-def down_call(a_parts, w, n_src, rows, chunk, resid=None, partials=()):
-    d = w.shape[1]
+                rest[h][...] = acc_ref[h * rows // 2:(h + 1) * rows // 2, :].astype(jnp.bfloat16)
+
+
+def down_call(a_parts, w, n_src, n_f, blk, n_blk, resid=None, partials=()):
+    cols = w.shape[1]
     parts = len(a_parts)
+    rows = a_parts[0].shape[0]
     kj = w.shape[0] // n_src
     kp = kj // parts
     own = resid is not None
-    bn = min(1024, d)
-    nb = d // bn
     bm = min(256, rows)
+    fixed = lambda j: (0, 0)
     args = [*a_parts, w]
-    in_specs = [pl.BlockSpec((rows, kp), lambda n, j: (chunk, j))] * parts + [pl.BlockSpec((kj, bn), lambda n, j: (j, n))]
-    col = lambda n, j: (0, n)
+    in_specs = [pl.BlockSpec((rows, kp), lambda j: (0, j))] * parts + [pl.BlockSpec((kj, cols), lambda j: (j, 0))]
     if own:
-        args += [resid, *partials]
-        in_specs += [pl.BlockSpec((rows, bn), lambda n, j: (chunk, n))] + [pl.BlockSpec((rows // 2, bn), col)] * 2
-        out_specs = pl.BlockSpec((rows, bn), col)
-        out_shape = jax.ShapeDtypeStruct((rows, d), jnp.bfloat16)
+        args += [*resid, *partials]
+        in_specs += [pl.BlockSpec(r.shape, fixed, pipeline_mode=pl.Buffered(1)) for r in (*resid, *partials)]
+        out_specs = pl.BlockSpec((rows, cols), fixed)
+        out_shape = jax.ShapeDtypeStruct((rows, cols), jnp.bfloat16)
     else:
-        out_specs = [pl.BlockSpec((rows // 2, bn), col)] * 2
-        out_shape = [jax.ShapeDtypeStruct((rows // 2, d), jnp.bfloat16)] * 2
-    return pl.pallas_call(
-        functools.partial(down_kernel, bm, parts, own),
-        grid=(nb, n_src),
+        out_specs = [pl.BlockSpec((rows // 2, cols), fixed)] * 2
+        out_shape = [jax.ShapeDtypeStruct((rows // 2, cols), jnp.bfloat16)] * 2
+    return pl.pallas_call(
+        functools.partial(down_kernel, bm, parts, own, n_f, blk, n_blk),
+        grid=(n_src,),
         in_specs=in_specs,
         out_specs=out_specs,
         out_shape=out_shape,
-        scratch_shapes=[pltpu.VMEM((rows, bn), jnp.float32)],
-        compiler_params=params(),
-        cost_estimate=cost(2 * rows * d * kj * n_src, 2 * w.size + 4 * rows * d),
+        scratch_shapes=[pltpu.VMEM((rows, cols), jnp.float32)],
+        compiler_params=params(),
+        cost_estimate=cost(2 * rows * cols * kj * n_src, 2 * w.size + 4 * rows * cols),
         name="down",
     )(*args)
+
+
+def place_kernel(n_in, moves, n_f, blk, n_blk, idx_ref, *refs):
+    ins = refs[:n_in]
+    out_ref, sem = refs[-2:]
+    copies = []
+    for i, src_row, rows, call, who in moves:
+        lanes = ins[i].shape[1] // n_f
+        row = pl.multiple_of(idx_ref[who] * rows + call * rows * (idx_ref.shape[0] - 1), rows)
+        for f in range(n_f):
+            copies.append(pltpu.make_async_copy(
+                ins[i].at[src_row:src_row + rows, f * lanes:(f + 1) * lanes],
+                out_ref.at[pl.ds(row, rows), (f * n_blk + blk) * lanes:(f * n_blk + blk + 1) * lanes],
+                sem.at[len(copies)]))
+    for c in copies:
+        c.start()
+    for c in copies:
+        c.wait()
+
+
+def place_call(idx, pieces, moves, shape, n_f, blk, n_blk, out):
+    n_in = len(pieces)
+    args = list(pieces)
+    in_specs = [pl.BlockSpec(p.shape, lambda *_: (0, 0)) for p in pieces]
+    aliases = {}
+    if out is not None:
+        args.append(out)
+        in_specs.append(pl.BlockSpec(memory_space=pl.ANY))
+        aliases = {n_in + 1: 0}
+    return pl.pallas_call(
+        functools.partial(place_kernel, n_in, moves, n_f, blk, n_blk),
+        grid_spec=pltpu.PrefetchScalarGridSpec(
+            num_scalar_prefetch=1, grid=(1,), in_specs=in_specs, out_specs=pl.BlockSpec(memory_space=pl.ANY),
+            scratch_shapes=[pltpu.SemaphoreType.DMA((len(moves) * n_f,))]),
+        out_shape=jax.ShapeDtypeStruct(shape, jnp.bfloat16),
+        input_output_aliases=aliases,
+        compiler_params=params(),
+        cost_estimate=cost(1000000, 4 * sum(p.size for p in pieces)),
+        name="place",
+    )(idx, *args)
 
 
 def after(val, *deps):
@@ -372,7 +437,10 @@
         me = lax.axis_index(tp)
 
         w_qkv = lax.all_gather(jnp.concatenate([w_query, w_key, w_value], axis=1), 'fsdp', axis=0, tiled=True)
-        full_o = lax.all_gather(w_out, ('ta', 'tb', 'fsdp'), axis=1, tiled=True)
+        rounds = []
+        for s in range(1, n_tp):
+            rounds.append(shift(w_out, s))
+        full_o = lax.all_gather(jnp.concatenate([w_out, *rounds], axis=0), 'fsdp', axis=1, tiled=True)
         fl = w_gate.shape[1]
         n_src = 2
         swaps = []
@@ -392,48 +460,69 @@
         h = norm_call(x, norm_attn.reshape(1, d))
         q, k, v, vt = qkv_call(h, w_qkv, cos_t, sin_t, n_q, n_kv)
 
-        pieces = [[] for _ in range(n_tp)]
+        pieces = []
         gu_parts = []
         o = q
         for call in range(N_CALLS):
             gu_parts.append(joined(call, 1, o))
             o = att_call(after(q, gu_parts[call], o), k, vt, valid_len, call)
+            got = []
             for s in range(n_tp):
                 blk = lax.dynamic_slice_in_dim(o, (me + s) % n_tp * sub, sub, axis=0)
                 if s:
                     blk = shift(blk, s)
-                pieces[s].append(blk)
+                got.append(blk)
+            pieces.append(got)
         d_part = joined(2, 0, o)
         gu_full = [lax.all_gather(w, 'fsdp', axis=0, tiled=True) for w in gu_parts]
-        full_d = lax.all_gather(d_part, 'fsdp', axis=1, tiled=True)
-        o_pieces = [jnp.concatenate(p, axis=0) for p in pieces]
-        o_pieces[0] = after(o_pieces[0], d_part)
-        idx = jnp.stack([me] + [(me - s) % n_tp for s in range(n_tp)]).astype(jnp.int32)
-        resid, u = out_call(idx, o_pieces, full_o, x, norm_mlp.reshape(1, d), sub, n_tp)
-
-        u4 = u.reshape(N_CALLS, 2, sub // 2, d)
-        u_prev = shift(u4[:, 0], 1)
-        u_next = shift(u4[:, 1], -1)
-        a_own = [gu_call(u, gu_full[0], n_src)]
-        a_own.append(gu_call(after(u, a_own[0]), gu_full[1], n_src))
-        u_prev, u_next = lax.optimization_barrier((u_prev, u_next, a_own[1]))[:2]
-        u_recv = jnp.stack([u_prev, u_next], axis=1).reshape(u.shape)
-        a_recv = [gu_call(u_recv, gu_full[0], n_src)]
-        a_recv.append(gu_call(after(u_recv, a_recv[0]), gu_full[1], n_src))
-        partials = []
+        n_blk = w_down.shape[1] // HEAD_DIM
+        d_full = [lax.all_gather(d_part[:, b * HEAD_DIM:(b + 1) * HEAD_DIM], 'fsdp', axis=1, tiled=True) for b in range(n_blk)]
+
+        resid, u_own, u_prev, u_next = [], [], [], []
+        order = d_part
+        for call in range(N_CALLS):
+            got = pieces[call]
+            got[0] = after(got[0], order)
+            row = (call * n_tp + me).reshape(1).astype(jnp.int32)
+            r, ua, ub = out_call(row, got, full_o, x, norm_mlp.reshape(1, d))
+            order = r
+            resid.append(r)
+            u_own += [ua, ub]
+            u_prev.append(shift(ua, 1))
+            u_next.append(shift(ub, -1))
+        u_recv = u_prev + u_next
+
+        a_own = [gu_call(u_own, gu_full[0], n_src)]
+        a_own.append(gu_call([after(u_own[0], a_own[0])] + u_own[1:], gu_full[1], n_src))
+        a_recv = [gu_call([after(u_recv[0], a_own[1])] + u_recv[1:], gu_full[0], n_src)]
+        a_recv.append(gu_call([after(u_recv[0], a_recv[0])] + u_recv[1:], gu_full[1], n_src))
+
         order = a_recv[1]
-        for c in range(N_CALLS):
-            p_prev, p_next = down_call([after(a_recv[0], order), a_recv[1]], full_d, n_src, sub, c)
-            order = p_prev
+        mine, far = [], []
+        for b in range(n_blk):
+            p_prev, p_next = down_call([after(a_recv[0], order), a_recv[1]], d_full[b], n_src, n_fs, b, n_blk)
             b_next = shift(p_prev, -1)
             b_prev = shift(p_next, 1)
-            partials.append((b_next, b_prev))
-        outs = []
-        for c in range(N_CALLS):
-            mine = down_call([after(a_own[0], order), a_own[1]], full_d, n_src, sub, c, resid, partials[c])
-            order = mine
-            outs.append(lax.all_gather(after(mine, *outs), tp, axis=0, tiled=True))
-        hidden = jnp.concatenate(outs, axis=0).reshape(1, seq, d)
+            m = down_call([after(a_own[0], p_prev), a_own[1]], d_full[b], n_src, n_fs, b, n_blk, resid, (b_next, b_prev))
+            order = m
+            f_prev = shift(m, 1)
+            f_next = shift(m, -1)
+            far_0 = shift(f_prev[:sub], 1)
+            far_1 = shift(f_next[sub:], -1)
+            mine.append((m, f_prev, f_next))
+            far.append((far_0, far_1))
+        idx = jnp.stack([(me - s) % n_tp for s in range(n_tp)] + [me]).astype(jnp.int32)
+        near_moves = [(i, c * sub, sub, c, who) for i, who in ((0, 0), (1, 1), (2, n_tp - 1)) for c in range(N_CALLS)]
+        far_moves = [(0, 0, sub, 0, 2), (1, 0, sub, 1, 2)]
+        hidden = None
+        for b in range(n_blk):
+            near = list(mine[b])
+            if b == 0:
+                near[0] = after(near[0], order)
+            hidden = place_call(idx, near, near_moves, (seq, d), n_fs, b, n_blk, hidden)
+            hidden = place_call(idx, far[b], far_moves, (seq, d), n_fs, b, n_blk, hidden)
+        hidden = hidden.reshape(1, seq, d)
         return hidden, k.reshape(1, seq, n_kv, HEAD_DIM), v.reshape(1, seq, n_kv, HEAD_DIM)
 
+
     return jax.shard_map(local_layer, mesh=mesh2, in_specs=in_specs, out_specs=out_specs, check_vma=False)

time: 900 us -> 887 us (0.986)
  the two profiles are of different devices: /device:TPU:97 before, /device:TPU:98 now
where the time goes in v4:
time: 887 us; the launch traced here: 878 us
  Pallas kernels  464 us (52%)
  waiting for transfers between devices  293 us (33%)
  starting transfers between devices  43 us (5%)
  local copies, waits for them, and re-layouts  42.5 us (5%)
  other arithmetic  20 us (2%)
  between operations  15.7 us (2%)
    ppermute x34, waiting for transfers between devices, shift(): return lax.ppermute(val, tp, [(i, (i + s) % n_tp) for i in range(n_tp)])  257 us
    pallas_call x4, Pallas kernels, gu_call(): pl.pallas_call(functools.partial(gu_kernel, bm, n_u), grid=(n_src, nb), i...  147 us
    pallas_call x6, Pallas kernels, down_call(): pl.pallas_call(functools.partial(down_kernel, bm, parts, own, n_f, blk, n...  103 us
    pallas_call x2, Pallas kernels, att_call(): pl.pallas_call(functools.partial(att_kernel, bq, bk, per, first), grid=(n...  72.9 us
    ppermute x34, starting transfers between devices, shift(): return lax.ppermute(val, tp, [(i, (i + s) % n_tp) for i in range(n_tp)])  42.4 us
    pallas_call x1, Pallas kernels, qkv_call(): pl.pallas_call(functools.partial(qkv_kernel, n_q, n_kv), grid=(s // bm,),...  41.6 us
    pallas_call x2, Pallas kernels, out_call(): pl.pallas_call(functools.partial(out_kernel, n_src), grid_spec=pltpu.Pref...  40.9 us
    all_gather x2, waiting for transfers between devices, local_layer(): gu_full = [lax.all_gather(w, 'fsdp', axis=0, tiled=True) for w in gu_parts]  34.5 us
  transfers between devices with their start and end apart: 41, of which 20 were waited for; matrix products, arithmetic and copies ran while one was open for 6% of the time, Pallas kernels for 52%

profile of v4, /device:TPU:98, one launch (start us, length us, event | category | flops | bytes accessed | tf_op | source)
XLA Modules:
  0.0 877.7 jit_solution(1317717689672127445)
XLA Ops:
  15.5 24.2 %collective-permute-done.8 = bf16[768,384]{1,0:T(8,128)(2,1)S(1)} collective-permute-done((bf16[768,384]{1,0:T(8,128)(2,1)S(1)}, bf16[768,384]{1,0:T(8,128)(2,1)S(1)}, u32[]{:S(2)}, u32[]{:S(2)}) %collective-permute-start.8) | collective-permute-done | bytes 589856 | tf_op jit(solution)/shard_map/ppermute | solution.py:429
  51.0 27.5 %norm.1.h_ref = bf16[4096,3072]{1,0:T(8,128)(2,1)} custom-call(bf16[4096,3072]{1,0:T(8,128)(2,1)} %bitcast.10, bf16[1,3072]{1,0:T(2,128)(2,1)} %reshape.60.g_ref), custom_call_target="tpu_custom_call" | custom-call | flops 100663296 | bytes 50331648 | tf_op jit(solution)/shard_map/norm/pallas_call | solution.py:48
  78.6 8.2 fusion
  89.9 41.6 %qkv.1 = (bf16[6,4096,128]{2,1,0:T(8,128)(2,1)}, bf16[4096,256]{1,0:T(8,128)(2,1)}, bf16[4096,256]{1,0:T(8,128)(2,1)}, bf16[256,4096]{1,0:T(8,128)(2,1)}) custom-call(bf16[4096,3072]{1,0:T(8,128)(2,1)} %norm.1.h_ref, bf16[3072,1280]{1,0:T(8,128)(2,1)} %all-gather.8.cloned.1.call-done.w_ref, f32[4096,128]{1,0:T(8,128)} %get-tuple-element.87.cos_ref, ...), custom_call_target="tpu_custom_call" | custom-call | flops 32212254720 | bytes 43515904 | tf_op jit(solution)/shard_map/qkv/pallas_call | solution.py:85
  142.7 33.2 %attention.2 = bf16[2048,768]{1,0:T(8,128)(2,1)} custom-call(s32[1]{0:T(128)S(6)} %copy.28.len_ref, bf16[6,4096,128]{2,1,0:T(8,128)(2,1)} %get-tuple-element.42.q_ref, bf16[4096,256]{1,0:T(8,128)(2,1)} %get-tuple-element.39.k_ref, bf16[256,4096]{1,0:T(8,128)(2,1)} %get-tuple-element.40.vt_ref), custom_call_target="tpu_custom_call" | custom-call | flops 25769803776 | bytes 12582912 | tf_op jit(solution)/shard_map/attention/pallas_call | solution.py:186
  183.2 39.7 %attention.3 = bf16[2048,768]{1,0:T(8,128)(2,1)} custom-call(s32[1]{0:T(128)S(6)} %copy.28.len_ref, bf16[6,4096,128]{2,1,0:T(8,128)(2,1)} %get-tuple-element.42.q_ref, bf16[4096,256]{1,0:T(8,128)(2,1)} %get-tuple-element.39.k_ref, bf16[256,4096]{1,0:T(8,128)(2,1)} %get-tuple-element.40.vt_ref), custom_call_target="tpu_custom_call" | custom-call | flops 77309411328 | bytes 12582912 | tf_op jit(solution)/shard_map/attention/pallas_call | solution.py:186
  241.5 28.3 %collective-permute-done.3.refs_1_ = bf16[512,768]{1,0:T(8,128)(2,1)} collective-permute-done((bf16[512,768]{1,0:T(8,128)(2,1)}, bf16[512,768]{1,0:T(8,128)(2,1)}, u32[]{:S(2)}, u32[]{:S(2)}) %collective-permute-start.3) | collective-permute-done | bytes 786464 | tf_op jit(solution)/shard_map/ppermute | solution.py:429
  270.7 20.8 %w_out.2 = (bf16[512,3072]{1,0:T(8,128)(2,1)}, bf16[256,3072]{1,0:T(8,128)(2,1)}, bf16[256,3072]{1,0:T(8,128)(2,1)}) custom-call(s32[1]{0:T(128)} %bitcast.4.idx_ref, bf16[512,768]{1,0:T(8,128)(2,1)} %get-tuple-element.44.refs_0_, bf16[512,768]{1,0:T(8,128)(2,1)} %collective-permute-done.3.refs_1_, bf16[512,768]{1,0:T(8,128)(2,1)} %collective-permute-done.4.refs_2_, ...), custom_call_target="tpu_custom_call" | custom-call | flops 9663676416 | bytes 31457280 | tf_op jit(solution)/shard_map/w_out/pallas_call | solution.py:235
  294.6 20.1 %w_out.3 = (bf16[512,3072]{1,0:T(8,128)(2,1)}, bf16[256,3072]{1,0:T(8,128)(2,1)}, bf16[256,3072]{1,0:T(8,128)(2,1)}) custom-call(s32[1]{0:T(128)} %bitcast.7.idx_ref, bf16[512,768]{1,0:T(8,128)(2,1)} %get-tuple-element.48.refs_0_, bf16[512,768]{1,0:T(8,128)(2,1)} %collective-permute-done.9.refs_1_, bf16[512,768]{1,0:T(8,128)(2,1)} %collective-permute-done.10.refs_2_, ...), custom_call_target="tpu_custom_call" | custom-call | flops 9663676416 | bytes 31457280 | tf_op jit(solution)/shard_map/w_out/pallas_call | solution.py:235
  319.3 36.8 %gate_up.4.refs_0_ = bf16[1024,2048]{1,0:T(8,128)(2,1)} custom-call(bf16[256,3072]{1,0:T(8,128)(2,1)} %get-tuple-element.51.refs_0_, bf16[256,3072]{1,0:T(8,128)(2,1)} %get-tuple-element.46.refs_1_, bf16[256,3072]{1,0:T(8,128)(2,1)} %get-tuple-element.49.refs_2_, bf16[256,3072]{1,0:T(8,128)(2,1)} %get-tuple-element.50.refs_3_, ...), custom_call_target="tpu_custom_call" | custom-call | flops 25769803776 | bytes 35651584 | tf_op jit(solution)/shard_map/gate_up/pallas_call | solution.py:284
  356.1 34.5 %all-gather.14.cloned.1.call-done.refs_4_.refs_5_ = bf16[3072,4096]{1,0:T(8,128)(2,1)} async-done(((bf16[384,4096]{1,0:T(8,128)(2,1)}), bf16[3072,4096]{1,0:T(8,128)(2,1)}) %all-gather.14.cloned.1.call-update) | async-done | bytes 25165840 | tf_op jit(solution)/shard_map/all_gather | solution.py:477
  390.6 36.5 %gate_up.5.refs_1_ = bf16[1024,2048]{1,0:T(8,128)(2,1)} custom-call(bf16[256,3072]{1,0:T(8,128)(2,1)} %get-tuple-element.51.refs_0_, bf16[256,3072]{1,0:T(8,128)(2,1)} %get-tuple-element.46.refs_1_, bf16[256,3072]{1,0:T(8,128)(2,1)} %get-tuple-element.49.refs_2_, bf16[256,3072]{1,0:T(8,128)(2,1)} %get-tuple-element.50.refs_3_, ...), custom_call_target="tpu_custom_call" | custom-call | flops 25769803776 | bytes 35651584 | tf_op jit(solution)/shard_map/gate_up/pallas_call | solution.py:284
  427.2 37.1 %gate_up.6.refs_0_ = bf16[1024,2048]{1,0:T(8,128)(2,1)} custom-call(bf16[256,3072]{1,0:T(8,128)(2,1)} %collective-permute-done.12.refs_0_, bf16[256,3072]{1,0:T(8,128)(2,1)} %collective-permute-done.13.refs_1_, bf16[256,3072]{1,0:T(8,128)(2,1)} %collective-permute-done.14.refs_2_, bf16[256,3072]{1,0:T(8,128)(2,1)} %collective-permute-done.15.refs_3_, ...), custom_call_target="tpu_custom_call" | custom-call | flops 25769803776 | bytes 35651584 | tf_op jit(solution)/shard_map/gate_up/pallas_call | solution.py:284
  464.3 37.0 %gate_up.7.refs_1_ = bf16[1024,2048]{1,0:T(8,128)(2,1)} custom-call(bf16[256,3072]{1,0:T(8,128)(2,1)} %collective-permute-done.12.refs_0_, bf16[256,3072]{1,0:T(8,128)(2,1)} %collective-permute-done.13.refs_1_, bf16[256,3072]{1,0:T(8,128)(2,1)} %collective-permute-done.14.refs_2_, bf16[256,3072]{1,0:T(8,128)(2,1)} %collective-permute-done.15.refs_3_, ...), custom_call_target="tpu_custom_call" | custom-call | flops 25769803776 | bytes 35651584 | tf_op jit(solution)/shard_map/gate_up/pallas_call | solution.py:284
  501.3 15.3 %down.6 = (bf16[512,1024]{1,0:T(8,128)(2,1)}, bf16[512,1024]{1,0:T(8,128)(2,1)}) custom-call(bf16[1024,2048]{1,0:T(8,128)(2,1)} %gate_up.6.refs_0_, bf16[1024,2048]{1,0:T(8,128)(2,1)} %gate_up.7.refs_1_, bf16[4096,1024]{1,0:T(8,128)(2,1)} %all-gather.16.cloned.1.call-done.refs_2_), custom_call_target="tpu_custom_call" | custom-call | flops 8589934592 | bytes 12582912 | tf_op jit(solution)/shard_map/down/pallas_call | solution.py:360
  519.4 23.3 %collective-permute-done.16.refs_5_ = bf16[512,1024]{1,0:T(8,128)(2,1)} collective-permute-done((bf16[512,1024]{1,0:T(8,128)(2,1)}, bf16[512,1024]{1,0:T(8,128)(2,1)}, u32[]{:S(2)}, u32[]{:S(2)}) %collective-permute-start.16) | collective-permute-done | bytes 1048608 | tf_op jit(solution)/shard_map/ppermute | solution.py:429
  546.1 19.0 %down.7.refs_0_ = bf16[1024,1024]{1,0:T(8,128)(2,1)} custom-call(bf16[1024,2048]{1,0:T(8,128)(2,1)} %gate_up.4.refs_0_, bf16[1024,2048]{1,0:T(8,128)(2,1)} %gate_up.5.refs_1_, bf16[4096,1024]{1,0:T(8,128)(2,1)} %all-gather.16.cloned.1.call-done.refs_2_, bf16[512,3072]{1,0:T(8,128)(2,1)} %get-tuple-element.47.refs_3_, ...), custom_call_target="tpu_custom_call" | custom-call | flops 8589934592 | bytes 12582912 | tf_op jit(solution)/shard_map/down/pallas_call | solution.py:360
  565.1 15.3 %down.8 = (bf16[512,1024]{1,0:T(8,128)(2,1)}, bf16[512,1024]{1,0:T(8,128)(2,1)}) custom-call(bf16[1024,2048]{1,0:T(8,128)(2,1)} %gate_up.6.refs_0_, bf16[1024,2048]{1,0:T(8,128)(2,1)} %gate_up.7.refs_1_, bf16[4096,1024]{1,0:T(8,128)(2,1)} %all-gather.18.cloned.1.call-done.refs_2_), custom_call_target="tpu_custom_call" | custom-call | flops 8589934592 | bytes 12582912 | tf_op jit(solution)/shard_map/down/pallas_call | solution.py:360
  582.7 22.3 %collective-permute-done.18.refs_5_ = bf16[512,1024]{1,0:T(8,128)(2,1)} collective-permute-done((bf16[512,1024]{1,0:T(8,128)(2,1)}, bf16[512,1024]{1,0:T(8,128)(2,1)}, u32[]{:S(2)}, u32[]{:S(2)}) %collective-permute-start.18) | collective-permute-done | bytes 1048608 | tf_op jit(solution)/shard_map/ppermute | solution.py:429
  608.2 18.9 %down.9.refs_0_ = bf16[1024,1024]{1,0:T(8,128)(2,1)} custom-call(bf16[1024,2048]{1,0:T(8,128)(2,1)} %gate_up.4.refs_0_, bf16[1024,2048]{1,0:T(8,128)(2,1)} %gate_up.5.refs_1_, bf16[4096,1024]{1,0:T(8,128)(2,1)} %all-gather.18.cloned.1.call-done.refs_2_, bf16[512,3072]{1,0:T(8,128)(2,1)} %get-tuple-element.47.refs_3_, ...), custom_call_target="tpu_custom_call" | custom-call | flops 8589934592 | bytes 12582912 | tf_op jit(solution)/shard_map/down/pallas_call | solution.py:360
  627.1 15.3 %down.10 = (bf16[512,1024]{1,0:T(8,128)(2,1)}, bf16[512,1024]{1,0:T(8,128)(2,1)}) custom-call(bf16[1024,2048]{1,0:T(8,128)(2,1)} %gate_up.6.refs_0_, bf16[1024,2048]{1,0:T(8,128)(2,1)} %gate_up.7.refs_1_, bf16[4096,1024]{1,0:T(8,128)(2,1)} %all-gather.20.cloned.1.call-done.refs_2_), custom_call_target="tpu_custom_call" | custom-call | flops 8589934592 | bytes 12582912 | tf_op jit(solution)/shard_map/down/pallas_call | solution.py:360
  646.4 22.3 %collective-permute-done.20.refs_5_ = bf16[512,1024]{1,0:T(8,128)(2,1)} collective-permute-done((bf16[512,1024]{1,0:T(8,128)(2,1)}, bf16[512,1024]{1,0:T(8,128)(2,1)}, u32[]{:S(2)}, u32[]{:S(2)}) %collective-permute-start.20) | collective-permute-done | bytes 1048608 | tf_op jit(solution)/shard_map/ppermute | solution.py:429
  669.9 5.7 collective-permute-done.21.refs_6_
  675.6 19.1 %down.11.refs_0_ = bf16[1024,1024]{1,0:T(8,128)(2,1)} custom-call(bf16[1024,2048]{1,0:T(8,128)(2,1)} %gate_up.4.refs_0_, bf16[1024,2048]{1,0:T(8,128)(2,1)} %gate_up.5.refs_1_, bf16[4096,1024]{1,0:T(8,128)(2,1)} %all-gather.20.cloned.1.call-done.refs_2_, bf16[512,3072]{1,0:T(8,128)(2,1)} %get-tuple-element.47.refs_3_, ...), custom_call_target="tpu_custom_call" | custom-call | flops 8589934592 | bytes 12582912 | tf_op jit(solution)/shard_map/down/pallas_call | solution.py:360
  699.2 14.4 %collective-permute-done.32.refs_2_ = bf16[1024,1024]{1,0:T(8,128)(2,1)} collective-permute-done((bf16[1024,1024]{1,0:T(8,128)(2,1)}, bf16[1024,1024]{1,0:T(8,128)(2,1)}, u32[]{:S(2)}, u32[]{:S(2)}) %collective-permute-start.32) | collective-permute-done | bytes 2097184 | tf_op jit(solution)/shard_map/ppermute | solution.py:429
  722.8 35.7 %collective-permute-done.28.refs_2_ = bf16[1024,1024]{1,0:T(8,128)(2,1)} collective-permute-done((bf16[1024,1024]{1,0:T(8,128)(2,1)}, bf16[1024,1024]{1,0:T(8,128)(2,1)}, u32[]{:S(2)}, u32[]{:S(2)}) %collective-permute-start.28) | collective-permute-done | bytes 2097184 | tf_op jit(solution)/shard_map/ppermute | solution.py:429
  766.6 36.9 %collective-permute-done.24.refs_2_ = bf16[1024,1024]{1,0:T(8,128)(2,1)S(1)} collective-permute-done((bf16[1024,1024]{1,0:T(8,128)(2,1)}, bf16[1024,1024]{1,0:T(8,128)(2,1)S(1)}, u32[]{:S(2)}, u32[]{:S(2)}) %collective-permute-start.24) | collective-permute-done | bytes 2097184 | tf_op jit(solution)/shard_map/ppermute | solution.py:429
  815.4 6.6 place.6.refs_2_
  829.6 6.6 place.8.refs_2_
  836.2 12.2 %collective-permute-done.29.refs_1_ = bf16[512,1024]{1,0:T(8,128)(2,1)} collective-permute-done((bf16[512,1024]{1,0:T(8,128)(2,1)}, bf16[512,1024]{1,0:T(8,128)(2,1)}, u32[]{:S(2)}, u32[]{:S(2)}) %collective-permute-start.29) | collective-permute-done | bytes 1048608 | tf_op jit(solution)/shard_map/ppermute | solution.py:429
  852.1 6.6 place.10.refs_2_
  858.7 8.0 collective-permute-done.25.refs_1_
  (134 shorter events, 133.2 us)
Async XLA Ops:
  7.2 82.7 %all-gather.8.cloned.1.call-start = ((), (), s32[]{:S(2)}) async-start(), calls=%async_computation | async-start | bytes 8847360 | tf_op jit(solution)/shard_map/all_gather | solution.py:439
  9.7 261.1 %all-gather.10.cloned.1.call-start = ((), (), s32[]{:S(2)}) async-start(), calls=%async_computation.1 | async-start | bytes 21233664 | tf_op jit(solution)/shard_map/all_gather | solution.py:443
  44.9 274.5 %all-gather.12.cloned.1.call-start = ((), (), s32[]{:S(2)}) async-start(), calls=%async_computation.2 | async-start | bytes 28311552 | tf_op jit(solution)/shard_map/all_gather | solution.py:477
  49.2 83.8 %collective-permute-start = (bf16[384,2048]{1,0:T(8,128)(2,1)}, bf16[384,2048]{1,0:T(8,128)(2,1)}, u32[]{:S(2)}, u32[]{:S(2)}) collective-permute-start(bf16[384,2048]{1,0:T(8,128)(2,1)} %pad_maximum_fusion.3), channel_id=1, source_target_pairs={{0,16},{8,24},{16,0},{24,8},{1,17},{9,25},{17,1},{25,9},{2,18},{10... | collective-permute-start | bytes 4718600 | tf_op jit(solution)/shard_map/ppermute | solution.py:429
  136.2 254.4 %all-gather.14.cloned.1.call-start = ((), (), s32[]{:S(2)}) async-start(), calls=%async_computation.3 | async-start | bytes 28311552 | tf_op jit(solution)/shard_map/all_gather | solution.py:477
  139.1 38.3 %collective-permute-start.1 = (bf16[384,2048]{1,0:T(8,128)(2,1)}, bf16[384,2048]{1,0:T(8,128)(2,1)}, u32[]{:S(2)}, u32[]{:S(2)}) collective-permute-start(bf16[384,2048]{1,0:T(8,128)(2,1)} %pad_maximum_fusion.4), channel_id=1, source_target_pairs={{0,16},{8,24},{16,0},{24,8},{1,17},{9,25},{17,1},{25,9},{2,18},{10... | collective-permute-start | bytes 4718600 | tf_op jit(solution)/shard_map/ppermute | solution.py:429
  180.7 320.7 %all-gather.16.cloned.1.call-start = ((), (), s32[]{:S(2)}) async-start(), calls=%async_computation.4 | async-start | bytes 9437184 | tf_op jit(solution)/shard_map/all_gather | solution.py:479
  180.7 43.8 %collective-permute-start.2 = (bf16[2048,384]{1,0:T(8,128)(2,1)}, bf16[2048,384]{1,0:T(8,128)(2,1)}, u32[]{:S(2)}, u32[]{:S(2)}) collective-permute-start(bf16[2048,384]{1,0:T(8,128)(2,1)} %param.21), channel_id=1, source_target_pairs={{0,16},{8,24},{16,0},{24,8},{1,17},{9,25},{17,1},{25,9},{2,18},{10... | collective-permute-start | bytes 4718600 | tf_op jit(solution)/shard_map/ppermute | solution.py:429
  228.2 336.8 %all-gather.18.cloned.1.call-start = ((), (), s32[]{:S(2)}) async-start(), calls=%async_computation.5 | async-start | bytes 9437184 | tf_op jit(solution)/shard_map/all_gather | solution.py:479
  228.9 398.2 %all-gather.20.cloned.1.call-start = ((), (), s32[]{:S(2)}) async-start(), calls=%async_computation.6 | async-start | bytes 9437184 | tf_op jit(solution)/shard_map/all_gather | solution.py:479
  231.0 38.7 %collective-permute-start.3 = (bf16[512,768]{1,0:T(8,128)(2,1)}, bf16[512,768]{1,0:T(8,128)(2,1)}, u32[]{:S(2)}, u32[]{:S(2)}) collective-permute-start(bf16[512,768]{1,0:T(8,128)(2,1)} %get-tuple-element.78), channel_id=1, source_target_pairs={{0,8},{8,16},{16,24},{24,0},{1,9},{9,17},{17,25},{25,1},{2,10},{10... | collective-permute-start | bytes 2359304 | tf_op jit(solution)/shard_map/ppermute | solution.py:429
  231.0 39.0 %collective-permute-start.4 = (bf16[512,768]{1,0:T(8,128)(2,1)}, bf16[512,768]{1,0:T(8,128)(2,1)}, u32[]{:S(2)}, u32[]{:S(2)}) collective-permute-start(bf16[512,768]{1,0:T(8,128)(2,1)} %get-tuple-element.77), channel_id=1, source_target_pairs={{0,16},{8,24},{16,0},{24,8},{1,17},{9,25},{17,1},{25,9},{2,18},{10... | collective-permute-start | bytes 2359304 | tf_op jit(solution)/shard_map/ppermute | solution.py:429
  232.6 38.1 %collective-permute-start.5 = (bf16[512,768]{1,0:T(8,128)(2,1)}, bf16[512,768]{1,0:T(8,128)(2,1)}, u32[]{:S(2)}, u32[]{:S(2)}) collective-permute-start(bf16[512,768]{1,0:T(8,128)(2,1)} %get-tuple-element.76), channel_id=1, source_target_pairs={{0,24},{8,0},{16,8},{24,16},{1,25},{9,1},{17,9},{25,17},{2,26},{10... | collective-permute-start | bytes 2359304 | tf_op jit(solution)/shard_map/ppermute | solution.py:429
  239.2 55.4 %collective-permute-start.9 = (bf16[512,768]{1,0:T(8,128)(2,1)}, bf16[512,768]{1,0:T(8,128)(2,1)}, u32[]{:S(2)}, u32[]{:S(2)}) collective-permute-start(bf16[512,768]{1,0:T(8,128)(2,1)} %get-tuple-element.74), channel_id=1, source_target_pairs={{0,8},{8,16},{16,24},{24,0},{1,9},{9,17},{17,25},{25,1},{2,10},{10... | collective-permute-start | bytes 2359304 | tf_op jit(solution)/shard_map/ppermute | solution.py:429
  239.3 55.3 %collective-permute-start.10 = (bf16[512,768]{1,0:T(8,128)(2,1)}, bf16[512,768]{1,0:T(8,128)(2,1)}, u32[]{:S(2)}, u32[]{:S(2)}) collective-permute-start(bf16[512,768]{1,0:T(8,128)(2,1)} %get-tuple-element.73), channel_id=1, source_target_pairs={{0,16},{8,24},{16,0},{24,8},{1,17},{9,25},{17,1},{25,9},{2,18},{10... | collective-permute-start | bytes 2359304 | tf_op jit(solution)/shard_map/ppermute | solution.py:429
  291.5 135.6 %collective-permute-start.12 = (bf16[256,3072]{1,0:T(8,128)(2,1)}, bf16[256,3072]{1,0:T(8,128)(2,1)}, u32[]{:S(2)}, u32[]{:S(2)}) collective-permute-start(bf16[256,3072]{1,0:T(8,128)(2,1)} %get-tuple-element.51.refs_0_), channel_id=1, source_target_pairs={{0,8},{8,16},{16,24},{24,0},{1,9},{9,17},{17,25},{25,1},{2,10},{10... | collective-permute-start | bytes 4718600 | tf_op jit(solution)/shard_map/ppermute | solution.py:429
  314.7 112.5 %collective-permute-start.13 = (bf16[256,3072]{1,0:T(8,128)(2,1)}, bf16[256,3072]{1,0:T(8,128)(2,1)}, u32[]{:S(2)}, u32[]{:S(2)}) collective-permute-start(bf16[256,3072]{1,0:T(8,128)(2,1)} %get-tuple-element.49.refs_2_), channel_id=1, source_target_pairs={{0,8},{8,16},{16,24},{24,0},{1,9},{9,17},{17,25},{25,1},{2,10},{10... | collective-permute-start | bytes 4718600 | tf_op jit(solution)/shard_map/ppermute | solution.py:429
  315.7 111.5 %collective-permute-start.14 = (bf16[256,3072]{1,0:T(8,128)(2,1)}, bf16[256,3072]{1,0:T(8,128)(2,1)}, u32[]{:S(2)}, u32[]{:S(2)}) collective-permute-start(bf16[256,3072]{1,0:T(8,128)(2,1)} %get-tuple-element.46.refs_1_), channel_id=1, source_target_pairs={{0,24},{8,0},{16,8},{24,16},{1,25},{9,1},{17,9},{25,17},{2,26},{10... | collective-permute-start | bytes 4718600 | tf_op jit(solution)/shard_map/ppermute | solution.py:429
  317.9 109.3 %collective-permute-start.15 = (bf16[256,3072]{1,0:T(8,128)(2,1)}, bf16[256,3072]{1,0:T(8,128)(2,1)}, u32[]{:S(2)}, u32[]{:S(2)}) collective-permute-start(bf16[256,3072]{1,0:T(8,128)(2,1)} %get-tuple-element.50.refs_3_), channel_id=1, source_target_pairs={{0,24},{8,0},{16,8},{24,16},{1,25},{9,1},{17,9},{25,17},{2,26},{10... | collective-permute-start | bytes 4718600 | tf_op jit(solution)/shard_map/ppermute | solution.py:429
  582.4 112.8 %collective-permute-start.30 = (bf16[1024,1024]{1,0:T(8,128)(2,1)}, bf16[1024,1024]{1,0:T(8,128)(2,1)}, u32[]{:S(2)}, u32[]{:S(2)}) collective-permute-start(bf16[1024,1024]{1,0:T(8,128)(2,1)} %down.7.refs_0_), channel_id=1, source_target_pairs={{0,8},{8,16},{16,24},{24,0},{1,9},{9,17},{17,25},{25,1},{2,10},{10... | collective-permute-start | bytes 6291464 | tf_op jit(solution)/shard_map/ppermute | solution.py:429
  642.3 33.3 %collective-permute-start.21 = (bf16[512,1024]{1,0:T(8,128)(2,1)}, bf16[512,1024]{1,0:T(8,128)(2,1)}, u32[]{:S(2)}, u32[]{:S(2)}) collective-permute-start(bf16[512,1024]{1,0:T(8,128)(2,1)} %get-tuple-element.66), channel_id=1, source_target_pairs={{0,8},{8,16},{16,24},{24,0},{1,9},{9,17},{17,25},{25,1},{2,10},{10... | collective-permute-start | bytes 3145736 | tf_op jit(solution)/shard_map/ppermute | solution.py:429
  644.4 69.3 %collective-permute-start.32 = (bf16[1024,1024]{1,0:T(8,128)(2,1)}, bf16[1024,1024]{1,0:T(8,128)(2,1)}, u32[]{:S(2)}, u32[]{:S(2)}) collective-permute-start(bf16[1024,1024]{1,0:T(8,128)(2,1)} %down.7.refs_0_), channel_id=1, source_target_pairs={{0,24},{8,0},{16,8},{24,16},{1,25},{9,1},{17,9},{25,17},{2,26},{10... | collective-permute-start | bytes 6291464 | tf_op jit(solution)/shard_map/ppermute | solution.py:429
  645.6 75.0 %collective-permute-start.26 = (bf16[1024,1024]{1,0:T(8,128)(2,1)}, bf16[1024,1024]{1,0:T(8,128)(2,1)}, u32[]{:S(2)}, u32[]{:S(2)}) collective-permute-start(bf16[1024,1024]{1,0:T(8,128)(2,1)} %down.9.refs_0_), channel_id=1, source_target_pairs={{0,8},{8,16},{16,24},{24,0},{1,9},{9,17},{17,25},{25,1},{2,10},{10... | collective-permute-start | bytes 6291464 | tf_op jit(solution)/shard_map/ppermute | solution.py:429
  668.7 89.9 %collective-permute-start.28 = (bf16[1024,1024]{1,0:T(8,128)(2,1)}, bf16[1024,1024]{1,0:T(8,128)(2,1)}, u32[]{:S(2)}, u32[]{:S(2)}) collective-permute-start(bf16[1024,1024]{1,0:T(8,128)(2,1)} %down.9.refs_0_), channel_id=1, source_target_pairs={{0,24},{8,0},{16,8},{24,16},{1,25},{9,1},{17,9},{25,17},{2,26},{10... | collective-permute-start | bytes 6291464 | tf_op jit(solution)/shard_map/ppermute | solution.py:429
  694.7 70.7 %collective-permute-start.22 = (bf16[1024,1024]{1,0:T(8,128)(2,1)}, bf16[1024,1024]{1,0:T(8,128)(2,1)S(1)}, u32[]{:S(2)}, u32[]{:S(2)}) collective-permute-start(bf16[1024,1024]{1,0:T(8,128)(2,1)} %down.11.refs_0_), channel_id=1, source_target_pairs={{0,8},{8,16},{16,24},{24,0},{1,9},{9,17},{17,25},{25,1},{2,10},{10... | collective-permute-start | bytes 6291464 | tf_op jit(solution)/shard_map/ppermute | solution.py:429
  695.2 108.2 %collective-permute-start.24 = (bf16[1024,1024]{1,0:T(8,128)(2,1)}, bf16[1024,1024]{1,0:T(8,128)(2,1)S(1)}, u32[]{:S(2)}, u32[]{:S(2)}) collective-permute-start(bf16[1024,1024]{1,0:T(8,128)(2,1)} %down.11.refs_0_), channel_id=1, source_target_pairs={{0,24},{8,0},{16,8},{24,16},{1,25},{9,1},{17,9},{25,17},{2,26},{10... | collective-permute-start | bytes 6291464 | tf_op jit(solution)/shard_map/ppermute | solution.py:429
  713.6 91.4 %collective-permute-start.31 = (bf16[512,1024]{1,0:T(8,128)(2,1)S(1)}, bf16[512,1024]{1,0:T(8,128)(2,1)S(1)}, u32[]{:S(2)}, u32[]{:S(2)}) collective-permute-start(bf16[512,1024]{1,0:T(8,128)(2,1)S(1)} %slice.59), channel_id=1, source_target_pairs={{0,8},{8,16},{16,24},{24,0},{1,9},{9,17},{17,25},{25,1},{2,10},{10... | collective-permute-start | bytes 3145736 | tf_op jit(solution)/shard_map/ppermute | solution.py:429
  720.5 105.4 %collective-permute-start.33 = (bf16[512,1024]{1,0:T(8,128)(2,1)}, bf16[512,1024]{1,0:T(8,128)(2,1)}, u32[]{:S(2)}, u32[]{:S(2)}) collective-permute-start(bf16[512,1024]{1,0:T(8,128)(2,1)} %slice.60), channel_id=1, source_target_pairs={{0,24},{8,0},{16,8},{24,16},{1,25},{9,1},{17,9},{25,17},{2,26},{10... | collective-permute-start | bytes 3145736 | tf_op jit(solution)/shard_map/ppermute | solution.py:429
  758.6 77.6 %collective-permute-start.27 = (bf16[512,1024]{1,0:T(8,128)(2,1)}, bf16[512,1024]{1,0:T(8,128)(2,1)}, u32[]{:S(2)}, u32[]{:S(2)}) collective-permute-start(bf16[512,1024]{1,0:T(8,128)(2,1)} %slice.57), channel_id=1, source_target_pairs={{0,8},{8,16},{16,24},{24,0},{1,9},{9,17},{17,25},{25,1},{2,10},{10... | collective-permute-start | bytes 3145736 | tf_op jit(solution)/shard_map/ppermute | solution.py:429
  765.4 83.1 %collective-permute-start.29 = (bf16[512,1024]{1,0:T(8,128)(2,1)}, bf16[512,1024]{1,0:T(8,128)(2,1)}, u32[]{:S(2)}, u32[]{:S(2)}) collective-permute-start(bf16[512,1024]{1,0:T(8,128)(2,1)} %slice.58), channel_id=1, source_target_pairs={{0,24},{8,0},{16,8},{24,16},{1,25},{9,1},{17,9},{25,17},{2,26},{10... | collective-permute-start | bytes 3145736 | tf_op jit(solution)/shard_map/ppermute | solution.py:429
  803.4 55.3 %collective-permute-start.23 = (bf16[512,1024]{1,0:T(8,128)(2,1)}, bf16[512,1024]{1,0:T(8,128)(2,1)}, u32[]{:S(2)}, u32[]{:S(2)}) collective-permute-start(bf16[512,1024]{1,0:T(8,128)(2,1)} %slice.55), channel_id=1, source_target_pairs={{0,8},{8,16},{16,24},{24,0},{1,9},{9,17},{17,25},{25,1},{2,10},{10... | collective-permute-start | bytes 3145736 | tf_op jit(solution)/shard_map/ppermute | solution.py:429
  806.1 60.6 %collective-permute-start.25 = (bf16[512,1024]{1,0:T(8,128)(2,1)}, bf16[512,1024]{1,0:T(8,128)(2,1)}, u32[]{:S(2)}, u32[]{:S(2)}) collective-permute-start(bf16[512,1024]{1,0:T(8,128)(2,1)} %slice.56), channel_id=1, source_target_pairs={{0,24},{8,0},{16,8},{24,16},{1,25},{9,1},{17,9},{25,17},{2,26},{10... | collective-permute-start | bytes 3145736 | tf_op jit(solution)/shard_map/ppermute | solution.py:429
  (22 other events, 309.1 us)
Sparse Core Ops, SparseCore 0:
  9.8 47.0 all-gather.7
  58.5 91.6 all-gather.9
  151.9 118.5 all-gather.11
  271.9 118.5 all-gather.13
  392.0 51.7 all-gather.15
  445.3 51.8 all-gather.17
  498.8 51.8 all-gather.19

commit v5 on v4

--- a/solution.py
+++ b/solution.py
@@ -255,18 +255,21 @@
     g_ref, up_ref, a_ref, u_all, sem = refs[n_u:]
     rows = u_all.shape[0]
     piece = rows // n_u
-
-    @pl.when((pl.program_id(0) == 0) & (pl.program_id(1) == 0))
+    first = (pl.program_id(0) == 0) & (pl.program_id(1) == 0)
+    copies = [pltpu.make_async_copy(u_refs[i], u_all.at[i * piece:(i + 1) * piece, :], sem.at[i]) for i in range(n_u)]
+
+    @pl.when(first)
     def _():
-        copies = [pltpu.make_async_copy(u_refs[i], u_all.at[i * piece:(i + 1) * piece, :], sem.at[i]) for i in range(n_u)]
         for c in copies:
             c.start()
-        for c in copies:
-            c.wait()
 
     @pl.loop(0, rows // bm)
     def _(m):
         r = pl.ds(pl.multiple_of(m * bm, bm), bm)
+        for i in range(n_u):
+            @pl.when(first & (m == i * piece // bm))
+            def _():
+                copies[i].wait()
         u = u_all[r, :]
         gate = jnp.dot(u, g_ref[...], preferred_element_type=jnp.float32)
         up = jnp.dot(u, up_ref[...], preferred_element_type=jnp.float32)
@@ -278,9 +281,9 @@
     rows, d = us[0].shape
     rows *= n_u
     half = w.shape[1] // (2 * n_src)
-    bn = min(512, half)
+    bn = math.gcd(256, half)
     nb = half // bn
-    bm = min(256, rows)
+    bm = min(512, rows)
     return pl.pallas_call(
         functools.partial(gu_kernel, bm, n_u),
         grid=(n_src, nb),
@@ -302,7 +305,6 @@
     rest = refs[parts + 1:]
     acc_ref = rest[-1]
     j = pl.program_id(0)
-    kp = a_refs[0].shape[1]
     rows, cols = acc_ref.shape
     lanes = cols // n_f
 
@@ -325,14 +327,19 @@
     def _(m):
         r = pl.ds(pl.multiple_of(m * bm, bm), bm)
         acc = acc_ref[r, :]
+        k0 = 0
         for p in range(parts):
-            acc = acc + jnp.dot(a_refs[p][r, :], w_ref[p * kp:(p + 1) * kp, :], preferred_element_type=jnp.float32)
+            kp = a_refs[p].shape[1]
+            acc = acc + jnp.dot(a_refs[p][r, :], w_ref[k0:k0 + kp, :], preferred_element_type=jnp.float32)
+            k0 += kp
         acc_ref[r, :] = acc
 
     @pl.when(j == pl.num_programs(0) - 1)
     def _():
         if own:
-            rest[N_CALLS + 2][...] = acc_ref[...].astype(jnp.bfloat16)
+            sub = rows // N_CALLS
+            for c in range(N_CALLS):
+                rest[N_CALLS + 2 + c][...] = acc_ref[c * sub:(c + 1) * sub, :].astype(jnp.bfloat16)
         else:
             for h in range(2):
                 rest[h][...] = acc_ref[h * rows // 2:(h + 1) * rows // 2, :].astype(jnp.bfloat16)
@@ -343,20 +350,17 @@
     parts = len(a_parts)
     rows = a_parts[0].shape[0]
     kj = w.shape[0] // n_src
-    kp = kj // parts
     own = resid is not None
     bm = min(256, rows)
     fixed = lambda j: (0, 0)
     args = [*a_parts, w]
-    in_specs = [pl.BlockSpec((rows, kp), lambda j: (0, j))] * parts + [pl.BlockSpec((kj, cols), lambda j: (j, 0))]
+    in_specs = [pl.BlockSpec((rows, a.shape[1] // n_src), lambda j: (0, j)) for a in a_parts] + [pl.BlockSpec((kj, cols), lambda j: (j, 0))]
     if own:
         args += [*resid, *partials]
         in_specs += [pl.BlockSpec(r.shape, fixed, pipeline_mode=pl.Buffered(1)) for r in (*resid, *partials)]
-        out_specs = pl.BlockSpec((rows, cols), fixed)
-        out_shape = jax.ShapeDtypeStruct((rows, cols), jnp.bfloat16)
-    else:
-        out_specs = [pl.BlockSpec((rows // 2, cols), fixed)] * 2
-        out_shape = [jax.ShapeDtypeStruct((rows // 2, cols), jnp.bfloat16)] * 2
+    n_out = N_CALLS if own else 2
+    out_specs = [pl.BlockSpec((rows // n_out, cols), fixed)] * n_out
+    out_shape = [jax.ShapeDtypeStruct((rows // n_out, cols), jnp.bfloat16)] * n_out
     return pl.pallas_call(
         functools.partial(down_kernel, bm, parts, own, n_f, blk, n_blk),
         grid=(n_src,),
@@ -444,8 +448,8 @@
         fl = w_gate.shape[1]
         n_src = 2
         swaps = []
-        for p in range(2):
-            cut = slice(p * fl // 2, (p + 1) * fl // 2)
+        lead = fl * 5 // 8
+        for cut in (slice(0, lead), slice(lead, fl)):
             local = jnp.concatenate([w_gate[:, cut], w_up[:, cut]], axis=1)
             swaps.append((local, shift(local, 2)))
         swaps.append((w_down, shift(w_down, 2)))
@@ -492,35 +496,45 @@
             u_next.append(shift(ub, -1))
         u_recv = u_prev + u_next
 
-        a_own = [gu_call(u_own, gu_full[0], n_src)]
-        a_own.append(gu_call([after(u_own[0], a_own[0])] + u_own[1:], gu_full[1], n_src))
-        a_recv = [gu_call([after(u_recv[0], a_own[1])] + u_recv[1:], gu_full[0], n_src)]
-        a_recv.append(gu_call([after(u_recv[0], a_recv[0])] + u_recv[1:], gu_full[1], n_src))
+        rows_of = {0: u_own, 1: u_recv}
+        acts = {0: [], 1: []}
+        order = resid[-1]
+        for p, who in ((0, 0), (0, 1), (1, 0), (1, 1)):
+            us = rows_of[who]
+            acts[who].append(gu_call([after(us[0], order)] + us[1:], gu_full[p], n_src))
+            order = acts[who][-1]
+        a_own, a_recv = acts[0], acts[1]
 
         order = a_recv[1]
-        mine, far = [], []
+        mine = []
         for b in range(n_blk):
             p_prev, p_next = down_call([after(a_recv[0], order), a_recv[1]], d_full[b], n_src, n_fs, b, n_blk)
             b_next = shift(p_prev, -1)
             b_prev = shift(p_next, 1)
             m = down_call([after(a_own[0], p_prev), a_own[1]], d_full[b], n_src, n_fs, b, n_blk, resid, (b_next, b_prev))
-            order = m
-            f_prev = shift(m, 1)
-            f_next = shift(m, -1)
-            far_0 = shift(f_prev[:sub], 1)
-            far_1 = shift(f_next[sub:], -1)
-            mine.append((m, f_prev, f_next))
-            far.append((far_0, far_1))
+            order = m[0]
+            near = {}
+            for c in range(N_CALLS):
+                near[0, c] = shift(m[c], 1)
+            for c in reversed(range(N_CALLS)):
+                near[1, c] = shift(m[c], -1)
+            mine.append((m, near))
         idx = jnp.stack([(me - s) % n_tp for s in range(n_tp)] + [me]).astype(jnp.int32)
-        near_moves = [(i, c * sub, sub, c, who) for i, who in ((0, 0), (1, 1), (2, n_tp - 1)) for c in range(N_CALLS)]
-        far_moves = [(0, 0, sub, 0, 2), (1, 0, sub, 1, 2)]
+        near_moves = [(i * N_CALLS + c, 0, sub, c, who) for i, who in enumerate((0, 1, n_tp - 1)) for c in range(N_CALLS)]
+        far_moves = [(0, 0, sub, 0, 2), (1, 0, sub, N_CALLS - 1, 2)]
         hidden = None
         for b in range(n_blk):
-            near = list(mine[b])
+            m, near = mine[b]
+            src = (near[0, 0], near[1, N_CALLS - 1])
+            if b == n_blk - 1:
+                src = tuple(after(v, hidden) for v in src)
+            far_0 = shift(src[0], 1)
+            far_1 = shift(src[1], -1)
+            pieces = [*m, *(near[g, c] for g in range(2) for c in range(N_CALLS))]
             if b == 0:
-                near[0] = after(near[0], order)
-            hidden = place_call(idx, near, near_moves, (seq, d), n_fs, b, n_blk, hidden)
-            hidden = place_call(idx, far[b], far_moves, (seq, d), n_fs, b, n_blk, hidden)
+                pieces[0] = after(pieces[0], order)
+            hidden = place_call(idx, pieces, near_moves, (seq, d), n_fs, b, n_blk, hidden)
+            hidden = place_call(idx, (far_0, far_1), far_moves, (seq, d), n_fs, b, n_blk, hidden)
         hidden = hidden.reshape(1, seq, d)
         return hidden, k.reshape(1, seq, n_kv, HEAD_DIM), v.reshape(1, seq, n_kv, HEAD_DIM)
 

time: 887 us -> 865 us (0.975)
  the two profiles are of different devices: /device:TPU:98 before, /device:TPU:102 now
where the time goes in v5:
time: 865 us; the launch traced here: 855 us
  Pallas kernels  477 us (55%)
  waiting for transfers between devices  261 us (30%)
  starting transfers between devices  51.3 us (6%)
  local copies, waits for them, and re-layouts  31.6 us (4%)
  other arithmetic  18.6 us (2%)
  between operations  15.7 us (2%)
    ppermute x40, waiting for transfers between devices, shift(): return lax.ppermute(val, tp, [(i, (i + s) % n_tp) for i in range(n_tp)])  260 us
    pallas_call x4, Pallas kernels, gu_call(): pl.pallas_call(functools.partial(gu_kernel, bm, n_u), grid=(n_src, nb), i...  136 us
    pallas_call x6, Pallas kernels, down_call(): pl.pallas_call(functools.partial(down_kernel, bm, parts, own, n_f, blk, n...  102 us
    pallas_call x2, Pallas kernels, att_call(): pl.pallas_call(functools.partial(att_kernel, bq, bk, per, first), grid=(n...  99.2 us
    ppermute x40, starting transfers between devices, shift(): return lax.ppermute(val, tp, [(i, (i + s) % n_tp) for i in range(n_tp)])  50.7 us
    pallas_call x1, Pallas kernels, qkv_call(): pl.pallas_call(functools.partial(qkv_kernel, n_q, n_kv), grid=(s // bm,),...  41.6 us
    pallas_call x2, Pallas kernels, out_call(): pl.pallas_call(functools.partial(out_kernel, n_src), grid_spec=pltpu.Pref...  40.2 us
    pallas_call x6, Pallas kernels, place_call(): pl.pallas_call(functools.partial(place_kernel, n_in, moves, n_f, blk, n_b...  30.4 us
  transfers between devices with their start and end apart: 47, of which 22 were waited for; matrix products, arithmetic and copies ran while one was open for 5% of the time, Pallas kernels for 55%

profile of v5, /device:TPU:102, one launch (start us, length us, event | category | flops | bytes accessed | tf_op | source)
XLA Modules:
  0.0 855.4 jit_solution(15231032398051395454)
XLA Ops:
  15.5 24.2 %collective-permute-done.8 = bf16[768,384]{1,0:T(8,128)(2,1)S(1)} collective-permute-done((bf16[768,384]{1,0:T(8,128)(2,1)S(1)}, bf16[768,384]{1,0:T(8,128)(2,1)S(1)}, u32[]{:S(2)}, u32[]{:S(2)}) %collective-permute-start.8) | collective-permute-done | bytes 589856 | tf_op jit(solution)/shard_map/ppermute | solution.py:433
  49.8 27.5 %norm.1.h_ref = bf16[4096,3072]{1,0:T(8,128)(2,1)} custom-call(bf16[4096,3072]{1,0:T(8,128)(2,1)} %bitcast.10, bf16[1,3072]{1,0:T(2,128)(2,1)} %reshape.60.g_ref), custom_call_target="tpu_custom_call" | custom-call | flops 100663296 | bytes 50331648 | tf_op jit(solution)/shard_map/norm/pallas_call | solution.py:48
  77.3 8.2 fusion
  88.6 41.6 %qkv.1 = (bf16[6,4096,128]{2,1,0:T(8,128)(2,1)}, bf16[4096,256]{1,0:T(8,128)(2,1)}, bf16[4096,256]{1,0:T(8,128)(2,1)}, bf16[256,4096]{1,0:T(8,128)(2,1)}) custom-call(bf16[4096,3072]{1,0:T(8,128)(2,1)} %norm.1.h_ref, bf16[3072,1280]{1,0:T(8,128)(2,1)} %all-gather.8.cloned.1.call-done.w_ref, f32[4096,128]{1,0:T(8,128)} %get-tuple-element.101.cos_ref, ...), custom_call_target="tpu_custom_call" | custom-call | flops 32212254720 | bytes 43515904 | tf_op jit(solution)/shard_map/qkv/pallas_call | solution.py:85
  142.2 35.5 %attention.2 = bf16[2048,768]{1,0:T(8,128)(2,1)} custom-call(s32[1]{0:T(128)S(6)} %copy.28.len_ref, bf16[6,4096,128]{2,1,0:T(8,128)(2,1)} %get-tuple-element.51.q_ref, bf16[4096,256]{1,0:T(8,128)(2,1)} %get-tuple-element.48.k_ref, bf16[256,4096]{1,0:T(8,128)(2,1)} %get-tuple-element.49.vt_ref), custom_call_target="tpu_custom_call" | custom-call | flops 25769803776 | bytes 12582912 | tf_op jit(solution)/shard_map/attention/pallas_call | solution.py:186
  182.8 63.7 %attention.3 = bf16[2048,768]{1,0:T(8,128)(2,1)} custom-call(s32[1]{0:T(128)S(6)} %copy.28.len_ref, bf16[6,4096,128]{2,1,0:T(8,128)(2,1)} %get-tuple-element.51.q_ref, bf16[4096,256]{1,0:T(8,128)(2,1)} %get-tuple-element.48.k_ref, bf16[256,4096]{1,0:T(8,128)(2,1)} %get-tuple-element.49.vt_ref), custom_call_target="tpu_custom_call" | custom-call | flops 77309411328 | bytes 12582912 | tf_op jit(solution)/shard_map/attention/pallas_call | solution.py:186
  266.0 8.1 collective-permute-done.3.refs_1_
  274.4 16.2 %collective-permute-done.4.refs_2_ = bf16[512,768]{1,0:T(8,128)(2,1)} collective-permute-done((bf16[512,768]{1,0:T(8,128)(2,1)}, bf16[512,768]{1,0:T(8,128)(2,1)}, u32[]{:S(2)}, u32[]{:S(2)}) %collective-permute-start.4) | collective-permute-done | bytes 786464 | tf_op jit(solution)/shard_map/ppermute | solution.py:433
  294.9 20.3 %w_out.2 = (bf16[512,3072]{1,0:T(8,128)(2,1)}, bf16[256,3072]{1,0:T(8,128)(2,1)}, bf16[256,3072]{1,0:T(8,128)(2,1)}) custom-call(s32[1]{0:T(128)} %bitcast.4.idx_ref, bf16[512,768]{1,0:T(8,128)(2,1)} %get-tuple-element.53.refs_0_, bf16[512,768]{1,0:T(8,128)(2,1)} %collective-permute-done.3.refs_1_, bf16[512,768]{1,0:T(8,128)(2,1)} %collective-permute-done.4.refs_2_, ...), custom_call_target="tpu_custom_call" | custom-call | flops 9663676416 | bytes 31457280 | tf_op jit(solution)/shard_map/w_out/pallas_call | solution.py:235
  317.0 7.3 collective-permute-done.10.refs_2_
  326.8 19.9 %w_out.3 = (bf16[512,3072]{1,0:T(8,128)(2,1)}, bf16[256,3072]{1,0:T(8,128)(2,1)}, bf16[256,3072]{1,0:T(8,128)(2,1)}) custom-call(s32[1]{0:T(128)} %bitcast.7.idx_ref, bf16[512,768]{1,0:T(8,128)(2,1)} %get-tuple-element.56.refs_0_, bf16[512,768]{1,0:T(8,128)(2,1)} %collective-permute-done.9.refs_1_, bf16[512,768]{1,0:T(8,128)(2,1)} %collective-permute-done.10.refs_2_, ...), custom_call_target="tpu_custom_call" | custom-call | flops 9663676416 | bytes 31457280 | tf_op jit(solution)/shard_map/w_out/pallas_call | solution.py:235
  352.6 41.4 %gate_up.4.refs_0_ = bf16[1024,2560]{1,0:T(8,128)(2,1)} custom-call(bf16[256,3072]{1,0:T(8,128)(2,1)} %get-tuple-element.63.refs_0_, bf16[256,3072]{1,0:T(8,128)(2,1)} %get-tuple-element.59.refs_1_, bf16[256,3072]{1,0:T(8,128)(2,1)} %get-tuple-element.60.refs_2_, bf16[256,3072]{1,0:T(8,128)(2,1)} %get-tuple-element.61.refs_3_, ...), custom_call_target="tpu_custom_call" | custom-call | flops 32212254720 | bytes 42991616 | tf_op jit(solution)/shard_map/gate_up/pallas_call | solution.py:287
  394.5 25.7 %collective-permute-done.15.refs_3_ = bf16[256,3072]{1,0:T(8,128)(2,1)} collective-permute-done((bf16[256,3072]{1,0:T(8,128)(2,1)}, bf16[256,3072]{1,0:T(8,128)(2,1)}, u32[]{:S(2)}, u32[]{:S(2)}) %collective-permute-start.15) | collective-permute-done | bytes 1572896 | tf_op jit(solution)/shard_map/ppermute | solution.py:433
  420.2 41.3 %gate_up.5.refs_0_ = bf16[1024,2560]{1,0:T(8,128)(2,1)} custom-call(bf16[256,3072]{1,0:T(8,128)(2,1)} %collective-permute-done.12.refs_0_, bf16[256,3072]{1,0:T(8,128)(2,1)} %collective-permute-done.13.refs_1_, bf16[256,3072]{1,0:T(8,128)(2,1)} %collective-permute-done.14.refs_2_, bf16[256,3072]{1,0:T(8,128)(2,1)} %collective-permute-done.15.refs_3_, ...), custom_call_target="tpu_custom_call" | custom-call | flops 32212254720 | bytes 42991616 | tf_op jit(solution)/shard_map/gate_up/pallas_call | solution.py:287
  461.6 26.8 %gate_up.6.refs_1_ = bf16[1024,1536]{1,0:T(8,128)(2,1)} custom-call(bf16[256,3072]{1,0:T(8,128)(2,1)} %get-tuple-element.63.refs_0_, bf16[256,3072]{1,0:T(8,128)(2,1)} %get-tuple-element.59.refs_1_, bf16[256,3072]{1,0:T(8,128)(2,1)} %get-tuple-element.60.refs_2_, bf16[256,3072]{1,0:T(8,128)(2,1)} %get-tuple-element.61.refs_3_, ...), custom_call_target="tpu_custom_call" | custom-call | flops 19327352832 | bytes 28311552 | tf_op jit(solution)/shard_map/gate_up/pallas_call | solution.py:287
  488.4 26.8 %gate_up.7.refs_1_ = bf16[1024,1536]{1,0:T(8,128)(2,1)} custom-call(bf16[256,3072]{1,0:T(8,128)(2,1)} %collective-permute-done.12.refs_0_, bf16[256,3072]{1,0:T(8,128)(2,1)} %collective-permute-done.13.refs_1_, bf16[256,3072]{1,0:T(8,128)(2,1)} %collective-permute-done.14.refs_2_, bf16[256,3072]{1,0:T(8,128)(2,1)} %collective-permute-done.15.refs_3_, ...), custom_call_target="tpu_custom_call" | custom-call | flops 19327352832 | bytes 28311552 | tf_op jit(solution)/shard_map/gate_up/pallas_call | solution.py:287
  515.2 15.3 %down.6 = (bf16[512,1024]{1,0:T(8,128)(2,1)}, bf16[512,1024]{1,0:T(8,128)(2,1)}) custom-call(bf16[1024,2560]{1,0:T(8,128)(2,1)} %gate_up.5.refs_0_, bf16[1024,1536]{1,0:T(8,128)(2,1)} %gate_up.7.refs_1_, bf16[4096,1024]{1,0:T(8,128)(2,1)} %all-gather.16.cloned.1.call-done.refs_2_), custom_call_target="tpu_custom_call" | custom-call | flops 8589934592 | bytes 12582912 | tf_op jit(solution)/shard_map/down/pallas_call | solution.py:364
  532.6 23.1 %collective-permute-done.16.refs_5_ = bf16[512,1024]{1,0:T(8,128)(2,1)} collective-permute-done((bf16[512,1024]{1,0:T(8,128)(2,1)}, bf16[512,1024]{1,0:T(8,128)(2,1)}, u32[]{:S(2)}, u32[]{:S(2)}) %collective-permute-start.16) | collective-permute-done | bytes 1048608 | tf_op jit(solution)/shard_map/ppermute | solution.py:433
  559.2 18.5 %down.7 = (bf16[512,1024]{1,0:T(8,128)(2,1)}, bf16[512,1024]{1,0:T(8,128)(2,1)}) custom-call(bf16[1024,2560]{1,0:T(8,128)(2,1)} %gate_up.4.refs_0_, bf16[1024,1536]{1,0:T(8,128)(2,1)} %gate_up.6.refs_1_, bf16[4096,1024]{1,0:T(8,128)(2,1)} %all-gather.16.cloned.1.call-done.refs_2_, bf16[512,3072]{1,0:T(8,128)(2,1)} %get-tuple-element.55.refs_3_, ...), custom_call_target="tpu_custom_call" | custom-call | flops 8589934592 | bytes 12582912 | tf_op jit(solution)/shard_map/down/pallas_call | solution.py:364
  577.7 15.3 %down.8 = (bf16[512,1024]{1,0:T(8,128)(2,1)}, bf16[512,1024]{1,0:T(8,128)(2,1)}) custom-call(bf16[1024,2560]{1,0:T(8,128)(2,1)} %gate_up.5.refs_0_, bf16[1024,1536]{1,0:T(8,128)(2,1)} %gate_up.7.refs_1_, bf16[4096,1024]{1,0:T(8,128)(2,1)} %all-gather.18.cloned.1.call-done.refs_2_), custom_call_target="tpu_custom_call" | custom-call | flops 8589934592 | bytes 12582912 | tf_op jit(solution)/shard_map/down/pallas_call | solution.py:364
  598.3 21.1 %collective-permute-done.18.refs_5_ = bf16[512,1024]{1,0:T(8,128)(2,1)} collective-permute-done((bf16[512,1024]{1,0:T(8,128)(2,1)}, bf16[512,1024]{1,0:T(8,128)(2,1)}, u32[]{:S(2)}, u32[]{:S(2)}) %collective-permute-start.18) | collective-permute-done | bytes 1048608 | tf_op jit(solution)/shard_map/ppermute | solution.py:433
  620.8 18.6 %down.9 = (bf16[512,1024]{1,0:T(8,128)(2,1)}, bf16[512,1024]{1,0:T(8,128)(2,1)}) custom-call(bf16[1024,2560]{1,0:T(8,128)(2,1)} %gate_up.4.refs_0_, bf16[1024,1536]{1,0:T(8,128)(2,1)} %gate_up.6.refs_1_, bf16[4096,1024]{1,0:T(8,128)(2,1)} %all-gather.18.cloned.1.call-done.refs_2_, bf16[512,3072]{1,0:T(8,128)(2,1)} %get-tuple-element.55.refs_3_, ...), custom_call_target="tpu_custom_call" | custom-call | flops 8589934592 | bytes 12582912 | tf_op jit(solution)/shard_map/down/pallas_call | solution.py:364
  639.5 15.3 %down.10 = (bf16[512,1024]{1,0:T(8,128)(2,1)}, bf16[512,1024]{1,0:T(8,128)(2,1)}) custom-call(bf16[1024,2560]{1,0:T(8,128)(2,1)} %gate_up.5.refs_0_, bf16[1024,1536]{1,0:T(8,128)(2,1)} %gate_up.7.refs_1_, bf16[4096,1024]{1,0:T(8,128)(2,1)} %all-gather.20.cloned.1.call-done.refs_2_), custom_call_target="tpu_custom_call" | custom-call | flops 8589934592 | bytes 12582912 | tf_op jit(solution)/shard_map/down/pallas_call | solution.py:364
  657.6 7.9 collective-permute-done.33.refs_3_
  667.5 19.2 %collective-permute-done.20.refs_5_ = bf16[512,1024]{1,0:T(8,128)(2,1)} collective-permute-done((bf16[512,1024]{1,0:T(8,128)(2,1)}, bf16[512,1024]{1,0:T(8,128)(2,1)}, u32[]{:S(2)}, u32[]{:S(2)}) %collective-permute-start.20) | collective-permute-done | bytes 1048608 | tf_op jit(solution)/shard_map/ppermute | solution.py:433
  690.0 20.4 %collective-permute-done.23.refs_2_ = bf16[512,1024]{1,0:T(8,128)(2,1)} collective-permute-done((bf16[512,1024]{1,0:T(8,128)(2,1)}, bf16[512,1024]{1,0:T(8,128)(2,1)}, u32[]{:S(2)}, u32[]{:S(2)}) %collective-permute-start.23) | collective-permute-done | bytes 1048608 | tf_op jit(solution)/shard_map/ppermute | solution.py:433
  710.4 18.9 %down.11 = (bf16[512,1024]{1,0:T(8,128)(2,1)}, bf16[512,1024]{1,0:T(8,128)(2,1)}) custom-call(bf16[1024,2560]{1,0:T(8,128)(2,1)} %gate_up.4.refs_0_, bf16[1024,1536]{1,0:T(8,128)(2,1)} %gate_up.6.refs_1_, bf16[4096,1024]{1,0:T(8,128)(2,1)} %all-gather.20.cloned.1.call-done.refs_2_, bf16[512,3072]{1,0:T(8,128)(2,1)} %get-tuple-element.55.refs_3_, ...), custom_call_target="tpu_custom_call" | custom-call | flops 8589934592 | bytes 12582912 | tf_op jit(solution)/shard_map/down/pallas_call | solution.py:364
  732.9 22.5 %collective-permute-done.30.refs_0_ = bf16[512,1024]{1,0:T(8,128)(2,1)} collective-permute-done((bf16[512,1024]{1,0:T(8,128)(2,1)}, bf16[512,1024]{1,0:T(8,128)(2,1)}, u32[]{:S(2)}, u32[]{:S(2)}) %collective-permute-start.30) | collective-permute-done | bytes 1048608 | tf_op jit(solution)/shard_map/ppermute | solution.py:433
  769.5 6.5 place.8.refs_2_
  783.0 17.3 %collective-permute-done.22.refs_2_ = bf16[512,1024]{1,0:T(8,128)(2,1)} collective-permute-done((bf16[512,1024]{1,0:T(8,128)(2,1)}, bf16[512,1024]{1,0:T(8,128)(2,1)}, u32[]{:S(2)}, u32[]{:S(2)}) %collective-permute-start.22) | collective-permute-done | bytes 1048608 | tf_op jit(solution)/shard_map/ppermute | solution.py:433
  809.5 13.3 %collective-permute-done.38.refs_3_ = bf16[512,1024]{1,0:T(8,128)(2,1)} collective-permute-done((bf16[512,1024]{1,0:T(8,128)(2,1)}, bf16[512,1024]{1,0:T(8,128)(2,1)}, u32[]{:S(2)}, u32[]{:S(2)}) %collective-permute-start.38) | collective-permute-done | bytes 1048608 | tf_op jit(solution)/shard_map/ppermute | solution.py:433
  829.3 15.1 %collective-permute-done.35.refs_0_ = bf16[512,1024]{1,0:T(8,128)(2,1)} collective-permute-done((bf16[512,1024]{1,0:T(8,128)(2,1)}, bf16[512,1024]{1,0:T(8,128)(2,1)}, u32[]{:S(2)}, u32[]{:S(2)}) %collective-permute-start.35) | collective-permute-done | bytes 1048608 | tf_op jit(solution)/shard_map/ppermute | solution.py:433
  (135 shorter events, 136.9 us)
Async XLA Ops:
  7.2 81.5 %all-gather.8.cloned.1.call-start = ((), (), s32[]{:S(2)}) async-start(), calls=%async_computation | async-start | bytes 8847360 | tf_op jit(solution)/shard_map/all_gather | solution.py:443
  9.6 285.2 %all-gather.10.cloned.1.call-start = ((), (), s32[]{:S(2)}) async-start(), calls=%async_computation.1 | async-start | bytes 21233664 | tf_op jit(solution)/shard_map/all_gather | solution.py:447
  45.0 307.6 %all-gather.12.cloned.1.call-start = ((), (), s32[]{:S(2)}) async-start(), calls=%async_computation.2 | async-start | bytes 35389440 | tf_op jit(solution)/shard_map/all_gather | solution.py:481
  47.9 85.4 %collective-permute-start = (bf16[384,2560]{1,0:T(8,128)(2,1)}, bf16[384,2560]{1,0:T(8,128)(2,1)}, u32[]{:S(2)}, u32[]{:S(2)}) collective-permute-start(bf16[384,2560]{1,0:T(8,128)(2,1)} %pad_maximum_fusion.3), channel_id=1, source_target_pairs={{0,16},{8,24},{16,0},{24,8},{1,17},{9,25},{17,1},{25,9},{2,18},{10... | collective-permute-start | bytes 5898248 | tf_op jit(solution)/shard_map/ppermute | solution.py:433
  136.3 325.2 %all-gather.14.cloned.1.call-start = ((), (), s32[]{:S(2)}) async-start(), calls=%async_computation.3 | async-start | bytes 21233664 | tf_op jit(solution)/shard_map/all_gather | solution.py:481
  182.2 333.1 %all-gather.16.cloned.1.call-start = ((), (), s32[]{:S(2)}) async-start(), calls=%async_computation.4 | async-start | bytes 9437184 | tf_op jit(solution)/shard_map/all_gather | solution.py:483
  182.3 65.8 %collective-permute-start.2 = (bf16[2048,384]{1,0:T(8,128)(2,1)}, bf16[2048,384]{1,0:T(8,128)(2,1)}, u32[]{:S(2)}, u32[]{:S(2)}) collective-permute-start(bf16[2048,384]{1,0:T(8,128)(2,1)} %param.21), channel_id=1, source_target_pairs={{0,16},{8,24},{16,0},{24,8},{1,17},{9,25},{17,1},{25,9},{2,18},{10... | collective-permute-start | bytes 4718600 | tf_op jit(solution)/shard_map/ppermute | solution.py:433
  251.7 326.0 %all-gather.18.cloned.1.call-start = ((), (), s32[]{:S(2)}) async-start(), calls=%async_computation.5 | async-start | bytes 9437184 | tf_op jit(solution)/shard_map/all_gather | solution.py:483
  252.3 387.1 %all-gather.20.cloned.1.call-start = ((), (), s32[]{:S(2)}) async-start(), calls=%async_computation.6 | async-start | bytes 9437184 | tf_op jit(solution)/shard_map/all_gather | solution.py:483
  264.6 52.4 %collective-permute-start.9 = (bf16[512,768]{1,0:T(8,128)(2,1)}, bf16[512,768]{1,0:T(8,128)(2,1)}, u32[]{:S(2)}, u32[]{:S(2)}) collective-permute-start(bf16[512,768]{1,0:T(8,128)(2,1)} %get-tuple-element.92), channel_id=1, source_target_pairs={{0,8},{8,16},{16,24},{24,0},{1,9},{9,17},{17,25},{25,1},{2,10},{10... | collective-permute-start | bytes 2359304 | tf_op jit(solution)/shard_map/ppermute | solution.py:433
  264.6 59.7 %collective-permute-start.10 = (bf16[512,768]{1,0:T(8,128)(2,1)}, bf16[512,768]{1,0:T(8,128)(2,1)}, u32[]{:S(2)}, u32[]{:S(2)}) collective-permute-start(bf16[512,768]{1,0:T(8,128)(2,1)} %get-tuple-element.91), channel_id=1, source_target_pairs={{0,16},{8,24},{16,0},{24,8},{1,17},{9,25},{17,1},{25,9},{2,18},{10... | collective-permute-start | bytes 2359304 | tf_op jit(solution)/shard_map/ppermute | solution.py:433
  274.1 52.7 %collective-permute-start.11 = (bf16[512,768]{1,0:T(8,128)(2,1)}, bf16[512,768]{1,0:T(8,128)(2,1)}, u32[]{:S(2)}, u32[]{:S(2)}) collective-permute-start(bf16[512,768]{1,0:T(8,128)(2,1)} %get-tuple-element.90), channel_id=1, source_target_pairs={{0,24},{8,0},{16,8},{24,16},{1,25},{9,1},{17,9},{25,17},{2,26},{10... | collective-permute-start | bytes 2359304 | tf_op jit(solution)/shard_map/ppermute | solution.py:433
  315.1 78.9 %collective-permute-start.12 = (bf16[256,3072]{1,0:T(8,128)(2,1)}, bf16[256,3072]{1,0:T(8,128)(2,1)}, u32[]{:S(2)}, u32[]{:S(2)}) collective-permute-start(bf16[256,3072]{1,0:T(8,128)(2,1)} %get-tuple-element.63.refs_0_), channel_id=1, source_target_pairs={{0,8},{8,16},{16,24},{24,0},{1,9},{9,17},{17,25},{25,1},{2,10},{10... | collective-permute-start | bytes 4718600 | tf_op jit(solution)/shard_map/ppermute | solution.py:433
  346.7 47.8 %collective-permute-start.13 = (bf16[256,3072]{1,0:T(8,128)(2,1)}, bf16[256,3072]{1,0:T(8,128)(2,1)}, u32[]{:S(2)}, u32[]{:S(2)}) collective-permute-start(bf16[256,3072]{1,0:T(8,128)(2,1)} %get-tuple-element.60.refs_2_), channel_id=1, source_target_pairs={{0,8},{8,16},{16,24},{24,0},{1,9},{9,17},{17,25},{25,1},{2,10},{10... | collective-permute-start | bytes 4718600 | tf_op jit(solution)/shard_map/ppermute | solution.py:433
  349.2 45.2 %collective-permute-start.14 = (bf16[256,3072]{1,0:T(8,128)(2,1)}, bf16[256,3072]{1,0:T(8,128)(2,1)}, u32[]{:S(2)}, u32[]{:S(2)}) collective-permute-start(bf16[256,3072]{1,0:T(8,128)(2,1)} %get-tuple-element.59.refs_1_), channel_id=1, source_target_pairs={{0,24},{8,0},{16,8},{24,16},{1,25},{9,1},{17,9},{25,17},{2,26},{10... | collective-permute-start | bytes 4718600 | tf_op jit(solution)/shard_map/ppermute | solution.py:433
  350.4 69.8 %collective-permute-start.15 = (bf16[256,3072]{1,0:T(8,128)(2,1)}, bf16[256,3072]{1,0:T(8,128)(2,1)}, u32[]{:S(2)}, u32[]{:S(2)}) collective-permute-start(bf16[256,3072]{1,0:T(8,128)(2,1)} %get-tuple-element.61.refs_3_), channel_id=1, source_target_pairs={{0,24},{8,0},{16,8},{24,16},{1,25},{9,1},{17,9},{25,17},{2,26},{10... | collective-permute-start | bytes 4718600 | tf_op jit(solution)/shard_map/ppermute | solution.py:433
  595.0 59.8 %collective-permute-start.29 = (bf16[512,1024]{1,0:T(8,128)(2,1)}, bf16[512,1024]{1,0:T(8,128)(2,1)}, u32[]{:S(2)}, u32[]{:S(2)}) collective-permute-start(bf16[512,1024]{1,0:T(8,128)(2,1)} %get-tuple-element.82.refs_0_), channel_id=1, source_target_pairs={{0,8},{8,16},{16,24},{24,0},{1,9},{9,17},{17,25},{25,1},{2,10},{10... | collective-permute-start | bytes 3145736 | tf_op jit(solution)/shard_map/ppermute | solution.py:433
  595.0 61.7 %collective-permute-start.31 = (bf16[512,1024]{1,0:T(8,128)(2,1)}, bf16[512,1024]{1,0:T(8,128)(2,1)}, u32[]{:S(2)}, u32[]{:S(2)}) collective-permute-start(bf16[512,1024]{1,0:T(8,128)(2,1)} %get-tuple-element.81.refs_1_), channel_id=1, source_target_pairs={{0,24},{8,0},{16,8},{24,16},{1,25},{9,1},{17,9},{25,17},{2,26},{10... | collective-permute-start | bytes 3145736 | tf_op jit(solution)/shard_map/ppermute | solution.py:433
  598.3 67.2 %collective-permute-start.33 = (bf16[512,1024]{1,0:T(8,128)(2,1)}, bf16[512,1024]{1,0:T(8,128)(2,1)}, u32[]{:S(2)}, u32[]{:S(2)}) collective-permute-start(bf16[512,1024]{1,0:T(8,128)(2,1)} %get-tuple-element.81.refs_1_), channel_id=1, source_target_pairs={{0,8},{8,16},{16,24},{24,0},{1,9},{9,17},{17,25},{25,1},{2,10},{10... | collective-permute-start | bytes 3145736 | tf_op jit(solution)/shard_map/ppermute | solution.py:433
  619.3 46.2 %collective-permute-start.34 = (bf16[512,1024]{1,0:T(8,128)(2,1)}, bf16[512,1024]{1,0:T(8,128)(2,1)}, u32[]{:S(2)}, u32[]{:S(2)}) collective-permute-start(bf16[512,1024]{1,0:T(8,128)(2,1)} %get-tuple-element.82.refs_0_), channel_id=1, source_target_pairs={{0,24},{8,0},{16,8},{24,16},{1,25},{9,1},{17,9},{25,17},{2,26},{10... | collective-permute-start | bytes 3145736 | tf_op jit(solution)/shard_map/ppermute | solution.py:433
  656.8 53.7 %collective-permute-start.23 = (bf16[512,1024]{1,0:T(8,128)(2,1)}, bf16[512,1024]{1,0:T(8,128)(2,1)}, u32[]{:S(2)}, u32[]{:S(2)}) collective-permute-start(bf16[512,1024]{1,0:T(8,128)(2,1)} %get-tuple-element.74.refs_0_), channel_id=1, source_target_pairs={{0,8},{8,16},{16,24},{24,0},{1,9},{9,17},{17,25},{25,1},{2,10},{10... | collective-permute-start | bytes 3145736 | tf_op jit(solution)/shard_map/ppermute | solution.py:433
  665.5 63.8 %collective-permute-start.25 = (bf16[512,1024]{1,0:T(8,128)(2,1)}, bf16[512,1024]{1,0:T(8,128)(2,1)}, u32[]{:S(2)}, u32[]{:S(2)}) collective-permute-start(bf16[512,1024]{1,0:T(8,128)(2,1)} %get-tuple-element.80.refs_1_), channel_id=1, source_target_pairs={{0,24},{8,0},{16,8},{24,16},{1,25},{9,1},{17,9},{25,17},{2,26},{10... | collective-permute-start | bytes 3145736 | tf_op jit(solution)/shard_map/ppermute | solution.py:433
  665.5 67.4 %collective-permute-start.27 = (bf16[512,1024]{1,0:T(8,128)(2,1)}, bf16[512,1024]{1,0:T(8,128)(2,1)}, u32[]{:S(2)}, u32[]{:S(2)}) collective-permute-start(bf16[512,1024]{1,0:T(8,128)(2,1)} %get-tuple-element.80.refs_1_), channel_id=1, source_target_pairs={{0,8},{8,16},{16,24},{24,0},{1,9},{9,17},{17,25},{25,1},{2,10},{10... | collective-permute-start | bytes 3145736 | tf_op jit(solution)/shard_map/ppermute | solution.py:433
  686.7 68.6 %collective-permute-start.30 = (bf16[512,1024]{1,0:T(8,128)(2,1)}, bf16[512,1024]{1,0:T(8,128)(2,1)}, u32[]{:S(2)}, u32[]{:S(2)}) collective-permute-start(bf16[512,1024]{1,0:T(8,128)(2,1)} %collective-permute-done.29.refs_2_), channel_id=1, source_target_pairs={{0,8},{8,16},{16,24},{24,0},{1,9},{9,17},{17,25},{25,1},{2,10},{10... | collective-permute-start | bytes 3145736 | tf_op jit(solution)/shard_map/ppermute | solution.py:433
  688.0 68.2 %collective-permute-start.32 = (bf16[512,1024]{1,0:T(8,128)(2,1)}, bf16[512,1024]{1,0:T(8,128)(2,1)}, u32[]{:S(2)}, u32[]{:S(2)}) collective-permute-start(bf16[512,1024]{1,0:T(8,128)(2,1)} %collective-permute-done.31.refs_5_), channel_id=1, source_target_pairs={{0,24},{8,0},{16,8},{24,16},{1,25},{9,1},{17,9},{25,17},{2,26},{10... | collective-permute-start | bytes 3145736 | tf_op jit(solution)/shard_map/ppermute | solution.py:433
  710.4 58.9 %collective-permute-start.28 = (bf16[512,1024]{1,0:T(8,128)(2,1)}, bf16[512,1024]{1,0:T(8,128)(2,1)}, u32[]{:S(2)}, u32[]{:S(2)}) collective-permute-start(bf16[512,1024]{1,0:T(8,128)(2,1)} %get-tuple-element.74.refs_0_), channel_id=1, source_target_pairs={{0,24},{8,0},{16,8},{24,16},{1,25},{9,1},{17,9},{25,17},{2,26},{10... | collective-permute-start | bytes 3145736 | tf_op jit(solution)/shard_map/ppermute | solution.py:433
  729.3 48.5 %collective-permute-start.24 = (bf16[512,1024]{1,0:T(8,128)(2,1)}, bf16[512,1024]{1,0:T(8,128)(2,1)}, u32[]{:S(2)}, u32[]{:S(2)}) collective-permute-start(bf16[512,1024]{1,0:T(8,128)(2,1)} %collective-permute-done.23.refs_2_), channel_id=1, source_target_pairs={{0,8},{8,16},{16,24},{24,0},{1,9},{9,17},{17,25},{25,1},{2,10},{10... | collective-permute-start | bytes 3145736 | tf_op jit(solution)/shard_map/ppermute | solution.py:433
  732.9 46.4 %collective-permute-start.26 = (bf16[512,1024]{1,0:T(8,128)(2,1)}, bf16[512,1024]{1,0:T(8,128)(2,1)}, u32[]{:S(2)}, u32[]{:S(2)}) collective-permute-start(bf16[512,1024]{1,0:T(8,128)(2,1)} %collective-permute-done.25.refs_5_), channel_id=1, source_target_pairs={{0,24},{8,0},{16,8},{24,16},{1,25},{9,1},{17,9},{25,17},{2,26},{10... | collective-permute-start | bytes 3145736 | tf_op jit(solution)/shard_map/ppermute | solution.py:433
  755.4 44.9 %collective-permute-start.22 = (bf16[512,1024]{1,0:T(8,128)(2,1)}, bf16[512,1024]{1,0:T(8,128)(2,1)}, u32[]{:S(2)}, u32[]{:S(2)}) collective-permute-start(bf16[512,1024]{1,0:T(8,128)(2,1)} %get-tuple-element.79.refs_0_), channel_id=1, source_target_pairs={{0,8},{8,16},{16,24},{24,0},{1,9},{9,17},{17,25},{25,1},{2,10},{10... | collective-permute-start | bytes 3145736 | tf_op jit(solution)/shard_map/ppermute | solution.py:433
  756.2 44.9 %collective-permute-start.36 = (bf16[512,1024]{1,0:T(8,128)(2,1)}, bf16[512,1024]{1,0:T(8,128)(2,1)}, u32[]{:S(2)}, u32[]{:S(2)}) collective-permute-start(bf16[512,1024]{1,0:T(8,128)(2,1)} %get-tuple-element.84.refs_1_), channel_id=1, source_target_pairs={{0,24},{8,0},{16,8},{24,16},{1,25},{9,1},{17,9},{25,17},{2,26},{10... | collective-permute-start | bytes 3145736 | tf_op jit(solution)/shard_map/ppermute | solution.py:433
  769.4 53.4 %collective-permute-start.38 = (bf16[512,1024]{1,0:T(8,128)(2,1)}, bf16[512,1024]{1,0:T(8,128)(2,1)}, u32[]{:S(2)}, u32[]{:S(2)}) collective-permute-start(bf16[512,1024]{1,0:T(8,128)(2,1)} %get-tuple-element.84.refs_1_), channel_id=1, source_target_pairs={{0,8},{8,16},{16,24},{24,0},{1,9},{9,17},{17,25},{25,1},{2,10},{10... | collective-permute-start | bytes 3145736 | tf_op jit(solution)/shard_map/ppermute | solution.py:433
  777.8 44.9 %collective-permute-start.39 = (bf16[512,1024]{1,0:T(8,128)(2,1)}, bf16[512,1024]{1,0:T(8,128)(2,1)}, u32[]{:S(2)}, u32[]{:S(2)}) collective-permute-start(bf16[512,1024]{1,0:T(8,128)(2,1)} %get-tuple-element.79.refs_0_), channel_id=1, source_target_pairs={{0,24},{8,0},{16,8},{24,16},{1,25},{9,1},{17,9},{25,17},{2,26},{10... | collective-permute-start | bytes 3145736 | tf_op jit(solution)/shard_map/ppermute | solution.py:433
  (26 other events, 523.8 us)
Sparse Core Ops, SparseCore 0:
  9.8 45.7 all-gather.7
  57.2 91.5 all-gather.9
  151.0 145.3 all-gather.11
  297.8 91.8 all-gather.13
  391.1 52.1 all-gather.15
  444.8 51.7 all-gather.17
  498.2 51.7 all-gather.19

commit v6 on v5

--- a/solution.py
+++ b/solution.py
@@ -299,92 +299,77 @@
     )(*us, w, w)
 
 
-def down_kernel(bm, parts, own, n_f, blk, n_blk, *refs):
+def down_kernel(bm, parts, n_src, own, meta_ref, *refs):
     a_refs = refs[:parts]
     w_ref = refs[parts]
     rest = refs[parts + 1:]
-    acc_ref = rest[-1]
-    j = pl.program_id(0)
-    rows, cols = acc_ref.shape
-    lanes = cols // n_f
-
-    @pl.when(j == 0)
-    def _():
-        if own:
-            quarter = rows // (2 * N_CALLS)
-            for c in range(N_CALLS):
-                for h in range(2):
-                    r = slice((2 * c + h) * quarter, (2 * c + h + 1) * quarter)
-                    for f in range(n_f):
-                        src = slice((f * n_blk + blk) * lanes, (f * n_blk + blk + 1) * lanes)
-                        dst = slice(f * lanes, (f + 1) * lanes)
-                        part = rest[N_CALLS + h][c * quarter:(c + 1) * quarter, dst].astype(jnp.float32)
-                        acc_ref[r, dst] = rest[c][h * quarter:(h + 1) * quarter, src].astype(jnp.float32) + part
-        else:
-            acc_ref[...] = jnp.zeros_like(acc_ref)
+    rows = a_refs[0].shape[0]
+    n = pl.program_id(0)
+    steps = pl.num_programs(0)
+    bn = w_ref.shape[1]
+    kj = w_ref.shape[0] // n_src
 
     @pl.loop(0, rows // bm)
     def _(m):
         r = pl.ds(pl.multiple_of(m * bm, bm), bm)
-        acc = acc_ref[r, :]
-        k0 = 0
-        for p in range(parts):
-            kp = a_refs[p].shape[1]
-            acc = acc + jnp.dot(a_refs[p][r, :], w_ref[k0:k0 + kp, :], preferred_element_type=jnp.float32)
-            k0 += kp
-        acc_ref[r, :] = acc
-
-    @pl.when(j == pl.num_programs(0) - 1)
-    def _():
-        if own:
-            sub = rows // N_CALLS
-            for c in range(N_CALLS):
-                rest[N_CALLS + 2 + c][...] = acc_ref[c * sub:(c + 1) * sub, :].astype(jnp.bfloat16)
-        else:
-            for h in range(2):
-                rest[h][...] = acc_ref[h * rows // 2:(h + 1) * rows // 2, :].astype(jnp.bfloat16)
-
-
-def down_call(a_parts, w, n_src, n_f, blk, n_blk, resid=None, partials=()):
-    cols = w.shape[1]
+        acc = None
+        for j in range(n_src):
+            k0 = j * kj
+            for p in range(parts):
+                kp = a_refs[p].shape[1] // n_src
+                part = jnp.dot(a_refs[p][r, j * kp:(j + 1) * kp], w_ref[k0:k0 + kp, :], preferred_element_type=jnp.float32)
+                acc = part if acc is None else acc + part
+                k0 += kp
+        out = pl.ds(pl.multiple_of(m // 2 * bm, bm), bm)
+        for h in range(2):
+            @pl.when(m % 2 == h)
+            def _():
+                if own:
+                    for i in range(bn // HEAD_DIM):
+                        lanes = slice(i * HEAD_DIM, (i + 1) * HEAD_DIM)
+                        col = pl.ds(pl.multiple_of(meta_ref[steps + n * (bn // HEAD_DIM) + i] * HEAD_DIM, HEAD_DIM), HEAD_DIM)
+                        part = acc[:, lanes] + rest[1 + h][out, lanes].astype(jnp.float32)
+                        rest[3][r, lanes] = (rest[0][r, col].astype(jnp.float32) + part).astype(jnp.bfloat16)
+                else:
+                    rest[h][out, :] = acc.astype(jnp.bfloat16)
+
+
+def down_call(a_parts, w, meta, n_src, bn, steps, resid=None, partials=()):
     parts = len(a_parts)
     rows = a_parts[0].shape[0]
-    kj = w.shape[0] // n_src
+    cols = steps * bn
     own = resid is not None
-    bm = min(256, rows)
-    fixed = lambda j: (0, 0)
+    fixed = lambda n, meta: (0, 0)
+    step = lambda n, meta: (0, n)
+    once = dict(pipeline_mode=pl.Buffered(1))
     args = [*a_parts, w]
-    in_specs = [pl.BlockSpec((rows, a.shape[1] // n_src), lambda j: (0, j)) for a in a_parts] + [pl.BlockSpec((kj, cols), lambda j: (j, 0))]
+    in_specs = [pl.BlockSpec(a.shape, fixed, **once) for a in a_parts] + [pl.BlockSpec((w.shape[0], bn), lambda n, meta: (0, meta[n]))]
     if own:
-        args += [*resid, *partials]
-        in_specs += [pl.BlockSpec(r.shape, fixed, pipeline_mode=pl.Buffered(1)) for r in (*resid, *partials)]
-    n_out = N_CALLS if own else 2
-    out_specs = [pl.BlockSpec((rows // n_out, cols), fixed)] * n_out
-    out_shape = [jax.ShapeDtypeStruct((rows // n_out, cols), jnp.bfloat16)] * n_out
-    return pl.pallas_call(
-        functools.partial(down_kernel, bm, parts, own, n_f, blk, n_blk),
-        grid=(n_src,),
-        in_specs=in_specs,
-        out_specs=out_specs,
-        out_shape=out_shape,
-        scratch_shapes=[pltpu.VMEM((rows, cols), jnp.float32)],
-        compiler_params=params(),
-        cost_estimate=cost(2 * rows * cols * kj * n_src, 2 * w.size + 4 * rows * cols),
+        args += [resid, *partials]
+        in_specs += [pl.BlockSpec(resid.shape, fixed, **once)] + [pl.BlockSpec((rows // 2, bn), step)] * 2
+    n_out = 1 if own else 2
+    return pl.pallas_call(
+        functools.partial(down_kernel, rows // (2 * N_CALLS), parts, n_src, own),
+        grid_spec=pltpu.PrefetchScalarGridSpec(
+            num_scalar_prefetch=1, grid=(steps,), in_specs=in_specs, out_specs=[pl.BlockSpec((rows // n_out, bn), step)] * n_out),
+        out_shape=[jax.ShapeDtypeStruct((rows // n_out, cols), jnp.bfloat16)] * n_out,
+        compiler_params=params(),
+        cost_estimate=cost(2 * rows * cols * w.shape[0], 2 * w.size + 4 * rows * cols),
         name="down",
-    )(*args)
-
-
-def place_kernel(n_in, moves, n_f, blk, n_blk, idx_ref, *refs):
+    )(meta, *args)
+
+
+def place_kernel(n_in, moves, n_tp, skip, idx_ref, *refs):
     ins = refs[:n_in]
     out_ref, sem = refs[-2:]
     copies = []
     for i, src_row, rows, call, who in moves:
-        lanes = ins[i].shape[1] // n_f
-        row = pl.multiple_of(idx_ref[who] * rows + call * rows * (idx_ref.shape[0] - 1), rows)
-        for f in range(n_f):
+        row = pl.multiple_of((call * n_tp + idx_ref[who]) * rows, rows)
+        for q in range(ins[i].shape[1] // HEAD_DIM):
+            col = pl.multiple_of(idx_ref[n_tp + skip + q] * HEAD_DIM, HEAD_DIM)
             copies.append(pltpu.make_async_copy(
-                ins[i].at[src_row:src_row + rows, f * lanes:(f + 1) * lanes],
-                out_ref.at[pl.ds(row, rows), (f * n_blk + blk) * lanes:(f * n_blk + blk + 1) * lanes],
+                ins[i].at[src_row:src_row + rows, q * HEAD_DIM:(q + 1) * HEAD_DIM],
+                out_ref.at[pl.ds(row, rows), pl.ds(col, HEAD_DIM)],
                 sem.at[len(copies)]))
     for c in copies:
         c.start()
@@ -392,7 +377,7 @@
         c.wait()
 
 
-def place_call(idx, pieces, moves, shape, n_f, blk, n_blk, out):
+def place_call(idx, pieces, moves, shape, n_tp, skip, out):
     n_in = len(pieces)
     args = list(pieces)
     in_specs = [pl.BlockSpec(p.shape, lambda *_: (0, 0)) for p in pieces]
@@ -401,11 +386,12 @@
         args.append(out)
         in_specs.append(pl.BlockSpec(memory_space=pl.ANY))
         aliases = {n_in + 1: 0}
-    return pl.pallas_call(
-        functools.partial(place_kernel, n_in, moves, n_f, blk, n_blk),
+    n_copies = sum(pieces[m[0]].shape[1] // HEAD_DIM for m in moves)
+    return pl.pallas_call(
+        functools.partial(place_kernel, n_in, moves, n_tp, skip),
         grid_spec=pltpu.PrefetchScalarGridSpec(
             num_scalar_prefetch=1, grid=(1,), in_specs=in_specs, out_specs=pl.BlockSpec(memory_space=pl.ANY),
-            scratch_shapes=[pltpu.SemaphoreType.DMA((len(moves) * n_f,))]),
+            scratch_shapes=[pltpu.SemaphoreType.DMA((n_copies,))]),
         out_shape=jax.ShapeDtypeStruct(shape, jnp.bfloat16),
         input_output_aliases=aliases,
         compiler_params=params(),
@@ -480,6 +466,8 @@
         d_part = joined(2, 0, o)
         gu_full = [lax.all_gather(w, 'fsdp', axis=0, tiled=True) for w in gu_parts]
         n_blk = w_down.shape[1] // HEAD_DIM
+        d_pair = lax.ppermute(d_part, 'fsdp', [(i, i ^ 1) for i in range(n_fs)])
+        d_near = jnp.concatenate([d_part, d_pair], axis=1)
         d_full = [lax.all_gather(d_part[:, b * HEAD_DIM:(b + 1) * HEAD_DIM], 'fsdp', axis=1, tiled=True) for b in range(n_blk)]
 
         resid, u_own, u_prev, u_next = [], [], [], []
@@ -494,47 +482,55 @@
             u_own += [ua, ub]
             u_prev.append(shift(ua, 1))
             u_next.append(shift(ub, -1))
-        u_recv = u_prev + u_next
-
-        rows_of = {0: u_own, 1: u_recv}
-        acts = {0: [], 1: []}
-        order = resid[-1]
-        for p, who in ((0, 0), (0, 1), (1, 0), (1, 1)):
-            us = rows_of[who]
-            acts[who].append(gu_call([after(us[0], order)] + us[1:], gu_full[p], n_src))
-            order = acts[who][-1]
-        a_own, a_recv = acts[0], acts[1]
-
+        u_recv = [u_prev[0], u_next[0], u_prev[1], u_next[1]]
+        resid = jnp.concatenate(resid, axis=0)
+
+        def gate_up(p, who, dep):
+            us = (u_own, u_recv)[who]
+            return gu_call([after(us[0], dep)] + us[1:], gu_full[p], n_src)
+
+        a_own = [gate_up(0, 0, resid)]
+        a_recv = [gate_up(0, 1, a_own[0])]
+        a_recv.append(gate_up(1, 1, a_recv[0]))
+
+        fs = lax.axis_index('fsdp')
+        chip, n_chip = fs // 2, n_fs // 2
+        others = [(chip + 1 + i) % n_chip for i in range(n_chip - 1)]
+        bn = 2 * HEAD_DIM
+        blocks = [(d_near, list(range(n_blk)), [fs * n_blk + i for i in range(n_blk)] + [(fs ^ 1) * n_blk + i for i in range(n_blk)])]
+        for b in range(n_blk):
+            units = sum(([2 * o_ * n_blk + b, (2 * o_ + 1) * n_blk + b] for o_ in others), [])
+            blocks.append((d_full[b], others, units))
         order = a_recv[1]
         mine = []
-        for b in range(n_blk):
-            p_prev, p_next = down_call([after(a_recv[0], order), a_recv[1]], d_full[b], n_src, n_fs, b, n_blk)
+        for b, (w, sel, units) in enumerate(blocks):
+            meta = jnp.stack([jnp.asarray(v, jnp.int32) for v in [*sel, *units]])
+            p_prev, p_next = down_call([after(a_recv[0], order), a_recv[1]], w, meta, n_src, bn, len(sel))
             b_next = shift(p_prev, -1)
             b_prev = shift(p_next, 1)
-            m = down_call([after(a_own[0], p_prev), a_own[1]], d_full[b], n_src, n_fs, b, n_blk, resid, (b_next, b_prev))
-            order = m[0]
+            if b == 0:
+                a_own.append(gate_up(1, 0, p_prev))
+            m, = down_call([after(a_own[0], p_prev), a_own[1]], w, meta, n_src, bn, len(sel), resid, (b_next, b_prev))
+            order = m
             near = {}
-            for c in range(N_CALLS):
-                near[0, c] = shift(m[c], 1)
-            for c in reversed(range(N_CALLS)):
-                near[1, c] = shift(m[c], -1)
+            for g, by in enumerate((1, -1)):
+                near[g] = shift(m, by)
             mine.append((m, near))
-        idx = jnp.stack([(me - s) % n_tp for s in range(n_tp)] + [me]).astype(jnp.int32)
-        near_moves = [(i * N_CALLS + c, 0, sub, c, who) for i, who in enumerate((0, 1, n_tp - 1)) for c in range(N_CALLS)]
+        idx = jnp.stack([jnp.asarray(v, jnp.int32) for v in [(me - s) % n_tp for s in range(n_tp)] + sum((u for _, _, u in blocks), [])])
+        near_moves = [(i, c * sub, sub, c, who) for i, who in enumerate((0, 1, n_tp - 1)) for c in range(N_CALLS)]
         far_moves = [(0, 0, sub, 0, 2), (1, 0, sub, N_CALLS - 1, 2)]
         hidden = None
-        for b in range(n_blk):
+        skip = 0
+        last = len(blocks) - 1
+        for b in range(len(blocks)):
             m, near = mine[b]
-            src = (near[0, 0], near[1, N_CALLS - 1])
-            if b == n_blk - 1:
-                src = tuple(after(v, hidden) for v in src)
-            far_0 = shift(src[0], 1)
-            far_1 = shift(src[1], -1)
-            pieces = [*m, *(near[g, c] for g in range(2) for c in range(N_CALLS))]
-            if b == 0:
-                pieces[0] = after(pieces[0], order)
-            hidden = place_call(idx, pieces, near_moves, (seq, d), n_fs, b, n_blk, hidden)
-            hidden = place_call(idx, (far_0, far_1), far_moves, (seq, d), n_fs, b, n_blk, hidden)
+            src = (near[0], near[1]) if b < last else (after(near[0], hidden), after(near[1], hidden))
+            far_0 = shift(src[0][:sub], 1)
+            far_1 = shift(src[1][sub:], -1)
+            pieces = [after(m, order) if b == 0 else m, near[0], near[1]]
+            hidden = place_call(idx, pieces, near_moves, (seq, d), n_tp, skip, hidden)
+            hidden = place_call(idx, (far_0, far_1), far_moves, (seq, d), n_tp, skip, hidden)
+            skip += len(blocks[b][2])
         hidden = hidden.reshape(1, seq, d)
         return hidden, k.reshape(1, seq, n_kv, HEAD_DIM), v.reshape(1, seq, n_kv, HEAD_DIM)
 

time: 865 us -> 914 us (1.057)
  the two profiles are of different devices: /device:TPU:102 before, /device:TPU:97 now
where the time goes in v6:
time: 914 us; the launch traced here: 900 us
  Pallas kernels  491 us (54%)
  waiting for transfers between devices  239 us (26%)
  starting transfers between devices  72.2 us (8%)
  local copies, waits for them, and re-layouts  58.3 us (6%)
  other arithmetic  23.7 us (3%)
  between operations  15.4 us (2%)
    ppermute x40, waiting for transfers between devices, shift(): return lax.ppermute(val, tp, [(i, (i + s) % n_tp) for i in range(n_tp)])  239 us
    pallas_call x4, Pallas kernels, gu_call(): pl.pallas_call(functools.partial(gu_kernel, bm, n_u), grid=(n_src, nb), i...  137 us
    pallas_call x8, Pallas kernels, down_call(): pl.pallas_call(functools.partial(down_kernel, rows // (2 * N_CALLS), part...  125 us
    pallas_call x2, Pallas kernels, att_call(): pl.pallas_call(functools.partial(att_kernel, bq, bk, per, first), grid=(n...  83.8 us
    ppermute x40, starting transfers between devices, shift(): return lax.ppermute(val, tp, [(i, (i + s) % n_tp) for i in range(n_tp)])  47.3 us
    pallas_call x1, Pallas kernels, qkv_call(): pl.pallas_call(functools.partial(qkv_kernel, n_q, n_kv), grid=(s // bm,),...  41.5 us
    pallas_call x2, Pallas kernels, out_call(): pl.pallas_call(functools.partial(out_kernel, n_src), grid_spec=pltpu.Pref...  41 us
    pallas_call x8, Pallas kernels, place_call(): pl.pallas_call(functools.partial(place_kernel, n_in, moves, n_tp, skip),...  34.9 us
  transfers between devices with their start and end apart: 48, of which 19 were waited for; matrix products, arithmetic and copies ran while one was open for 8% of the time, Pallas kernels for 54%

profile of v6, /device:TPU:97, one launch (start us, length us, event | category | flops | bytes accessed | tf_op | source)
XLA Modules:
  0.0 900.1 jit_solution(4598839834722135082)
XLA Ops:
  16.7 11.5 %collective-permute-done.6 = bf16[768,384]{1,0:T(8,128)(2,1)S(1)} collective-permute-done((bf16[768,384]{1,0:T(8,128)(2,1)S(1)}, bf16[768,384]{1,0:T(8,128)(2,1)S(1)}, u32[]{:S(2)}, u32[]{:S(2)}) %collective-permute-start.6) | collective-permute-done | bytes 589856 | tf_op jit(solution)/shard_map/ppermute | solution.py:419
  28.2 13.4 %collective-permute-done.7 = bf16[768,384]{1,0:T(8,128)(2,1)S(1)} collective-permute-done((bf16[768,384]{1,0:T(8,128)(2,1)S(1)}, bf16[768,384]{1,0:T(8,128)(2,1)S(1)}, u32[]{:S(2)}, u32[]{:S(2)}) %collective-permute-start.7) | collective-permute-done | bytes 589856 | tf_op jit(solution)/shard_map/ppermute | solution.py:419
  49.2 27.8 %norm.1.h_ref = bf16[4096,3072]{1,0:T(8,128)(2,1)} custom-call(bf16[4096,3072]{1,0:T(8,128)(2,1)} %bitcast.37, bf16[1,3072]{1,0:T(2,128)(2,1)} %reshape.63.g_ref), custom_call_target="tpu_custom_call" | custom-call | flops 100663296 | bytes 50331648 | tf_op jit(solution)/shard_map/norm/pallas_call | solution.py:48
  77.0 8.2 fusion
  88.3 41.5 %qkv.1 = (bf16[6,4096,128]{2,1,0:T(8,128)(2,1)}, bf16[4096,256]{1,0:T(8,128)(2,1)}, bf16[4096,256]{1,0:T(8,128)(2,1)}, bf16[256,4096]{1,0:T(8,128)(2,1)}) custom-call(bf16[4096,3072]{1,0:T(8,128)(2,1)} %norm.1.h_ref, bf16[3072,1280]{1,0:T(8,128)(2,1)} %all-gather.8.cloned.1.call-done.w_ref, f32[4096,128]{1,0:T(8,128)} %get-tuple-element.97.cos_ref, ...), custom_call_target="tpu_custom_call" | custom-call | flops 32212254720 | bytes 43515904 | tf_op jit(solution)/shard_map/qkv/pallas_call | solution.py:85
  139.6 35.4 %attention.2 = bf16[2048,768]{1,0:T(8,128)(2,1)} custom-call(s32[1]{0:T(128)S(6)} %copy.33.len_ref, bf16[6,4096,128]{2,1,0:T(8,128)(2,1)} %get-tuple-element.49.q_ref, bf16[4096,256]{1,0:T(8,128)(2,1)} %get-tuple-element.46.k_ref, bf16[256,4096]{1,0:T(8,128)(2,1)} %get-tuple-element.47.vt_ref), custom_call_target="tpu_custom_call" | custom-call | flops 25769803776 | bytes 12582912 | tf_op jit(solution)/shard_map/attention/pallas_call | solution.py:186
  181.9 48.5 %attention.3 = bf16[2048,768]{1,0:T(8,128)(2,1)} custom-call(s32[1]{0:T(128)S(6)} %copy.33.len_ref, bf16[6,4096,128]{2,1,0:T(8,128)(2,1)} %get-tuple-element.49.q_ref, bf16[4096,256]{1,0:T(8,128)(2,1)} %get-tuple-element.46.k_ref, bf16[256,4096]{1,0:T(8,128)(2,1)} %get-tuple-element.47.vt_ref), custom_call_target="tpu_custom_call" | custom-call | flops 77309411328 | bytes 12582912 | tf_op jit(solution)/shard_map/attention/pallas_call | solution.py:186
  236.5 24.0 %collective-permute-start.16 = (bf16[4096,384]{1,0:T(8,128)(2,1)S(1)}, bf16[4096,384]{1,0:T(8,128)(2,1)}, u32[]{:S(2)}, u32[]{:S(2)}) collective-permute-start(bf16[4096,384]{1,0:T(8,128)(2,1)S(1)} %constant_dynamic-update-slice_fusion.4), channel_id=1, source_target_pairs={{0,1},{1,0},{2,3},{3,2},{4,5},{5,4},{6,7},{7,6},{8,9},{9,8},{10,11... | collective-permute-start | bytes 9437192 | tf_op jit(solution)/shard_map/ppermute | solution.py:469
  286.8 17.6 %collective-permute-done.4.refs_2_ = bf16[512,768]{1,0:T(8,128)(2,1)} collective-permute-done((bf16[512,768]{1,0:T(8,128)(2,1)}, bf16[512,768]{1,0:T(8,128)(2,1)}, u32[]{:S(2)}, u32[]{:S(2)}) %collective-permute-start.4) | collective-permute-done | bytes 786464 | tf_op jit(solution)/shard_map/ppermute | solution.py:419
  304.3 20.9 %w_out.2 = (bf16[512,3072]{1,0:T(8,128)(2,1)}, bf16[256,3072]{1,0:T(8,128)(2,1)}, bf16[256,3072]{1,0:T(8,128)(2,1)}) custom-call(s32[1]{0:T(128)} %bitcast.31.idx_ref, bf16[512,768]{1,0:T(8,128)(2,1)} %get-tuple-element.51.refs_0_, bf16[512,768]{1,0:T(8,128)(2,1)} %collective-permute-done.3.refs_1_, bf16[512,768]{1,0:T(8,128)(2,1)} %collective-permute-done.4.refs_2_, ...), custom_call_target="tpu_custom_call" | custom-call | flops 9663676416 | bytes 31457280 | tf_op jit(solution)/shard_map/w_out/pallas_call | solution.py:235
  338.5 20.1 %w_out.3 = (bf16[512,3072]{1,0:T(8,128)(2,1)}, bf16[256,3072]{1,0:T(8,128)(2,1)}, bf16[256,3072]{1,0:T(8,128)(2,1)}) custom-call(s32[1]{0:T(128)} %bitcast.34.idx_ref, bf16[512,768]{1,0:T(8,128)(2,1)} %get-tuple-element.54.refs_0_, bf16[512,768]{1,0:T(8,128)(2,1)} %collective-permute-done.9.refs_1_, bf16[512,768]{1,0:T(8,128)(2,1)} %collective-permute-done.10.refs_2_, ...), custom_call_target="tpu_custom_call" | custom-call | flops 9663676416 | bytes 31457280 | tf_op jit(solution)/shard_map/w_out/pallas_call | solution.py:235
  366.1 41.4 %gate_up.4.refs_0_ = bf16[1024,2560]{1,0:T(8,128)(2,1)} custom-call(bf16[256,3072]{1,0:T(8,128)(2,1)} %get-tuple-element.65.refs_0_, bf16[256,3072]{1,0:T(8,128)(2,1)} %get-tuple-element.57.refs_1_, bf16[256,3072]{1,0:T(8,128)(2,1)} %get-tuple-element.58.refs_2_, bf16[256,3072]{1,0:T(8,128)(2,1)} %get-tuple-element.59.refs_3_, ...), custom_call_target="tpu_custom_call" | custom-call | flops 32212254720 | bytes 42991616 | tf_op jit(solution)/shard_map/gate_up/pallas_call | solution.py:287
  407.6 24.9 %collective-permute-done.13.refs_1_ = bf16[256,3072]{1,0:T(8,128)(2,1)} collective-permute-done((bf16[256,3072]{1,0:T(8,128)(2,1)}, bf16[256,3072]{1,0:T(8,128)(2,1)}, u32[]{:S(2)}, u32[]{:S(2)}) %collective-permute-start.13) | collective-permute-done | bytes 1572896 | tf_op jit(solution)/shard_map/ppermute | solution.py:419
  432.5 41.5 %gate_up.5.refs_0_ = bf16[1024,2560]{1,0:T(8,128)(2,1)} custom-call(bf16[256,3072]{1,0:T(8,128)(2,1)} %collective-permute-done.12.refs_0_, bf16[256,3072]{1,0:T(8,128)(2,1)} %collective-permute-done.13.refs_1_, bf16[256,3072]{1,0:T(8,128)(2,1)} %collective-permute-done.14.refs_2_, bf16[256,3072]{1,0:T(8,128)(2,1)} %collective-permute-done.15.refs_3_, ...), custom_call_target="tpu_custom_call" | custom-call | flops 32212254720 | bytes 42991616 | tf_op jit(solution)/shard_map/gate_up/pallas_call | solution.py:287
  474.0 26.9 %gate_up.6.refs_1_ = bf16[1024,1536]{1,0:T(8,128)(2,1)} custom-call(bf16[256,3072]{1,0:T(8,128)(2,1)} %collective-permute-done.12.refs_0_, bf16[256,3072]{1,0:T(8,128)(2,1)} %collective-permute-done.13.refs_1_, bf16[256,3072]{1,0:T(8,128)(2,1)} %collective-permute-done.14.refs_2_, bf16[256,3072]{1,0:T(8,128)(2,1)} %collective-permute-done.15.refs_3_, ...), custom_call_target="tpu_custom_call" | custom-call | flops 19327352832 | bytes 28311552 | tf_op jit(solution)/shard_map/gate_up/pallas_call | solution.py:287
  500.9 14.3 %down.8 = (bf16[512,768]{1,0:T(8,128)(2,1)}, bf16[512,768]{1,0:T(8,128)(2,1)}) custom-call(s32[9]{0:T(128)} %stack.173.meta_ref, bf16[1024,2560]{1,0:T(8,128)(2,1)} %gate_up.5.refs_0_, bf16[1024,1536]{1,0:T(8,128)(2,1)} %gate_up.6.refs_1_, bf16[4096,768]{1,0:T(8,128)(2,1)} %pad_maximum_fusion.refs_2_), custom_call_target="tpu_custom_call" | custom-call | flops 6442450944 | bytes 9437184 | tf_op jit(solution)/shard_map/down/pallas_call | solution.py:351
  518.2 26.8 %gate_up.7.refs_1_ = bf16[1024,1536]{1,0:T(8,128)(2,1)} custom-call(bf16[256,3072]{1,0:T(8,128)(2,1)} %get-tuple-element.65.refs_0_, bf16[256,3072]{1,0:T(8,128)(2,1)} %get-tuple-element.57.refs_1_, bf16[256,3072]{1,0:T(8,128)(2,1)} %get-tuple-element.58.refs_2_, bf16[256,3072]{1,0:T(8,128)(2,1)} %get-tuple-element.59.refs_3_, ...), custom_call_target="tpu_custom_call" | custom-call | flops 19327352832 | bytes 28311552 | tf_op jit(solution)/shard_map/gate_up/pallas_call | solution.py:287
  545.1 17.3 %down.9.refs_0_ = bf16[1024,768]{1,0:T(8,128)(2,1)} custom-call(s32[9]{0:T(128)} %stack.173.meta_ref, bf16[1024,2560]{1,0:T(8,128)(2,1)} %gate_up.4.refs_0_, bf16[1024,1536]{1,0:T(8,128)(2,1)} %gate_up.7.refs_1_, bf16[4096,768]{1,0:T(8,128)(2,1)} %pad_maximum_fusion.refs_2_, bf16[1024,3072]{1,0:T(8,128)(2,1)} %constant_dynamic-update-slice_fusion.6.refs_3_, ...), custom_call_target="tpu_custom_call" | custom-call | flops 6442450944 | bytes 9437184 | tf_op jit(solution)/shard_map/down/pallas_call | solution.py:351
  562.4 14.2 %down.10 = (bf16[512,768]{1,0:T(8,128)(2,1)}, bf16[512,768]{1,0:T(8,128)(2,1)}) custom-call(s32[9]{0:T(128)} %stack.172.meta_ref, bf16[1024,2560]{1,0:T(8,128)(2,1)} %gate_up.5.refs_0_, bf16[1024,1536]{1,0:T(8,128)(2,1)} %gate_up.6.refs_1_, bf16[4096,1024]{1,0:T(8,128)(2,1)} %all-gather.16.cloned.1.call-done.refs_2_), custom_call_target="tpu_custom_call" | custom-call | flops 6442450944 | bytes 11534336 | tf_op jit(solution)/shard_map/down/pallas_call | solution.py:351
  579.8 14.2 %collective-permute-done.19.refs_4_ = bf16[512,768]{1,0:T(8,128)(2,1)} collective-permute-done((bf16[512,768]{1,0:T(8,128)(2,1)}, bf16[512,768]{1,0:T(8,128)(2,1)}, u32[]{:S(2)}, u32[]{:S(2)}) %collective-permute-start.19) | collective-permute-done | bytes 786464 | tf_op jit(solution)/shard_map/ppermute | solution.py:419
  597.1 16.9 %down.11.refs_0_ = bf16[1024,768]{1,0:T(8,128)(2,1)} custom-call(s32[9]{0:T(128)} %stack.172.meta_ref, bf16[1024,2560]{1,0:T(8,128)(2,1)} %gate_up.4.refs_0_, bf16[1024,1536]{1,0:T(8,128)(2,1)} %gate_up.7.refs_1_, bf16[4096,1024]{1,0:T(8,128)(2,1)} %all-gather.16.cloned.1.call-done.refs_2_, bf16[1024,3072]{1,0:T(8,128)(2,1)} %constant_dynamic-update-slice_fusion.6.refs_3_, ...), custom_call_target="tpu_custom_call" | custom-call | flops 6442450944 | bytes 11534336 | tf_op jit(solution)/shard_map/down/pallas_call | solution.py:351
  614.0 14.3 %down.12 = (bf16[512,768]{1,0:T(8,128)(2,1)}, bf16[512,768]{1,0:T(8,128)(2,1)}) custom-call(s32[9]{0:T(128)} %stack.171.meta_ref, bf16[1024,2560]{1,0:T(8,128)(2,1)} %gate_up.5.refs_0_, bf16[1024,1536]{1,0:T(8,128)(2,1)} %gate_up.6.refs_1_, bf16[4096,1024]{1,0:T(8,128)(2,1)} %all-gather.18.cloned.1.call-done.refs_2_), custom_call_target="tpu_custom_call" | custom-call | flops 6442450944 | bytes 11534336 | tf_op jit(solution)/shard_map/down/pallas_call | solution.py:351
  633.1 11.0 %collective-permute-done.21.refs_4_ = bf16[512,768]{1,0:T(8,128)(2,1)} collective-permute-done((bf16[512,768]{1,0:T(8,128)(2,1)}, bf16[512,768]{1,0:T(8,128)(2,1)}, u32[]{:S(2)}, u32[]{:S(2)}) %collective-permute-start.21) | collective-permute-done | bytes 786464 | tf_op jit(solution)/shard_map/ppermute | solution.py:419
  645.7 16.9 %down.13.refs_0_ = bf16[1024,768]{1,0:T(8,128)(2,1)} custom-call(s32[9]{0:T(128)} %stack.171.meta_ref, bf16[1024,2560]{1,0:T(8,128)(2,1)} %gate_up.4.refs_0_, bf16[1024,1536]{1,0:T(8,128)(2,1)} %gate_up.7.refs_1_, bf16[4096,1024]{1,0:T(8,128)(2,1)} %all-gather.18.cloned.1.call-done.refs_2_, bf16[1024,3072]{1,0:T(8,128)(2,1)} %constant_dynamic-update-slice_fusion.6.refs_3_, ...), custom_call_target="tpu_custom_call" | custom-call | flops 6442450944 | bytes 11534336 | tf_op jit(solution)/shard_map/down/pallas_call | solution.py:351
  662.6 14.3 %down.14 = (bf16[512,768]{1,0:T(8,128)(2,1)}, bf16[512,768]{1,0:T(8,128)(2,1)}) custom-call(s32[9]{0:T(128)} %stack.170.meta_ref, bf16[1024,2560]{1,0:T(8,128)(2,1)} %gate_up.5.refs_0_, bf16[1024,1536]{1,0:T(8,128)(2,1)} %gate_up.6.refs_1_, bf16[4096,1024]{1,0:T(8,128)(2,1)} %all-gather.20.cloned.1.call-done.refs_2_), custom_call_target="tpu_custom_call" | custom-call | flops 6442450944 | bytes 11534336 | tf_op jit(solution)/shard_map/down/pallas_call | solution.py:351
  681.1 10.7 %collective-permute-done.23.refs_4_ = bf16[512,768]{1,0:T(8,128)(2,1)} collective-permute-done((bf16[512,768]{1,0:T(8,128)(2,1)}, bf16[512,768]{1,0:T(8,128)(2,1)}, u32[]{:S(2)}, u32[]{:S(2)}) %collective-permute-start.23) | collective-permute-done | bytes 786464 | tf_op jit(solution)/shard_map/ppermute | solution.py:419
  691.8 21.3 %collective-permute-done.30.refs_1_ = bf16[1024,768]{1,0:T(8,128)(2,1)} collective-permute-done((bf16[1024,768]{1,0:T(8,128)(2,1)}, bf16[1024,768]{1,0:T(8,128)(2,1)}, u32[]{:S(2)}, u32[]{:S(2)}) %collective-permute-start.30) | collective-permute-done | bytes 1572896 | tf_op jit(solution)/shard_map/ppermute | solution.py:419
  717.3 46.4 %collective-permute-done.24.refs_5_ = bf16[512,768]{1,0:T(8,128)(2,1)} collective-permute-done((bf16[512,768]{1,0:T(8,128)(2,1)}, bf16[512,768]{1,0:T(8,128)(2,1)}, u32[]{:S(2)}, u32[]{:S(2)}) %collective-permute-start.24) | collective-permute-done | bytes 786464 | tf_op jit(solution)/shard_map/ppermute | solution.py:419
  763.6 16.7 %collective-permute-done.35.refs_0_ = bf16[512,768]{1,0:T(8,128)(2,1)S(1)} collective-permute-done((bf16[512,768]{1,0:T(8,128)(2,1)S(1)}, bf16[512,768]{1,0:T(8,128)(2,1)S(1)}, u32[]{:S(2)}, u32[]{:S(2)}) %collective-permute-start.35) | collective-permute-done | bytes 786464 | tf_op jit(solution)/shard_map/ppermute | solution.py:419
  781.3 16.9 %down.15.refs_0_ = bf16[1024,768]{1,0:T(8,128)(2,1)} custom-call(s32[9]{0:T(128)} %stack.170.meta_ref, bf16[1024,2560]{1,0:T(8,128)(2,1)} %gate_up.4.refs_0_, bf16[1024,1536]{1,0:T(8,128)(2,1)} %gate_up.7.refs_1_, bf16[4096,1024]{1,0:T(8,128)(2,1)} %all-gather.20.cloned.1.call-done.refs_2_, bf16[1024,3072]{1,0:T(8,128)(2,1)} %constant_dynamic-update-slice_fusion.6.refs_3_, ...), custom_call_target="tpu_custom_call" | custom-call | flops 6442450944 | bytes 11534336 | tf_op jit(solution)/shard_map/down/pallas_call | solution.py:351
  827.5 19.7 %collective-permute-done.33.refs_1_ = bf16[512,768]{1,0:T(8,128)(2,1)} collective-permute-done((bf16[512,768]{1,0:T(8,128)(2,1)}, bf16[512,768]{1,0:T(8,128)(2,1)}, u32[]{:S(2)}, u32[]{:S(2)}) %collective-permute-start.33) | collective-permute-done | bytes 786464 | tf_op jit(solution)/shard_map/ppermute | solution.py:419
  855.9 8.1 collective-permute-done.29.refs_1_
  (158 shorter events, 181.2 us)
Async XLA Ops:
  7.2 81.1 %all-gather.8.cloned.1.call-start = ((), (), s32[]{:S(2)}) async-start(), calls=%async_computation | async-start | bytes 8847360 | tf_op jit(solution)/shard_map/all_gather | solution.py:429
  9.7 294.6 %all-gather.10.cloned.1.call-start = ((), (), s32[]{:S(2)}) async-start(), calls=%async_computation.1 | async-start | bytes 21233664 | tf_op jit(solution)/shard_map/all_gather | solution.py:433
  43.4 322.7 %all-gather.12.cloned.1.call-start = ((), (), s32[]{:S(2)}) async-start(), calls=%async_computation.2 | async-start | bytes 35389440 | tf_op jit(solution)/shard_map/all_gather | solution.py:467
  46.4 86.4 %collective-permute-start = (bf16[384,2560]{1,0:T(8,128)(2,1)}, bf16[384,2560]{1,0:T(8,128)(2,1)}, u32[]{:S(2)}, u32[]{:S(2)}) collective-permute-start(bf16[384,2560]{1,0:T(8,128)(2,1)} %pad_maximum_fusion.4), channel_id=1, source_target_pairs={{0,16},{8,24},{16,0},{24,8},{1,17},{9,25},{17,1},{25,9},{2,18},{10... | collective-permute-start | bytes 5898248 | tf_op jit(solution)/shard_map/ppermute | solution.py:419
  136.1 337.9 %all-gather.14.cloned.1.call-start = ((), (), s32[]{:S(2)}) async-start(), calls=%async_computation.3 | async-start | bytes 21233664 | tf_op jit(solution)/shard_map/all_gather | solution.py:467
  138.4 38.0 %collective-permute-start.1 = (bf16[384,1536]{1,0:T(8,128)(2,1)}, bf16[384,1536]{1,0:T(8,128)(2,1)}, u32[]{:S(2)}, u32[]{:S(2)}) collective-permute-start(bf16[384,1536]{1,0:T(8,128)(2,1)} %pad_maximum_fusion.5), channel_id=1, source_target_pairs={{0,16},{8,24},{16,0},{24,8},{1,17},{9,25},{17,1},{25,9},{2,18},{10... | collective-permute-start | bytes 3538952 | tf_op jit(solution)/shard_map/ppermute | solution.py:419
  179.3 383.0 %all-gather.16.cloned.1.call-start = ((), (), s32[]{:S(2)}) async-start(), calls=%async_computation.4 | async-start | bytes 9437184 | tf_op jit(solution)/shard_map/all_gather | solution.py:471
  179.4 52.6 %collective-permute-start.2 = (bf16[2048,384]{1,0:T(8,128)(2,1)}, bf16[2048,384]{1,0:T(8,128)(2,1)}, u32[]{:S(2)}, u32[]{:S(2)}) collective-permute-start(bf16[2048,384]{1,0:T(8,128)(2,1)} %param.21), channel_id=1, source_target_pairs={{0,16},{8,24},{16,0},{24,8},{1,17},{9,25},{17,1},{25,9},{2,18},{10... | collective-permute-start | bytes 4718600 | tf_op jit(solution)/shard_map/ppermute | solution.py:419
  235.8 378.2 %all-gather.18.cloned.1.call-start = ((), (), s32[]{:S(2)}) async-start(), calls=%async_computation.5 | async-start | bytes 9437184 | tf_op jit(solution)/shard_map/all_gather | solution.py:471
  236.4 426.1 %all-gather.20.cloned.1.call-start = ((), (), s32[]{:S(2)}) async-start(), calls=%async_computation.6 | async-start | bytes 9437184 | tf_op jit(solution)/shard_map/all_gather | solution.py:471
  267.2 37.1 %collective-permute-start.4 = (bf16[512,768]{1,0:T(8,128)(2,1)}, bf16[512,768]{1,0:T(8,128)(2,1)}, u32[]{:S(2)}, u32[]{:S(2)}) collective-permute-start(bf16[512,768]{1,0:T(8,128)(2,1)} %get-tuple-element.91), channel_id=1, source_target_pairs={{0,16},{8,24},{16,0},{24,8},{1,17},{9,25},{17,1},{25,9},{2,18},{10... | collective-permute-start | bytes 2359304 | tf_op jit(solution)/shard_map/ppermute | solution.py:419
  271.4 59.6 %collective-permute-start.10 = (bf16[512,768]{1,0:T(8,128)(2,1)}, bf16[512,768]{1,0:T(8,128)(2,1)}, u32[]{:S(2)}, u32[]{:S(2)}) collective-permute-start(bf16[512,768]{1,0:T(8,128)(2,1)} %get-tuple-element.87), channel_id=1, source_target_pairs={{0,16},{8,24},{16,0},{24,8},{1,17},{9,25},{17,1},{25,9},{2,18},{10... | collective-permute-start | bytes 2359304 | tf_op jit(solution)/shard_map/ppermute | solution.py:419
  273.0 64.5 %collective-permute-start.11 = (bf16[512,768]{1,0:T(8,128)(2,1)}, bf16[512,768]{1,0:T(8,128)(2,1)}, u32[]{:S(2)}, u32[]{:S(2)}) collective-permute-start(bf16[512,768]{1,0:T(8,128)(2,1)} %get-tuple-element.86), channel_id=1, source_target_pairs={{0,24},{8,0},{16,8},{24,16},{1,25},{9,1},{17,9},{25,17},{2,26},{10... | collective-permute-start | bytes 2359304 | tf_op jit(solution)/shard_map/ppermute | solution.py:419
  286.6 51.9 %collective-permute-start.9 = (bf16[512,768]{1,0:T(8,128)(2,1)}, bf16[512,768]{1,0:T(8,128)(2,1)}, u32[]{:S(2)}, u32[]{:S(2)}) collective-permute-start(bf16[512,768]{1,0:T(8,128)(2,1)} %get-tuple-element.88), channel_id=1, source_target_pairs={{0,8},{8,16},{16,24},{24,0},{1,9},{9,17},{17,25},{25,1},{2,10},{10... | collective-permute-start | bytes 2359304 | tf_op jit(solution)/shard_map/ppermute | solution.py:419
  325.3 82.3 %collective-permute-start.12 = (bf16[256,3072]{1,0:T(8,128)(2,1)}, bf16[256,3072]{1,0:T(8,128)(2,1)}, u32[]{:S(2)}, u32[]{:S(2)}) collective-permute-start(bf16[256,3072]{1,0:T(8,128)(2,1)} %get-tuple-element.65.refs_0_), channel_id=1, source_target_pairs={{0,8},{8,16},{16,24},{24,0},{1,9},{9,17},{17,25},{25,1},{2,10},{10... | collective-permute-start | bytes 4718600 | tf_op jit(solution)/shard_map/ppermute | solution.py:419
  362.4 45.2 %collective-permute-start.14 = (bf16[256,3072]{1,0:T(8,128)(2,1)}, bf16[256,3072]{1,0:T(8,128)(2,1)}, u32[]{:S(2)}, u32[]{:S(2)}) collective-permute-start(bf16[256,3072]{1,0:T(8,128)(2,1)} %get-tuple-element.58.refs_2_), channel_id=1, source_target_pairs={{0,8},{8,16},{16,24},{24,0},{1,9},{9,17},{17,25},{25,1},{2,10},{10... | collective-permute-start | bytes 4718600 | tf_op jit(solution)/shard_map/ppermute | solution.py:419
  363.1 44.5 %collective-permute-start.15 = (bf16[256,3072]{1,0:T(8,128)(2,1)}, bf16[256,3072]{1,0:T(8,128)(2,1)}, u32[]{:S(2)}, u32[]{:S(2)}) collective-permute-start(bf16[256,3072]{1,0:T(8,128)(2,1)} %get-tuple-element.59.refs_3_), channel_id=1, source_target_pairs={{0,24},{8,0},{16,8},{24,16},{1,25},{9,1},{17,9},{25,17},{2,26},{10... | collective-permute-start | bytes 4718600 | tf_op jit(solution)/shard_map/ppermute | solution.py:419
  365.1 67.4 %collective-permute-start.13 = (bf16[256,3072]{1,0:T(8,128)(2,1)}, bf16[256,3072]{1,0:T(8,128)(2,1)}, u32[]{:S(2)}, u32[]{:S(2)}) collective-permute-start(bf16[256,3072]{1,0:T(8,128)(2,1)} %get-tuple-element.57.refs_1_), channel_id=1, source_target_pairs={{0,24},{8,0},{16,8},{24,16},{1,25},{9,1},{17,9},{25,17},{2,26},{10... | collective-permute-start | bytes 4718600 | tf_op jit(solution)/shard_map/ppermute | solution.py:419
  630.4 48.9 %collective-permute-start.34 = (bf16[1024,768]{1,0:T(8,128)(2,1)}, bf16[1024,768]{1,0:T(8,128)(2,1)}, u32[]{:S(2)}, u32[]{:S(2)}) collective-permute-start(bf16[1024,768]{1,0:T(8,128)(2,1)} %down.9.refs_0_), channel_id=1, source_target_pairs={{0,8},{8,16},{16,24},{24,0},{1,9},{9,17},{17,25},{25,1},{2,10},{10... | collective-permute-start | bytes 4718600 | tf_op jit(solution)/shard_map/ppermute | solution.py:419
  630.5 50.1 %collective-permute-start.36 = (bf16[1024,768]{1,0:T(8,128)(2,1)}, bf16[1024,768]{1,0:T(8,128)(2,1)}, u32[]{:S(2)}, u32[]{:S(2)}) collective-permute-start(bf16[1024,768]{1,0:T(8,128)(2,1)} %down.9.refs_0_), channel_id=1, source_target_pairs={{0,24},{8,0},{16,8},{24,16},{1,25},{9,1},{17,9},{25,17},{2,26},{10... | collective-permute-start | bytes 4718600 | tf_op jit(solution)/shard_map/ppermute | solution.py:419
  633.1 80.0 %collective-permute-start.30 = (bf16[1024,768]{1,0:T(8,128)(2,1)}, bf16[1024,768]{1,0:T(8,128)(2,1)}, u32[]{:S(2)}, u32[]{:S(2)}) collective-permute-start(bf16[1024,768]{1,0:T(8,128)(2,1)} %down.11.refs_0_), channel_id=1, source_target_pairs={{0,8},{8,16},{16,24},{24,0},{1,9},{9,17},{17,25},{25,1},{2,10},{10... | collective-permute-start | bytes 4718600 | tf_op jit(solution)/shard_map/ppermute | solution.py:419
  677.2 121.0 %collective-permute-start.32 = (bf16[1024,768]{1,0:T(8,128)(2,1)}, bf16[1024,768]{1,0:T(8,128)(2,1)}, u32[]{:S(2)}, u32[]{:S(2)}) collective-permute-start(bf16[1024,768]{1,0:T(8,128)(2,1)} %down.11.refs_0_), channel_id=1, source_target_pairs={{0,24},{8,0},{16,8},{24,16},{1,25},{9,1},{17,9},{25,17},{2,26},{10... | collective-permute-start | bytes 4718600 | tf_op jit(solution)/shard_map/ppermute | solution.py:419
  679.4 121.5 %collective-permute-start.26 = (bf16[1024,768]{1,0:T(8,128)(2,1)}, bf16[1024,768]{1,0:T(8,128)(2,1)}, u32[]{:S(2)}, u32[]{:S(2)}) collective-permute-start(bf16[1024,768]{1,0:T(8,128)(2,1)} %down.13.refs_0_), channel_id=1, source_target_pairs={{0,8},{8,16},{16,24},{24,0},{1,9},{9,17},{17,25},{25,1},{2,10},{10... | collective-permute-start | bytes 4718600 | tf_op jit(solution)/shard_map/ppermute | solution.py:419
  680.6 83.1 %collective-permute-start.24 = (bf16[512,768]{1,0:T(8,128)(2,1)}, bf16[512,768]{1,0:T(8,128)(2,1)}, u32[]{:S(2)}, u32[]{:S(2)}) collective-permute-start(bf16[512,768]{1,0:T(8,128)(2,1)} %get-tuple-element.78), channel_id=1, source_target_pairs={{0,8},{8,16},{16,24},{24,0},{1,9},{9,17},{17,25},{25,1},{2,10},{10... | collective-permute-start | bytes 2359304 | tf_op jit(solution)/shard_map/ppermute | solution.py:419
  691.8 88.6 %collective-permute-start.35 = (bf16[512,768]{1,0:T(8,128)(2,1)S(1)}, bf16[512,768]{1,0:T(8,128)(2,1)S(1)}, u32[]{:S(2)}, u32[]{:S(2)}) collective-permute-start(bf16[512,768]{1,0:T(8,128)(2,1)S(1)} %slice.67), channel_id=1, source_target_pairs={{0,8},{8,16},{16,24},{24,0},{1,9},{9,17},{17,25},{25,1},{2,10},{10... | collective-permute-start | bytes 2359304 | tf_op jit(solution)/shard_map/ppermute | solution.py:419
  713.1 90.0 %collective-permute-start.28 = (bf16[1024,768]{1,0:T(8,128)(2,1)}, bf16[1024,768]{1,0:T(8,128)(2,1)}, u32[]{:S(2)}, u32[]{:S(2)}) collective-permute-start(bf16[1024,768]{1,0:T(8,128)(2,1)} %down.13.refs_0_), channel_id=1, source_target_pairs={{0,24},{8,0},{16,8},{24,16},{1,25},{9,1},{17,9},{25,17},{2,26},{10... | collective-permute-start | bytes 4718600 | tf_op jit(solution)/shard_map/ppermute | solution.py:419
  763.6 46.2 %collective-permute-start.37 = (bf16[512,768]{1,0:T(8,128)(2,1)}, bf16[512,768]{1,0:T(8,128)(2,1)}, u32[]{:S(2)}, u32[]{:S(2)}) collective-permute-start(bf16[512,768]{1,0:T(8,128)(2,1)} %slice.68), channel_id=1, source_target_pairs={{0,24},{8,0},{16,8},{24,16},{1,25},{9,1},{17,9},{25,17},{2,26},{10... | collective-permute-start | bytes 2359304 | tf_op jit(solution)/shard_map/ppermute | solution.py:419
  798.2 69.0 %collective-permute-start.39 = (bf16[1024,768]{1,0:T(8,128)(2,1)}, bf16[1024,768]{1,0:T(8,128)(2,1)}, u32[]{:S(2)}, u32[]{:S(2)}) collective-permute-start(bf16[1024,768]{1,0:T(8,128)(2,1)} %down.15.refs_0_), channel_id=1, source_target_pairs={{0,24},{8,0},{16,8},{24,16},{1,25},{9,1},{17,9},{25,17},{2,26},{10... | collective-permute-start | bytes 4718600 | tf_op jit(solution)/shard_map/ppermute | solution.py:419
  800.9 66.4 %collective-permute-start.25 = (bf16[1024,768]{1,0:T(8,128)(2,1)}, bf16[1024,768]{1,0:T(8,128)(2,1)}, u32[]{:S(2)}, u32[]{:S(2)}) collective-permute-start(bf16[1024,768]{1,0:T(8,128)(2,1)} %down.15.refs_0_), channel_id=1, source_target_pairs={{0,8},{8,16},{16,24},{24,0},{1,9},{9,17},{17,25},{25,1},{2,10},{10... | collective-permute-start | bytes 4718600 | tf_op jit(solution)/shard_map/ppermute | solution.py:419
  803.0 44.1 %collective-permute-start.33 = (bf16[512,768]{1,0:T(8,128)(2,1)}, bf16[512,768]{1,0:T(8,128)(2,1)}, u32[]{:S(2)}, u32[]{:S(2)}) collective-permute-start(bf16[512,768]{1,0:T(8,128)(2,1)} %slice.66), channel_id=1, source_target_pairs={{0,24},{8,0},{16,8},{24,16},{1,25},{9,1},{17,9},{25,17},{2,26},{10... | collective-permute-start | bytes 2359304 | tf_op jit(solution)/shard_map/ppermute | solution.py:419
  809.9 46.0 %collective-permute-start.27 = (bf16[512,768]{1,0:T(8,128)(2,1)}, bf16[512,768]{1,0:T(8,128)(2,1)}, u32[]{:S(2)}, u32[]{:S(2)}) collective-permute-start(bf16[512,768]{1,0:T(8,128)(2,1)} %slice.63), channel_id=1, source_target_pairs={{0,8},{8,16},{16,24},{24,0},{1,9},{9,17},{17,25},{25,1},{2,10},{10... | collective-permute-start | bytes 2359304 | tf_op jit(solution)/shard_map/ppermute | solution.py:419
  809.9 54.1 %collective-permute-start.29 = (bf16[512,768]{1,0:T(8,128)(2,1)}, bf16[512,768]{1,0:T(8,128)(2,1)}, u32[]{:S(2)}, u32[]{:S(2)}) collective-permute-start(bf16[512,768]{1,0:T(8,128)(2,1)} %slice.64), channel_id=1, source_target_pairs={{0,24},{8,0},{16,8},{24,16},{1,25},{9,1},{17,9},{25,17},{2,26},{10... | collective-permute-start | bytes 2359304 | tf_op jit(solution)/shard_map/ppermute | solution.py:419
  (28 other events, 418.1 us)
Sparse Core Ops, SparseCore 0:
  9.8 49.2 all-gather.7
  60.7 91.0 all-gather.9
  153.3 145.2 all-gather.11
  300.0 92.0 all-gather.13
  393.6 51.5 all-gather.15
  446.6 51.8 all-gather.17
  500.1 51.7 all-gather.19

commit v7 on v6

--- a/solution.py
+++ b/solution.py
@@ -44,7 +44,7 @@
 
 def norm_call(x, gain):
     s, d = x.shape
-    bm = min(256, s)
+    bm = min(512, s)
     return pl.pallas_call(
         norm_kernel,
         grid=(s // bm,),
@@ -334,22 +334,22 @@
                     rest[h][out, :] = acc.astype(jnp.bfloat16)
 
 
-def down_call(a_parts, w, meta, n_src, bn, steps, resid=None, partials=()):
+def down_call(a_parts, w, meta, n_src, bn, steps, rows, call=0, resid=None, partials=()):
     parts = len(a_parts)
-    rows = a_parts[0].shape[0]
     cols = steps * bn
     own = resid is not None
-    fixed = lambda n, meta: (0, 0)
+    half = rows // 2
     step = lambda n, meta: (0, n)
     once = dict(pipeline_mode=pl.Buffered(1))
     args = [*a_parts, w]
-    in_specs = [pl.BlockSpec(a.shape, fixed, **once) for a in a_parts] + [pl.BlockSpec((w.shape[0], bn), lambda n, meta: (0, meta[n]))]
+    in_specs = [pl.BlockSpec((rows, a.shape[1]), lambda n, meta, b=(call if a.shape[0] > rows else 0): (b, 0), **once) for a in a_parts]
+    in_specs += [pl.BlockSpec((w.shape[0], bn), lambda n, meta: (0, meta[n]))]
     if own:
         args += [resid, *partials]
-        in_specs += [pl.BlockSpec(resid.shape, fixed, **once)] + [pl.BlockSpec((rows // 2, bn), step)] * 2
+        in_specs += [pl.BlockSpec(resid.shape, lambda n, meta: (0, 0), **once)] + [pl.BlockSpec((half, bn), lambda n, meta: (call, n))] * 2
     n_out = 1 if own else 2
     return pl.pallas_call(
-        functools.partial(down_kernel, rows // (2 * N_CALLS), parts, n_src, own),
+        functools.partial(down_kernel, half if own else half // N_CALLS, parts, n_src, own),
         grid_spec=pltpu.PrefetchScalarGridSpec(
             num_scalar_prefetch=1, grid=(steps,), in_specs=in_specs, out_specs=[pl.BlockSpec((rows // n_out, bn), step)] * n_out),
         out_shape=[jax.ShapeDtypeStruct((rows // n_out, cols), jnp.bfloat16)] * n_out,
@@ -483,15 +483,14 @@
             u_prev.append(shift(ua, 1))
             u_next.append(shift(ub, -1))
         u_recv = [u_prev[0], u_next[0], u_prev[1], u_next[1]]
-        resid = jnp.concatenate(resid, axis=0)
-
-        def gate_up(p, who, dep):
-            us = (u_own, u_recv)[who]
+
+        def gate_up(p, us, dep):
             return gu_call([after(us[0], dep)] + us[1:], gu_full[p], n_src)
 
-        a_own = [gate_up(0, 0, resid)]
-        a_recv = [gate_up(0, 1, a_own[0])]
-        a_recv.append(gate_up(1, 1, a_recv[0]))
+        a_own = gate_up(0, u_own, resid[-1])
+        a_recv = [gate_up(0, u_recv, a_own)]
+        a_recv.append(gate_up(1, u_recv, a_recv[0]))
+        a_late = []
 
         fs = lax.axis_index('fsdp')
         chip, n_chip = fs // 2, n_fs // 2
@@ -505,29 +504,36 @@
         mine = []
         for b, (w, sel, units) in enumerate(blocks):
             meta = jnp.stack([jnp.asarray(v, jnp.int32) for v in [*sel, *units]])
-            p_prev, p_next = down_call([after(a_recv[0], order), a_recv[1]], w, meta, n_src, bn, len(sel))
+            p_prev, p_next = down_call([after(a_recv[0], order), a_recv[1]], w, meta, n_src, bn, len(sel), N_CALLS * sub)
             b_next = shift(p_prev, -1)
             b_prev = shift(p_next, 1)
-            if b == 0:
-                a_own.append(gate_up(1, 0, p_prev))
-            m, = down_call([after(a_own[0], p_prev), a_own[1]], w, meta, n_src, bn, len(sel), resid, (b_next, b_prev))
-            order = m
-            near = {}
-            for g, by in enumerate((1, -1)):
-                near[g] = shift(m, by)
+            order = p_prev
+            m, near = [], {}
+            for c in range(N_CALLS):
+                if b == 0:
+                    a_late.append(gate_up(1, u_own[2 * c:2 * c + 2], order))
+                    order = a_late[c]
+                m += down_call([after(a_own, order), a_late[c]], w, meta, n_src, bn, len(sel), sub, c, resid[c], (b_next, b_prev))
+                order = m[c]
+                for g, by in enumerate((1, -1)):
+                    near[g, c] = shift(m[c], by)
             mine.append((m, near))
         idx = jnp.stack([jnp.asarray(v, jnp.int32) for v in [(me - s) % n_tp for s in range(n_tp)] + sum((u for _, _, u in blocks), [])])
-        near_moves = [(i, c * sub, sub, c, who) for i, who in enumerate((0, 1, n_tp - 1)) for c in range(N_CALLS)]
+        near_moves = [(i * N_CALLS + c, 0, sub, c, who) for i, who in enumerate((0, 1, n_tp - 1)) for c in range(N_CALLS)]
         far_moves = [(0, 0, sub, 0, 2), (1, 0, sub, N_CALLS - 1, 2)]
         hidden = None
         skip = 0
         last = len(blocks) - 1
         for b in range(len(blocks)):
             m, near = mine[b]
-            src = (near[0], near[1]) if b < last else (after(near[0], hidden), after(near[1], hidden))
-            far_0 = shift(src[0][:sub], 1)
-            far_1 = shift(src[1][sub:], -1)
-            pieces = [after(m, order) if b == 0 else m, near[0], near[1]]
+            src = (near[0, 0], near[1, N_CALLS - 1])
+            if b == last:
+                src = tuple(after(v, hidden) for v in src)
+            far_0 = shift(src[0], 1)
+            far_1 = shift(src[1], -1)
+            pieces = [*m, *(near[g, c] for g in range(2) for c in range(N_CALLS))]
+            if b == 0:
+                pieces[0] = after(pieces[0], order)
             hidden = place_call(idx, pieces, near_moves, (seq, d), n_tp, skip, hidden)
             hidden = place_call(idx, (far_0, far_1), far_moves, (seq, d), n_tp, skip, hidden)
             skip += len(blocks[b][2])

time: 914 us -> 875 us (0.957)
  waiting for transfers between devices: 239 us -> 198 us
  local copies, waits for them, and re-layouts: 58.3 us -> 33.9 us
  Pallas kernels: 491 us -> 507 us
    ppermute x40 -> x48, waiting for transfers between devices: 239 us -> 197 us  [shift(): return lax.ppermute(val, tp, [(i, (i + s) % n_tp) for i in range(n_tp)])]
    slice x8 -> x0, local copies, waits for them, and re-layouts: 15.8 us -> none  [the longest x4 8.4 us: local_layer(): far_1 = shift(src[1][sub:], -1)]
    pallas_call x8 -> x12, Pallas kernels: 125 us -> 140 us  [down_call(): pl.pallas_call(functools.partial(down_kernel, half if own else half // N_...]
    ppermute x40 -> x48, starting transfers between devices: 47.3 us -> 55.5 us  [shift(): return lax.ppermute(val, tp, [(i, (i + s) % n_tp) for i in range(n_tp)])]
    pallas_call x4 -> x5, Pallas kernels: 137 us -> 142 us  [gu_call(): pl.pallas_call(functools.partial(gu_kernel, bm, n_u), grid=(n_src, nb), i...]
  transfers between devices with their start and end apart: 48 -> 56, of which waited for: 19 -> 27; matrix products, arithmetic and copies ran while one was open for 8% -> 6% of each run, Pallas kernels for 54% -> 59%
where the time goes in v7:
time: 875 us; the launch traced here: 859 us
  Pallas kernels  507 us (58%)
  waiting for transfers between devices  198 us (23%)
  starting transfers between devices  80.4 us (9%)
  local copies, waits for them, and re-layouts  33.9 us (4%)
  other arithmetic  23.6 us (3%)
  between operations  15.4 us (2%)
    ppermute x48, waiting for transfers between devices, shift(): return lax.ppermute(val, tp, [(i, (i + s) % n_tp) for i in range(n_tp)])  197 us
    pallas_call x5, Pallas kernels, gu_call(): pl.pallas_call(functools.partial(gu_kernel, bm, n_u), grid=(n_src, nb), i...  142 us
    pallas_call x12, Pallas kernels, down_call(): pl.pallas_call(functools.partial(down_kernel, half if own else half // N_...  140 us
    pallas_call x2, Pallas kernels, att_call(): pl.pallas_call(functools.partial(att_kernel, bq, bk, per, first), grid=(n...  83.8 us
    ppermute x48, starting transfers between devices, shift(): return lax.ppermute(val, tp, [(i, (i + s) % n_tp) for i in range(n_tp)])  55.5 us
    pallas_call x1, Pallas kernels, qkv_call(): pl.pallas_call(functools.partial(qkv_kernel, n_q, n_kv), grid=(s // bm,),...  41.3 us
    pallas_call x2, Pallas kernels, out_call(): pl.pallas_call(functools.partial(out_kernel, n_src), grid_spec=pltpu.Pref...  40.8 us
    pallas_call x8, Pallas kernels, place_call(): pl.pallas_call(functools.partial(place_kernel, n_in, moves, n_tp, skip),...  34.8 us
  transfers between devices with their start and end apart: 56, of which 27 were waited for; matrix products, arithmetic and copies ran while one was open for 6% of the time, Pallas kernels for 59%

profile of v7, /device:TPU:97, one launch (start us, length us, event | category | flops | bytes accessed | tf_op | source)
XLA Modules:
  0.0 858.8 jit_solution(8192594219623857094)
XLA Ops:
  16.7 11.5 %collective-permute-done.6 = bf16[768,384]{1,0:T(8,128)(2,1)S(1)} collective-permute-done((bf16[768,384]{1,0:T(8,128)(2,1)S(1)}, bf16[768,384]{1,0:T(8,128)(2,1)S(1)}, u32[]{:S(2)}, u32[]{:S(2)}) %collective-permute-start.6) | collective-permute-done | bytes 589856 | tf_op jit(solution)/shard_map/ppermute | solution.py:419
  28.2 13.4 %collective-permute-done.7 = bf16[768,384]{1,0:T(8,128)(2,1)S(1)} collective-permute-done((bf16[768,384]{1,0:T(8,128)(2,1)S(1)}, bf16[768,384]{1,0:T(8,128)(2,1)S(1)}, u32[]{:S(2)}, u32[]{:S(2)}) %collective-permute-start.7) | collective-permute-done | bytes 589856 | tf_op jit(solution)/shard_map/ppermute | solution.py:419
  49.1 24.4 %norm.1.h_ref = bf16[4096,3072]{1,0:T(8,128)(2,1)} custom-call(bf16[4096,3072]{1,0:T(8,128)(2,1)} %bitcast.37, bf16[1,3072]{1,0:T(2,128)(2,1)} %reshape.63.g_ref), custom_call_target="tpu_custom_call" | custom-call | flops 100663296 | bytes 50331648 | tf_op jit(solution)/shard_map/norm/pallas_call | solution.py:48
  84.9 41.3 %qkv.1 = (bf16[6,4096,128]{2,1,0:T(8,128)(2,1)}, bf16[4096,256]{1,0:T(8,128)(2,1)}, bf16[4096,256]{1,0:T(8,128)(2,1)}, bf16[256,4096]{1,0:T(8,128)(2,1)}) custom-call(bf16[4096,3072]{1,0:T(8,128)(2,1)} %norm.1.h_ref, bf16[3072,1280]{1,0:T(8,128)(2,1)} %all-gather.8.cloned.1.call-done.w_ref, f32[4096,128]{1,0:T(8,128)} %get-tuple-element.107.cos_ref, ...), custom_call_target="tpu_custom_call" | custom-call | flops 32212254720 | bytes 43515904 | tf_op jit(solution)/shard_map/qkv/pallas_call | solution.py:85
  136.2 35.4 %attention.2 = bf16[2048,768]{1,0:T(8,128)(2,1)} custom-call(s32[1]{0:T(128)S(6)} %copy.32.len_ref, bf16[6,4096,128]{2,1,0:T(8,128)(2,1)} %get-tuple-element.54.q_ref, bf16[4096,256]{1,0:T(8,128)(2,1)} %get-tuple-element.51.k_ref, bf16[256,4096]{1,0:T(8,128)(2,1)} %get-tuple-element.52.vt_ref), custom_call_target="tpu_custom_call" | custom-call | flops 25769803776 | bytes 12582912 | tf_op jit(solution)/shard_map/attention/pallas_call | solution.py:186
  178.2 48.4 %attention.3 = bf16[2048,768]{1,0:T(8,128)(2,1)} custom-call(s32[1]{0:T(128)S(6)} %copy.32.len_ref, bf16[6,4096,128]{2,1,0:T(8,128)(2,1)} %get-tuple-element.54.q_ref, bf16[4096,256]{1,0:T(8,128)(2,1)} %get-tuple-element.51.k_ref, bf16[256,4096]{1,0:T(8,128)(2,1)} %get-tuple-element.52.vt_ref), custom_call_target="tpu_custom_call" | custom-call | flops 77309411328 | bytes 12582912 | tf_op jit(solution)/shard_map/attention/pallas_call | solution.py:186
  232.7 24.3 %collective-permute-start.16 = (bf16[4096,384]{1,0:T(8,128)(2,1)S(1)}, bf16[4096,384]{1,0:T(8,128)(2,1)}, u32[]{:S(2)}, u32[]{:S(2)}) collective-permute-start(bf16[4096,384]{1,0:T(8,128)(2,1)S(1)} %constant_dynamic-update-slice_fusion.4), channel_id=1, source_target_pairs={{0,1},{1,0},{2,3},{3,2},{4,5},{5,4},{6,7},{7,6},{8,9},{9,8},{10,11... | collective-permute-start | bytes 9437192 | tf_op jit(solution)/shard_map/ppermute | solution.py:469
  283.2 16.7 %collective-permute-done.4.refs_2_ = bf16[512,768]{1,0:T(8,128)(2,1)} collective-permute-done((bf16[512,768]{1,0:T(8,128)(2,1)}, bf16[512,768]{1,0:T(8,128)(2,1)}, u32[]{:S(2)}, u32[]{:S(2)}) %collective-permute-start.4) | collective-permute-done | bytes 786464 | tf_op jit(solution)/shard_map/ppermute | solution.py:419
  300.3 20.7 %w_out.2 = (bf16[512,3072]{1,0:T(8,128)(2,1)}, bf16[256,3072]{1,0:T(8,128)(2,1)}, bf16[256,3072]{1,0:T(8,128)(2,1)}) custom-call(s32[1]{0:T(128)} %bitcast.31.idx_ref, bf16[512,768]{1,0:T(8,128)(2,1)} %get-tuple-element.56.refs_0_, bf16[512,768]{1,0:T(8,128)(2,1)} %collective-permute-done.3.refs_1_, bf16[512,768]{1,0:T(8,128)(2,1)} %collective-permute-done.4.refs_2_, ...), custom_call_target="tpu_custom_call" | custom-call | flops 9663676416 | bytes 31457280 | tf_op jit(solution)/shard_map/w_out/pallas_call | solution.py:235
  322.9 11.0 %collective-permute-done.11.refs_3_ = bf16[512,768]{1,0:T(8,128)(2,1)} collective-permute-done((bf16[512,768]{1,0:T(8,128)(2,1)}, bf16[512,768]{1,0:T(8,128)(2,1)}, u32[]{:S(2)}, u32[]{:S(2)}) %collective-permute-start.11) | collective-permute-done | bytes 786464 | tf_op jit(solution)/shard_map/ppermute | solution.py:419
  334.2 20.0 %w_out.3 = (bf16[512,3072]{1,0:T(8,128)(2,1)}, bf16[256,3072]{1,0:T(8,128)(2,1)}, bf16[256,3072]{1,0:T(8,128)(2,1)}) custom-call(s32[1]{0:T(128)} %bitcast.34.idx_ref, bf16[512,768]{1,0:T(8,128)(2,1)} %get-tuple-element.59.refs_0_, bf16[512,768]{1,0:T(8,128)(2,1)} %collective-permute-done.9.refs_1_, bf16[512,768]{1,0:T(8,128)(2,1)} %collective-permute-done.10.refs_2_, ...), custom_call_target="tpu_custom_call" | custom-call | flops 9663676416 | bytes 31457280 | tf_op jit(solution)/shard_map/w_out/pallas_call | solution.py:235
  358.5 41.6 %gate_up.5.refs_0_ = bf16[1024,2560]{1,0:T(8,128)(2,1)} custom-call(bf16[256,3072]{1,0:T(8,128)(2,1)} %get-tuple-element.69.refs_0_, bf16[256,3072]{1,0:T(8,128)(2,1)} %get-tuple-element.62.refs_1_, bf16[256,3072]{1,0:T(8,128)(2,1)} %get-tuple-element.72.refs_2_.refs_0_, bf16[256,3072]{1,0:T(8,128)(2,1)} %get-tuple-element.64.refs_3_.refs_1_, ...), custom_call_target="tpu_custom_call" | custom-call | flops 32212254720 | bytes 42991616 | tf_op jit(solution)/shard_map/gate_up/pallas_call | solution.py:287
  401.6 22.8 %collective-permute-done.13.refs_1_ = bf16[256,3072]{1,0:T(8,128)(2,1)} collective-permute-done((bf16[256,3072]{1,0:T(8,128)(2,1)}, bf16[256,3072]{1,0:T(8,128)(2,1)}, u32[]{:S(2)}, u32[]{:S(2)}) %collective-permute-start.13) | collective-permute-done | bytes 1572896 | tf_op jit(solution)/shard_map/ppermute | solution.py:419
  424.3 41.4 %gate_up.6.refs_0_ = bf16[1024,2560]{1,0:T(8,128)(2,1)} custom-call(bf16[256,3072]{1,0:T(8,128)(2,1)} %collective-permute-done.12.refs_0_, bf16[256,3072]{1,0:T(8,128)(2,1)} %collective-permute-done.13.refs_1_, bf16[256,3072]{1,0:T(8,128)(2,1)} %collective-permute-done.14.refs_2_, bf16[256,3072]{1,0:T(8,128)(2,1)} %collective-permute-done.15.refs_3_, ...), custom_call_target="tpu_custom_call" | custom-call | flops 32212254720 | bytes 42991616 | tf_op jit(solution)/shard_map/gate_up/pallas_call | solution.py:287
  465.8 26.8 %gate_up.7.refs_1_ = bf16[1024,1536]{1,0:T(8,128)(2,1)} custom-call(bf16[256,3072]{1,0:T(8,128)(2,1)} %collective-permute-done.12.refs_0_, bf16[256,3072]{1,0:T(8,128)(2,1)} %collective-permute-done.13.refs_1_, bf16[256,3072]{1,0:T(8,128)(2,1)} %collective-permute-done.14.refs_2_, bf16[256,3072]{1,0:T(8,128)(2,1)} %collective-permute-done.15.refs_3_, ...), custom_call_target="tpu_custom_call" | custom-call | flops 19327352832 | bytes 28311552 | tf_op jit(solution)/shard_map/gate_up/pallas_call | solution.py:287
  492.6 14.7 %down.12 = (bf16[512,768]{1,0:T(8,128)(2,1)}, bf16[512,768]{1,0:T(8,128)(2,1)}) custom-call(s32[9]{0:T(128)} %stack.173.meta_ref, bf16[1024,2560]{1,0:T(8,128)(2,1)} %gate_up.6.refs_0_, bf16[1024,1536]{1,0:T(8,128)(2,1)} %gate_up.7.refs_1_, bf16[4096,768]{1,0:T(8,128)(2,1)} %pad_maximum_fusion.refs_2_), custom_call_target="tpu_custom_call" | custom-call | flops 6442450944 | bytes 9437184 | tf_op jit(solution)/shard_map/down/pallas_call | solution.py:351
  510.3 16.3 %gate_up.8.refs_1_ = bf16[512,1536]{1,0:T(8,128)(2,1)} custom-call(bf16[256,3072]{1,0:T(8,128)(2,1)} %get-tuple-element.69.refs_0_, bf16[256,3072]{1,0:T(8,128)(2,1)} %get-tuple-element.62.refs_1_, bf16[3072,3072]{1,0:T(8,128)(2,1)} %all-gather.14.cloned.1.call-done.refs_4_.refs_5_.refs_2_.refs_3_, ...), custom_call_target="tpu_custom_call" | custom-call | flops 9663676416 | bytes 23592960 | tf_op jit(solution)/shard_map/gate_up/pallas_call | solution.py:287
  528.4 10.3 %down.13.refs_0_ = bf16[512,768]{1,0:T(8,128)(2,1)} custom-call(s32[9]{0:T(128)} %stack.173.meta_ref, bf16[1024,2560]{1,0:T(8,128)(2,1)} %gate_up.5.refs_0_, bf16[512,1536]{1,0:T(8,128)(2,1)} %gate_up.8.refs_1_, bf16[4096,768]{1,0:T(8,128)(2,1)} %pad_maximum_fusion.refs_2_, bf16[512,3072]{1,0:T(8,128)(2,1)} %get-tuple-element.58.refs_3_, ...), custom_call_target="tpu_custom_call" | custom-call | flops 3221225472 | bytes 7864320 | tf_op jit(solution)/shard_map/down/pallas_call | solution.py:351
  538.7 16.3 %gate_up.9.refs_1_ = bf16[512,1536]{1,0:T(8,128)(2,1)} custom-call(bf16[256,3072]{1,0:T(8,128)(2,1)} %get-tuple-element.72.refs_2_.refs_0_, bf16[256,3072]{1,0:T(8,128)(2,1)} %get-tuple-element.64.refs_3_.refs_1_, bf16[3072,3072]{1,0:T(8,128)(2,1)} %all-gather.14.cloned.1.call-done.refs_4_.refs_5_.refs_2_.refs_3_, ...), custom_call_target="tpu_custom_call" | custom-call | flops 9663676416 | bytes 23592960 | tf_op jit(solution)/shard_map/gate_up/pallas_call | solution.py:287
  555.0 10.3 %down.14.refs_1_ = bf16[512,768]{1,0:T(8,128)(2,1)} custom-call(s32[9]{0:T(128)} %stack.173.meta_ref, bf16[1024,2560]{1,0:T(8,128)(2,1)} %gate_up.5.refs_0_, bf16[512,1536]{1,0:T(8,128)(2,1)} %gate_up.9.refs_1_, bf16[4096,768]{1,0:T(8,128)(2,1)} %pad_maximum_fusion.refs_2_, bf16[512,3072]{1,0:T(8,128)(2,1)} %get-tuple-element.60.refs_3_, ...), custom_call_target="tpu_custom_call" | custom-call | flops 3221225472 | bytes 7864320 | tf_op jit(solution)/shard_map/down/pallas_call | solution.py:351
  565.4 14.2 %down.15 = (bf16[512,768]{1,0:T(8,128)(2,1)}, bf16[512,768]{1,0:T(8,128)(2,1)}) custom-call(s32[9]{0:T(128)} %stack.172.meta_ref, bf16[1024,2560]{1,0:T(8,128)(2,1)} %gate_up.6.refs_0_, bf16[1024,1536]{1,0:T(8,128)(2,1)} %gate_up.7.refs_1_, bf16[4096,1024]{1,0:T(8,128)(2,1)} %all-gather.16.cloned.1.call-done.refs_2_), custom_call_target="tpu_custom_call" | custom-call | flops 6442450944 | bytes 11534336 | tf_op jit(solution)/shard_map/down/pallas_call | solution.py:351
  583.9 11.6 %collective-permute-done.19.refs_4_ = bf16[512,768]{1,0:T(8,128)(2,1)} collective-permute-done((bf16[512,768]{1,0:T(8,128)(2,1)}, bf16[512,768]{1,0:T(8,128)(2,1)}, u32[]{:S(2)}, u32[]{:S(2)}) %collective-permute-start.19) | collective-permute-done | bytes 786464 | tf_op jit(solution)/shard_map/ppermute | solution.py:419
  598.0 10.3 %down.16.refs_0_ = bf16[512,768]{1,0:T(8,128)(2,1)} custom-call(s32[9]{0:T(128)} %stack.172.meta_ref, bf16[1024,2560]{1,0:T(8,128)(2,1)} %gate_up.5.refs_0_, bf16[512,1536]{1,0:T(8,128)(2,1)} %gate_up.8.refs_1_, bf16[4096,1024]{1,0:T(8,128)(2,1)} %all-gather.16.cloned.1.call-done.refs_2_, bf16[512,3072]{1,0:T(8,128)(2,1)} %get-tuple-element.58.refs_3_, ...), custom_call_target="tpu_custom_call" | custom-call | flops 3221225472 | bytes 9961472 | tf_op jit(solution)/shard_map/down/pallas_call | solution.py:351
  618.5 14.2 %down.18 = (bf16[512,768]{1,0:T(8,128)(2,1)}, bf16[512,768]{1,0:T(8,128)(2,1)}) custom-call(s32[9]{0:T(128)} %stack.171.meta_ref, bf16[1024,2560]{1,0:T(8,128)(2,1)} %gate_up.6.refs_0_, bf16[1024,1536]{1,0:T(8,128)(2,1)} %gate_up.7.refs_1_, bf16[4096,1024]{1,0:T(8,128)(2,1)} %all-gather.18.cloned.1.call-done.refs_2_), custom_call_target="tpu_custom_call" | custom-call | flops 6442450944 | bytes 11534336 | tf_op jit(solution)/shard_map/down/pallas_call | solution.py:351
  646.5 10.3 %down.19.refs_0_ = bf16[512,768]{1,0:T(8,128)(2,1)} custom-call(s32[9]{0:T(128)} %stack.171.meta_ref, bf16[1024,2560]{1,0:T(8,128)(2,1)} %gate_up.5.refs_0_, bf16[512,1536]{1,0:T(8,128)(2,1)} %gate_up.8.refs_1_, bf16[4096,1024]{1,0:T(8,128)(2,1)} %all-gather.18.cloned.1.call-done.refs_2_, bf16[512,3072]{1,0:T(8,128)(2,1)} %get-tuple-element.58.refs_3_, ...), custom_call_target="tpu_custom_call" | custom-call | flops 3221225472 | bytes 9961472 | tf_op jit(solution)/shard_map/down/pallas_call | solution.py:351
  656.8 10.3 %down.20.refs_1_ = bf16[512,768]{1,0:T(8,128)(2,1)} custom-call(s32[9]{0:T(128)} %stack.171.meta_ref, bf16[1024,2560]{1,0:T(8,128)(2,1)} %gate_up.5.refs_0_, bf16[512,1536]{1,0:T(8,128)(2,1)} %gate_up.9.refs_1_, bf16[4096,1024]{1,0:T(8,128)(2,1)} %all-gather.18.cloned.1.call-done.refs_2_, bf16[512,3072]{1,0:T(8,128)(2,1)} %get-tuple-element.60.refs_3_, ...), custom_call_target="tpu_custom_call" | custom-call | flops 3221225472 | bytes 9961472 | tf_op jit(solution)/shard_map/down/pallas_call | solution.py:351
  680.2 14.2 %down.21 = (bf16[512,768]{1,0:T(8,128)(2,1)}, bf16[512,768]{1,0:T(8,128)(2,1)}) custom-call(s32[9]{0:T(128)} %stack.170.meta_ref, bf16[1024,2560]{1,0:T(8,128)(2,1)} %gate_up.6.refs_0_, bf16[1024,1536]{1,0:T(8,128)(2,1)} %gate_up.7.refs_1_, bf16[4096,1024]{1,0:T(8,128)(2,1)} %all-gather.20.cloned.1.call-done.refs_2_), custom_call_target="tpu_custom_call" | custom-call | flops 6442450944 | bytes 11534336 | tf_op jit(solution)/shard_map/down/pallas_call | solution.py:351
  697.7 15.9 %collective-permute-done.32.refs_2_ = bf16[512,768]{1,0:T(8,128)(2,1)} collective-permute-done((bf16[512,768]{1,0:T(8,128)(2,1)}, bf16[512,768]{1,0:T(8,128)(2,1)}, u32[]{:S(2)}, u32[]{:S(2)}) %collective-permute-start.32) | collective-permute-done | bytes 786464 | tf_op jit(solution)/shard_map/ppermute | solution.py:419
  715.1 13.6 %collective-permute-done.23.refs_4_ = bf16[512,768]{1,0:T(8,128)(2,1)} collective-permute-done((bf16[512,768]{1,0:T(8,128)(2,1)}, bf16[512,768]{1,0:T(8,128)(2,1)}, u32[]{:S(2)}, u32[]{:S(2)}) %collective-permute-start.23) | collective-permute-done | bytes 786464 | tf_op jit(solution)/shard_map/ppermute | solution.py:419
  730.5 10.3 %down.22.refs_0_ = bf16[512,768]{1,0:T(8,128)(2,1)} custom-call(s32[9]{0:T(128)} %stack.170.meta_ref, bf16[1024,2560]{1,0:T(8,128)(2,1)} %gate_up.5.refs_0_, bf16[512,1536]{1,0:T(8,128)(2,1)} %gate_up.8.refs_1_, bf16[4096,1024]{1,0:T(8,128)(2,1)} %all-gather.20.cloned.1.call-done.refs_2_, bf16[512,3072]{1,0:T(8,128)(2,1)} %get-tuple-element.58.refs_3_, ...), custom_call_target="tpu_custom_call" | custom-call | flops 3221225472 | bytes 9961472 | tf_op jit(solution)/shard_map/down/pallas_call | solution.py:351
  747.6 14.8 %collective-permute-done.28.refs_5_ = bf16[512,768]{1,0:T(8,128)(2,1)} collective-permute-done((bf16[512,768]{1,0:T(8,128)(2,1)}, bf16[512,768]{1,0:T(8,128)(2,1)}, u32[]{:S(2)}, u32[]{:S(2)}) %collective-permute-start.28) | collective-permute-done | bytes 786464 | tf_op jit(solution)/shard_map/ppermute | solution.py:419
  764.7 10.3 %down.23.refs_1_ = bf16[512,768]{1,0:T(8,128)(2,1)} custom-call(s32[9]{0:T(128)} %stack.170.meta_ref, bf16[1024,2560]{1,0:T(8,128)(2,1)} %gate_up.5.refs_0_, bf16[512,1536]{1,0:T(8,128)(2,1)} %gate_up.9.refs_1_, bf16[4096,1024]{1,0:T(8,128)(2,1)} %all-gather.20.cloned.1.call-done.refs_2_, bf16[512,3072]{1,0:T(8,128)(2,1)} %get-tuple-element.60.refs_3_, ...), custom_call_target="tpu_custom_call" | custom-call | flops 3221225472 | bytes 9961472 | tf_op jit(solution)/shard_map/down/pallas_call | solution.py:351
  (167 shorter events, 225.6 us)
Async XLA Ops:
  7.2 77.7 %all-gather.8.cloned.1.call-start = ((), (), s32[]{:S(2)}) async-start(), calls=%async_computation | async-start | bytes 8847360 | tf_op jit(solution)/shard_map/all_gather | solution.py:429
  9.6 290.6 %all-gather.10.cloned.1.call-start = ((), (), s32[]{:S(2)}) async-start(), calls=%async_computation.1 | async-start | bytes 21233664 | tf_op jit(solution)/shard_map/all_gather | solution.py:433
  43.4 315.1 %all-gather.12.cloned.1.call-start = ((), (), s32[]{:S(2)}) async-start(), calls=%async_computation.2 | async-start | bytes 35389440 | tf_op jit(solution)/shard_map/all_gather | solution.py:467
  46.3 82.8 %collective-permute-start = (bf16[384,2560]{1,0:T(8,128)(2,1)}, bf16[384,2560]{1,0:T(8,128)(2,1)}, u32[]{:S(2)}, u32[]{:S(2)}) collective-permute-start(bf16[384,2560]{1,0:T(8,128)(2,1)} %pad_maximum_fusion.4), channel_id=1, source_target_pairs={{0,16},{8,24},{16,0},{24,8},{1,17},{9,25},{17,1},{25,9},{2,18},{10... | collective-permute-start | bytes 5898248 | tf_op jit(solution)/shard_map/ppermute | solution.py:419
  132.3 333.5 %all-gather.14.cloned.1.call-start = ((), (), s32[]{:S(2)}) async-start(), calls=%async_computation.3 | async-start | bytes 21233664 | tf_op jit(solution)/shard_map/all_gather | solution.py:467
  134.5 38.5 %collective-permute-start.1 = (bf16[384,1536]{1,0:T(8,128)(2,1)}, bf16[384,1536]{1,0:T(8,128)(2,1)}, u32[]{:S(2)}, u32[]{:S(2)}) collective-permute-start(bf16[384,1536]{1,0:T(8,128)(2,1)} %pad_maximum_fusion.5), channel_id=1, source_target_pairs={{0,16},{8,24},{16,0},{24,8},{1,17},{9,25},{17,1},{25,9},{2,18},{10... | collective-permute-start | bytes 3538952 | tf_op jit(solution)/shard_map/ppermute | solution.py:419
  176.0 389.4 %all-gather.16.cloned.1.call-start = ((), (), s32[]{:S(2)}) async-start(), calls=%async_computation.4 | async-start | bytes 9437184 | tf_op jit(solution)/shard_map/all_gather | solution.py:471
  176.1 52.2 %collective-permute-start.2 = (bf16[2048,384]{1,0:T(8,128)(2,1)}, bf16[2048,384]{1,0:T(8,128)(2,1)}, u32[]{:S(2)}, u32[]{:S(2)}) collective-permute-start(bf16[2048,384]{1,0:T(8,128)(2,1)} %param.21), channel_id=1, source_target_pairs={{0,16},{8,24},{16,0},{24,8},{1,17},{9,25},{17,1},{25,9},{2,18},{10... | collective-permute-start | bytes 4718600 | tf_op jit(solution)/shard_map/ppermute | solution.py:419
  232.0 386.6 %all-gather.18.cloned.1.call-start = ((), (), s32[]{:S(2)}) async-start(), calls=%async_computation.5 | async-start | bytes 9437184 | tf_op jit(solution)/shard_map/all_gather | solution.py:471
  232.6 447.6 %all-gather.20.cloned.1.call-start = ((), (), s32[]{:S(2)}) async-start(), calls=%async_computation.6 | async-start | bytes 9437184 | tf_op jit(solution)/shard_map/all_gather | solution.py:471
  267.4 55.5 %collective-permute-start.10 = (bf16[512,768]{1,0:T(8,128)(2,1)}, bf16[512,768]{1,0:T(8,128)(2,1)}, u32[]{:S(2)}, u32[]{:S(2)}) collective-permute-start(bf16[512,768]{1,0:T(8,128)(2,1)} %get-tuple-element.97), channel_id=1, source_target_pairs={{0,16},{8,24},{16,0},{24,8},{1,17},{9,25},{17,1},{25,9},{2,18},{10... | collective-permute-start | bytes 2359304 | tf_op jit(solution)/shard_map/ppermute | solution.py:419
  269.4 64.5 %collective-permute-start.11 = (bf16[512,768]{1,0:T(8,128)(2,1)}, bf16[512,768]{1,0:T(8,128)(2,1)}, u32[]{:S(2)}, u32[]{:S(2)}) collective-permute-start(bf16[512,768]{1,0:T(8,128)(2,1)} %get-tuple-element.96), channel_id=1, source_target_pairs={{0,24},{8,0},{16,8},{24,16},{1,25},{9,1},{17,9},{25,17},{2,26},{10... | collective-permute-start | bytes 2359304 | tf_op jit(solution)/shard_map/ppermute | solution.py:419
  283.0 51.2 %collective-permute-start.9 = (bf16[512,768]{1,0:T(8,128)(2,1)}, bf16[512,768]{1,0:T(8,128)(2,1)}, u32[]{:S(2)}, u32[]{:S(2)}) collective-permute-start(bf16[512,768]{1,0:T(8,128)(2,1)} %get-tuple-element.98), channel_id=1, source_target_pairs={{0,8},{8,16},{16,24},{24,0},{1,9},{9,17},{17,25},{25,1},{2,10},{10... | collective-permute-start | bytes 2359304 | tf_op jit(solution)/shard_map/ppermute | solution.py:419
  321.0 79.1 %collective-permute-start.12 = (bf16[256,3072]{1,0:T(8,128)(2,1)}, bf16[256,3072]{1,0:T(8,128)(2,1)}, u32[]{:S(2)}, u32[]{:S(2)}) collective-permute-start(bf16[256,3072]{1,0:T(8,128)(2,1)} %get-tuple-element.69.refs_0_), channel_id=1, source_target_pairs={{0,8},{8,16},{16,24},{24,0},{1,9},{9,17},{17,25},{25,1},{2,10},{10... | collective-permute-start | bytes 4718600 | tf_op jit(solution)/shard_map/ppermute | solution.py:419
  354.2 47.4 %collective-permute-start.14 = (bf16[256,3072]{1,0:T(8,128)(2,1)}, bf16[256,3072]{1,0:T(8,128)(2,1)}, u32[]{:S(2)}, u32[]{:S(2)}) collective-permute-start(bf16[256,3072]{1,0:T(8,128)(2,1)} %get-tuple-element.72.refs_2_.refs_0_), channel_id=1, source_target_pairs={{0,8},{8,16},{16,24},{24,0},{1,9},{9,17},{17,25},{25,1},{2,10},{10... | collective-permute-start | bytes 4718600 | tf_op jit(solution)/shard_map/ppermute | solution.py:419
  355.3 46.2 %collective-permute-start.15 = (bf16[256,3072]{1,0:T(8,128)(2,1)}, bf16[256,3072]{1,0:T(8,128)(2,1)}, u32[]{:S(2)}, u32[]{:S(2)}) collective-permute-start(bf16[256,3072]{1,0:T(8,128)(2,1)} %get-tuple-element.64.refs_3_.refs_1_), channel_id=1, source_target_pairs={{0,24},{8,0},{16,8},{24,16},{1,25},{9,1},{17,9},{25,17},{2,26},{10... | collective-permute-start | bytes 4718600 | tf_op jit(solution)/shard_map/ppermute | solution.py:419
  357.0 67.3 %collective-permute-start.13 = (bf16[256,3072]{1,0:T(8,128)(2,1)}, bf16[256,3072]{1,0:T(8,128)(2,1)}, u32[]{:S(2)}, u32[]{:S(2)}) collective-permute-start(bf16[256,3072]{1,0:T(8,128)(2,1)} %get-tuple-element.62.refs_1_), channel_id=1, source_target_pairs={{0,24},{8,0},{16,8},{24,16},{1,25},{9,1},{17,9},{25,17},{2,26},{10... | collective-permute-start | bytes 4718600 | tf_op jit(solution)/shard_map/ppermute | solution.py:419
  581.7 52.6 %collective-permute-start.40 = (bf16[512,768]{1,0:T(8,128)(2,1)}, bf16[512,768]{1,0:T(8,128)(2,1)}, u32[]{:S(2)}, u32[]{:S(2)}) collective-permute-start(bf16[512,768]{1,0:T(8,128)(2,1)} %down.14.refs_1_), channel_id=1, source_target_pairs={{0,24},{8,0},{16,8},{24,16},{1,25},{9,1},{17,9},{25,17},{2,26},{10... | collective-permute-start | bytes 2359304 | tf_op jit(solution)/shard_map/ppermute | solution.py:419
  583.9 53.0 %collective-permute-start.38 = (bf16[512,768]{1,0:T(8,128)(2,1)}, bf16[512,768]{1,0:T(8,128)(2,1)}, u32[]{:S(2)}, u32[]{:S(2)}) collective-permute-start(bf16[512,768]{1,0:T(8,128)(2,1)} %down.13.refs_0_), channel_id=1, source_target_pairs={{0,8},{8,16},{16,24},{24,0},{1,9},{9,17},{17,25},{25,1},{2,10},{10... | collective-permute-start | bytes 2359304 | tf_op jit(solution)/shard_map/ppermute | solution.py:419
  636.9 41.2 %collective-permute-start.41 = (bf16[512,768]{1,0:T(8,128)(2,1)}, bf16[512,768]{1,0:T(8,128)(2,1)}, u32[]{:S(2)}, u32[]{:S(2)}) collective-permute-start(bf16[512,768]{1,0:T(8,128)(2,1)} %collective-permute-done.40.refs_5_), channel_id=1, source_target_pairs={{0,24},{8,0},{16,8},{24,16},{1,25},{9,1},{17,9},{25,17},{2,26},{10... | collective-permute-start | bytes 2359304 | tf_op jit(solution)/shard_map/ppermute | solution.py:419
  644.4 50.6 %collective-permute-start.34 = (bf16[512,768]{1,0:T(8,128)(2,1)}, bf16[512,768]{1,0:T(8,128)(2,1)}, u32[]{:S(2)}, u32[]{:S(2)}) collective-permute-start(bf16[512,768]{1,0:T(8,128)(2,1)} %down.17.refs_1_), channel_id=1, source_target_pairs={{0,24},{8,0},{16,8},{24,16},{1,25},{9,1},{17,9},{25,17},{2,26},{10... | collective-permute-start | bytes 2359304 | tf_op jit(solution)/shard_map/ppermute | solution.py:419
  646.5 48.0 %collective-permute-start.39 = (bf16[512,768]{1,0:T(8,128)(2,1)}, bf16[512,768]{1,0:T(8,128)(2,1)}, u32[]{:S(2)}, u32[]{:S(2)}) collective-permute-start(bf16[512,768]{1,0:T(8,128)(2,1)} %collective-permute-done.38.refs_2_), channel_id=1, source_target_pairs={{0,8},{8,16},{16,24},{24,0},{1,9},{9,17},{17,25},{25,1},{2,10},{10... | collective-permute-start | bytes 2359304 | tf_op jit(solution)/shard_map/ppermute | solution.py:419
  667.2 46.4 %collective-permute-start.32 = (bf16[512,768]{1,0:T(8,128)(2,1)}, bf16[512,768]{1,0:T(8,128)(2,1)}, u32[]{:S(2)}, u32[]{:S(2)}) collective-permute-start(bf16[512,768]{1,0:T(8,128)(2,1)} %down.16.refs_0_), channel_id=1, source_target_pairs={{0,8},{8,16},{16,24},{24,0},{1,9},{9,17},{17,25},{25,1},{2,10},{10... | collective-permute-start | bytes 2359304 | tf_op jit(solution)/shard_map/ppermute | solution.py:419
  696.7 48.8 %collective-permute-start.35 = (bf16[512,768]{1,0:T(8,128)(2,1)}, bf16[512,768]{1,0:T(8,128)(2,1)}, u32[]{:S(2)}, u32[]{:S(2)}) collective-permute-start(bf16[512,768]{1,0:T(8,128)(2,1)} %collective-permute-done.34.refs_5_), channel_id=1, source_target_pairs={{0,24},{8,0},{16,8},{24,16},{1,25},{9,1},{17,9},{25,17},{2,26},{10... | collective-permute-start | bytes 2359304 | tf_op jit(solution)/shard_map/ppermute | solution.py:419
  713.6 48.8 %collective-permute-start.28 = (bf16[512,768]{1,0:T(8,128)(2,1)}, bf16[512,768]{1,0:T(8,128)(2,1)}, u32[]{:S(2)}, u32[]{:S(2)}) collective-permute-start(bf16[512,768]{1,0:T(8,128)(2,1)} %down.20.refs_1_), channel_id=1, source_target_pairs={{0,24},{8,0},{16,8},{24,16},{1,25},{9,1},{17,9},{25,17},{2,26},{10... | collective-permute-start | bytes 2359304 | tf_op jit(solution)/shard_map/ppermute | solution.py:419
  713.6 50.9 %collective-permute-start.26 = (bf16[512,768]{1,0:T(8,128)(2,1)}, bf16[512,768]{1,0:T(8,128)(2,1)}, u32[]{:S(2)}, u32[]{:S(2)}) collective-permute-start(bf16[512,768]{1,0:T(8,128)(2,1)} %down.19.refs_0_), channel_id=1, source_target_pairs={{0,8},{8,16},{16,24},{24,0},{1,9},{9,17},{17,25},{25,1},{2,10},{10... | collective-permute-start | bytes 2359304 | tf_op jit(solution)/shard_map/ppermute | solution.py:419
  728.7 46.2 %collective-permute-start.33 = (bf16[512,768]{1,0:T(8,128)(2,1)}, bf16[512,768]{1,0:T(8,128)(2,1)}, u32[]{:S(2)}, u32[]{:S(2)}) collective-permute-start(bf16[512,768]{1,0:T(8,128)(2,1)} %collective-permute-done.32.refs_2_), channel_id=1, source_target_pairs={{0,8},{8,16},{16,24},{24,0},{1,9},{9,17},{17,25},{25,1},{2,10},{10... | collective-permute-start | bytes 2359304 | tf_op jit(solution)/shard_map/ppermute | solution.py:419
  730.5 50.6 %collective-permute-start.30 = (bf16[512,768]{1,0:T(8,128)(2,1)}, bf16[512,768]{1,0:T(8,128)(2,1)}, u32[]{:S(2)}, u32[]{:S(2)}) collective-permute-start(bf16[512,768]{1,0:T(8,128)(2,1)} %down.20.refs_1_), channel_id=1, source_target_pairs={{0,8},{8,16},{16,24},{24,0},{1,9},{9,17},{17,25},{25,1},{2,10},{10... | collective-permute-start | bytes 2359304 | tf_op jit(solution)/shard_map/ppermute | solution.py:419
  745.6 53.6 %collective-permute-start.31 = (bf16[512,768]{1,0:T(8,128)(2,1)}, bf16[512,768]{1,0:T(8,128)(2,1)}, u32[]{:S(2)}, u32[]{:S(2)}) collective-permute-start(bf16[512,768]{1,0:T(8,128)(2,1)} %down.19.refs_0_), channel_id=1, source_target_pairs={{0,24},{8,0},{16,8},{24,16},{1,25},{9,1},{17,9},{25,17},{2,26},{10... | collective-permute-start | bytes 2359304 | tf_op jit(solution)/shard_map/ppermute | solution.py:419
  762.4 42.3 %collective-permute-start.29 = (bf16[512,768]{1,0:T(8,128)(2,1)}, bf16[512,768]{1,0:T(8,128)(2,1)}, u32[]{:S(2)}, u32[]{:S(2)}) collective-permute-start(bf16[512,768]{1,0:T(8,128)(2,1)} %collective-permute-done.28.refs_5_), channel_id=1, source_target_pairs={{0,24},{8,0},{16,8},{24,16},{1,25},{9,1},{17,9},{25,17},{2,26},{10... | collective-permute-start | bytes 2359304 | tf_op jit(solution)/shard_map/ppermute | solution.py:419
  764.5 43.0 %collective-permute-start.27 = (bf16[512,768]{1,0:T(8,128)(2,1)}, bf16[512,768]{1,0:T(8,128)(2,1)}, u32[]{:S(2)}, u32[]{:S(2)}) collective-permute-start(bf16[512,768]{1,0:T(8,128)(2,1)} %collective-permute-done.26.refs_2_), channel_id=1, source_target_pairs={{0,8},{8,16},{16,24},{24,0},{1,9},{9,17},{17,25},{25,1},{2,10},{10... | collective-permute-start | bytes 2359304 | tf_op jit(solution)/shard_map/ppermute | solution.py:419
  774.9 38.0 %collective-permute-start.45 = (bf16[512,768]{1,0:T(8,128)(2,1)}, bf16[512,768]{1,0:T(8,128)(2,1)}, u32[]{:S(2)}, u32[]{:S(2)}) collective-permute-start(bf16[512,768]{1,0:T(8,128)(2,1)} %down.23.refs_1_), channel_id=1, source_target_pairs={{0,24},{8,0},{16,8},{24,16},{1,25},{9,1},{17,9},{25,17},{2,26},{10... | collective-permute-start | bytes 2359304 | tf_op jit(solution)/shard_map/ppermute | solution.py:419
  (35 other events, 714.5 us)
Sparse Core Ops, SparseCore 0:
  9.8 49.2 all-gather.7
  60.6 91.0 all-gather.9
  153.3 145.2 all-gather.11
  300.0 92.0 all-gather.13
  393.6 51.5 all-gather.15
  446.6 51.8 all-gather.17
  500.1 51.8 all-gather.19

commit v8 on v7

--- a/solution.py
+++ b/solution.py
@@ -38,8 +38,20 @@
     return (vals_f32 * inv * gain).astype(jnp.bfloat16)
 
 
+def norm_into(x_ref, gain, store):
+    rows = min(16, x_ref.shape[0])
+
+    @pl.loop(0, x_ref.shape[0] // rows)
+    def _(i):
+        r = pl.ds(pl.multiple_of(i * rows, rows), rows)
+        store(r, norm_rows(x_ref[r, :].astype(jnp.float32), gain))
+
+
 def norm_kernel(x_ref, g_ref, h_ref):
-    h_ref[...] = norm_rows(x_ref[...].astype(jnp.float32), g_ref[...].astype(jnp.float32))
+    def store(r, val):
+        h_ref[r, :] = val
+
+    norm_into(x_ref, g_ref[...].astype(jnp.float32), store)
 
 
 def norm_call(x, gain):
@@ -220,9 +232,12 @@
     @pl.when(n == pl.num_programs(0) - 1)
     def _():
         r_ref[...] = y_ref[...]
-        u = norm_rows(y_ref[...].astype(jnp.float32), g_ref[...].astype(jnp.float32))
-        ua_ref[...] = u[:half]
-        ub_ref[...] = u[half:]
+        gain = g_ref[...].astype(jnp.float32)
+        for part, u_ref in enumerate((ua_ref, ub_ref)):
+            def store(r, val, u_ref=u_ref):
+                u_ref[r, :] = val
+
+            norm_into(y_ref.at[part * half:(part + 1) * half, :], gain, store)
 
 
 def out_call(idx, o_pieces, w, x, gain):
@@ -299,18 +314,41 @@
     )(*us, w, w)
 
 
-def down_kernel(bm, parts, n_src, own, meta_ref, *refs):
-    a_refs = refs[:parts]
+def down_kernel(bm, parts, n_src, own, row0, meta_ref, *refs):
+    a_any = refs[:parts]
     w_ref = refs[parts]
     rest = refs[parts + 1:]
+    resid_any = rest[0] if own else None
+    partials = rest[1:3] if own else ()
+    outs = rest[3:4] if own else rest[:2]
+    scratch = rest[4:] if own else rest[2:]
+    a_refs, sem = scratch[:parts], scratch[parts]
     rows = a_refs[0].shape[0]
     n = pl.program_id(0)
-    steps = pl.num_programs(0)
     bn = w_ref.shape[1]
     kj = w_ref.shape[0] // n_src
-
-    @pl.loop(0, rows // bm)
+    n_m = rows // bm
+    copies = [[pltpu.make_async_copy(a_any[p].at[row0[p] + i * bm:row0[p] + (i + 1) * bm, :], a_refs[p].at[i * bm:(i + 1) * bm, :], sem.at[p, i])
+               for p in range(parts)] for i in range(n_m)]
+    more = []
+    if own:
+        r_ref, r_sem = scratch[parts + 1:]
+        for q in range(r_ref.shape[1] // HEAD_DIM):
+            col = pl.multiple_of(meta_ref[r_ref.shape[1] // bn + q] * HEAD_DIM, HEAD_DIM)
+            more.append(pltpu.make_async_copy(resid_any.at[:, pl.ds(col, HEAD_DIM)], r_ref.at[:, q * HEAD_DIM:(q + 1) * HEAD_DIM], r_sem.at[q]))
+
+    @pl.when(n == 0)
+    def _():
+        for c in sum(copies, []) + more:
+            c.start()
+
+    @pl.loop(0, n_m)
     def _(m):
+        for i in range(n_m):
+            @pl.when((n == 0) & (m == i))
+            def _():
+                for c in copies[i]:
+                    c.wait()
         r = pl.ds(pl.multiple_of(m * bm, bm), bm)
         acc = None
         for j in range(n_src):
@@ -320,18 +358,23 @@
                 part = jnp.dot(a_refs[p][r, j * kp:(j + 1) * kp], w_ref[k0:k0 + kp, :], preferred_element_type=jnp.float32)
                 acc = part if acc is None else acc + part
                 k0 += kp
-        out = pl.ds(pl.multiple_of(m // 2 * bm, bm), bm)
-        for h in range(2):
-            @pl.when(m % 2 == h)
+        if own:
+            @pl.when((n == 0) & (m == 0))
             def _():
-                if own:
-                    for i in range(bn // HEAD_DIM):
-                        lanes = slice(i * HEAD_DIM, (i + 1) * HEAD_DIM)
-                        col = pl.ds(pl.multiple_of(meta_ref[steps + n * (bn // HEAD_DIM) + i] * HEAD_DIM, HEAD_DIM), HEAD_DIM)
-                        part = acc[:, lanes] + rest[1 + h][out, lanes].astype(jnp.float32)
-                        rest[3][r, lanes] = (rest[0][r, col].astype(jnp.float32) + part).astype(jnp.bfloat16)
-                else:
-                    rest[h][out, :] = acc.astype(jnp.bfloat16)
+                for c in more:
+                    c.wait()
+
+            for h in range(2):
+                @pl.when(m == h)
+                def _():
+                    base = r_ref[r, pl.ds(pl.multiple_of(n * bn, bn), bn)].astype(jnp.float32)
+                    outs[0][r, :] = (base + (acc + partials[h][...].astype(jnp.float32))).astype(jnp.bfloat16)
+        else:
+            out = pl.ds(pl.multiple_of(m // 2 * bm, bm), bm)
+            for h in range(2):
+                @pl.when(m % 2 == h)
+                def _():
+                    outs[h][out, :] = acc.astype(jnp.bfloat16)
 
 
 def down_call(a_parts, w, meta, n_src, bn, steps, rows, call=0, resid=None, partials=()):
@@ -339,19 +382,23 @@
     cols = steps * bn
     own = resid is not None
     half = rows // 2
+    bm = half if own else half // N_CALLS
     step = lambda n, meta: (0, n)
-    once = dict(pipeline_mode=pl.Buffered(1))
+    anywhere = pl.BlockSpec(memory_space=pl.ANY)
     args = [*a_parts, w]
-    in_specs = [pl.BlockSpec((rows, a.shape[1]), lambda n, meta, b=(call if a.shape[0] > rows else 0): (b, 0), **once) for a in a_parts]
-    in_specs += [pl.BlockSpec((w.shape[0], bn), lambda n, meta: (0, meta[n]))]
+    in_specs = [anywhere] * parts + [pl.BlockSpec((w.shape[0], bn), lambda n, meta: (0, meta[n]))]
+    scratch = [pltpu.VMEM((rows, a.shape[1]), jnp.bfloat16) for a in a_parts] + [pltpu.SemaphoreType.DMA((parts, rows // bm))]
     if own:
         args += [resid, *partials]
-        in_specs += [pl.BlockSpec(resid.shape, lambda n, meta: (0, 0), **once)] + [pl.BlockSpec((half, bn), lambda n, meta: (call, n))] * 2
+        in_specs += [anywhere] + [pl.BlockSpec((half, bn), lambda n, meta: (call, n))] * 2
+        scratch += [pltpu.VMEM((rows, cols), jnp.bfloat16), pltpu.SemaphoreType.DMA((cols // HEAD_DIM,))]
     n_out = 1 if own else 2
+    row0 = tuple(call * rows if a.shape[0] > rows else 0 for a in a_parts)
     return pl.pallas_call(
-        functools.partial(down_kernel, half if own else half // N_CALLS, parts, n_src, own),
+        functools.partial(down_kernel, bm, parts, n_src, own, row0),
         grid_spec=pltpu.PrefetchScalarGridSpec(
-            num_scalar_prefetch=1, grid=(steps,), in_specs=in_specs, out_specs=[pl.BlockSpec((rows // n_out, bn), step)] * n_out),
+            num_scalar_prefetch=1, grid=(steps,), in_specs=in_specs, out_specs=[pl.BlockSpec((rows // n_out, bn), step)] * n_out,
+            scratch_shapes=scratch),
         out_shape=[jax.ShapeDtypeStruct((rows // n_out, cols), jnp.bfloat16)] * n_out,
         compiler_params=params(),
         cost_estimate=cost(2 * rows * cols * w.shape[0], 2 * w.size + 4 * rows * cols),
@@ -500,14 +547,41 @@
         for b in range(n_blk):
             units = sum(([2 * o_ * n_blk + b, (2 * o_ + 1) * n_blk + b] for o_ in others), [])
             blocks.append((d_full[b], others, units))
+        idx = jnp.stack([jnp.asarray(v, jnp.int32) for v in [(me - s) % n_tp for s in range(n_tp)] + sum((u for _, _, u in blocks), [])])
+        near_moves = [(i * N_CALLS + c, 0, sub, c, who) for i, who in enumerate((0, 1, n_tp - 1)) for c in range(N_CALLS)]
+        far_moves = [(0, 0, sub, 0, 2), (1, 0, sub, N_CALLS - 1, 2)]
+        skip = [sum(len(u) for _, _, u in blocks[:b]) for b in range(len(blocks))]
+        last = len(blocks) - 1
+        mine, far = [], []
+
+        def place_near(b, out, *deps):
+            m, near = mine[b]
+            pieces = [*m, *(near[g, c] for g in range(2) for c in range(N_CALLS))]
+            pieces[0] = after(pieces[0], *deps)
+            return place_call(idx, pieces, near_moves, (seq, d), n_tp, skip[b], out)
+
+        def place_far(b, out):
+            return place_call(idx, far[b], far_moves, (seq, d), n_tp, skip[b], out)
+
+        def relay(b, *deps):
+            near = mine[b][1]
+            far_0 = shift(after(near[0, 0], *deps), 1)
+            far_1 = shift(after(near[1, N_CALLS - 1], *deps), -1)
+            far.append((far_0, far_1))
+
         order = a_recv[1]
-        mine = []
+        hidden = None
         for b, (w, sel, units) in enumerate(blocks):
             meta = jnp.stack([jnp.asarray(v, jnp.int32) for v in [*sel, *units]])
             p_prev, p_next = down_call([after(a_recv[0], order), a_recv[1]], w, meta, n_src, bn, len(sel), N_CALLS * sub)
             b_next = shift(p_prev, -1)
             b_prev = shift(p_next, 1)
             order = p_prev
+            if b >= 1:
+                relay(b - 1)
+            if b >= 2:
+                hidden = place_far(b - 2, place_near(b - 2, hidden, order))
+                order = hidden
             m, near = [], {}
             for c in range(N_CALLS):
                 if b == 0:
@@ -518,25 +592,9 @@
                 for g, by in enumerate((1, -1)):
                     near[g, c] = shift(m[c], by)
             mine.append((m, near))
-        idx = jnp.stack([jnp.asarray(v, jnp.int32) for v in [(me - s) % n_tp for s in range(n_tp)] + sum((u for _, _, u in blocks), [])])
-        near_moves = [(i * N_CALLS + c, 0, sub, c, who) for i, who in enumerate((0, 1, n_tp - 1)) for c in range(N_CALLS)]
-        far_moves = [(0, 0, sub, 0, 2), (1, 0, sub, N_CALLS - 1, 2)]
-        hidden = None
-        skip = 0
-        last = len(blocks) - 1
-        for b in range(len(blocks)):
-            m, near = mine[b]
-            src = (near[0, 0], near[1, N_CALLS - 1])
-            if b == last:
-                src = tuple(after(v, hidden) for v in src)
-            far_0 = shift(src[0], 1)
-            far_1 = shift(src[1], -1)
-            pieces = [*m, *(near[g, c] for g in range(2) for c in range(N_CALLS))]
-            if b == 0:
-                pieces[0] = after(pieces[0], order)
-            hidden = place_call(idx, pieces, near_moves, (seq, d), n_tp, skip, hidden)
-            hidden = place_call(idx, (far_0, far_1), far_moves, (seq, d), n_tp, skip, hidden)
-            skip += len(blocks[b][2])
+        hidden = place_far(last - 1, place_near(last - 1, hidden, order))
+        relay(last, hidden)
+        hidden = place_far(last, place_near(last, hidden))
         hidden = hidden.reshape(1, seq, d)
         return hidden, k.reshape(1, seq, n_kv, HEAD_DIM), v.reshape(1, seq, n_kv, HEAD_DIM)
 

time: 875 us -> 870 us (level)
  waiting for transfers between devices: 198 us -> 179 us
  Pallas kernels: 507 us -> 521 us
    ppermute x48, waiting for transfers between devices: 197 us -> 178 us  [shift(): return lax.ppermute(val, tp, [(i, (i + s) % n_tp) for i in range(n_tp)])]
    pallas_call x1, Pallas kernels: 24.4 us -> 37.8 us  [norm_call(): pl.pallas_call(norm_kernel, grid=(s // bm,), in_specs=[pl.BlockSpec((bm,...]
  transfers between devices with their start and end apart: 56 -> 56, of which waited for: 27 -> 22; matrix products, arithmetic and copies ran while one was open for 6% -> 6% of each run, Pallas kernels for 59% -> 60%
where the time goes in v8:
time: 870 us; the launch traced here: 860 us
  Pallas kernels  521 us (60%)
  waiting for transfers between devices  179 us (21%)
  starting transfers between devices  87.1 us (10%)
  local copies, waits for them, and re-layouts  33.7 us (4%)
  other arithmetic  23.7 us (3%)
  between operations  15.8 us (2%)
    ppermute x48, waiting for transfers between devices, shift(): return lax.ppermute(val, tp, [(i, (i + s) % n_tp) for i in range(n_tp)])  178 us
    pallas_call x5, Pallas kernels, gu_call(): pl.pallas_call(functools.partial(gu_kernel, bm, n_u), grid=(n_src, nb), i...  143 us
    pallas_call x12, Pallas kernels, down_call(): pl.pallas_call(functools.partial(down_kernel, bm, parts, n_src, own, row0...  135 us
    pallas_call x2, Pallas kernels, att_call(): pl.pallas_call(functools.partial(att_kernel, bq, bk, per, first), grid=(n...  83.9 us
    ppermute x48, starting transfers between devices, shift(): return lax.ppermute(val, tp, [(i, (i + s) % n_tp) for i in range(n_tp)])  62.4 us
    pallas_call x2, Pallas kernels, out_call(): pl.pallas_call(functools.partial(out_kernel, n_src), grid_spec=pltpu.Pref...  45 us
    pallas_call x1, Pallas kernels, qkv_call(): pl.pallas_call(functools.partial(qkv_kernel, n_q, n_kv), grid=(s // bm,),...  41.4 us
    pallas_call x1, Pallas kernels, norm_call(): pl.pallas_call(norm_kernel, grid=(s // bm,), in_specs=[pl.BlockSpec((bm,...  37.8 us
  transfers between devices with their start and end apart: 56, of which 22 were waited for; matrix products, arithmetic and copies ran while one was open for 6% of the time, Pallas kernels for 60%

profile of v8, /device:TPU:97, one launch (start us, length us, event | category | flops | bytes accessed | tf_op | source)
XLA Modules:
  0.0 859.9 jit_solution(3269779832268491602)
XLA Ops:
  16.7 11.5 %collective-permute-done.6 = bf16[768,384]{1,0:T(8,128)(2,1)S(1)} collective-permute-done((bf16[768,384]{1,0:T(8,128)(2,1)S(1)}, bf16[768,384]{1,0:T(8,128)(2,1)S(1)}, u32[]{:S(2)}, u32[]{:S(2)}) %collective-permute-start.6) | collective-permute-done | bytes 589856 | tf_op jit(solution)/shard_map/ppermute | solution.py:466
  28.2 13.4 %collective-permute-done.7 = bf16[768,384]{1,0:T(8,128)(2,1)S(1)} collective-permute-done((bf16[768,384]{1,0:T(8,128)(2,1)S(1)}, bf16[768,384]{1,0:T(8,128)(2,1)S(1)}, u32[]{:S(2)}, u32[]{:S(2)}) %collective-permute-start.7) | collective-permute-done | bytes 589856 | tf_op jit(solution)/shard_map/ppermute | solution.py:466
  49.1 37.8 %norm.1.h_ref = bf16[4096,3072]{1,0:T(8,128)(2,1)} custom-call(bf16[4096,3072]{1,0:T(8,128)(2,1)} %bitcast.37, bf16[1,3072]{1,0:T(2,128)(2,1)} %reshape.63.g_ref), custom_call_target="tpu_custom_call" | custom-call | flops 100663296 | bytes 50331648 | tf_op jit(solution)/shard_map/norm/pallas_call | solution.py:60
  98.3 41.4 %qkv.1 = (bf16[6,4096,128]{2,1,0:T(8,128)(2,1)}, bf16[4096,256]{1,0:T(8,128)(2,1)}, bf16[4096,256]{1,0:T(8,128)(2,1)}, bf16[256,4096]{1,0:T(8,128)(2,1)}) custom-call(bf16[4096,3072]{1,0:T(8,128)(2,1)} %norm.1.h_ref, bf16[3072,1280]{1,0:T(8,128)(2,1)} %all-gather.8.cloned.1.call-done.w_ref, f32[4096,128]{1,0:T(8,128)} %get-tuple-element.111.cos_ref, ...), custom_call_target="tpu_custom_call" | custom-call | flops 32212254720 | bytes 43515904 | tf_op jit(solution)/shard_map/qkv/pallas_call | solution.py:97
  150.2 35.4 %attention.2 = bf16[2048,768]{1,0:T(8,128)(2,1)} custom-call(s32[1]{0:T(128)S(6)} %copy.32.len_ref, bf16[6,4096,128]{2,1,0:T(8,128)(2,1)} %get-tuple-element.56.q_ref, bf16[4096,256]{1,0:T(8,128)(2,1)} %get-tuple-element.53.k_ref, bf16[256,4096]{1,0:T(8,128)(2,1)} %get-tuple-element.54.vt_ref), custom_call_target="tpu_custom_call" | custom-call | flops 25769803776 | bytes 12582912 | tf_op jit(solution)/shard_map/attention/pallas_call | solution.py:198
  191.7 48.5 %attention.3 = bf16[2048,768]{1,0:T(8,128)(2,1)} custom-call(s32[1]{0:T(128)S(6)} %copy.32.len_ref, bf16[6,4096,128]{2,1,0:T(8,128)(2,1)} %get-tuple-element.56.q_ref, bf16[4096,256]{1,0:T(8,128)(2,1)} %get-tuple-element.53.k_ref, bf16[256,4096]{1,0:T(8,128)(2,1)} %get-tuple-element.54.vt_ref), custom_call_target="tpu_custom_call" | custom-call | flops 77309411328 | bytes 12582912 | tf_op jit(solution)/shard_map/attention/pallas_call | solution.py:198
  246.2 24.1 %collective-permute-start.16 = (bf16[4096,384]{1,0:T(8,128)(2,1)S(1)}, bf16[4096,384]{1,0:T(8,128)(2,1)}, u32[]{:S(2)}, u32[]{:S(2)}) collective-permute-start(bf16[4096,384]{1,0:T(8,128)(2,1)S(1)} %constant_dynamic-update-slice_fusion.4), channel_id=1, source_target_pairs={{0,1},{1,0},{2,3},{3,2},{4,5},{5,4},{6,7},{7,6},{8,9},{9,8},{10,11... | collective-permute-start | bytes 9437192 | tf_op jit(solution)/shard_map/ppermute | solution.py:516
  296.6 17.0 %collective-permute-done.4.refs_2_ = bf16[512,768]{1,0:T(8,128)(2,1)} collective-permute-done((bf16[512,768]{1,0:T(8,128)(2,1)}, bf16[512,768]{1,0:T(8,128)(2,1)}, u32[]{:S(2)}, u32[]{:S(2)}) %collective-permute-start.4) | collective-permute-done | bytes 786464 | tf_op jit(solution)/shard_map/ppermute | solution.py:466
  313.6 22.7 %w_out.2 = (bf16[512,3072]{1,0:T(8,128)(2,1)}, bf16[256,3072]{1,0:T(8,128)(2,1)}, bf16[256,3072]{1,0:T(8,128)(2,1)}) custom-call(s32[1]{0:T(128)} %bitcast.31.idx_ref, bf16[512,768]{1,0:T(8,128)(2,1)} %get-tuple-element.58.refs_0_, bf16[512,768]{1,0:T(8,128)(2,1)} %collective-permute-done.3.refs_1_, bf16[512,768]{1,0:T(8,128)(2,1)} %collective-permute-done.4.refs_2_, ...), custom_call_target="tpu_custom_call" | custom-call | flops 9663676416 | bytes 31457280 | tf_op jit(solution)/shard_map/w_out/pallas_call | solution.py:250
  347.8 22.4 %w_out.3 = (bf16[512,3072]{1,0:T(8,128)(2,1)}, bf16[256,3072]{1,0:T(8,128)(2,1)}, bf16[256,3072]{1,0:T(8,128)(2,1)}) custom-call(s32[1]{0:T(128)} %bitcast.34.idx_ref, bf16[512,768]{1,0:T(8,128)(2,1)} %get-tuple-element.61.refs_0_, bf16[512,768]{1,0:T(8,128)(2,1)} %collective-permute-done.9.refs_1_, bf16[512,768]{1,0:T(8,128)(2,1)} %collective-permute-done.10.refs_2_, ...), custom_call_target="tpu_custom_call" | custom-call | flops 9663676416 | bytes 31457280 | tf_op jit(solution)/shard_map/w_out/pallas_call | solution.py:250
  374.3 41.4 %gate_up.5.refs_0_ = bf16[1024,2560]{1,0:T(8,128)(2,1)} custom-call(bf16[256,3072]{1,0:T(8,128)(2,1)} %get-tuple-element.71.refs_0_, bf16[256,3072]{1,0:T(8,128)(2,1)} %get-tuple-element.64.refs_1_, bf16[256,3072]{1,0:T(8,128)(2,1)} %get-tuple-element.74.refs_2_.refs_0_, bf16[256,3072]{1,0:T(8,128)(2,1)} %get-tuple-element.66.refs_3_.refs_1_, ...), custom_call_target="tpu_custom_call" | custom-call | flops 32212254720 | bytes 42991616 | tf_op jit(solution)/shard_map/gate_up/pallas_call | solution.py:302
  415.7 24.5 %collective-permute-done.13.refs_1_ = bf16[256,3072]{1,0:T(8,128)(2,1)} collective-permute-done((bf16[256,3072]{1,0:T(8,128)(2,1)}, bf16[256,3072]{1,0:T(8,128)(2,1)}, u32[]{:S(2)}, u32[]{:S(2)}) %collective-permute-start.13) | collective-permute-done | bytes 1572896 | tf_op jit(solution)/shard_map/ppermute | solution.py:466
  440.2 41.6 %gate_up.6.refs_0_ = bf16[1024,2560]{1,0:T(8,128)(2,1)} custom-call(bf16[256,3072]{1,0:T(8,128)(2,1)} %collective-permute-done.12.refs_0_, bf16[256,3072]{1,0:T(8,128)(2,1)} %collective-permute-done.13.refs_1_, bf16[256,3072]{1,0:T(8,128)(2,1)} %collective-permute-done.14.refs_2_, bf16[256,3072]{1,0:T(8,128)(2,1)} %collective-permute-done.15.refs_3_, ...), custom_call_target="tpu_custom_call" | custom-call | flops 32212254720 | bytes 42991616 | tf_op jit(solution)/shard_map/gate_up/pallas_call | solution.py:302
  481.9 27.3 %gate_up.7.refs_1_ = bf16[1024,1536]{1,0:T(8,128)(2,1)} custom-call(bf16[256,3072]{1,0:T(8,128)(2,1)} %collective-permute-done.12.refs_0_, bf16[256,3072]{1,0:T(8,128)(2,1)} %collective-permute-done.13.refs_1_, bf16[256,3072]{1,0:T(8,128)(2,1)} %collective-permute-done.14.refs_2_, bf16[256,3072]{1,0:T(8,128)(2,1)} %collective-permute-done.15.refs_3_, ...), custom_call_target="tpu_custom_call" | custom-call | flops 19327352832 | bytes 28311552 | tf_op jit(solution)/shard_map/gate_up/pallas_call | solution.py:302
  509.1 13.8 %down.12 = (bf16[512,768]{1,0:T(8,128)(2,1)}, bf16[512,768]{1,0:T(8,128)(2,1)}) custom-call(s32[9]{0:T(128)} %stack.172.meta_ref, bf16[1024,2560]{1,0:T(8,128)(2,1)} %gate_up.6.refs_0_, bf16[1024,1536]{1,0:T(8,128)(2,1)} %gate_up.7.refs_1_, bf16[4096,768]{1,0:T(8,128)(2,1)} %pad_maximum_fusion.refs_2_), custom_call_target="tpu_custom_call" | custom-call | flops 6442450944 | bytes 9437184 | tf_op jit(solution)/shard_map/down/pallas_call | solution.py:397
  526.1 16.7 %gate_up.8.refs_1_ = bf16[512,1536]{1,0:T(8,128)(2,1)} custom-call(bf16[256,3072]{1,0:T(8,128)(2,1)} %get-tuple-element.71.refs_0_, bf16[256,3072]{1,0:T(8,128)(2,1)} %get-tuple-element.64.refs_1_, bf16[3072,3072]{1,0:T(8,128)(2,1)} %all-gather.14.cloned.1.call-done.refs_4_.refs_5_.refs_2_.refs_3_, ...), custom_call_target="tpu_custom_call" | custom-call | flops 9663676416 | bytes 23592960 | tf_op jit(solution)/shard_map/gate_up/pallas_call | solution.py:302
  544.5 10.2 %down.13.refs_0_ = bf16[512,768]{1,0:T(8,128)(2,1)} custom-call(s32[9]{0:T(128)} %stack.172.meta_ref, bf16[1024,2560]{1,0:T(8,128)(2,1)} %gate_up.5.refs_0_, bf16[512,1536]{1,0:T(8,128)(2,1)} %gate_up.8.refs_1_, bf16[4096,768]{1,0:T(8,128)(2,1)} %pad_maximum_fusion.refs_2_, bf16[512,3072]{1,0:T(8,128)(2,1)} %get-tuple-element.60.refs_3_, ...), custom_call_target="tpu_custom_call" | custom-call | flops 3221225472 | bytes 7864320 | tf_op jit(solution)/shard_map/down/pallas_call | solution.py:397
  554.7 16.1 %gate_up.9.refs_1_ = bf16[512,1536]{1,0:T(8,128)(2,1)} custom-call(bf16[256,3072]{1,0:T(8,128)(2,1)} %get-tuple-element.74.refs_2_.refs_0_, bf16[256,3072]{1,0:T(8,128)(2,1)} %get-tuple-element.66.refs_3_.refs_1_, bf16[3072,3072]{1,0:T(8,128)(2,1)} %all-gather.14.cloned.1.call-done.refs_4_.refs_5_.refs_2_.refs_3_, ...), custom_call_target="tpu_custom_call" | custom-call | flops 9663676416 | bytes 23592960 | tf_op jit(solution)/shard_map/gate_up/pallas_call | solution.py:302
  570.8 9.9 %down.14.refs_1_ = bf16[512,768]{1,0:T(8,128)(2,1)} custom-call(s32[9]{0:T(128)} %stack.172.meta_ref, bf16[1024,2560]{1,0:T(8,128)(2,1)} %gate_up.5.refs_0_, bf16[512,1536]{1,0:T(8,128)(2,1)} %gate_up.9.refs_1_, bf16[4096,768]{1,0:T(8,128)(2,1)} %pad_maximum_fusion.refs_2_, bf16[512,3072]{1,0:T(8,128)(2,1)} %get-tuple-element.62.refs_3_, ...), custom_call_target="tpu_custom_call" | custom-call | flops 3221225472 | bytes 7864320 | tf_op jit(solution)/shard_map/down/pallas_call | solution.py:397
  580.8 13.7 %down.15 = (bf16[512,768]{1,0:T(8,128)(2,1)}, bf16[512,768]{1,0:T(8,128)(2,1)}) custom-call(s32[9]{0:T(128)} %stack.171.meta_ref, bf16[1024,2560]{1,0:T(8,128)(2,1)} %gate_up.6.refs_0_, bf16[1024,1536]{1,0:T(8,128)(2,1)} %gate_up.7.refs_1_, bf16[4096,1024]{1,0:T(8,128)(2,1)} %all-gather.16.cloned.1.call-done.refs_2_), custom_call_target="tpu_custom_call" | custom-call | flops 6442450944 | bytes 11534336 | tf_op jit(solution)/shard_map/down/pallas_call | solution.py:397
  598.6 12.3 %collective-permute-done.19.refs_4_ = bf16[512,768]{1,0:T(8,128)(2,1)} collective-permute-done((bf16[512,768]{1,0:T(8,128)(2,1)}, bf16[512,768]{1,0:T(8,128)(2,1)}, u32[]{:S(2)}, u32[]{:S(2)}) %collective-permute-start.19) | collective-permute-done | bytes 786464 | tf_op jit(solution)/shard_map/ppermute | solution.py:466
  613.6 10.0 %down.16.refs_0_ = bf16[512,768]{1,0:T(8,128)(2,1)} custom-call(s32[9]{0:T(128)} %stack.171.meta_ref, bf16[1024,2560]{1,0:T(8,128)(2,1)} %gate_up.5.refs_0_, bf16[512,1536]{1,0:T(8,128)(2,1)} %gate_up.8.refs_1_, bf16[4096,1024]{1,0:T(8,128)(2,1)} %all-gather.16.cloned.1.call-done.refs_2_, bf16[512,3072]{1,0:T(8,128)(2,1)} %get-tuple-element.60.refs_3_, ...), custom_call_target="tpu_custom_call" | custom-call | flops 3221225472 | bytes 9961472 | tf_op jit(solution)/shard_map/down/pallas_call | solution.py:397
  623.6 10.0 %down.17.refs_1_ = bf16[512,768]{1,0:T(8,128)(2,1)} custom-call(s32[9]{0:T(128)} %stack.171.meta_ref, bf16[1024,2560]{1,0:T(8,128)(2,1)} %gate_up.5.refs_0_, bf16[512,1536]{1,0:T(8,128)(2,1)} %gate_up.9.refs_1_, bf16[4096,1024]{1,0:T(8,128)(2,1)} %all-gather.16.cloned.1.call-done.refs_2_, bf16[512,3072]{1,0:T(8,128)(2,1)} %get-tuple-element.62.refs_3_, ...), custom_call_target="tpu_custom_call" | custom-call | flops 3221225472 | bytes 9961472 | tf_op jit(solution)/shard_map/down/pallas_call | solution.py:397
  635.1 13.7 %down.18 = (bf16[512,768]{1,0:T(8,128)(2,1)}, bf16[512,768]{1,0:T(8,128)(2,1)}) custom-call(s32[9]{0:T(128)} %stack.173.meta_ref, bf16[1024,2560]{1,0:T(8,128)(2,1)} %gate_up.6.refs_0_, bf16[1024,1536]{1,0:T(8,128)(2,1)} %gate_up.7.refs_1_, bf16[4096,1024]{1,0:T(8,128)(2,1)} %all-gather.18.cloned.1.call-done.refs_2_), custom_call_target="tpu_custom_call" | custom-call | flops 6442450944 | bytes 11534336 | tf_op jit(solution)/shard_map/down/pallas_call | solution.py:397
  681.0 10.0 %down.19.refs_0_ = bf16[512,768]{1,0:T(8,128)(2,1)} custom-call(s32[9]{0:T(128)} %stack.173.meta_ref, bf16[1024,2560]{1,0:T(8,128)(2,1)} %gate_up.5.refs_0_, bf16[512,1536]{1,0:T(8,128)(2,1)} %gate_up.8.refs_1_, bf16[4096,1024]{1,0:T(8,128)(2,1)} %all-gather.18.cloned.1.call-done.refs_2_, bf16[512,3072]{1,0:T(8,128)(2,1)} %get-tuple-element.60.refs_3_, ...), custom_call_target="tpu_custom_call" | custom-call | flops 3221225472 | bytes 9961472 | tf_op jit(solution)/shard_map/down/pallas_call | solution.py:397
  691.0 9.9 %down.20.refs_1_ = bf16[512,768]{1,0:T(8,128)(2,1)} custom-call(s32[9]{0:T(128)} %stack.173.meta_ref, bf16[1024,2560]{1,0:T(8,128)(2,1)} %gate_up.5.refs_0_, bf16[512,1536]{1,0:T(8,128)(2,1)} %gate_up.9.refs_1_, bf16[4096,1024]{1,0:T(8,128)(2,1)} %all-gather.18.cloned.1.call-done.refs_2_, bf16[512,3072]{1,0:T(8,128)(2,1)} %get-tuple-element.62.refs_3_, ...), custom_call_target="tpu_custom_call" | custom-call | flops 3221225472 | bytes 9961472 | tf_op jit(solution)/shard_map/down/pallas_call | solution.py:397
  702.5 13.7 %down.21 = (bf16[512,768]{1,0:T(8,128)(2,1)}, bf16[512,768]{1,0:T(8,128)(2,1)}) custom-call(s32[9]{0:T(128)} %stack.170.meta_ref, bf16[1024,2560]{1,0:T(8,128)(2,1)} %gate_up.6.refs_0_, bf16[1024,1536]{1,0:T(8,128)(2,1)} %gate_up.7.refs_1_, bf16[4096,1024]{1,0:T(8,128)(2,1)} %all-gather.20.cloned.1.call-done.refs_2_), custom_call_target="tpu_custom_call" | custom-call | flops 6442450944 | bytes 11534336 | tf_op jit(solution)/shard_map/down/pallas_call | solution.py:397
  748.7 10.0 %down.22.refs_0_ = bf16[512,768]{1,0:T(8,128)(2,1)} custom-call(s32[9]{0:T(128)} %stack.170.meta_ref, bf16[1024,2560]{1,0:T(8,128)(2,1)} %gate_up.5.refs_0_, bf16[512,1536]{1,0:T(8,128)(2,1)} %gate_up.8.refs_1_, bf16[4096,1024]{1,0:T(8,128)(2,1)} %all-gather.20.cloned.1.call-done.refs_2_, bf16[512,3072]{1,0:T(8,128)(2,1)} %get-tuple-element.60.refs_3_, ...), custom_call_target="tpu_custom_call" | custom-call | flops 3221225472 | bytes 9961472 | tf_op jit(solution)/shard_map/down/pallas_call | solution.py:397
  765.3 9.9 %down.23.refs_1_ = bf16[512,768]{1,0:T(8,128)(2,1)} custom-call(s32[9]{0:T(128)} %stack.170.meta_ref, bf16[1024,2560]{1,0:T(8,128)(2,1)} %gate_up.5.refs_0_, bf16[512,1536]{1,0:T(8,128)(2,1)} %gate_up.9.refs_1_, bf16[4096,1024]{1,0:T(8,128)(2,1)} %all-gather.20.cloned.1.call-done.refs_2_, bf16[512,3072]{1,0:T(8,128)(2,1)} %get-tuple-element.62.refs_3_, ...), custom_call_target="tpu_custom_call" | custom-call | flops 3221225472 | bytes 9961472 | tf_op jit(solution)/shard_map/down/pallas_call | solution.py:397
  802.3 10.9 %collective-permute-done.45.refs_5_ = bf16[512,768]{1,0:T(8,128)(2,1)} collective-permute-done((bf16[512,768]{1,0:T(8,128)(2,1)}, bf16[512,768]{1,0:T(8,128)(2,1)}, u32[]{:S(2)}, u32[]{:S(2)}) %collective-permute-start.45) | collective-permute-done | bytes 786464 | tf_op jit(solution)/shard_map/ppermute | solution.py:466
  823.0 9.4 %collective-permute-done.47.refs_3_ = bf16[512,768]{1,0:T(8,128)(2,1)} collective-permute-done((bf16[512,768]{1,0:T(8,128)(2,1)}, bf16[512,768]{1,0:T(8,128)(2,1)}, u32[]{:S(2)}, u32[]{:S(2)}) %collective-permute-start.47) | collective-permute-done | bytes 786464 | tf_op jit(solution)/shard_map/ppermute | solution.py:466
  837.9 9.0 %collective-permute-done.46.refs_1_ = bf16[512,768]{1,0:T(8,128)(2,1)} collective-permute-done((bf16[512,768]{1,0:T(8,128)(2,1)}, bf16[512,768]{1,0:T(8,128)(2,1)}, u32[]{:S(2)}, u32[]{:S(2)}) %collective-permute-start.46) | collective-permute-done | bytes 786464 | tf_op jit(solution)/shard_map/ppermute | solution.py:466
  (167 shorter events, 226.1 us)
Async XLA Ops:
  7.2 91.1 %all-gather.8.cloned.1.call-start = ((), (), s32[]{:S(2)}) async-start(), calls=%async_computation | async-start | bytes 8847360 | tf_op jit(solution)/shard_map/all_gather | solution.py:476
  9.6 304.0 %all-gather.10.cloned.1.call-start = ((), (), s32[]{:S(2)}) async-start(), calls=%async_computation.1 | async-start | bytes 21233664 | tf_op jit(solution)/shard_map/all_gather | solution.py:480
  43.3 330.9 %all-gather.12.cloned.1.call-start = ((), (), s32[]{:S(2)}) async-start(), calls=%async_computation.2 | async-start | bytes 35389440 | tf_op jit(solution)/shard_map/all_gather | solution.py:514
  46.3 96.4 %collective-permute-start = (bf16[384,2560]{1,0:T(8,128)(2,1)}, bf16[384,2560]{1,0:T(8,128)(2,1)}, u32[]{:S(2)}, u32[]{:S(2)}) collective-permute-start(bf16[384,2560]{1,0:T(8,128)(2,1)} %pad_maximum_fusion.4), channel_id=1, source_target_pairs={{0,16},{8,24},{16,0},{24,8},{1,17},{9,25},{17,1},{25,9},{2,18},{10... | collective-permute-start | bytes 5898248 | tf_op jit(solution)/shard_map/ppermute | solution.py:466
  145.7 336.1 %all-gather.14.cloned.1.call-start = ((), (), s32[]{:S(2)}) async-start(), calls=%async_computation.3 | async-start | bytes 21233664 | tf_op jit(solution)/shard_map/all_gather | solution.py:514
  148.1 38.9 %collective-permute-start.1 = (bf16[384,1536]{1,0:T(8,128)(2,1)}, bf16[384,1536]{1,0:T(8,128)(2,1)}, u32[]{:S(2)}, u32[]{:S(2)}) collective-permute-start(bf16[384,1536]{1,0:T(8,128)(2,1)} %pad_maximum_fusion.5), channel_id=1, source_target_pairs={{0,16},{8,24},{16,0},{24,8},{1,17},{9,25},{17,1},{25,9},{2,18},{10... | collective-permute-start | bytes 3538952 | tf_op jit(solution)/shard_map/ppermute | solution.py:466
  189.9 390.9 %all-gather.16.cloned.1.call-start = ((), (), s32[]{:S(2)}) async-start(), calls=%async_computation.4 | async-start | bytes 9437184 | tf_op jit(solution)/shard_map/all_gather | solution.py:518
  189.9 51.9 %collective-permute-start.2 = (bf16[2048,384]{1,0:T(8,128)(2,1)}, bf16[2048,384]{1,0:T(8,128)(2,1)}, u32[]{:S(2)}, u32[]{:S(2)}) collective-permute-start(bf16[2048,384]{1,0:T(8,128)(2,1)} %param.21), channel_id=1, source_target_pairs={{0,16},{8,24},{16,0},{24,8},{1,17},{9,25},{17,1},{25,9},{2,18},{10... | collective-permute-start | bytes 4718600 | tf_op jit(solution)/shard_map/ppermute | solution.py:466
  245.5 389.6 %all-gather.18.cloned.1.call-start = ((), (), s32[]{:S(2)}) async-start(), calls=%async_computation.5 | async-start | bytes 9437184 | tf_op jit(solution)/shard_map/all_gather | solution.py:518
  246.1 456.3 %all-gather.20.cloned.1.call-start = ((), (), s32[]{:S(2)}) async-start(), calls=%async_computation.6 | async-start | bytes 9437184 | tf_op jit(solution)/shard_map/all_gather | solution.py:518
  246.2 36.4 %collective-permute-start.16 = (bf16[4096,384]{1,0:T(8,128)(2,1)S(1)}, bf16[4096,384]{1,0:T(8,128)(2,1)}, u32[]{:S(2)}, u32[]{:S(2)}) collective-permute-start(bf16[4096,384]{1,0:T(8,128)(2,1)S(1)} %constant_dynamic-update-slice_fusion.4), channel_id=1, source_target_pairs={{0,1},{1,0},{2,3},{3,2},{4,5},{5,4},{6,7},{7,6},{8,9},{9,8},{10,11... | collective-permute-start | bytes 9437192 | tf_op jit(solution)/shard_map/ppermute | solution.py:516
  276.6 37.0 %collective-permute-start.4 = (bf16[512,768]{1,0:T(8,128)(2,1)}, bf16[512,768]{1,0:T(8,128)(2,1)}, u32[]{:S(2)}, u32[]{:S(2)}) collective-permute-start(bf16[512,768]{1,0:T(8,128)(2,1)} %get-tuple-element.105), channel_id=1, source_target_pairs={{0,16},{8,24},{16,0},{24,8},{1,17},{9,25},{17,1},{25,9},{2,18},{10... | collective-permute-start | bytes 2359304 | tf_op jit(solution)/shard_map/ppermute | solution.py:466
  281.1 57.5 %collective-permute-start.10 = (bf16[512,768]{1,0:T(8,128)(2,1)}, bf16[512,768]{1,0:T(8,128)(2,1)}, u32[]{:S(2)}, u32[]{:S(2)}) collective-permute-start(bf16[512,768]{1,0:T(8,128)(2,1)} %get-tuple-element.101), channel_id=1, source_target_pairs={{0,16},{8,24},{16,0},{24,8},{1,17},{9,25},{17,1},{25,9},{2,18},{10... | collective-permute-start | bytes 2359304 | tf_op jit(solution)/shard_map/ppermute | solution.py:466
  282.7 64.6 %collective-permute-start.11 = (bf16[512,768]{1,0:T(8,128)(2,1)}, bf16[512,768]{1,0:T(8,128)(2,1)}, u32[]{:S(2)}, u32[]{:S(2)}) collective-permute-start(bf16[512,768]{1,0:T(8,128)(2,1)} %get-tuple-element.100), channel_id=1, source_target_pairs={{0,24},{8,0},{16,8},{24,16},{1,25},{9,1},{17,9},{25,17},{2,26},{10... | collective-permute-start | bytes 2359304 | tf_op jit(solution)/shard_map/ppermute | solution.py:466
  296.3 51.5 %collective-permute-start.9 = (bf16[512,768]{1,0:T(8,128)(2,1)}, bf16[512,768]{1,0:T(8,128)(2,1)}, u32[]{:S(2)}, u32[]{:S(2)}) collective-permute-start(bf16[512,768]{1,0:T(8,128)(2,1)} %get-tuple-element.102), channel_id=1, source_target_pairs={{0,8},{8,16},{16,24},{24,0},{1,9},{9,17},{17,25},{25,1},{2,10},{10... | collective-permute-start | bytes 2359304 | tf_op jit(solution)/shard_map/ppermute | solution.py:466
  336.3 79.4 %collective-permute-start.12 = (bf16[256,3072]{1,0:T(8,128)(2,1)}, bf16[256,3072]{1,0:T(8,128)(2,1)}, u32[]{:S(2)}, u32[]{:S(2)}) collective-permute-start(bf16[256,3072]{1,0:T(8,128)(2,1)} %get-tuple-element.71.refs_0_), channel_id=1, source_target_pairs={{0,8},{8,16},{16,24},{24,0},{1,9},{9,17},{17,25},{25,1},{2,10},{10... | collective-permute-start | bytes 4718600 | tf_op jit(solution)/shard_map/ppermute | solution.py:466
  370.1 45.6 %collective-permute-start.14 = (bf16[256,3072]{1,0:T(8,128)(2,1)}, bf16[256,3072]{1,0:T(8,128)(2,1)}, u32[]{:S(2)}, u32[]{:S(2)}) collective-permute-start(bf16[256,3072]{1,0:T(8,128)(2,1)} %get-tuple-element.74.refs_2_.refs_0_), channel_id=1, source_target_pairs={{0,8},{8,16},{16,24},{24,0},{1,9},{9,17},{17,25},{25,1},{2,10},{10... | collective-permute-start | bytes 4718600 | tf_op jit(solution)/shard_map/ppermute | solution.py:466
  371.2 44.6 %collective-permute-start.15 = (bf16[256,3072]{1,0:T(8,128)(2,1)}, bf16[256,3072]{1,0:T(8,128)(2,1)}, u32[]{:S(2)}, u32[]{:S(2)}) collective-permute-start(bf16[256,3072]{1,0:T(8,128)(2,1)} %get-tuple-element.66.refs_3_.refs_1_), channel_id=1, source_target_pairs={{0,24},{8,0},{16,8},{24,16},{1,25},{9,1},{17,9},{25,17},{2,26},{10... | collective-permute-start | bytes 4718600 | tf_op jit(solution)/shard_map/ppermute | solution.py:466
  372.8 67.4 %collective-permute-start.13 = (bf16[256,3072]{1,0:T(8,128)(2,1)}, bf16[256,3072]{1,0:T(8,128)(2,1)}, u32[]{:S(2)}, u32[]{:S(2)}) collective-permute-start(bf16[256,3072]{1,0:T(8,128)(2,1)} %get-tuple-element.64.refs_1_), channel_id=1, source_target_pairs={{0,24},{8,0},{16,8},{24,16},{1,25},{9,1},{17,9},{25,17},{2,26},{10... | collective-permute-start | bytes 4718600 | tf_op jit(solution)/shard_map/ppermute | solution.py:466
  596.0 37.5 %collective-permute-start.27 = (bf16[512,768]{1,0:T(8,128)(2,1)}, bf16[512,768]{1,0:T(8,128)(2,1)}, u32[]{:S(2)}, u32[]{:S(2)}) collective-permute-start(bf16[512,768]{1,0:T(8,128)(2,1)} %down.14.refs_1_), channel_id=1, source_target_pairs={{0,24},{8,0},{16,8},{24,16},{1,25},{9,1},{17,9},{25,17},{2,26},{10... | collective-permute-start | bytes 2359304 | tf_op jit(solution)/shard_map/ppermute | solution.py:466
  598.6 51.6 %collective-permute-start.29 = (bf16[512,768]{1,0:T(8,128)(2,1)}, bf16[512,768]{1,0:T(8,128)(2,1)}, u32[]{:S(2)}, u32[]{:S(2)}) collective-permute-start(bf16[512,768]{1,0:T(8,128)(2,1)} %down.14.refs_1_), channel_id=1, source_target_pairs={{0,8},{8,16},{16,24},{24,0},{1,9},{9,17},{17,25},{25,1},{2,10},{10... | collective-permute-start | bytes 2359304 | tf_op jit(solution)/shard_map/ppermute | solution.py:466
  610.9 39.4 %collective-permute-start.30 = (bf16[512,768]{1,0:T(8,128)(2,1)}, bf16[512,768]{1,0:T(8,128)(2,1)}, u32[]{:S(2)}, u32[]{:S(2)}) collective-permute-start(bf16[512,768]{1,0:T(8,128)(2,1)} %down.13.refs_0_), channel_id=1, source_target_pairs={{0,24},{8,0},{16,8},{24,16},{1,25},{9,1},{17,9},{25,17},{2,26},{10... | collective-permute-start | bytes 2359304 | tf_op jit(solution)/shard_map/ppermute | solution.py:466
  650.3 50.6 %collective-permute-start.23 = (bf16[512,768]{1,0:T(8,128)(2,1)}, bf16[512,768]{1,0:T(8,128)(2,1)}, u32[]{:S(2)}, u32[]{:S(2)}) collective-permute-start(bf16[512,768]{1,0:T(8,128)(2,1)} %down.17.refs_1_), channel_id=1, source_target_pairs={{0,24},{8,0},{16,8},{24,16},{1,25},{9,1},{17,9},{25,17},{2,26},{10... | collective-permute-start | bytes 2359304 | tf_op jit(solution)/shard_map/ppermute | solution.py:466
  661.5 39.6 %collective-permute-start.21 = (bf16[512,768]{1,0:T(8,128)(2,1)}, bf16[512,768]{1,0:T(8,128)(2,1)}, u32[]{:S(2)}, u32[]{:S(2)}) collective-permute-start(bf16[512,768]{1,0:T(8,128)(2,1)} %down.16.refs_0_), channel_id=1, source_target_pairs={{0,8},{8,16},{16,24},{24,0},{1,9},{9,17},{17,25},{25,1},{2,10},{10... | collective-permute-start | bytes 2359304 | tf_op jit(solution)/shard_map/ppermute | solution.py:466
  668.2 49.4 %collective-permute-start.33 = (bf16[512,768]{1,0:T(8,128)(2,1)}, bf16[512,768]{1,0:T(8,128)(2,1)}, u32[]{:S(2)}, u32[]{:S(2)}) collective-permute-start(bf16[512,768]{1,0:T(8,128)(2,1)} %down.17.refs_1_), channel_id=1, source_target_pairs={{0,8},{8,16},{16,24},{24,0},{1,9},{9,17},{17,25},{25,1},{2,10},{10... | collective-permute-start | bytes 2359304 | tf_op jit(solution)/shard_map/ppermute | solution.py:466
  678.3 39.4 %collective-permute-start.34 = (bf16[512,768]{1,0:T(8,128)(2,1)}, bf16[512,768]{1,0:T(8,128)(2,1)}, u32[]{:S(2)}, u32[]{:S(2)}) collective-permute-start(bf16[512,768]{1,0:T(8,128)(2,1)} %down.16.refs_0_), channel_id=1, source_target_pairs={{0,24},{8,0},{16,8},{24,16},{1,25},{9,1},{17,9},{25,17},{2,26},{10... | collective-permute-start | bytes 2359304 | tf_op jit(solution)/shard_map/ppermute | solution.py:466
  717.7 44.9 %collective-permute-start.40 = (bf16[512,768]{1,0:T(8,128)(2,1)}, bf16[512,768]{1,0:T(8,128)(2,1)}, u32[]{:S(2)}, u32[]{:S(2)}) collective-permute-start(bf16[512,768]{1,0:T(8,128)(2,1)} %down.20.refs_1_), channel_id=1, source_target_pairs={{0,24},{8,0},{16,8},{24,16},{1,25},{9,1},{17,9},{25,17},{2,26},{10... | collective-permute-start | bytes 2359304 | tf_op jit(solution)/shard_map/ppermute | solution.py:466
  728.9 36.4 %collective-permute-start.38 = (bf16[512,768]{1,0:T(8,128)(2,1)}, bf16[512,768]{1,0:T(8,128)(2,1)}, u32[]{:S(2)}, u32[]{:S(2)}) collective-permute-start(bf16[512,768]{1,0:T(8,128)(2,1)} %down.19.refs_0_), channel_id=1, source_target_pairs={{0,8},{8,16},{16,24},{24,0},{1,9},{9,17},{17,25},{25,1},{2,10},{10... | collective-permute-start | bytes 2359304 | tf_op jit(solution)/shard_map/ppermute | solution.py:466
  731.3 50.6 %collective-permute-start.42 = (bf16[512,768]{1,0:T(8,128)(2,1)}, bf16[512,768]{1,0:T(8,128)(2,1)}, u32[]{:S(2)}, u32[]{:S(2)}) collective-permute-start(bf16[512,768]{1,0:T(8,128)(2,1)} %down.20.refs_1_), channel_id=1, source_target_pairs={{0,8},{8,16},{16,24},{24,0},{1,9},{9,17},{17,25},{25,1},{2,10},{10... | collective-permute-start | bytes 2359304 | tf_op jit(solution)/shard_map/ppermute | solution.py:466
  745.7 36.1 %collective-permute-start.43 = (bf16[512,768]{1,0:T(8,128)(2,1)}, bf16[512,768]{1,0:T(8,128)(2,1)}, u32[]{:S(2)}, u32[]{:S(2)}) collective-permute-start(bf16[512,768]{1,0:T(8,128)(2,1)} %down.19.refs_0_), channel_id=1, source_target_pairs={{0,24},{8,0},{16,8},{24,16},{1,25},{9,1},{17,9},{25,17},{2,26},{10... | collective-permute-start | bytes 2359304 | tf_op jit(solution)/shard_map/ppermute | solution.py:466
  775.2 37.9 %collective-permute-start.45 = (bf16[512,768]{1,0:T(8,128)(2,1)}, bf16[512,768]{1,0:T(8,128)(2,1)}, u32[]{:S(2)}, u32[]{:S(2)}) collective-permute-start(bf16[512,768]{1,0:T(8,128)(2,1)} %down.23.refs_1_), channel_id=1, source_target_pairs={{0,24},{8,0},{16,8},{24,16},{1,25},{9,1},{17,9},{25,17},{2,26},{10... | collective-permute-start | bytes 2359304 | tf_op jit(solution)/shard_map/ppermute | solution.py:466
  781.9 50.6 %collective-permute-start.47 = (bf16[512,768]{1,0:T(8,128)(2,1)}, bf16[512,768]{1,0:T(8,128)(2,1)}, u32[]{:S(2)}, u32[]{:S(2)}) collective-permute-start(bf16[512,768]{1,0:T(8,128)(2,1)} %down.23.refs_1_), channel_id=1, source_target_pairs={{0,8},{8,16},{16,24},{24,0},{1,9},{9,17},{17,25},{25,1},{2,10},{10... | collective-permute-start | bytes 2359304 | tf_op jit(solution)/shard_map/ppermute | solution.py:466
  (35 other events, 747.7 us)
Sparse Core Ops, SparseCore 0:
  9.7 49.2 all-gather.7
  60.7 91.1 all-gather.9
  153.4 145.1 all-gather.11
  300.1 92.0 all-gather.13
  393.6 51.5 all-gather.15
  446.7 51.7 all-gather.17
  500.0 51.7 all-gather.19

commit v9 on v8

--- a/solution.py
+++ b/solution.py
@@ -38,20 +38,8 @@
     return (vals_f32 * inv * gain).astype(jnp.bfloat16)
 
 
-def norm_into(x_ref, gain, store):
-    rows = min(16, x_ref.shape[0])
-
-    @pl.loop(0, x_ref.shape[0] // rows)
-    def _(i):
-        r = pl.ds(pl.multiple_of(i * rows, rows), rows)
-        store(r, norm_rows(x_ref[r, :].astype(jnp.float32), gain))
-
-
 def norm_kernel(x_ref, g_ref, h_ref):
-    def store(r, val):
-        h_ref[r, :] = val
-
-    norm_into(x_ref, g_ref[...].astype(jnp.float32), store)
+    h_ref[...] = norm_rows(x_ref[...].astype(jnp.float32), g_ref[...].astype(jnp.float32))
 
 
 def norm_call(x, gain):
@@ -232,12 +220,9 @@
     @pl.when(n == pl.num_programs(0) - 1)
     def _():
         r_ref[...] = y_ref[...]
-        gain = g_ref[...].astype(jnp.float32)
-        for part, u_ref in enumerate((ua_ref, ub_ref)):
-            def store(r, val, u_ref=u_ref):
-                u_ref[r, :] = val
-
-            norm_into(y_ref.at[part * half:(part + 1) * half, :], gain, store)
+        u = norm_rows(y_ref[...].astype(jnp.float32), g_ref[...].astype(jnp.float32))
+        ua_ref[...] = u[:half]
+        ub_ref[...] = u[half:]
 
 
 def out_call(idx, o_pieces, w, x, gain):
@@ -358,23 +343,22 @@
                 part = jnp.dot(a_refs[p][r, j * kp:(j + 1) * kp], w_ref[k0:k0 + kp, :], preferred_element_type=jnp.float32)
                 acc = part if acc is None else acc + part
                 k0 += kp
+        half = bm // 2
         if own:
             @pl.when((n == 0) & (m == 0))
             def _():
                 for c in more:
                     c.wait()
 
+            cols = pl.ds(pl.multiple_of(n * bn, bn), bn)
             for h in range(2):
-                @pl.when(m == h)
-                def _():
-                    base = r_ref[r, pl.ds(pl.multiple_of(n * bn, bn), bn)].astype(jnp.float32)
-                    outs[0][r, :] = (base + (acc + partials[h][...].astype(jnp.float32))).astype(jnp.bfloat16)
+                rr = slice(h * half, (h + 1) * half)
+                part = acc[rr] + partials[h][...].astype(jnp.float32)
+                outs[0][rr, :] = (r_ref[rr, cols].astype(jnp.float32) + part).astype(jnp.bfloat16)
         else:
-            out = pl.ds(pl.multiple_of(m // 2 * bm, bm), bm)
+            out = pl.ds(pl.multiple_of(m * half, half), half)
             for h in range(2):
-                @pl.when(m % 2 == h)
-                def _():
-                    outs[h][out, :] = acc.astype(jnp.bfloat16)
+                outs[h][out, :] = acc[h * half:(h + 1) * half].astype(jnp.bfloat16)
 
 
 def down_call(a_parts, w, meta, n_src, bn, steps, rows, call=0, resid=None, partials=()):
@@ -382,7 +366,7 @@
     cols = steps * bn
     own = resid is not None
     half = rows // 2
-    bm = half if own else half // N_CALLS
+    bm = rows if own else rows // N_CALLS
     step = lambda n, meta: (0, n)
     anywhere = pl.BlockSpec(memory_space=pl.ANY)
     args = [*a_parts, w]

time: 870 us -> 855 us (0.983)
  Pallas kernels: 521 us -> 503 us
    pallas_call x1, Pallas kernels: 37.8 us -> 24.4 us  [norm_call(): pl.pallas_call(norm_kernel, grid=(s // bm,), in_specs=[pl.BlockSpec((bm,...]
  transfers between devices with their start and end apart: 56 -> 56, of which waited for: 22 -> 24; matrix products, arithmetic and copies ran while one was open for 6% -> 6% of each run, Pallas kernels for 60% -> 59%
where the time goes in v9:
time: 855 us; the launch traced here: 843 us
  Pallas kernels  503 us (59%)
  waiting for transfers between devices  176 us (21%)
  starting transfers between devices  91.7 us (11%)
  local copies, waits for them, and re-layouts  33.7 us (4%)
  other arithmetic  23.5 us (3%)
  between operations  15.5 us (2%)
    ppermute x48, waiting for transfers between devices, shift(): return lax.ppermute(val, tp, [(i, (i + s) % n_tp) for i in range(n_tp)])  176 us
    pallas_call x5, Pallas kernels, gu_call(): pl.pallas_call(functools.partial(gu_kernel, bm, n_u), grid=(n_src, nb), i...  143 us
    pallas_call x12, Pallas kernels, down_call(): pl.pallas_call(functools.partial(down_kernel, bm, parts, n_src, own, row0...  135 us
    pallas_call x2, Pallas kernels, att_call(): pl.pallas_call(functools.partial(att_kernel, bq, bk, per, first), grid=(n...  83.8 us
    ppermute x48, starting transfers between devices, shift(): return lax.ppermute(val, tp, [(i, (i + s) % n_tp) for i in range(n_tp)])  66.8 us
    pallas_call x1, Pallas kernels, qkv_call(): pl.pallas_call(functools.partial(qkv_kernel, n_q, n_kv), grid=(s // bm,),...  41.2 us
    pallas_call x2, Pallas kernels, out_call(): pl.pallas_call(functools.partial(out_kernel, n_src), grid_spec=pltpu.Pref...  40.9 us
    pallas_call x8, Pallas kernels, place_call(): pl.pallas_call(functools.partial(place_kernel, n_in, moves, n_tp, skip),...  34.8 us
  transfers between devices with their start and end apart: 56, of which 24 were waited for; matrix products, arithmetic and copies ran while one was open for 6% of the time, Pallas kernels for 59%

profile of v9, /device:TPU:97, one launch (start us, length us, event | category | flops | bytes accessed | tf_op | source)
XLA Modules:
  0.0 843.4 jit_solution(11353947568831184117)
XLA Ops:
  16.7 11.5 %collective-permute-done.6 = bf16[768,384]{1,0:T(8,128)(2,1)S(1)} collective-permute-done((bf16[768,384]{1,0:T(8,128)(2,1)S(1)}, bf16[768,384]{1,0:T(8,128)(2,1)S(1)}, u32[]{:S(2)}, u32[]{:S(2)}) %collective-permute-start.6) | collective-permute-done | bytes 589856 | tf_op jit(solution)/shard_map/ppermute | solution.py:450
  28.2 13.4 %collective-permute-done.7 = bf16[768,384]{1,0:T(8,128)(2,1)S(1)} collective-permute-done((bf16[768,384]{1,0:T(8,128)(2,1)S(1)}, bf16[768,384]{1,0:T(8,128)(2,1)S(1)}, u32[]{:S(2)}, u32[]{:S(2)}) %collective-permute-start.7) | collective-permute-done | bytes 589856 | tf_op jit(solution)/shard_map/ppermute | solution.py:450
  49.1 24.4 %norm.1.h_ref = bf16[4096,3072]{1,0:T(8,128)(2,1)} custom-call(bf16[4096,3072]{1,0:T(8,128)(2,1)} %bitcast.37, bf16[1,3072]{1,0:T(2,128)(2,1)} %reshape.63.g_ref), custom_call_target="tpu_custom_call" | custom-call | flops 100663296 | bytes 50331648 | tf_op jit(solution)/shard_map/norm/pallas_call | solution.py:48
  84.9 41.2 %qkv.1 = (bf16[6,4096,128]{2,1,0:T(8,128)(2,1)}, bf16[4096,256]{1,0:T(8,128)(2,1)}, bf16[4096,256]{1,0:T(8,128)(2,1)}, bf16[256,4096]{1,0:T(8,128)(2,1)}) custom-call(bf16[4096,3072]{1,0:T(8,128)(2,1)} %norm.1.h_ref, bf16[3072,1280]{1,0:T(8,128)(2,1)} %all-gather.8.cloned.1.call-done.w_ref, f32[4096,128]{1,0:T(8,128)} %get-tuple-element.111.cos_ref, ...), custom_call_target="tpu_custom_call" | custom-call | flops 32212254720 | bytes 43515904 | tf_op jit(solution)/shard_map/qkv/pallas_call | solution.py:85
  136.1 35.4 %attention.2 = bf16[2048,768]{1,0:T(8,128)(2,1)} custom-call(s32[1]{0:T(128)S(6)} %copy.32.len_ref, bf16[6,4096,128]{2,1,0:T(8,128)(2,1)} %get-tuple-element.56.q_ref, bf16[4096,256]{1,0:T(8,128)(2,1)} %get-tuple-element.53.k_ref, bf16[256,4096]{1,0:T(8,128)(2,1)} %get-tuple-element.54.vt_ref), custom_call_target="tpu_custom_call" | custom-call | flops 25769803776 | bytes 12582912 | tf_op jit(solution)/shard_map/attention/pallas_call | solution.py:186
  178.2 48.5 %attention.3 = bf16[2048,768]{1,0:T(8,128)(2,1)} custom-call(s32[1]{0:T(128)S(6)} %copy.32.len_ref, bf16[6,4096,128]{2,1,0:T(8,128)(2,1)} %get-tuple-element.56.q_ref, bf16[4096,256]{1,0:T(8,128)(2,1)} %get-tuple-element.53.k_ref, bf16[256,4096]{1,0:T(8,128)(2,1)} %get-tuple-element.54.vt_ref), custom_call_target="tpu_custom_call" | custom-call | flops 77309411328 | bytes 12582912 | tf_op jit(solution)/shard_map/attention/pallas_call | solution.py:186
  232.7 24.3 %collective-permute-start.16 = (bf16[4096,384]{1,0:T(8,128)(2,1)S(1)}, bf16[4096,384]{1,0:T(8,128)(2,1)}, u32[]{:S(2)}, u32[]{:S(2)}) collective-permute-start(bf16[4096,384]{1,0:T(8,128)(2,1)S(1)} %constant_dynamic-update-slice_fusion.4), channel_id=1, source_target_pairs={{0,1},{1,0},{2,3},{3,2},{4,5},{5,4},{6,7},{7,6},{8,9},{9,8},{10,11... | collective-permute-start | bytes 9437192 | tf_op jit(solution)/shard_map/ppermute | solution.py:500
  283.2 16.7 %collective-permute-done.4.refs_2_ = bf16[512,768]{1,0:T(8,128)(2,1)} collective-permute-done((bf16[512,768]{1,0:T(8,128)(2,1)}, bf16[512,768]{1,0:T(8,128)(2,1)}, u32[]{:S(2)}, u32[]{:S(2)}) %collective-permute-start.4) | collective-permute-done | bytes 786464 | tf_op jit(solution)/shard_map/ppermute | solution.py:450
  300.2 20.7 %w_out.2 = (bf16[512,3072]{1,0:T(8,128)(2,1)}, bf16[256,3072]{1,0:T(8,128)(2,1)}, bf16[256,3072]{1,0:T(8,128)(2,1)}) custom-call(s32[1]{0:T(128)} %bitcast.31.idx_ref, bf16[512,768]{1,0:T(8,128)(2,1)} %get-tuple-element.58.refs_0_, bf16[512,768]{1,0:T(8,128)(2,1)} %collective-permute-done.3.refs_1_, bf16[512,768]{1,0:T(8,128)(2,1)} %collective-permute-done.4.refs_2_, ...), custom_call_target="tpu_custom_call" | custom-call | flops 9663676416 | bytes 31457280 | tf_op jit(solution)/shard_map/w_out/pallas_call | solution.py:235
  322.8 11.1 %collective-permute-done.11.refs_3_ = bf16[512,768]{1,0:T(8,128)(2,1)} collective-permute-done((bf16[512,768]{1,0:T(8,128)(2,1)}, bf16[512,768]{1,0:T(8,128)(2,1)}, u32[]{:S(2)}, u32[]{:S(2)}) %collective-permute-start.11) | collective-permute-done | bytes 786464 | tf_op jit(solution)/shard_map/ppermute | solution.py:450
  334.1 20.1 %w_out.3 = (bf16[512,3072]{1,0:T(8,128)(2,1)}, bf16[256,3072]{1,0:T(8,128)(2,1)}, bf16[256,3072]{1,0:T(8,128)(2,1)}) custom-call(s32[1]{0:T(128)} %bitcast.34.idx_ref, bf16[512,768]{1,0:T(8,128)(2,1)} %get-tuple-element.61.refs_0_, bf16[512,768]{1,0:T(8,128)(2,1)} %collective-permute-done.9.refs_1_, bf16[512,768]{1,0:T(8,128)(2,1)} %collective-permute-done.10.refs_2_, ...), custom_call_target="tpu_custom_call" | custom-call | flops 9663676416 | bytes 31457280 | tf_op jit(solution)/shard_map/w_out/pallas_call | solution.py:235
  358.5 41.6 %gate_up.5.refs_0_ = bf16[1024,2560]{1,0:T(8,128)(2,1)} custom-call(bf16[256,3072]{1,0:T(8,128)(2,1)} %get-tuple-element.71.refs_0_, bf16[256,3072]{1,0:T(8,128)(2,1)} %get-tuple-element.64.refs_1_, bf16[256,3072]{1,0:T(8,128)(2,1)} %get-tuple-element.74.refs_2_.refs_0_, bf16[256,3072]{1,0:T(8,128)(2,1)} %get-tuple-element.66.refs_3_.refs_1_, ...), custom_call_target="tpu_custom_call" | custom-call | flops 32212254720 | bytes 42991616 | tf_op jit(solution)/shard_map/gate_up/pallas_call | solution.py:287
  401.5 22.7 %collective-permute-done.13.refs_1_ = bf16[256,3072]{1,0:T(8,128)(2,1)} collective-permute-done((bf16[256,3072]{1,0:T(8,128)(2,1)}, bf16[256,3072]{1,0:T(8,128)(2,1)}, u32[]{:S(2)}, u32[]{:S(2)}) %collective-permute-start.13) | collective-permute-done | bytes 1572896 | tf_op jit(solution)/shard_map/ppermute | solution.py:450
  424.3 41.4 %gate_up.6.refs_0_ = bf16[1024,2560]{1,0:T(8,128)(2,1)} custom-call(bf16[256,3072]{1,0:T(8,128)(2,1)} %collective-permute-done.12.refs_0_, bf16[256,3072]{1,0:T(8,128)(2,1)} %collective-permute-done.13.refs_1_, bf16[256,3072]{1,0:T(8,128)(2,1)} %collective-permute-done.14.refs_2_, bf16[256,3072]{1,0:T(8,128)(2,1)} %collective-permute-done.15.refs_3_, ...), custom_call_target="tpu_custom_call" | custom-call | flops 32212254720 | bytes 42991616 | tf_op jit(solution)/shard_map/gate_up/pallas_call | solution.py:287
  465.7 26.8 %gate_up.7.refs_1_ = bf16[1024,1536]{1,0:T(8,128)(2,1)} custom-call(bf16[256,3072]{1,0:T(8,128)(2,1)} %collective-permute-done.12.refs_0_, bf16[256,3072]{1,0:T(8,128)(2,1)} %collective-permute-done.13.refs_1_, bf16[256,3072]{1,0:T(8,128)(2,1)} %collective-permute-done.14.refs_2_, bf16[256,3072]{1,0:T(8,128)(2,1)} %collective-permute-done.15.refs_3_, ...), custom_call_target="tpu_custom_call" | custom-call | flops 19327352832 | bytes 28311552 | tf_op jit(solution)/shard_map/gate_up/pallas_call | solution.py:287
  492.5 13.3 %down.12 = (bf16[512,768]{1,0:T(8,128)(2,1)}, bf16[512,768]{1,0:T(8,128)(2,1)}) custom-call(s32[9]{0:T(128)} %stack.172.meta_ref, bf16[1024,2560]{1,0:T(8,128)(2,1)} %gate_up.6.refs_0_, bf16[1024,1536]{1,0:T(8,128)(2,1)} %gate_up.7.refs_1_, bf16[4096,768]{1,0:T(8,128)(2,1)} %pad_maximum_fusion.refs_2_), custom_call_target="tpu_custom_call" | custom-call | flops 6442450944 | bytes 9437184 | tf_op jit(solution)/shard_map/down/pallas_call | solution.py:381
  508.8 16.6 %gate_up.8.refs_1_ = bf16[512,1536]{1,0:T(8,128)(2,1)} custom-call(bf16[256,3072]{1,0:T(8,128)(2,1)} %get-tuple-element.71.refs_0_, bf16[256,3072]{1,0:T(8,128)(2,1)} %get-tuple-element.64.refs_1_, bf16[3072,3072]{1,0:T(8,128)(2,1)} %all-gather.14.cloned.1.call-done.refs_4_.refs_5_.refs_2_.refs_3_, ...), custom_call_target="tpu_custom_call" | custom-call | flops 9663676416 | bytes 23592960 | tf_op jit(solution)/shard_map/gate_up/pallas_call | solution.py:287
  527.0 10.3 %down.13.refs_0_ = bf16[512,768]{1,0:T(8,128)(2,1)} custom-call(s32[9]{0:T(128)} %stack.172.meta_ref, bf16[1024,2560]{1,0:T(8,128)(2,1)} %gate_up.5.refs_0_, bf16[512,1536]{1,0:T(8,128)(2,1)} %gate_up.8.refs_1_, bf16[4096,768]{1,0:T(8,128)(2,1)} %pad_maximum_fusion.refs_2_, bf16[512,3072]{1,0:T(8,128)(2,1)} %get-tuple-element.60.refs_3_, ...), custom_call_target="tpu_custom_call" | custom-call | flops 3221225472 | bytes 7864320 | tf_op jit(solution)/shard_map/down/pallas_call | solution.py:381
  537.3 16.5 %gate_up.9.refs_1_ = bf16[512,1536]{1,0:T(8,128)(2,1)} custom-call(bf16[256,3072]{1,0:T(8,128)(2,1)} %get-tuple-element.74.refs_2_.refs_0_, bf16[256,3072]{1,0:T(8,128)(2,1)} %get-tuple-element.66.refs_3_.refs_1_, bf16[3072,3072]{1,0:T(8,128)(2,1)} %all-gather.14.cloned.1.call-done.refs_4_.refs_5_.refs_2_.refs_3_, ...), custom_call_target="tpu_custom_call" | custom-call | flops 9663676416 | bytes 23592960 | tf_op jit(solution)/shard_map/gate_up/pallas_call | solution.py:287
  553.7 10.3 %down.14.refs_1_ = bf16[512,768]{1,0:T(8,128)(2,1)} custom-call(s32[9]{0:T(128)} %stack.172.meta_ref, bf16[1024,2560]{1,0:T(8,128)(2,1)} %gate_up.5.refs_0_, bf16[512,1536]{1,0:T(8,128)(2,1)} %gate_up.9.refs_1_, bf16[4096,768]{1,0:T(8,128)(2,1)} %pad_maximum_fusion.refs_2_, bf16[512,3072]{1,0:T(8,128)(2,1)} %get-tuple-element.62.refs_3_, ...), custom_call_target="tpu_custom_call" | custom-call | flops 3221225472 | bytes 7864320 | tf_op jit(solution)/shard_map/down/pallas_call | solution.py:381
  564.0 13.0 %down.15 = (bf16[512,768]{1,0:T(8,128)(2,1)}, bf16[512,768]{1,0:T(8,128)(2,1)}) custom-call(s32[9]{0:T(128)} %stack.171.meta_ref, bf16[1024,2560]{1,0:T(8,128)(2,1)} %gate_up.6.refs_0_, bf16[1024,1536]{1,0:T(8,128)(2,1)} %gate_up.7.refs_1_, bf16[4096,1024]{1,0:T(8,128)(2,1)} %all-gather.16.cloned.1.call-done.refs_2_), custom_call_target="tpu_custom_call" | custom-call | flops 6442450944 | bytes 11534336 | tf_op jit(solution)/shard_map/down/pallas_call | solution.py:381
  582.1 11.9 %collective-permute-done.19.refs_4_ = bf16[512,768]{1,0:T(8,128)(2,1)} collective-permute-done((bf16[512,768]{1,0:T(8,128)(2,1)}, bf16[512,768]{1,0:T(8,128)(2,1)}, u32[]{:S(2)}, u32[]{:S(2)}) %collective-permute-start.19) | collective-permute-done | bytes 786464 | tf_op jit(solution)/shard_map/ppermute | solution.py:450
  597.4 10.3 %down.16.refs_0_ = bf16[512,768]{1,0:T(8,128)(2,1)} custom-call(s32[9]{0:T(128)} %stack.171.meta_ref, bf16[1024,2560]{1,0:T(8,128)(2,1)} %gate_up.5.refs_0_, bf16[512,1536]{1,0:T(8,128)(2,1)} %gate_up.8.refs_1_, bf16[4096,1024]{1,0:T(8,128)(2,1)} %all-gather.16.cloned.1.call-done.refs_2_, bf16[512,3072]{1,0:T(8,128)(2,1)} %get-tuple-element.60.refs_3_, ...), custom_call_target="tpu_custom_call" | custom-call | flops 3221225472 | bytes 9961472 | tf_op jit(solution)/shard_map/down/pallas_call | solution.py:381
  607.7 10.3 %down.17.refs_1_ = bf16[512,768]{1,0:T(8,128)(2,1)} custom-call(s32[9]{0:T(128)} %stack.171.meta_ref, bf16[1024,2560]{1,0:T(8,128)(2,1)} %gate_up.5.refs_0_, bf16[512,1536]{1,0:T(8,128)(2,1)} %gate_up.9.refs_1_, bf16[4096,1024]{1,0:T(8,128)(2,1)} %all-gather.16.cloned.1.call-done.refs_2_, bf16[512,3072]{1,0:T(8,128)(2,1)} %get-tuple-element.62.refs_3_, ...), custom_call_target="tpu_custom_call" | custom-call | flops 3221225472 | bytes 9961472 | tf_op jit(solution)/shard_map/down/pallas_call | solution.py:381
  619.6 13.0 %down.18 = (bf16[512,768]{1,0:T(8,128)(2,1)}, bf16[512,768]{1,0:T(8,128)(2,1)}) custom-call(s32[9]{0:T(128)} %stack.173.meta_ref, bf16[1024,2560]{1,0:T(8,128)(2,1)} %gate_up.6.refs_0_, bf16[1024,1536]{1,0:T(8,128)(2,1)} %gate_up.7.refs_1_, bf16[4096,1024]{1,0:T(8,128)(2,1)} %all-gather.18.cloned.1.call-done.refs_2_), custom_call_target="tpu_custom_call" | custom-call | flops 6442450944 | bytes 11534336 | tf_op jit(solution)/shard_map/down/pallas_call | solution.py:381
  664.8 10.2 %down.19.refs_0_ = bf16[512,768]{1,0:T(8,128)(2,1)} custom-call(s32[9]{0:T(128)} %stack.173.meta_ref, bf16[1024,2560]{1,0:T(8,128)(2,1)} %gate_up.5.refs_0_, bf16[512,1536]{1,0:T(8,128)(2,1)} %gate_up.8.refs_1_, bf16[4096,1024]{1,0:T(8,128)(2,1)} %all-gather.18.cloned.1.call-done.refs_2_, bf16[512,3072]{1,0:T(8,128)(2,1)} %get-tuple-element.60.refs_3_, ...), custom_call_target="tpu_custom_call" | custom-call | flops 3221225472 | bytes 9961472 | tf_op jit(solution)/shard_map/down/pallas_call | solution.py:381
  675.1 10.3 %down.20.refs_1_ = bf16[512,768]{1,0:T(8,128)(2,1)} custom-call(s32[9]{0:T(128)} %stack.173.meta_ref, bf16[1024,2560]{1,0:T(8,128)(2,1)} %gate_up.5.refs_0_, bf16[512,1536]{1,0:T(8,128)(2,1)} %gate_up.9.refs_1_, bf16[4096,1024]{1,0:T(8,128)(2,1)} %all-gather.18.cloned.1.call-done.refs_2_, bf16[512,3072]{1,0:T(8,128)(2,1)} %get-tuple-element.62.refs_3_, ...), custom_call_target="tpu_custom_call" | custom-call | flops 3221225472 | bytes 9961472 | tf_op jit(solution)/shard_map/down/pallas_call | solution.py:381
  687.1 13.0 %down.21 = (bf16[512,768]{1,0:T(8,128)(2,1)}, bf16[512,768]{1,0:T(8,128)(2,1)}) custom-call(s32[9]{0:T(128)} %stack.170.meta_ref, bf16[1024,2560]{1,0:T(8,128)(2,1)} %gate_up.6.refs_0_, bf16[1024,1536]{1,0:T(8,128)(2,1)} %gate_up.7.refs_1_, bf16[4096,1024]{1,0:T(8,128)(2,1)} %all-gather.20.cloned.1.call-done.refs_2_), custom_call_target="tpu_custom_call" | custom-call | flops 6442450944 | bytes 11534336 | tf_op jit(solution)/shard_map/down/pallas_call | solution.py:381
  732.2 10.3 %down.22.refs_0_ = bf16[512,768]{1,0:T(8,128)(2,1)} custom-call(s32[9]{0:T(128)} %stack.170.meta_ref, bf16[1024,2560]{1,0:T(8,128)(2,1)} %gate_up.5.refs_0_, bf16[512,1536]{1,0:T(8,128)(2,1)} %gate_up.8.refs_1_, bf16[4096,1024]{1,0:T(8,128)(2,1)} %all-gather.20.cloned.1.call-done.refs_2_, bf16[512,3072]{1,0:T(8,128)(2,1)} %get-tuple-element.60.refs_3_, ...), custom_call_target="tpu_custom_call" | custom-call | flops 3221225472 | bytes 9961472 | tf_op jit(solution)/shard_map/down/pallas_call | solution.py:381
  749.1 10.3 %down.23.refs_1_ = bf16[512,768]{1,0:T(8,128)(2,1)} custom-call(s32[9]{0:T(128)} %stack.170.meta_ref, bf16[1024,2560]{1,0:T(8,128)(2,1)} %gate_up.5.refs_0_, bf16[512,1536]{1,0:T(8,128)(2,1)} %gate_up.9.refs_1_, bf16[4096,1024]{1,0:T(8,128)(2,1)} %all-gather.20.cloned.1.call-done.refs_2_, bf16[512,3072]{1,0:T(8,128)(2,1)} %get-tuple-element.62.refs_3_, ...), custom_call_target="tpu_custom_call" | custom-call | flops 3221225472 | bytes 9961472 | tf_op jit(solution)/shard_map/down/pallas_call | solution.py:381
  786.1 10.2 %collective-permute-done.45.refs_5_ = bf16[512,768]{1,0:T(8,128)(2,1)} collective-permute-done((bf16[512,768]{1,0:T(8,128)(2,1)}, bf16[512,768]{1,0:T(8,128)(2,1)}, u32[]{:S(2)}, u32[]{:S(2)}) %collective-permute-start.45) | collective-permute-done | bytes 786464 | tf_op jit(solution)/shard_map/ppermute | solution.py:450
  806.8 9.4 %collective-permute-done.47.refs_3_ = bf16[512,768]{1,0:T(8,128)(2,1)} collective-permute-done((bf16[512,768]{1,0:T(8,128)(2,1)}, bf16[512,768]{1,0:T(8,128)(2,1)}, u32[]{:S(2)}, u32[]{:S(2)}) %collective-permute-start.47) | collective-permute-done | bytes 786464 | tf_op jit(solution)/shard_map/ppermute | solution.py:450
  (167 shorter events, 229.0 us)
Async XLA Ops:
  7.2 77.7 %all-gather.8.cloned.1.call-start = ((), (), s32[]{:S(2)}) async-start(), calls=%async_computation | async-start | bytes 8847360 | tf_op jit(solution)/shard_map/all_gather | solution.py:460
  9.6 290.6 %all-gather.10.cloned.1.call-start = ((), (), s32[]{:S(2)}) async-start(), calls=%async_computation.1 | async-start | bytes 21233664 | tf_op jit(solution)/shard_map/all_gather | solution.py:464
  43.3 315.2 %all-gather.12.cloned.1.call-start = ((), (), s32[]{:S(2)}) async-start(), calls=%async_computation.2 | async-start | bytes 35389440 | tf_op jit(solution)/shard_map/all_gather | solution.py:498
  46.3 82.9 %collective-permute-start = (bf16[384,2560]{1,0:T(8,128)(2,1)}, bf16[384,2560]{1,0:T(8,128)(2,1)}, u32[]{:S(2)}, u32[]{:S(2)}) collective-permute-start(bf16[384,2560]{1,0:T(8,128)(2,1)} %pad_maximum_fusion.4), channel_id=1, source_target_pairs={{0,16},{8,24},{16,0},{24,8},{1,17},{9,25},{17,1},{25,9},{2,18},{10... | collective-permute-start | bytes 5898248 | tf_op jit(solution)/shard_map/ppermute | solution.py:450
  132.2 333.4 %all-gather.14.cloned.1.call-start = ((), (), s32[]{:S(2)}) async-start(), calls=%async_computation.3 | async-start | bytes 21233664 | tf_op jit(solution)/shard_map/all_gather | solution.py:498
  134.5 38.5 %collective-permute-start.1 = (bf16[384,1536]{1,0:T(8,128)(2,1)}, bf16[384,1536]{1,0:T(8,128)(2,1)}, u32[]{:S(2)}, u32[]{:S(2)}) collective-permute-start(bf16[384,1536]{1,0:T(8,128)(2,1)} %pad_maximum_fusion.5), channel_id=1, source_target_pairs={{0,16},{8,24},{16,0},{24,8},{1,17},{9,25},{17,1},{25,9},{2,18},{10... | collective-permute-start | bytes 3538952 | tf_op jit(solution)/shard_map/ppermute | solution.py:450
  176.0 388.1 %all-gather.16.cloned.1.call-start = ((), (), s32[]{:S(2)}) async-start(), calls=%async_computation.4 | async-start | bytes 9437184 | tf_op jit(solution)/shard_map/all_gather | solution.py:502
  176.0 52.2 %collective-permute-start.2 = (bf16[2048,384]{1,0:T(8,128)(2,1)}, bf16[2048,384]{1,0:T(8,128)(2,1)}, u32[]{:S(2)}, u32[]{:S(2)}) collective-permute-start(bf16[2048,384]{1,0:T(8,128)(2,1)} %param.21), channel_id=1, source_target_pairs={{0,16},{8,24},{16,0},{24,8},{1,17},{9,25},{17,1},{25,9},{2,18},{10... | collective-permute-start | bytes 4718600 | tf_op jit(solution)/shard_map/ppermute | solution.py:450
  231.9 387.6 %all-gather.18.cloned.1.call-start = ((), (), s32[]{:S(2)}) async-start(), calls=%async_computation.5 | async-start | bytes 9437184 | tf_op jit(solution)/shard_map/all_gather | solution.py:502
  232.6 454.5 %all-gather.20.cloned.1.call-start = ((), (), s32[]{:S(2)}) async-start(), calls=%async_computation.6 | async-start | bytes 9437184 | tf_op jit(solution)/shard_map/all_gather | solution.py:502
  262.8 37.1 %collective-permute-start.4 = (bf16[512,768]{1,0:T(8,128)(2,1)}, bf16[512,768]{1,0:T(8,128)(2,1)}, u32[]{:S(2)}, u32[]{:S(2)}) collective-permute-start(bf16[512,768]{1,0:T(8,128)(2,1)} %get-tuple-element.105), channel_id=1, source_target_pairs={{0,16},{8,24},{16,0},{24,8},{1,17},{9,25},{17,1},{25,9},{2,18},{10... | collective-permute-start | bytes 2359304 | tf_op jit(solution)/shard_map/ppermute | solution.py:450
  267.3 55.5 %collective-permute-start.10 = (bf16[512,768]{1,0:T(8,128)(2,1)}, bf16[512,768]{1,0:T(8,128)(2,1)}, u32[]{:S(2)}, u32[]{:S(2)}) collective-permute-start(bf16[512,768]{1,0:T(8,128)(2,1)} %get-tuple-element.101), channel_id=1, source_target_pairs={{0,16},{8,24},{16,0},{24,8},{1,17},{9,25},{17,1},{25,9},{2,18},{10... | collective-permute-start | bytes 2359304 | tf_op jit(solution)/shard_map/ppermute | solution.py:450
  269.4 64.5 %collective-permute-start.11 = (bf16[512,768]{1,0:T(8,128)(2,1)}, bf16[512,768]{1,0:T(8,128)(2,1)}, u32[]{:S(2)}, u32[]{:S(2)}) collective-permute-start(bf16[512,768]{1,0:T(8,128)(2,1)} %get-tuple-element.100), channel_id=1, source_target_pairs={{0,24},{8,0},{16,8},{24,16},{1,25},{9,1},{17,9},{25,17},{2,26},{10... | collective-permute-start | bytes 2359304 | tf_op jit(solution)/shard_map/ppermute | solution.py:450
  283.0 51.1 %collective-permute-start.9 = (bf16[512,768]{1,0:T(8,128)(2,1)}, bf16[512,768]{1,0:T(8,128)(2,1)}, u32[]{:S(2)}, u32[]{:S(2)}) collective-permute-start(bf16[512,768]{1,0:T(8,128)(2,1)} %get-tuple-element.102), channel_id=1, source_target_pairs={{0,8},{8,16},{16,24},{24,0},{1,9},{9,17},{17,25},{25,1},{2,10},{10... | collective-permute-start | bytes 2359304 | tf_op jit(solution)/shard_map/ppermute | solution.py:450
  321.0 79.1 %collective-permute-start.12 = (bf16[256,3072]{1,0:T(8,128)(2,1)}, bf16[256,3072]{1,0:T(8,128)(2,1)}, u32[]{:S(2)}, u32[]{:S(2)}) collective-permute-start(bf16[256,3072]{1,0:T(8,128)(2,1)} %get-tuple-element.71.refs_0_), channel_id=1, source_target_pairs={{0,8},{8,16},{16,24},{24,0},{1,9},{9,17},{17,25},{25,1},{2,10},{10... | collective-permute-start | bytes 4718600 | tf_op jit(solution)/shard_map/ppermute | solution.py:450
  354.2 47.3 %collective-permute-start.14 = (bf16[256,3072]{1,0:T(8,128)(2,1)}, bf16[256,3072]{1,0:T(8,128)(2,1)}, u32[]{:S(2)}, u32[]{:S(2)}) collective-permute-start(bf16[256,3072]{1,0:T(8,128)(2,1)} %get-tuple-element.74.refs_2_.refs_0_), channel_id=1, source_target_pairs={{0,8},{8,16},{16,24},{24,0},{1,9},{9,17},{17,25},{25,1},{2,10},{10... | collective-permute-start | bytes 4718600 | tf_op jit(solution)/shard_map/ppermute | solution.py:450
  355.3 46.2 %collective-permute-start.15 = (bf16[256,3072]{1,0:T(8,128)(2,1)}, bf16[256,3072]{1,0:T(8,128)(2,1)}, u32[]{:S(2)}, u32[]{:S(2)}) collective-permute-start(bf16[256,3072]{1,0:T(8,128)(2,1)} %get-tuple-element.66.refs_3_.refs_1_), channel_id=1, source_target_pairs={{0,24},{8,0},{16,8},{24,16},{1,25},{9,1},{17,9},{25,17},{2,26},{10... | collective-permute-start | bytes 4718600 | tf_op jit(solution)/shard_map/ppermute | solution.py:450
  357.0 67.2 %collective-permute-start.13 = (bf16[256,3072]{1,0:T(8,128)(2,1)}, bf16[256,3072]{1,0:T(8,128)(2,1)}, u32[]{:S(2)}, u32[]{:S(2)}) collective-permute-start(bf16[256,3072]{1,0:T(8,128)(2,1)} %get-tuple-element.64.refs_1_), channel_id=1, source_target_pairs={{0,24},{8,0},{16,8},{24,16},{1,25},{9,1},{17,9},{25,17},{2,26},{10... | collective-permute-start | bytes 4718600 | tf_op jit(solution)/shard_map/ppermute | solution.py:450
  578.8 39.2 %collective-permute-start.27 = (bf16[512,768]{1,0:T(8,128)(2,1)}, bf16[512,768]{1,0:T(8,128)(2,1)}, u32[]{:S(2)}, u32[]{:S(2)}) collective-permute-start(bf16[512,768]{1,0:T(8,128)(2,1)} %down.14.refs_1_), channel_id=1, source_target_pairs={{0,24},{8,0},{16,8},{24,16},{1,25},{9,1},{17,9},{25,17},{2,26},{10... | collective-permute-start | bytes 2359304 | tf_op jit(solution)/shard_map/ppermute | solution.py:450
  582.1 51.9 %collective-permute-start.29 = (bf16[512,768]{1,0:T(8,128)(2,1)}, bf16[512,768]{1,0:T(8,128)(2,1)}, u32[]{:S(2)}, u32[]{:S(2)}) collective-permute-start(bf16[512,768]{1,0:T(8,128)(2,1)} %down.14.refs_1_), channel_id=1, source_target_pairs={{0,8},{8,16},{16,24},{24,0},{1,9},{9,17},{17,25},{25,1},{2,10},{10... | collective-permute-start | bytes 2359304 | tf_op jit(solution)/shard_map/ppermute | solution.py:450
  594.0 40.2 %collective-permute-start.30 = (bf16[512,768]{1,0:T(8,128)(2,1)}, bf16[512,768]{1,0:T(8,128)(2,1)}, u32[]{:S(2)}, u32[]{:S(2)}) collective-permute-start(bf16[512,768]{1,0:T(8,128)(2,1)} %down.13.refs_0_), channel_id=1, source_target_pairs={{0,24},{8,0},{16,8},{24,16},{1,25},{9,1},{17,9},{25,17},{2,26},{10... | collective-permute-start | bytes 2359304 | tf_op jit(solution)/shard_map/ppermute | solution.py:450
  634.2 51.2 %collective-permute-start.23 = (bf16[512,768]{1,0:T(8,128)(2,1)}, bf16[512,768]{1,0:T(8,128)(2,1)}, u32[]{:S(2)}, u32[]{:S(2)}) collective-permute-start(bf16[512,768]{1,0:T(8,128)(2,1)} %down.17.refs_1_), channel_id=1, source_target_pairs={{0,24},{8,0},{16,8},{24,16},{1,25},{9,1},{17,9},{25,17},{2,26},{10... | collective-permute-start | bytes 2359304 | tf_op jit(solution)/shard_map/ppermute | solution.py:450
  644.6 41.1 %collective-permute-start.21 = (bf16[512,768]{1,0:T(8,128)(2,1)}, bf16[512,768]{1,0:T(8,128)(2,1)}, u32[]{:S(2)}, u32[]{:S(2)}) collective-permute-start(bf16[512,768]{1,0:T(8,128)(2,1)} %down.16.refs_0_), channel_id=1, source_target_pairs={{0,8},{8,16},{16,24},{24,0},{1,9},{9,17},{17,25},{25,1},{2,10},{10... | collective-permute-start | bytes 2359304 | tf_op jit(solution)/shard_map/ppermute | solution.py:450
  651.3 50.3 %collective-permute-start.33 = (bf16[512,768]{1,0:T(8,128)(2,1)}, bf16[512,768]{1,0:T(8,128)(2,1)}, u32[]{:S(2)}, u32[]{:S(2)}) collective-permute-start(bf16[512,768]{1,0:T(8,128)(2,1)} %down.17.refs_1_), channel_id=1, source_target_pairs={{0,8},{8,16},{16,24},{24,0},{1,9},{9,17},{17,25},{25,1},{2,10},{10... | collective-permute-start | bytes 2359304 | tf_op jit(solution)/shard_map/ppermute | solution.py:450
  661.4 40.3 %collective-permute-start.34 = (bf16[512,768]{1,0:T(8,128)(2,1)}, bf16[512,768]{1,0:T(8,128)(2,1)}, u32[]{:S(2)}, u32[]{:S(2)}) collective-permute-start(bf16[512,768]{1,0:T(8,128)(2,1)} %down.16.refs_0_), channel_id=1, source_target_pairs={{0,24},{8,0},{16,8},{24,16},{1,25},{9,1},{17,9},{25,17},{2,26},{10... | collective-permute-start | bytes 2359304 | tf_op jit(solution)/shard_map/ppermute | solution.py:450
  701.7 44.0 %collective-permute-start.40 = (bf16[512,768]{1,0:T(8,128)(2,1)}, bf16[512,768]{1,0:T(8,128)(2,1)}, u32[]{:S(2)}, u32[]{:S(2)}) collective-permute-start(bf16[512,768]{1,0:T(8,128)(2,1)} %down.20.refs_1_), channel_id=1, source_target_pairs={{0,24},{8,0},{16,8},{24,16},{1,25},{9,1},{17,9},{25,17},{2,26},{10... | collective-permute-start | bytes 2359304 | tf_op jit(solution)/shard_map/ppermute | solution.py:450
  712.0 37.1 %collective-permute-start.38 = (bf16[512,768]{1,0:T(8,128)(2,1)}, bf16[512,768]{1,0:T(8,128)(2,1)}, u32[]{:S(2)}, u32[]{:S(2)}) collective-permute-start(bf16[512,768]{1,0:T(8,128)(2,1)} %down.19.refs_0_), channel_id=1, source_target_pairs={{0,8},{8,16},{16,24},{24,0},{1,9},{9,17},{17,25},{25,1},{2,10},{10... | collective-permute-start | bytes 2359304 | tf_op jit(solution)/shard_map/ppermute | solution.py:450
  715.1 50.6 %collective-permute-start.42 = (bf16[512,768]{1,0:T(8,128)(2,1)}, bf16[512,768]{1,0:T(8,128)(2,1)}, u32[]{:S(2)}, u32[]{:S(2)}) collective-permute-start(bf16[512,768]{1,0:T(8,128)(2,1)} %down.20.refs_1_), channel_id=1, source_target_pairs={{0,8},{8,16},{16,24},{24,0},{1,9},{9,17},{17,25},{25,1},{2,10},{10... | collective-permute-start | bytes 2359304 | tf_op jit(solution)/shard_map/ppermute | solution.py:450
  728.8 36.8 %collective-permute-start.43 = (bf16[512,768]{1,0:T(8,128)(2,1)}, bf16[512,768]{1,0:T(8,128)(2,1)}, u32[]{:S(2)}, u32[]{:S(2)}) collective-permute-start(bf16[512,768]{1,0:T(8,128)(2,1)} %down.19.refs_0_), channel_id=1, source_target_pairs={{0,24},{8,0},{16,8},{24,16},{1,25},{9,1},{17,9},{25,17},{2,26},{10... | collective-permute-start | bytes 2359304 | tf_op jit(solution)/shard_map/ppermute | solution.py:450
  759.4 36.8 %collective-permute-start.45 = (bf16[512,768]{1,0:T(8,128)(2,1)}, bf16[512,768]{1,0:T(8,128)(2,1)}, u32[]{:S(2)}, u32[]{:S(2)}) collective-permute-start(bf16[512,768]{1,0:T(8,128)(2,1)} %down.23.refs_1_), channel_id=1, source_target_pairs={{0,24},{8,0},{16,8},{24,16},{1,25},{9,1},{17,9},{25,17},{2,26},{10... | collective-permute-start | bytes 2359304 | tf_op jit(solution)/shard_map/ppermute | solution.py:450
  765.7 50.6 %collective-permute-start.47 = (bf16[512,768]{1,0:T(8,128)(2,1)}, bf16[512,768]{1,0:T(8,128)(2,1)}, u32[]{:S(2)}, u32[]{:S(2)}) collective-permute-start(bf16[512,768]{1,0:T(8,128)(2,1)} %down.23.refs_1_), channel_id=1, source_target_pairs={{0,8},{8,16},{16,24},{24,0},{1,9},{9,17},{17,25},{25,1},{2,10},{10... | collective-permute-start | bytes 2359304 | tf_op jit(solution)/shard_map/ppermute | solution.py:450
  779.4 36.8 %collective-permute-start.48 = (bf16[512,768]{1,0:T(8,128)(2,1)}, bf16[512,768]{1,0:T(8,128)(2,1)}, u32[]{:S(2)}, u32[]{:S(2)}) collective-permute-start(bf16[512,768]{1,0:T(8,128)(2,1)} %down.22.refs_0_), channel_id=1, source_target_pairs={{0,24},{8,0},{16,8},{24,16},{1,25},{9,1},{17,9},{25,17},{2,26},{10... | collective-permute-start | bytes 2359304 | tf_op jit(solution)/shard_map/ppermute | solution.py:450
  (35 other events, 741.9 us)
Sparse Core Ops, SparseCore 0:
  9.7 49.2 all-gather.7
  60.6 91.0 all-gather.9
  153.3 145.2 all-gather.11
  300.0 92.0 all-gather.13
  393.5 51.5 all-gather.15
  446.6 51.7 all-gather.17
  500.0 51.8 all-gather.19

commit v10 on v9

--- a/solution.py
+++ b/solution.py
@@ -555,12 +555,23 @@
 
         order = a_recv[1]
         hidden = None
-        for b, (w, sel, units) in enumerate(blocks):
+        asked = []
+
+        def ask(b, dep):
+            w, sel, units = blocks[b]
             meta = jnp.stack([jnp.asarray(v, jnp.int32) for v in [*sel, *units]])
-            p_prev, p_next = down_call([after(a_recv[0], order), a_recv[1]], w, meta, n_src, bn, len(sel), N_CALLS * sub)
+            p_prev, p_next = down_call([after(a_recv[0], dep), a_recv[1]], w, meta, n_src, bn, len(sel), N_CALLS * sub)
             b_next = shift(p_prev, -1)
             b_prev = shift(p_next, 1)
-            order = p_prev
+            asked.append((meta, b_next, b_prev))
+            return p_prev
+
+        for b, (w, sel, units) in enumerate(blocks):
+            if b < last:
+                order = ask(b, order)
+            if b == last - 1:
+                order = ask(last, order)
+            meta, b_next, b_prev = asked[b]
             if b >= 1:
                 relay(b - 1)
             if b >= 2:

time: 855 us -> 855 us (level)
  transfers between devices with their start and end apart: 56 -> 56, of which waited for: 24 -> 23; matrix products, arithmetic and copies ran while one was open for 6% -> 6% of each run, Pallas kernels for 59% -> 59%
where the time goes in v10:
time: 855 us; the launch traced here: 843 us
  Pallas kernels  503 us (59%)
  waiting for transfers between devices  179 us (21%)
  starting transfers between devices  88.8 us (10%)
  local copies, waits for them, and re-layouts  33.6 us (4%)
  other arithmetic  23.5 us (3%)
  between operations  15.5 us (2%)
    ppermute x48, waiting for transfers between devices, shift(): return lax.ppermute(val, tp, [(i, (i + s) % n_tp) for i in range(n_tp)])  178 us
    pallas_call x5, Pallas kernels, gu_call(): pl.pallas_call(functools.partial(gu_kernel, bm, n_u), grid=(n_src, nb), i...  143 us
    pallas_call x12, Pallas kernels, down_call(): pl.pallas_call(functools.partial(down_kernel, bm, parts, n_src, own, row0...  135 us
    pallas_call x2, Pallas kernels, att_call(): pl.pallas_call(functools.partial(att_kernel, bq, bk, per, first), grid=(n...  83.8 us
    ppermute x48, starting transfers between devices, shift(): return lax.ppermute(val, tp, [(i, (i + s) % n_tp) for i in range(n_tp)])  63.9 us
    pallas_call x1, Pallas kernels, qkv_call(): pl.pallas_call(functools.partial(qkv_kernel, n_q, n_kv), grid=(s // bm,),...  41.2 us
    pallas_call x2, Pallas kernels, out_call(): pl.pallas_call(functools.partial(out_kernel, n_src), grid_spec=pltpu.Pref...  40.9 us
    pallas_call x8, Pallas kernels, place_call(): pl.pallas_call(functools.partial(place_kernel, n_in, moves, n_tp, skip),...  34.8 us
  transfers between devices with their start and end apart: 56, of which 23 were waited for; matrix products, arithmetic and copies ran while one was open for 6% of the time, Pallas kernels for 59%

profile of v10, /device:TPU:97, one launch (start us, length us, event | category | flops | bytes accessed | tf_op | source)
XLA Modules:
  0.0 843.4 jit_solution(14286125355194974342)
XLA Ops:
  16.7 11.5 %collective-permute-done.6 = bf16[768,384]{1,0:T(8,128)(2,1)S(1)} collective-permute-done((bf16[768,384]{1,0:T(8,128)(2,1)S(1)}, bf16[768,384]{1,0:T(8,128)(2,1)S(1)}, u32[]{:S(2)}, u32[]{:S(2)}) %collective-permute-start.6) | collective-permute-done | bytes 589856 | tf_op jit(solution)/shard_map/ppermute | solution.py:450
  28.2 13.4 %collective-permute-done.7 = bf16[768,384]{1,0:T(8,128)(2,1)S(1)} collective-permute-done((bf16[768,384]{1,0:T(8,128)(2,1)S(1)}, bf16[768,384]{1,0:T(8,128)(2,1)S(1)}, u32[]{:S(2)}, u32[]{:S(2)}) %collective-permute-start.7) | collective-permute-done | bytes 589856 | tf_op jit(solution)/shard_map/ppermute | solution.py:450
  49.1 24.4 %norm.1.h_ref = bf16[4096,3072]{1,0:T(8,128)(2,1)} custom-call(bf16[4096,3072]{1,0:T(8,128)(2,1)} %bitcast.37, bf16[1,3072]{1,0:T(2,128)(2,1)} %reshape.63.g_ref), custom_call_target="tpu_custom_call" | custom-call | flops 100663296 | bytes 50331648 | tf_op jit(solution)/shard_map/norm/pallas_call | solution.py:48
  84.9 41.2 %qkv.1 = (bf16[6,4096,128]{2,1,0:T(8,128)(2,1)}, bf16[4096,256]{1,0:T(8,128)(2,1)}, bf16[4096,256]{1,0:T(8,128)(2,1)}, bf16[256,4096]{1,0:T(8,128)(2,1)}) custom-call(bf16[4096,3072]{1,0:T(8,128)(2,1)} %norm.1.h_ref, bf16[3072,1280]{1,0:T(8,128)(2,1)} %all-gather.8.cloned.1.call-done.w_ref, f32[4096,128]{1,0:T(8,128)} %get-tuple-element.111.cos_ref, ...), custom_call_target="tpu_custom_call" | custom-call | flops 32212254720 | bytes 43515904 | tf_op jit(solution)/shard_map/qkv/pallas_call | solution.py:85
  136.1 35.4 %attention.2 = bf16[2048,768]{1,0:T(8,128)(2,1)} custom-call(s32[1]{0:T(128)S(6)} %copy.32.len_ref, bf16[6,4096,128]{2,1,0:T(8,128)(2,1)} %get-tuple-element.56.q_ref, bf16[4096,256]{1,0:T(8,128)(2,1)} %get-tuple-element.53.k_ref, bf16[256,4096]{1,0:T(8,128)(2,1)} %get-tuple-element.54.vt_ref), custom_call_target="tpu_custom_call" | custom-call | flops 25769803776 | bytes 12582912 | tf_op jit(solution)/shard_map/attention/pallas_call | solution.py:186
  178.2 48.5 %attention.3 = bf16[2048,768]{1,0:T(8,128)(2,1)} custom-call(s32[1]{0:T(128)S(6)} %copy.32.len_ref, bf16[6,4096,128]{2,1,0:T(8,128)(2,1)} %get-tuple-element.56.q_ref, bf16[4096,256]{1,0:T(8,128)(2,1)} %get-tuple-element.53.k_ref, bf16[256,4096]{1,0:T(8,128)(2,1)} %get-tuple-element.54.vt_ref), custom_call_target="tpu_custom_call" | custom-call | flops 77309411328 | bytes 12582912 | tf_op jit(solution)/shard_map/attention/pallas_call | solution.py:186
  232.7 24.3 %collective-permute-start.16 = (bf16[4096,384]{1,0:T(8,128)(2,1)S(1)}, bf16[4096,384]{1,0:T(8,128)(2,1)}, u32[]{:S(2)}, u32[]{:S(2)}) collective-permute-start(bf16[4096,384]{1,0:T(8,128)(2,1)S(1)} %constant_dynamic-update-slice_fusion.4), channel_id=1, source_target_pairs={{0,1},{1,0},{2,3},{3,2},{4,5},{5,4},{6,7},{7,6},{8,9},{9,8},{10,11... | collective-permute-start | bytes 9437192 | tf_op jit(solution)/shard_map/ppermute | solution.py:500
  283.2 16.7 %collective-permute-done.4.refs_2_ = bf16[512,768]{1,0:T(8,128)(2,1)} collective-permute-done((bf16[512,768]{1,0:T(8,128)(2,1)}, bf16[512,768]{1,0:T(8,128)(2,1)}, u32[]{:S(2)}, u32[]{:S(2)}) %collective-permute-start.4) | collective-permute-done | bytes 786464 | tf_op jit(solution)/shard_map/ppermute | solution.py:450
  300.2 20.7 %w_out.2 = (bf16[512,3072]{1,0:T(8,128)(2,1)}, bf16[256,3072]{1,0:T(8,128)(2,1)}, bf16[256,3072]{1,0:T(8,128)(2,1)}) custom-call(s32[1]{0:T(128)} %bitcast.31.idx_ref, bf16[512,768]{1,0:T(8,128)(2,1)} %get-tuple-element.58.refs_0_, bf16[512,768]{1,0:T(8,128)(2,1)} %collective-permute-done.3.refs_1_, bf16[512,768]{1,0:T(8,128)(2,1)} %collective-permute-done.4.refs_2_, ...), custom_call_target="tpu_custom_call" | custom-call | flops 9663676416 | bytes 31457280 | tf_op jit(solution)/shard_map/w_out/pallas_call | solution.py:235
  322.8 11.1 %collective-permute-done.11.refs_3_ = bf16[512,768]{1,0:T(8,128)(2,1)} collective-permute-done((bf16[512,768]{1,0:T(8,128)(2,1)}, bf16[512,768]{1,0:T(8,128)(2,1)}, u32[]{:S(2)}, u32[]{:S(2)}) %collective-permute-start.11) | collective-permute-done | bytes 786464 | tf_op jit(solution)/shard_map/ppermute | solution.py:450
  334.1 20.1 %w_out.3 = (bf16[512,3072]{1,0:T(8,128)(2,1)}, bf16[256,3072]{1,0:T(8,128)(2,1)}, bf16[256,3072]{1,0:T(8,128)(2,1)}) custom-call(s32[1]{0:T(128)} %bitcast.34.idx_ref, bf16[512,768]{1,0:T(8,128)(2,1)} %get-tuple-element.61.refs_0_, bf16[512,768]{1,0:T(8,128)(2,1)} %collective-permute-done.9.refs_1_, bf16[512,768]{1,0:T(8,128)(2,1)} %collective-permute-done.10.refs_2_, ...), custom_call_target="tpu_custom_call" | custom-call | flops 9663676416 | bytes 31457280 | tf_op jit(solution)/shard_map/w_out/pallas_call | solution.py:235
  358.5 41.6 %gate_up.5.refs_0_ = bf16[1024,2560]{1,0:T(8,128)(2,1)} custom-call(bf16[256,3072]{1,0:T(8,128)(2,1)} %get-tuple-element.71.refs_0_, bf16[256,3072]{1,0:T(8,128)(2,1)} %get-tuple-element.64.refs_1_, bf16[256,3072]{1,0:T(8,128)(2,1)} %get-tuple-element.74.refs_2_.refs_0_, bf16[256,3072]{1,0:T(8,128)(2,1)} %get-tuple-element.66.refs_3_.refs_1_, ...), custom_call_target="tpu_custom_call" | custom-call | flops 32212254720 | bytes 42991616 | tf_op jit(solution)/shard_map/gate_up/pallas_call | solution.py:287
  401.5 22.7 %collective-permute-done.13.refs_1_ = bf16[256,3072]{1,0:T(8,128)(2,1)} collective-permute-done((bf16[256,3072]{1,0:T(8,128)(2,1)}, bf16[256,3072]{1,0:T(8,128)(2,1)}, u32[]{:S(2)}, u32[]{:S(2)}) %collective-permute-start.13) | collective-permute-done | bytes 1572896 | tf_op jit(solution)/shard_map/ppermute | solution.py:450
  424.3 41.4 %gate_up.6.refs_0_ = bf16[1024,2560]{1,0:T(8,128)(2,1)} custom-call(bf16[256,3072]{1,0:T(8,128)(2,1)} %collective-permute-done.12.refs_0_, bf16[256,3072]{1,0:T(8,128)(2,1)} %collective-permute-done.13.refs_1_, bf16[256,3072]{1,0:T(8,128)(2,1)} %collective-permute-done.14.refs_2_, bf16[256,3072]{1,0:T(8,128)(2,1)} %collective-permute-done.15.refs_3_, ...), custom_call_target="tpu_custom_call" | custom-call | flops 32212254720 | bytes 42991616 | tf_op jit(solution)/shard_map/gate_up/pallas_call | solution.py:287
  465.7 26.8 %gate_up.7.refs_1_ = bf16[1024,1536]{1,0:T(8,128)(2,1)} custom-call(bf16[256,3072]{1,0:T(8,128)(2,1)} %collective-permute-done.12.refs_0_, bf16[256,3072]{1,0:T(8,128)(2,1)} %collective-permute-done.13.refs_1_, bf16[256,3072]{1,0:T(8,128)(2,1)} %collective-permute-done.14.refs_2_, bf16[256,3072]{1,0:T(8,128)(2,1)} %collective-permute-done.15.refs_3_, ...), custom_call_target="tpu_custom_call" | custom-call | flops 19327352832 | bytes 28311552 | tf_op jit(solution)/shard_map/gate_up/pallas_call | solution.py:287
  492.5 13.3 %down.12 = (bf16[512,768]{1,0:T(8,128)(2,1)}, bf16[512,768]{1,0:T(8,128)(2,1)}) custom-call(s32[9]{0:T(128)} %stack.172.meta_ref, bf16[1024,2560]{1,0:T(8,128)(2,1)} %gate_up.6.refs_0_, bf16[1024,1536]{1,0:T(8,128)(2,1)} %gate_up.7.refs_1_, bf16[4096,768]{1,0:T(8,128)(2,1)} %pad_maximum_fusion.refs_2_), custom_call_target="tpu_custom_call" | custom-call | flops 6442450944 | bytes 9437184 | tf_op jit(solution)/shard_map/down/pallas_call | solution.py:381
  508.8 16.6 %gate_up.8.refs_1_ = bf16[512,1536]{1,0:T(8,128)(2,1)} custom-call(bf16[256,3072]{1,0:T(8,128)(2,1)} %get-tuple-element.71.refs_0_, bf16[256,3072]{1,0:T(8,128)(2,1)} %get-tuple-element.64.refs_1_, bf16[3072,3072]{1,0:T(8,128)(2,1)} %all-gather.14.cloned.1.call-done.refs_4_.refs_5_.refs_2_.refs_3_, ...), custom_call_target="tpu_custom_call" | custom-call | flops 9663676416 | bytes 23592960 | tf_op jit(solution)/shard_map/gate_up/pallas_call | solution.py:287
  527.0 10.3 %down.13.refs_0_ = bf16[512,768]{1,0:T(8,128)(2,1)} custom-call(s32[9]{0:T(128)} %stack.172.meta_ref, bf16[1024,2560]{1,0:T(8,128)(2,1)} %gate_up.5.refs_0_, bf16[512,1536]{1,0:T(8,128)(2,1)} %gate_up.8.refs_1_, bf16[4096,768]{1,0:T(8,128)(2,1)} %pad_maximum_fusion.refs_2_, bf16[512,3072]{1,0:T(8,128)(2,1)} %get-tuple-element.60.refs_3_, ...), custom_call_target="tpu_custom_call" | custom-call | flops 3221225472 | bytes 7864320 | tf_op jit(solution)/shard_map/down/pallas_call | solution.py:381
  537.3 16.5 %gate_up.9.refs_1_ = bf16[512,1536]{1,0:T(8,128)(2,1)} custom-call(bf16[256,3072]{1,0:T(8,128)(2,1)} %get-tuple-element.74.refs_2_.refs_0_, bf16[256,3072]{1,0:T(8,128)(2,1)} %get-tuple-element.66.refs_3_.refs_1_, bf16[3072,3072]{1,0:T(8,128)(2,1)} %all-gather.14.cloned.1.call-done.refs_4_.refs_5_.refs_2_.refs_3_, ...), custom_call_target="tpu_custom_call" | custom-call | flops 9663676416 | bytes 23592960 | tf_op jit(solution)/shard_map/gate_up/pallas_call | solution.py:287
  553.7 10.3 %down.14.refs_1_ = bf16[512,768]{1,0:T(8,128)(2,1)} custom-call(s32[9]{0:T(128)} %stack.172.meta_ref, bf16[1024,2560]{1,0:T(8,128)(2,1)} %gate_up.5.refs_0_, bf16[512,1536]{1,0:T(8,128)(2,1)} %gate_up.9.refs_1_, bf16[4096,768]{1,0:T(8,128)(2,1)} %pad_maximum_fusion.refs_2_, bf16[512,3072]{1,0:T(8,128)(2,1)} %get-tuple-element.62.refs_3_, ...), custom_call_target="tpu_custom_call" | custom-call | flops 3221225472 | bytes 7864320 | tf_op jit(solution)/shard_map/down/pallas_call | solution.py:381
  564.0 13.0 %down.15 = (bf16[512,768]{1,0:T(8,128)(2,1)}, bf16[512,768]{1,0:T(8,128)(2,1)}) custom-call(s32[9]{0:T(128)} %stack.171.meta_ref, bf16[1024,2560]{1,0:T(8,128)(2,1)} %gate_up.6.refs_0_, bf16[1024,1536]{1,0:T(8,128)(2,1)} %gate_up.7.refs_1_, bf16[4096,1024]{1,0:T(8,128)(2,1)} %all-gather.16.cloned.1.call-done.refs_2_), custom_call_target="tpu_custom_call" | custom-call | flops 6442450944 | bytes 11534336 | tf_op jit(solution)/shard_map/down/pallas_call | solution.py:381
  581.4 12.6 %collective-permute-done.19.refs_4_ = bf16[512,768]{1,0:T(8,128)(2,1)} collective-permute-done((bf16[512,768]{1,0:T(8,128)(2,1)}, bf16[512,768]{1,0:T(8,128)(2,1)}, u32[]{:S(2)}, u32[]{:S(2)}) %collective-permute-start.19) | collective-permute-done | bytes 786464 | tf_op jit(solution)/shard_map/ppermute | solution.py:450
  597.4 10.2 %down.16.refs_0_ = bf16[512,768]{1,0:T(8,128)(2,1)} custom-call(s32[9]{0:T(128)} %stack.171.meta_ref, bf16[1024,2560]{1,0:T(8,128)(2,1)} %gate_up.5.refs_0_, bf16[512,1536]{1,0:T(8,128)(2,1)} %gate_up.8.refs_1_, bf16[4096,1024]{1,0:T(8,128)(2,1)} %all-gather.16.cloned.1.call-done.refs_2_, bf16[512,3072]{1,0:T(8,128)(2,1)} %get-tuple-element.60.refs_3_, ...), custom_call_target="tpu_custom_call" | custom-call | flops 3221225472 | bytes 9961472 | tf_op jit(solution)/shard_map/down/pallas_call | solution.py:381
  607.7 10.3 %down.17.refs_1_ = bf16[512,768]{1,0:T(8,128)(2,1)} custom-call(s32[9]{0:T(128)} %stack.171.meta_ref, bf16[1024,2560]{1,0:T(8,128)(2,1)} %gate_up.5.refs_0_, bf16[512,1536]{1,0:T(8,128)(2,1)} %gate_up.9.refs_1_, bf16[4096,1024]{1,0:T(8,128)(2,1)} %all-gather.16.cloned.1.call-done.refs_2_, bf16[512,3072]{1,0:T(8,128)(2,1)} %get-tuple-element.62.refs_3_, ...), custom_call_target="tpu_custom_call" | custom-call | flops 3221225472 | bytes 9961472 | tf_op jit(solution)/shard_map/down/pallas_call | solution.py:381
  619.7 11.2 %collective-permute-done.29.refs_3_ = bf16[512,768]{1,0:T(8,128)(2,1)} collective-permute-done((bf16[512,768]{1,0:T(8,128)(2,1)}, bf16[512,768]{1,0:T(8,128)(2,1)}, u32[]{:S(2)}, u32[]{:S(2)}) %collective-permute-start.29) | collective-permute-done | bytes 786464 | tf_op jit(solution)/shard_map/ppermute | solution.py:450
  631.4 13.1 %down.18 = (bf16[512,768]{1,0:T(8,128)(2,1)}, bf16[512,768]{1,0:T(8,128)(2,1)}) custom-call(s32[9]{0:T(128)} %stack.173.meta_ref, bf16[1024,2560]{1,0:T(8,128)(2,1)} %gate_up.6.refs_0_, bf16[1024,1536]{1,0:T(8,128)(2,1)} %gate_up.7.refs_1_, bf16[4096,1024]{1,0:T(8,128)(2,1)} %all-gather.18.cloned.1.call-done.refs_2_), custom_call_target="tpu_custom_call" | custom-call | flops 6442450944 | bytes 11534336 | tf_op jit(solution)/shard_map/down/pallas_call | solution.py:381
  648.6 12.8 %collective-permute-done.28.refs_1_ = bf16[512,768]{1,0:T(8,128)(2,1)} collective-permute-done((bf16[512,768]{1,0:T(8,128)(2,1)}, bf16[512,768]{1,0:T(8,128)(2,1)}, u32[]{:S(2)}, u32[]{:S(2)}) %collective-permute-start.28) | collective-permute-done | bytes 786464 | tf_op jit(solution)/shard_map/ppermute | solution.py:450
  666.3 13.0 %down.19 = (bf16[512,768]{1,0:T(8,128)(2,1)}, bf16[512,768]{1,0:T(8,128)(2,1)}) custom-call(s32[9]{0:T(128)} %stack.170.meta_ref, bf16[1024,2560]{1,0:T(8,128)(2,1)} %gate_up.6.refs_0_, bf16[1024,1536]{1,0:T(8,128)(2,1)} %gate_up.7.refs_1_, bf16[4096,1024]{1,0:T(8,128)(2,1)} %all-gather.20.cloned.1.call-done.refs_2_), custom_call_target="tpu_custom_call" | custom-call | flops 6442450944 | bytes 11534336 | tf_op jit(solution)/shard_map/down/pallas_call | solution.py:381
  689.8 10.2 %down.20.refs_0_ = bf16[512,768]{1,0:T(8,128)(2,1)} custom-call(s32[9]{0:T(128)} %stack.173.meta_ref, bf16[1024,2560]{1,0:T(8,128)(2,1)} %gate_up.5.refs_0_, bf16[512,1536]{1,0:T(8,128)(2,1)} %gate_up.8.refs_1_, bf16[4096,1024]{1,0:T(8,128)(2,1)} %all-gather.18.cloned.1.call-done.refs_2_, bf16[512,3072]{1,0:T(8,128)(2,1)} %get-tuple-element.60.refs_3_, ...), custom_call_target="tpu_custom_call" | custom-call | flops 3221225472 | bytes 9961472 | tf_op jit(solution)/shard_map/down/pallas_call | solution.py:381
  700.2 10.3 %down.21.refs_1_ = bf16[512,768]{1,0:T(8,128)(2,1)} custom-call(s32[9]{0:T(128)} %stack.173.meta_ref, bf16[1024,2560]{1,0:T(8,128)(2,1)} %gate_up.5.refs_0_, bf16[512,1536]{1,0:T(8,128)(2,1)} %gate_up.9.refs_1_, bf16[4096,1024]{1,0:T(8,128)(2,1)} %all-gather.18.cloned.1.call-done.refs_2_, bf16[512,3072]{1,0:T(8,128)(2,1)} %get-tuple-element.62.refs_3_, ...), custom_call_target="tpu_custom_call" | custom-call | flops 3221225472 | bytes 9961472 | tf_op jit(solution)/shard_map/down/pallas_call | solution.py:381
  732.2 10.2 %down.22.refs_0_ = bf16[512,768]{1,0:T(8,128)(2,1)} custom-call(s32[9]{0:T(128)} %stack.170.meta_ref, bf16[1024,2560]{1,0:T(8,128)(2,1)} %gate_up.5.refs_0_, bf16[512,1536]{1,0:T(8,128)(2,1)} %gate_up.8.refs_1_, bf16[4096,1024]{1,0:T(8,128)(2,1)} %all-gather.20.cloned.1.call-done.refs_2_, bf16[512,3072]{1,0:T(8,128)(2,1)} %get-tuple-element.60.refs_3_, ...), custom_call_target="tpu_custom_call" | custom-call | flops 3221225472 | bytes 9961472 | tf_op jit(solution)/shard_map/down/pallas_call | solution.py:381
  749.1 10.3 %down.23.refs_1_ = bf16[512,768]{1,0:T(8,128)(2,1)} custom-call(s32[9]{0:T(128)} %stack.170.meta_ref, bf16[1024,2560]{1,0:T(8,128)(2,1)} %gate_up.5.refs_0_, bf16[512,1536]{1,0:T(8,128)(2,1)} %gate_up.9.refs_1_, bf16[4096,1024]{1,0:T(8,128)(2,1)} %all-gather.20.cloned.1.call-done.refs_2_, bf16[512,3072]{1,0:T(8,128)(2,1)} %get-tuple-element.62.refs_3_, ...), custom_call_target="tpu_custom_call" | custom-call | flops 3221225472 | bytes 9961472 | tf_op jit(solution)/shard_map/down/pallas_call | solution.py:381
  (167 shorter events, 223.8 us)
Async XLA Ops:
  7.2 77.7 %all-gather.8.cloned.1.call-start = ((), (), s32[]{:S(2)}) async-start(), calls=%async_computation | async-start | bytes 8847360 | tf_op jit(solution)/shard_map/all_gather | solution.py:460
  9.6 290.6 %all-gather.10.cloned.1.call-start = ((), (), s32[]{:S(2)}) async-start(), calls=%async_computation.1 | async-start | bytes 21233664 | tf_op jit(solution)/shard_map/all_gather | solution.py:464
  43.3 315.2 %all-gather.12.cloned.1.call-start = ((), (), s32[]{:S(2)}) async-start(), calls=%async_computation.2 | async-start | bytes 35389440 | tf_op jit(solution)/shard_map/all_gather | solution.py:498
  46.3 82.9 %collective-permute-start = (bf16[384,2560]{1,0:T(8,128)(2,1)}, bf16[384,2560]{1,0:T(8,128)(2,1)}, u32[]{:S(2)}, u32[]{:S(2)}) collective-permute-start(bf16[384,2560]{1,0:T(8,128)(2,1)} %pad_maximum_fusion.4), channel_id=1, source_target_pairs={{0,16},{8,24},{16,0},{24,8},{1,17},{9,25},{17,1},{25,9},{2,18},{10... | collective-permute-start | bytes 5898248 | tf_op jit(solution)/shard_map/ppermute | solution.py:450
  132.2 333.4 %all-gather.14.cloned.1.call-start = ((), (), s32[]{:S(2)}) async-start(), calls=%async_computation.3 | async-start | bytes 21233664 | tf_op jit(solution)/shard_map/all_gather | solution.py:498
  134.5 38.5 %collective-permute-start.1 = (bf16[384,1536]{1,0:T(8,128)(2,1)}, bf16[384,1536]{1,0:T(8,128)(2,1)}, u32[]{:S(2)}, u32[]{:S(2)}) collective-permute-start(bf16[384,1536]{1,0:T(8,128)(2,1)} %pad_maximum_fusion.5), channel_id=1, source_target_pairs={{0,16},{8,24},{16,0},{24,8},{1,17},{9,25},{17,1},{25,9},{2,18},{10... | collective-permute-start | bytes 3538952 | tf_op jit(solution)/shard_map/ppermute | solution.py:450
  176.0 388.1 %all-gather.16.cloned.1.call-start = ((), (), s32[]{:S(2)}) async-start(), calls=%async_computation.4 | async-start | bytes 9437184 | tf_op jit(solution)/shard_map/all_gather | solution.py:502
  176.0 52.2 %collective-permute-start.2 = (bf16[2048,384]{1,0:T(8,128)(2,1)}, bf16[2048,384]{1,0:T(8,128)(2,1)}, u32[]{:S(2)}, u32[]{:S(2)}) collective-permute-start(bf16[2048,384]{1,0:T(8,128)(2,1)} %param.21), channel_id=1, source_target_pairs={{0,16},{8,24},{16,0},{24,8},{1,17},{9,25},{17,1},{25,9},{2,18},{10... | collective-permute-start | bytes 4718600 | tf_op jit(solution)/shard_map/ppermute | solution.py:450
  231.9 399.5 %all-gather.18.cloned.1.call-start = ((), (), s32[]{:S(2)}) async-start(), calls=%async_computation.5 | async-start | bytes 9437184 | tf_op jit(solution)/shard_map/all_gather | solution.py:502
  232.6 433.7 %all-gather.20.cloned.1.call-start = ((), (), s32[]{:S(2)}) async-start(), calls=%async_computation.6 | async-start | bytes 9437184 | tf_op jit(solution)/shard_map/all_gather | solution.py:502
  262.8 37.1 %collective-permute-start.4 = (bf16[512,768]{1,0:T(8,128)(2,1)}, bf16[512,768]{1,0:T(8,128)(2,1)}, u32[]{:S(2)}, u32[]{:S(2)}) collective-permute-start(bf16[512,768]{1,0:T(8,128)(2,1)} %get-tuple-element.105), channel_id=1, source_target_pairs={{0,16},{8,24},{16,0},{24,8},{1,17},{9,25},{17,1},{25,9},{2,18},{10... | collective-permute-start | bytes 2359304 | tf_op jit(solution)/shard_map/ppermute | solution.py:450
  267.3 55.5 %collective-permute-start.10 = (bf16[512,768]{1,0:T(8,128)(2,1)}, bf16[512,768]{1,0:T(8,128)(2,1)}, u32[]{:S(2)}, u32[]{:S(2)}) collective-permute-start(bf16[512,768]{1,0:T(8,128)(2,1)} %get-tuple-element.101), channel_id=1, source_target_pairs={{0,16},{8,24},{16,0},{24,8},{1,17},{9,25},{17,1},{25,9},{2,18},{10... | collective-permute-start | bytes 2359304 | tf_op jit(solution)/shard_map/ppermute | solution.py:450
  269.4 64.5 %collective-permute-start.11 = (bf16[512,768]{1,0:T(8,128)(2,1)}, bf16[512,768]{1,0:T(8,128)(2,1)}, u32[]{:S(2)}, u32[]{:S(2)}) collective-permute-start(bf16[512,768]{1,0:T(8,128)(2,1)} %get-tuple-element.100), channel_id=1, source_target_pairs={{0,24},{8,0},{16,8},{24,16},{1,25},{9,1},{17,9},{25,17},{2,26},{10... | collective-permute-start | bytes 2359304 | tf_op jit(solution)/shard_map/ppermute | solution.py:450
  283.0 51.1 %collective-permute-start.9 = (bf16[512,768]{1,0:T(8,128)(2,1)}, bf16[512,768]{1,0:T(8,128)(2,1)}, u32[]{:S(2)}, u32[]{:S(2)}) collective-permute-start(bf16[512,768]{1,0:T(8,128)(2,1)} %get-tuple-element.102), channel_id=1, source_target_pairs={{0,8},{8,16},{16,24},{24,0},{1,9},{9,17},{17,25},{25,1},{2,10},{10... | collective-permute-start | bytes 2359304 | tf_op jit(solution)/shard_map/ppermute | solution.py:450
  321.0 79.1 %collective-permute-start.12 = (bf16[256,3072]{1,0:T(8,128)(2,1)}, bf16[256,3072]{1,0:T(8,128)(2,1)}, u32[]{:S(2)}, u32[]{:S(2)}) collective-permute-start(bf16[256,3072]{1,0:T(8,128)(2,1)} %get-tuple-element.71.refs_0_), channel_id=1, source_target_pairs={{0,8},{8,16},{16,24},{24,0},{1,9},{9,17},{17,25},{25,1},{2,10},{10... | collective-permute-start | bytes 4718600 | tf_op jit(solution)/shard_map/ppermute | solution.py:450
  354.2 47.3 %collective-permute-start.14 = (bf16[256,3072]{1,0:T(8,128)(2,1)}, bf16[256,3072]{1,0:T(8,128)(2,1)}, u32[]{:S(2)}, u32[]{:S(2)}) collective-permute-start(bf16[256,3072]{1,0:T(8,128)(2,1)} %get-tuple-element.74.refs_2_.refs_0_), channel_id=1, source_target_pairs={{0,8},{8,16},{16,24},{24,0},{1,9},{9,17},{17,25},{25,1},{2,10},{10... | collective-permute-start | bytes 4718600 | tf_op jit(solution)/shard_map/ppermute | solution.py:450
  355.3 46.2 %collective-permute-start.15 = (bf16[256,3072]{1,0:T(8,128)(2,1)}, bf16[256,3072]{1,0:T(8,128)(2,1)}, u32[]{:S(2)}, u32[]{:S(2)}) collective-permute-start(bf16[256,3072]{1,0:T(8,128)(2,1)} %get-tuple-element.66.refs_3_.refs_1_), channel_id=1, source_target_pairs={{0,24},{8,0},{16,8},{24,16},{1,25},{9,1},{17,9},{25,17},{2,26},{10... | collective-permute-start | bytes 4718600 | tf_op jit(solution)/shard_map/ppermute | solution.py:450
  357.0 67.2 %collective-permute-start.13 = (bf16[256,3072]{1,0:T(8,128)(2,1)}, bf16[256,3072]{1,0:T(8,128)(2,1)}, u32[]{:S(2)}, u32[]{:S(2)}) collective-permute-start(bf16[256,3072]{1,0:T(8,128)(2,1)} %get-tuple-element.64.refs_1_), channel_id=1, source_target_pairs={{0,24},{8,0},{16,8},{24,16},{1,25},{9,1},{17,9},{25,17},{2,26},{10... | collective-permute-start | bytes 4718600 | tf_op jit(solution)/shard_map/ppermute | solution.py:450
  578.8 39.3 %collective-permute-start.27 = (bf16[512,768]{1,0:T(8,128)(2,1)}, bf16[512,768]{1,0:T(8,128)(2,1)}, u32[]{:S(2)}, u32[]{:S(2)}) collective-permute-start(bf16[512,768]{1,0:T(8,128)(2,1)} %down.14.refs_1_), channel_id=1, source_target_pairs={{0,24},{8,0},{16,8},{24,16},{1,25},{9,1},{17,9},{25,17},{2,26},{10... | collective-permute-start | bytes 2359304 | tf_op jit(solution)/shard_map/ppermute | solution.py:450
  581.4 49.4 %collective-permute-start.29 = (bf16[512,768]{1,0:T(8,128)(2,1)}, bf16[512,768]{1,0:T(8,128)(2,1)}, u32[]{:S(2)}, u32[]{:S(2)}) collective-permute-start(bf16[512,768]{1,0:T(8,128)(2,1)} %down.14.refs_1_), channel_id=1, source_target_pairs={{0,8},{8,16},{16,24},{24,0},{1,9},{9,17},{17,25},{25,1},{2,10},{10... | collective-permute-start | bytes 2359304 | tf_op jit(solution)/shard_map/ppermute | solution.py:450
  594.0 50.6 %collective-permute-start.30 = (bf16[512,768]{1,0:T(8,128)(2,1)}, bf16[512,768]{1,0:T(8,128)(2,1)}, u32[]{:S(2)}, u32[]{:S(2)}) collective-permute-start(bf16[512,768]{1,0:T(8,128)(2,1)} %down.13.refs_0_), channel_id=1, source_target_pairs={{0,24},{8,0},{16,8},{24,16},{1,25},{9,1},{17,9},{25,17},{2,26},{10... | collective-permute-start | bytes 2359304 | tf_op jit(solution)/shard_map/ppermute | solution.py:450
  618.1 43.3 %collective-permute-start.28 = (bf16[512,768]{1,0:T(8,128)(2,1)}, bf16[512,768]{1,0:T(8,128)(2,1)}, u32[]{:S(2)}, u32[]{:S(2)}) collective-permute-start(bf16[512,768]{1,0:T(8,128)(2,1)} %collective-permute-done.27.refs_5_), channel_id=1, source_target_pairs={{0,24},{8,0},{16,8},{24,16},{1,25},{9,1},{17,9},{25,17},{2,26},{10... | collective-permute-start | bytes 2359304 | tf_op jit(solution)/shard_map/ppermute | solution.py:450
  618.2 43.2 %collective-permute-start.26 = (bf16[512,768]{1,0:T(8,128)(2,1)}, bf16[512,768]{1,0:T(8,128)(2,1)}, u32[]{:S(2)}, u32[]{:S(2)}) collective-permute-start(bf16[512,768]{1,0:T(8,128)(2,1)} %collective-permute-done.25.refs_2_), channel_id=1, source_target_pairs={{0,8},{8,16},{16,24},{24,0},{1,9},{9,17},{17,25},{25,1},{2,10},{10... | collective-permute-start | bytes 2359304 | tf_op jit(solution)/shard_map/ppermute | solution.py:450
  644.6 43.5 %collective-permute-start.31 = (bf16[512,768]{1,0:T(8,128)(2,1)}, bf16[512,768]{1,0:T(8,128)(2,1)}, u32[]{:S(2)}, u32[]{:S(2)}) collective-permute-start(bf16[512,768]{1,0:T(8,128)(2,1)} %get-tuple-element.82), channel_id=1, source_target_pairs={{0,24},{8,0},{16,8},{24,16},{1,25},{9,1},{17,9},{25,17},{2,26},{10... | collective-permute-start | bytes 2359304 | tf_op jit(solution)/shard_map/ppermute | solution.py:450
  647.3 40.9 %collective-permute-start.32 = (bf16[512,768]{1,0:T(8,128)(2,1)}, bf16[512,768]{1,0:T(8,128)(2,1)}, u32[]{:S(2)}, u32[]{:S(2)}) collective-permute-start(bf16[512,768]{1,0:T(8,128)(2,1)} %get-tuple-element.87), channel_id=1, source_target_pairs={{0,8},{8,16},{16,24},{24,0},{1,9},{9,17},{17,25},{25,1},{2,10},{10... | collective-permute-start | bytes 2359304 | tf_op jit(solution)/shard_map/ppermute | solution.py:450
  661.4 38.6 %collective-permute-start.33 = (bf16[512,768]{1,0:T(8,128)(2,1)}, bf16[512,768]{1,0:T(8,128)(2,1)}, u32[]{:S(2)}, u32[]{:S(2)}) collective-permute-start(bf16[512,768]{1,0:T(8,128)(2,1)} %down.17.refs_1_), channel_id=1, source_target_pairs={{0,8},{8,16},{16,24},{24,0},{1,9},{9,17},{17,25},{25,1},{2,10},{10... | collective-permute-start | bytes 2359304 | tf_op jit(solution)/shard_map/ppermute | solution.py:450
  661.4 49.1 %collective-permute-start.34 = (bf16[512,768]{1,0:T(8,128)(2,1)}, bf16[512,768]{1,0:T(8,128)(2,1)}, u32[]{:S(2)}, u32[]{:S(2)}) collective-permute-start(bf16[512,768]{1,0:T(8,128)(2,1)} %down.16.refs_0_), channel_id=1, source_target_pairs={{0,24},{8,0},{16,8},{24,16},{1,25},{9,1},{17,9},{25,17},{2,26},{10... | collective-permute-start | bytes 2359304 | tf_op jit(solution)/shard_map/ppermute | solution.py:450
  664.8 48.4 %collective-permute-start.24 = (bf16[512,768]{1,0:T(8,128)(2,1)}, bf16[512,768]{1,0:T(8,128)(2,1)}, u32[]{:S(2)}, u32[]{:S(2)}) collective-permute-start(bf16[512,768]{1,0:T(8,128)(2,1)} %collective-permute-done.23.refs_5_), channel_id=1, source_target_pairs={{0,24},{8,0},{16,8},{24,16},{1,25},{9,1},{17,9},{25,17},{2,26},{10... | collective-permute-start | bytes 2359304 | tf_op jit(solution)/shard_map/ppermute | solution.py:450
  688.1 40.7 %collective-permute-start.35 = (bf16[512,768]{1,0:T(8,128)(2,1)}, bf16[512,768]{1,0:T(8,128)(2,1)}, u32[]{:S(2)}, u32[]{:S(2)}) collective-permute-start(bf16[512,768]{1,0:T(8,128)(2,1)} %get-tuple-element.84), channel_id=1, source_target_pairs={{0,24},{8,0},{16,8},{24,16},{1,25},{9,1},{17,9},{25,17},{2,26},{10... | collective-permute-start | bytes 2359304 | tf_op jit(solution)/shard_map/ppermute | solution.py:450
  715.1 50.6 %collective-permute-start.42 = (bf16[512,768]{1,0:T(8,128)(2,1)}, bf16[512,768]{1,0:T(8,128)(2,1)}, u32[]{:S(2)}, u32[]{:S(2)}) collective-permute-start(bf16[512,768]{1,0:T(8,128)(2,1)} %down.21.refs_1_), channel_id=1, source_target_pairs={{0,8},{8,16},{16,24},{24,0},{1,9},{9,17},{17,25},{25,1},{2,10},{10... | collective-permute-start | bytes 2359304 | tf_op jit(solution)/shard_map/ppermute | solution.py:450
  759.4 36.8 %collective-permute-start.45 = (bf16[512,768]{1,0:T(8,128)(2,1)}, bf16[512,768]{1,0:T(8,128)(2,1)}, u32[]{:S(2)}, u32[]{:S(2)}) collective-permute-start(bf16[512,768]{1,0:T(8,128)(2,1)} %down.23.refs_1_), channel_id=1, source_target_pairs={{0,24},{8,0},{16,8},{24,16},{1,25},{9,1},{17,9},{25,17},{2,26},{10... | collective-permute-start | bytes 2359304 | tf_op jit(solution)/shard_map/ppermute | solution.py:450
  765.7 50.6 %collective-permute-start.47 = (bf16[512,768]{1,0:T(8,128)(2,1)}, bf16[512,768]{1,0:T(8,128)(2,1)}, u32[]{:S(2)}, u32[]{:S(2)}) collective-permute-start(bf16[512,768]{1,0:T(8,128)(2,1)} %down.23.refs_1_), channel_id=1, source_target_pairs={{0,8},{8,16},{16,24},{24,0},{1,9},{9,17},{17,25},{25,1},{2,10},{10... | collective-permute-start | bytes 2359304 | tf_op jit(solution)/shard_map/ppermute | solution.py:450
  (35 other events, 774.5 us)
Sparse Core Ops, SparseCore 0:
  9.7 49.2 all-gather.7
  60.6 91.0 all-gather.9
  153.3 145.2 all-gather.11
  300.0 92.0 all-gather.13
  393.5 51.5 all-gather.15
  446.6 51.7 all-gather.17
  500.0 51.8 all-gather.19
